TPU v7x, 256 devices: a whole 4x4x8 slice. The times are simulated.
256 devices in a mesh: sx: 8 (over x, core), sy: 32 (over z, y).
Axes of the slice: x: 4, y: 4, z: 8, core: 2. Of those that a mesh axis runs over, the one named last changes fastest.
Arguments:
- right_side: float32 [8, 8, 8, 65536], P(None, None, None, ('sx', 'sy')), may hold values from -8 to 8
- stretch: float32 [3, 65536], P(None, ('sx', 'sy')), may hold values from 0.3 to 3
- mass_term: float32 [65536], P(('sx', 'sy')), may hold values from 0.5 to 2
- slot_position: int32 [65536], P(('sx', 'sy')), may hold values from 0 to 255, as said below
- coarse_group: int32 [65536], P(('sx', 'sy')), may hold values from 0 to 4095, as said below
Outputs:
- smoothed: float32 [8, 8, 8, 65536], P(None, None, None, ('sx', 'sy'))
- fine_residual: float32 [8, 8, 8, 65536], P(None, None, None, ('sx', 'sy'))
- coarse_rhs: float32 [8, 4096], P(None, ('sx', 'sy'))
Inputs may be any that keep to these rules, and one draw needn't show every extreme that they name: `slot_position`: each device's block of 256 entries is a permutation of 0 to 255. `coarse_group`: group k is owned by the device of block index k // 16 (block index i * 32 + j); an element of device (i, j) belongs to a group owned by some device (i, j') of the same first index.
All inputs are finite; a program needn't handle non-finite values.
Results may differ from a plain program's by a relative error of at most 0.00013.
Values sent between devices are 32-bit elements; how exact they have to be, the bound alone decides.
No kernel may reach another device: no remote copies, remote signals or barrier semaphores. Data moves between devices by JAX's collectives and lax.ppermute only.
A program may use at most 128 MiB of HBM per device.

v0:
```python
import jax
import jax.numpy as jnp
import numpy as np
from jax import lax
from jax.experimental import pallas as pl
from jax.experimental.pallas import tpu as pltpu
from jax.sharding import PartitionSpec as P

NODES = 8
GRP_DEV = 16
LANES = 128
RELAX = 0.35
F32 = jnp.float32
BF16 = jnp.bfloat16


def split_np(a):
    a = np.asarray(a, np.float32)
    hi = np.asarray(jnp.asarray(a).astype(BF16).astype(F32))
    return hi, a - hi


def constants():
    n = NODES + 2
    col = np.arange(n, dtype=np.float64) + 1.0
    s = np.sqrt(2.0 / (n + 1.0)) * np.sin(np.pi * col[:, None] * col[None, :] / (n + 1.0))
    lam = 2.0 - 2.0 * np.cos(np.pi * col / (n + 1.0))
    fwd = np.zeros((104, 112))
    for q in range(n):
        for r in range(n):
            c = q * 8 + r - 1
            if r == 0:
                c = 80 + q
            if r == n - 1:
                c = 96 + q
            fwd[:100, c] = np.outer(s[:, q], s[:, r]).reshape(-1)
    fh, fl = split_np(fwd)
    a1 = np.concatenate([np.concatenate([fh, fh], 1), np.concatenate([fl, fl], 1)], 0)
    bh, bl = split_np(RELAX * fwd.T)
    a2 = np.concatenate([np.concatenate([bh, bh], 1), np.concatenate([bl, bl], 1)], 0)
    lam_j = np.ones((104, LANES), np.float32)
    lam_k = np.ones((104, LANES), np.float32)
    lam_j[:100] = np.repeat(lam, n)[:, None]
    lam_k[:100] = np.tile(lam, n)[:, None]
    t = np.arange(NODES) / (NODES - 1.0)
    w = np.stack([1.0 - t, t])
    wm = np.einsum("ax,by,cz->abcxyz", w, w, w).reshape(8, 512)
    wh, wl = split_np(wm)
    wm = np.concatenate([wh, wl], 0)
    return s, lam, a1, a2, lam_j, lam_k, wm


SINES, LAM, A_FWD, A_BWD, LAM_J, LAM_K, W_MOM = constants()


def split(x):
    hi = x.astype(BF16)
    return hi, (x - hi.astype(F32)).astype(BF16)


def dot(a, b):
    return lax.dot_general(a, b, (((1,), (0,)), ((), ())), preferred_element_type=F32)


def dot_t(a, b):
    return lax.dot_general(a, b, (((1,), (1,)), ((), ())), preferred_element_type=F32)


def flags():
    i = lax.axis_index("sx")
    j = lax.axis_index("sy")
    nx = lax.axis_size("sx")
    ny = lax.axis_size("sy")
    one = lambda c: jnp.where(c, 1.0, 0.0).astype(F32)
    return one(i > 0), one(i < nx - 1), one(j > 0), one(j < ny - 1)


def lane_up(x):
    lane = lax.broadcasted_iota(jnp.int32, x.shape, x.ndim - 1)
    return jnp.where(lane == LANES - 1, 0.0, pltpu.roll(x, LANES - 1, x.ndim - 1))


def lane_down(x):
    lane = lax.broadcasted_iota(jnp.int32, x.shape, x.ndim - 1)
    return jnp.where(lane == 0, 0.0, pltpu.roll(x, 1, x.ndim - 1))


def onehot(slot_row):
    p = lax.broadcasted_iota(jnp.int32, (256, 256), 0)
    return jnp.where(p == slot_row, 1.0, 0.0).astype(BF16)


def place_kernel(rhs_ref, stretch_ref, mass_ref, slot_ref, src_ref, coef_ref, lo_ref, hi_ref):
    oh = onehot(slot_ref[...])
    c = jnp.concatenate([stretch_ref[...], mass_ref[...], jnp.zeros((4, 256), F32)], 0)
    c1, rest = split(c)
    r1 = c - c1.astype(F32)
    c2 = r1.astype(BF16)
    c3 = (r1 - c2.astype(F32)).astype(BF16)
    cg = dot_t(c1, oh) + dot_t(c2, oh) + dot_t(c3, oh)
    coef = jnp.concatenate([cg[0:4, :LANES], cg[0:4, LANES:]], 0)
    coef_ref[...] = coef
    lo_ref[16] = coef
    hi_ref[16] = coef
    for x in range(8):
        a = rhs_ref[x * 64 : (x + 1) * 64, :]
        a1 = a.astype(BF16)
        e = a - a1.astype(F32)
        a2 = e.astype(BF16)
        a3 = (e - a2.astype(F32)).astype(BF16)
        g = dot_t(jnp.concatenate([a1, a2, a3], 0), oh)
        g = g[0:64] + g[64:128] + g[128:192]
        for b in range(2):
            block = g[:, b * LANES : (b + 1) * LANES].reshape(8, 8, LANES)
            src_ref[x, b * 8 : b * 8 + 8] = block
            if x == 0:
                lo_ref[b * 8 : b * 8 + 8] = block
            if x == 7:
                hi_ref[b * 8 : b * 8 + 8] = block


def block_solves(rext, coef_ref, a1_ref, a2_ref, lj_ref, lk_ref, spec, wout):
    for p in range(10):
        base = p * 192
        ends = []
        for z, shift in ((7, lane_down), (0, lane_up)):
            rows = [shift(rext[pl.ds(base + 64 * t + z, 8, stride=8), :]) for t in range(3)]
            ends.append(rows)
        halves = []
        for b in range(2):
            halves.append(
                jnp.concatenate(
                    [rext[base + 64 * b : base + 64 * b + 80, :]]
                    + ends[0][b : b + 2]
                    + ends[1][b : b + 2],
                    0,
                )
            )
        hi, lo = split(jnp.concatenate(halves, 1))
        r = dot(a1_ref[...], jnp.concatenate([hi, lo], 0))
        spec[p] = r[:104] + r[104:]

    even = [i for i in range(0, 10, 2)]
    odd = [i for i in range(1, 10, 2)]
    for b in range(2):
        lanes = slice(b * LANES, (b + 1) * LANES)
        cx, cy, cz, m = [
            jnp.broadcast_to(coef_ref[b * 4 + k : b * 4 + k + 1, :], (8, LANES)) for k in range(4)
        ]

        def chunk(t, carry):
            row = pl.ds(pl.multiple_of(t * 8, 8), 8)
            v = [spec[p, row, lanes] for p in range(10)]
            d0 = cy * lj_ref[row, :] + cz * lk_ref[row, :] + m
            s = [v[p] + v[9 - p] for p in range(5)]
            d = [v[p] - v[9 - p] for p in range(5)]
            z = [None] * 10
            for i in range(10):
                h = s if i % 2 == 0 else d
                acc = h[0] * float(SINES[i, 0])
                for p in range(1, 5):
                    acc = acc + h[p] * float(SINES[i, p])
                z[i] = acc / (d0 + cx * float(LAM[i]))
            for p in range(5):
                e = z[0] * float(SINES[0, p])
                o = z[1] * float(SINES[1, p])
                for i in even[1:]:
                    e = e + z[i] * float(SINES[i, p])
                for i in odd[1:]:
                    o = o + z[i] * float(SINES[i, p])
                spec[p, row, lanes] = e + o
                spec[9 - p, row, lanes] = e - o
            return carry

        lax.fori_loop(0, 13, chunk, 0)

    for p in range(10):
        base = p * 192
        hi, lo = split(spec[p])
        r = dot(a2_ref[...], jnp.concatenate([hi, lo], 0))
        r = r[:112] + r[112:]
        r0 = r[:, :LANES]
        r1 = r[:, LANES:]
        wout[base : base + 64, :] = r0[0:64]
        wout[base + 64 : base + 80, :] = r0[64:80] + r1[0:16]
        wout[base + 80 : base + 144, :] = r1[16:80]
        wout[base + 144 : base + 192, :] = jnp.zeros((48, LANES), F32)
        for off, z, shift in ((80, 7, lane_up), (96, 0, lane_down)):
            rows = [
                r0[off : off + 8],
                r0[off + 8 : off + 16] + r1[off : off + 8],
                r1[off + 8 : off + 16],
            ]
            for t in range(3):
                at = pl.ds(base + 64 * t + z, 8, stride=8)
                wout[at, :] = wout[at, :] + shift(rows[t])


def put(ref, p, y, value):
    n = value.shape[0]
    at = (p * 24 + y) * 8
    ref[at : at + n * 8, :] = value.reshape(n * 8, LANES)


def get(ref, p, y, n):
    at = (p * 24 + y) * 8
    return ref[at : at + n * 8, :].reshape(n, 8, LANES)


def first_kernel(
    src_ref, coef_ref, xl_ref, xr_ref, yd_ref, yu_ref, a1_ref, a2_ref, lj_ref, lk_ref,
    rext_ref, w_ref, to_left_ref, to_right_ref, to_down_ref, to_up_ref, spec, wout,
):
    left, right, down, up = flags()
    zero = jnp.zeros((6, 8, LANES), F32)
    for p in range(10):
        side = {0: left, 9: right}.get(p)
        if p == 0:
            line = xl_ref[0:16] * left
        elif p == 9:
            line = xr_ref[0:16] * right
        else:
            line = src_ref[p - 1]
        fd = down if side is None else down * side
        fu = up if side is None else up * side
        put(rext_ref, p, 0, yd_ref[p : p + 1] * fd)
        put(rext_ref, p, 1, line)
        put(rext_ref, p, 17, yu_ref[p : p + 1] * fu)
        put(rext_ref, p, 18, zero)
    block_solves(rext_ref, coef_ref, a1_ref, a2_ref, lj_ref, lk_ref, spec, wout)
    empty = jnp.zeros((3, 8, LANES), F32)
    to_up_ref[0] = empty
    to_up_ref[11] = empty
    to_down_ref[0] = empty
    to_down_ref[11] = empty
    for p in range(10):
        line = get(wout, p, 0, 18)
        w_ref[p] = line
        if p < 3:
            to_left_ref[p] = line
        if p > 6:
            to_right_ref[p - 7] = line
        side = {0: left, 9: right}.get(p)
        if side is not None:
            line = line * side
        to_down_ref[p + 1] = line[0:3]
        to_up_ref[p + 1] = line[15:18]


def edge_kernel(own_dn_ref, own_up_ref, l_dn_ref, l_up_ref, r_dn_ref, r_up_ref, dn_ref, up_ref):
    left, right, _, _ = flags()
    for own, l, r, out in (
        (own_dn_ref, l_dn_ref, r_dn_ref, dn_ref),
        (own_up_ref, l_up_ref, r_up_ref, up_ref),
    ):
        n = l.shape[0]
        m = own.shape[0]
        out[0:n] = own[0:n] + l[...] * left
        out[n : m - n] = own[n : m - n]
        out[m - n :] = own[m - n :] + r[...] * right


def neighbours_z(u):
    z = lax.broadcasted_iota(jnp.int32, u.shape, 1)
    s = pltpu.roll(u, 7, 1)
    above = jnp.where(z == 7, lane_up(s), s)
    s = pltpu.roll(u, 1, 1)
    below = jnp.where(z == 0, lane_down(s), s)
    return above, below


def second_kernel(
    rext_ref, coef_ref, xl_ref, xr_ref, yd_ref, yu_ref, w_ref, l_ref, r_ref, d_ref, u_ref,
    a1_ref, a2_ref, lj_ref, lk_ref,
    c_ref, to_left_ref, to_right_ref, to_down_ref, to_up_ref, h, cb, r1, spec, wout,
):
    left, right, down, up = flags()
    for x in range(12):
        if x == 0:
            g = l_ref[0] * left
        elif x == 1:
            g = (l_ref[1] + w_ref[0]) * left
        elif x == 2:
            g = l_ref[2] * left + w_ref[1]
        elif x == 9:
            g = w_ref[8] + r_ref[0] * right
        elif x == 10:
            g = (w_ref[9] + r_ref[1]) * right
        elif x == 11:
            g = r_ref[2] * right
        else:
            g = w_ref[x - 1]
        d = d_ref[x] * down
        u = u_ref[x] * up
        h[x, 0] = d[0]
        h[x, 1] = g[0] * down + d[1]
        h[x, 2] = g[1] + d[2]
        h[x, 3:17] = g[2:16]
        h[x, 17] = g[16] + u[0]
        h[x, 18] = g[17] * up + u[1]
        h[x, 19] = u[2]
    for a, own in ((0, xl_ref), (1, None), (2, xr_ref)):
        for b in range(4):
            for k in range(4):
                if b == 0:
                    row = yd_ref[10 + a, 4 + k : 5 + k, :]
                elif b == 3:
                    row = yu_ref[10 + a, k : k + 1, :]
                else:
                    at = (b - 1) * 4 + k
                    row = coef_ref[at : at + 1, :] if own is None else own[16, at : at + 1, :]
                cb[a, b, k] = jnp.broadcast_to(row, (8, LANES))
    zero = jnp.zeros((6, 8, LANES), F32)
    for p in range(10):
        a = 0 if p == 0 else 2 if p == 9 else 1
        for y, n, b in ((0, 1, 0), (1, 4, 1), (5, 4, 1), (9, 4, 2), (13, 4, 2), (17, 1, 3)):
            v = h[p + 1, y + 1 : y + 1 + n]
            above, below = neighbours_z(v)
            two = v + v
            res = get(rext_ref, p, y, n) - (
                cb[a, b, 0] * (two - h[p + 2, y + 1 : y + 1 + n] - h[p, y + 1 : y + 1 + n])
                + cb[a, b, 1] * (two - h[p + 1, y + 2 : y + 2 + n] - h[p + 1, y : y + n])
                + cb[a, b, 2] * (two - above - below)
                + cb[a, b, 3] * v
            )
            if p == 0:
                res = res * left
            if p == 9:
                res = res * right
            if y == 0:
                res = res * down
            if y == 17:
                res = res * up
            put(r1, p, y, res)
        put(r1, p, 18, zero)
    block_solves(r1, coef_ref, a1_ref, a2_ref, lj_ref, lk_ref, spec, wout)
    for p in range(10):
        line = get(wout, p, 0, 18)
        c_ref[p] = h[p + 1, 1:19] + line
        if p < 2:
            to_left_ref[p] = line
        if p > 7:
            to_right_ref[p - 8] = line
        side = {0: left, 9: right}.get(p)
        if side is not None:
            line = line * side
        to_down_ref[p] = line[0:2]
        to_up_ref[p] = line[16:18]


def last_kernel(
    src_ref, coef_ref, c_ref, l_ref, r_ref, d_ref, u_ref, slot_ref, group_ref, wm_ref,
    smooth_ref, res_ref, part_ref, h, mu, mr,
):
    left, right, down, up = flags()
    for p in range(10):
        g = c_ref[p]
        if p == 0:
            g = (g + l_ref[0]) * left
        elif p == 1:
            g = g + l_ref[1] * left
        elif p == 8:
            g = g + r_ref[0] * right
        elif p == 9:
            g = (g + r_ref[1]) * right
        d = d_ref[p] * down
        u = u_ref[p] * up
        h[p, 0] = g[0] * down + d[0]
        h[p, 1] = g[1] + d[1]
        h[p, 2:16] = g[2:16]
        h[p, 16] = g[16] + u[0]
        h[p, 17] = g[17] * up + u[1]
    for b in range(2):
        lanes = slice(b * LANES, (b + 1) * LANES)
        cf = [
            jnp.broadcast_to(coef_ref[b * 4 + k : b * 4 + k + 1, :], (8, LANES)) for k in range(4)
        ]
        for x in range(8):
            p = x + 1
            for y in (0, 4):
                yy = b * 8 + y + 1
                v = h[p, yy : yy + 4]
                above, below = neighbours_z(v)
                two = v + v
                res = src_ref[x, yy - 1 : yy + 3] - (
                    cf[0] * (two - h[p + 1, yy : yy + 4] - h[p - 1, yy : yy + 4])
                    + cf[1] * (two - h[p, yy + 1 : yy + 5] - h[p, yy - 1 : yy + 3])
                    + cf[2] * (two - above - below)
                    + cf[3] * v
                )
                at = (x * 8 + y) * 8
                mu[at : at + 32, lanes] = v.reshape(32, LANES)
                mr[at : at + 32, lanes] = res.reshape(32, LANES)
    oh = onehot(slot_ref[...])
    mom = jnp.zeros((16, 256), F32)
    for x in range(8):
        at = slice(x * 64, x * 64 + 64)
        uh, ul = split(mu[at, :])
        rh, rl = split(mr[at, :])
        o = dot(jnp.concatenate([uh, ul, rh, rl], 0), oh)
        smooth_ref[at, :] = o[0:64] + o[64:128]
        res_ref[at, :] = o[128:192] + o[192:256]
    for x in range(4):
        at = slice(x * 128, x * 128 + 128)
        rh, rl = split(mr[at, :])
        mom = mom + dot(wm_ref[:, at], rh) + dot(wm_ref[:, at], rl)
    mh, ml = split(mom[0:8] + mom[8:16])
    mom = dot(mh, oh) + dot(ml, oh)
    ny = part_ref.shape[0]
    col = group_ref[...] - lax.axis_index("sx") * (ny * GRP_DEV)
    owner = lax.shift_right_logical(col, 4)
    member = jnp.bitwise_and(col, 15)
    sel = lax.broadcasted_iota(jnp.int32, (ny, 256), 0)
    pick = jnp.where(sel == owner, 1.0, 0.0).astype(BF16)
    m16 = lax.broadcasted_iota(jnp.int32, (16, 256), 0) == member
    spread = jnp.concatenate(
        [jnp.where(m16, jnp.broadcast_to(mom[v : v + 1], (16, 256)), 0.0) for v in range(8)], 0
    )
    sh, sl = split(spread)
    part_ref[...] = dot_t(pick, sh) + dot_t(pick, sl)


def sd(*shape):
    return jax.ShapeDtypeStruct(shape, F32)


def ring(value, axis, by):
    n = lax.axis_size(axis)
    return lax.ppermute(value, axis, [(i, (i + by) % n) for i in range(n)])


def call(kernel, outs, scratch=(), **kw):
    return pl.pallas_call(
        kernel,
        out_shape=outs,
        scratch_shapes=[pltpu.VMEM(s, F32) for s in scratch],
        **kw,
    )


def edges(own_dn, own_up, from_left, from_right, first, last, layers):
    rows = own_dn.shape[0]
    n = last - first
    full = pl.BlockSpec((rows, layers, 8, LANES), lambda i: (0, 0, 0, 0))
    top = 18 // layers - 1
    lo = pl.BlockSpec((n, layers, 8, LANES), lambda i: (0, 0, 0, 0))
    hi = pl.BlockSpec((n, layers, 8, LANES), lambda i: (0, top, 0, 0))
    return pl.pallas_call(
        edge_kernel,
        grid=(1,),
        in_specs=[full, full, lo, hi, lo, hi],
        out_specs=[full, full],
        out_shape=[sd(rows, layers, 8, LANES)] * 2,
    )(own_dn, own_up, from_left, from_left, from_right, from_right)


def on_device(right_side, stretch, mass_term, slot_position, coarse_group):
    a1 = jnp.asarray(A_FWD, BF16)
    a2 = jnp.asarray(A_BWD, BF16)
    lj = jnp.asarray(LAM_J, F32)
    lk = jnp.asarray(LAM_K, F32)
    wm = jnp.asarray(W_MOM, BF16)
    slot = slot_position.reshape(1, 256)
    src, coef, lo, hi = call(
        place_kernel, [sd(8, 16, 8, LANES), sd(8, LANES), sd(17, 8, LANES), sd(17, 8, LANES)]
    )(right_side.reshape(512, 256), stretch, mass_term.reshape(1, 256), slot)
    xl = ring(hi, "sx", 1)
    xr = ring(lo, "sx", -1)
    c3 = coef[None]
    to_up = jnp.concatenate([xl[15:16], src[:, 15], xr[15:16], xl[16:17], c3, xr[16:17]], 0)
    to_dn = jnp.concatenate([xl[0:1], src[:, 0], xr[0:1], xl[16:17], c3, xr[16:17]], 0)
    yd = ring(to_up, "sy", 1)
    yu = ring(to_dn, "sy", -1)

    slab = sd(3, 18, 8, LANES)
    side = sd(12, 3, 8, LANES)
    rext, w, to_l, to_r, to_d, to_u = call(
        first_kernel,
        [sd(1920, LANES), sd(10, 18, 8, LANES), slab, slab, side, side],
        [(10, 104, 256), (1920, LANES)],
    )(src, coef, xl, xr, yd, yu, a1, a2, lj, lk)
    fl = ring(to_r, "sx", 1)
    fr = ring(to_l, "sx", -1)
    to_d, to_u = edges(to_d, to_u, fl, fr, 0, 3, 3)
    fd = ring(to_u, "sy", 1)
    fu = ring(to_d, "sy", -1)

    slab = sd(2, 18, 8, LANES)
    side = sd(10, 2, 8, LANES)
    c, to_l, to_r, to_d, to_u = call(
        second_kernel,
        [sd(10, 18, 8, LANES), slab, slab, side, side],
        [(12, 20, 8, LANES), (3, 4, 4, 8, LANES), (1920, LANES), (10, 104, 256), (1920, LANES)],
    )(rext, coef, xl, xr, yd, yu, w, fl, fr, fd, fu, a1, a2, lj, lk)
    fl = ring(to_r, "sx", 1)
    fr = ring(to_l, "sx", -1)
    to_d, to_u = edges(to_d, to_u, fl, fr, 0, 2, 2)
    fd = ring(to_u, "sy", 1)
    fu = ring(to_d, "sy", -1)

    ny = lax.axis_size("sy")
    smooth, res, part = call(
        last_kernel,
        [sd(512, 256), sd(512, 256), sd(ny, LANES)],
        [(10, 18, 8, LANES), (512, 256), (512, 256)],
    )(src, coef, c, fl, fr, fd, fu, slot, coarse_group.reshape(1, 256), wm)
    arrived = lax.all_to_all(part, "sy", split_axis=0, concat_axis=0, tiled=True)
    coarse = arrived.sum(axis=0).reshape(8, GRP_DEV)
    return smooth.reshape(8, 8, 8, 256), res.reshape(8, 8, 8, 256), coarse


def solution(mesh):
    split_all = P(None, None, None, ("sx", "sy"))
    flat = P(("sx", "sy"))
    return jax.shard_map(
        on_device,
        mesh=mesh,
        in_specs=(split_all, P(None, ("sx", "sy")), flat, flat, flat),
        out_specs=(split_all, split_all, P(None, ("sx", "sy"))),
        check_vma=False,
    )
```

profile of v0, /device:TPU:8, one launch (start us, length us, event | category | flops | bytes accessed | tf_op | source)
XLA Modules:
  0.0 92.1 jit_solution(9795595672727367516)
XLA Ops:
  0.6 2.5 %shard_map.121 = (f32[8,16,8,128]{3,2,1,0:T(8,128)}, f32[8,128]{1,0:T(8,128)}, f32[17,8,128]{2,1,0:T(8,128)}, f32[17,8,128]{2,1,0:T(8,128)}) custom-call(f32[512,256]{1,0:T(8,128)} %bitcast.20, f32[3,256]{1,0:T(4,128)} %stretch_ref.1, f32[1,256]{1,0:T(1,128)} %bitcast.24, s32[1,256]{1,0:T(1,128)} %bitcast.22), custom_call_target="tpu_custom_call" | custom-call | tf_op jit(solution)/shard_map/pallas_call | solution.py:464
  3.1 0.0 collective-permute-start
  3.1 3.0 %collective-permute-start.1 = (f32[17,8,128]{2,1,0:T(8,128)}, f32[17,8,128]{2,1,0:T(8,128)S(1)}, u32[]{:S(2)}, u32[]{:S(2)}) collective-permute-start(f32[17,8,128]{2,1,0:T(8,128)} %get-tuple-element.28), channel_id=1, source_target_pairs={{0,224},{32,0},{64,32},{96,64},{128,96},{160,128},{192,160},{224,1... | collective-permute-start | bytes 208904 | tf_op jit(solution)/shard_map/ppermute | solution.py:429
  6.1 2.2 %collective-permute-done.xl_ref = f32[17,8,128]{2,1,0:T(8,128)S(1)} collective-permute-done((f32[17,8,128]{2,1,0:T(8,128)}, f32[17,8,128]{2,1,0:T(8,128)S(1)}, u32[]{:S(2)}, u32[]{:S(2)}) %collective-permute-start) | collective-permute-done | bytes 69664 | tf_op jit(solution)/shard_map/ppermute | solution.py:429
  8.3 0.8 fusion
  9.1 0.0 collective-permute-done.1.xr_ref
  9.1 0.0 copy-start.5
  9.1 0.0 copy-done.4
  9.1 0.0 copy-start.12
  9.1 0.7 copy-done.12
  9.8 2.2 %collective-permute-start.3 = (f32[13,8,128]{2,1,0:T(8,128)S(1)}, f32[13,8,128]{2,1,0:T(8,128)S(1)}, u32[]{:S(2)}, u32[]{:S(2)}) collective-permute-start(f32[13,8,128]{2,1,0:T(8,128)S(1)} %get-tuple-element.49), channel_id=1, source_target_pairs={{0,31},{1,0},{2,1},{3,2},{4,3},{5,4},{6,5},{7,6},{8,7},{9,8},{10,9... | collective-permute-start | bytes 159752 | tf_op jit(solution)/shard_map/ppermute | solution.py:429
  12.0 0.0 collective-permute-start.2
  12.0 2.0 %collective-permute-done.3.yu_ref = f32[13,8,128]{2,1,0:T(8,128)S(1)} collective-permute-done((f32[13,8,128]{2,1,0:T(8,128)S(1)}, f32[13,8,128]{2,1,0:T(8,128)S(1)}, u32[]{:S(2)}, u32[]{:S(2)}) %collective-permute-start.3) | collective-permute-done | bytes 53280 | tf_op jit(solution)/shard_map/ppermute | solution.py:429
  14.0 6.7 %collective-permute-done.2.yd_ref = f32[13,8,128]{2,1,0:T(8,128)S(1)} collective-permute-done((f32[13,8,128]{2,1,0:T(8,128)S(1)}, f32[13,8,128]{2,1,0:T(8,128)S(1)}, u32[]{:S(2)}, u32[]{:S(2)}) %collective-permute-start.2) | collective-permute-done | bytes 53280 | tf_op jit(solution)/shard_map/ppermute | solution.py:429
  20.7 0.0 copy-done.5
  20.7 0.6 copy-done.7
  21.3 4.7 %shard_map.122 = (f32[1920,128]{1,0:T(8,128)}, f32[10,18,8,128]{3,2,1,0:T(8,128)}, f32[3,18,8,128]{3,2,1,0:T(8,128)}, f32[3,18,8,128]{3,2,1,0:T(8,128)}, f32[12,...) custom-call(f32[8,16,8,128]{3,2,1,0:T(8,128)} %get-tuple-element.25.src_ref, f32[8,128]{1,0:T(8,128)} %get-tuple-element.26.coef_ref, ...), custom_call_target="tpu_custom_call" | custom-call | tf_op jit(solution)/shard_map/pallas_call | solution.py:477
  26.0 0.0 collective-permute-start.4
  26.0 3.0 %collective-permute-start.5 = (f32[3,18,8,128]{3,2,1,0:T(8,128)}, f32[3,18,8,128]{3,2,1,0:T(8,128)S(1)}, u32[]{:S(2)}, u32[]{:S(2)}) collective-permute-start(f32[3,18,8,128]{3,2,1,0:T(8,128)} %get-tuple-element.32), channel_id=1, source_target_pairs={{0,224},{32,0},{64,32},{96,64},{128,96},{160,128},{192,160},{224,1... | collective-permute-start | bytes 663560 | tf_op jit(solution)/shard_map/ppermute | solution.py:429
  29.0 3.8 %collective-permute-done.4.l_dn_ref.l_up_ref.l_ref = f32[3,18,8,128]{3,2,1,0:T(8,128)S(1)} collective-permute-done((f32[3,18,8,128]{3,2,1,0:T(8,128)}, f32[3,18,8,128]{3,2,1,0:T(8,128)S(1)}, u32[]{:S(2)}, u32[]{:S(2)}) %collective-permute-start.4) | collective-permute-done | bytes 221216 | tf_op jit(solution)/shard_map/ppermute | solution.py:429
  32.8 0.0 collective-permute-done.5.r_dn_ref.r_up_ref.r_ref
  32.8 0.7 copy-done
  33.5 0.1 copy-done.1
  33.6 1.7 %shard_map.123 = (f32[12,3,8,128]{3,2,1,0:T(8,128)}, f32[12,3,8,128]{3,2,1,0:T(8,128)}) custom-call(f32[12,3,8,128]{3,2,1,0:T(8,128)} %get-tuple-element.33.own_dn_ref, f32[12,3,8,128]{3,2,1,0:T(8,128)} %get-tuple-element.34.own_up_ref, f32[3,18,8,128]{3,2,1,0:T(8,128)} %copy-done, f32[3,18,8,128]{3,2,1,0:T(8,128)} %copy-done, f32[3,18,8,128]{3,2,1,0:T(8,128)} %copy-done.1, ...), custom_call_target="tpu_custom_call" | custom-call | tf_op jit(solution)/shard_map/pallas_call | solution.py:448
  35.3 0.0 collective-permute-start.6
  35.3 5.3 %collective-permute-start.7 = (f32[12,3,8,128]{3,2,1,0:T(8,128)}, f32[12,3,8,128]{3,2,1,0:T(8,128)S(1)}, u32[]{:S(2)}, u32[]{:S(2)}) collective-permute-start(f32[12,3,8,128]{3,2,1,0:T(8,128)} %get-tuple-element.36), channel_id=1, source_target_pairs={{0,31},{1,0},{2,1},{3,2},{4,3},{5,4},{6,5},{7,6},{8,7},{9,8},{10,9... | collective-permute-start | bytes 442376 | tf_op jit(solution)/shard_map/ppermute | solution.py:429
  40.6 3.7 %collective-permute-done.6.d_ref = f32[12,3,8,128]{3,2,1,0:T(8,128)S(1)} collective-permute-done((f32[12,3,8,128]{3,2,1,0:T(8,128)}, f32[12,3,8,128]{3,2,1,0:T(8,128)S(1)}, u32[]{:S(2)}, u32[]{:S(2)}) %collective-permute-start.6) | collective-permute-done | bytes 147488 | tf_op jit(solution)/shard_map/ppermute | solution.py:429
  44.4 0.0 collective-permute-done.7.u_ref
  44.4 0.6 copy-done.8
  45.0 0.1 copy-done.9
  45.1 5.8 %shard_map.124 = (f32[10,18,8,128]{3,2,1,0:T(8,128)}, f32[2,18,8,128]{3,2,1,0:T(8,128)}, f32[2,18,8,128]{3,2,1,0:T(8,128)}, f32[10,2,8,128]{3,2,1,0:T(8,128)}, f32[10,2,8,128]{3,2,1,0:T(8,128)}) custom-call(f32[1920,128]{1,0:T(8,128)} %get-tuple-element.29.rext_ref, f32[8,128]{1,0:T(8,128)} %get-tuple-element.26.coef_ref, f32[17,8,128]{2,1,0:T(8,128)} %copy-done.4, ...), custom_call_target="tpu_custom_call" | custom-call | tf_op jit(solution)/shard_map/pallas_call | solution.py:490
  50.9 0.0 collective-permute-start.8
  50.9 3.0 %collective-permute-start.9 = (f32[2,18,8,128]{3,2,1,0:T(8,128)}, f32[2,18,8,128]{3,2,1,0:T(8,128)S(1)}, u32[]{:S(2)}, u32[]{:S(2)}) collective-permute-start(f32[2,18,8,128]{3,2,1,0:T(8,128)} %get-tuple-element.39), channel_id=1, source_target_pairs={{0,224},{32,0},{64,32},{96,64},{128,96},{160,128},{192,160},{224,1... | collective-permute-start | bytes 442376 | tf_op jit(solution)/shard_map/ppermute | solution.py:429
  53.9 3.0 %collective-permute-done.8.l_dn_ref.l_up_ref.l_ref = f32[2,18,8,128]{3,2,1,0:T(8,128)S(1)} collective-permute-done((f32[2,18,8,128]{3,2,1,0:T(8,128)}, f32[2,18,8,128]{3,2,1,0:T(8,128)S(1)}, u32[]{:S(2)}, u32[]{:S(2)}) %collective-permute-start.8) | collective-permute-done | bytes 147488 | tf_op jit(solution)/shard_map/ppermute | solution.py:429
  56.9 0.0 collective-permute-done.9.r_dn_ref.r_up_ref.r_ref
  56.9 0.6 copy-done.2
  57.5 0.1 copy-done.3
  57.6 1.6 %shard_map.125 = (f32[10,2,8,128]{3,2,1,0:T(8,128)}, f32[10,2,8,128]{3,2,1,0:T(8,128)}) custom-call(f32[10,2,8,128]{3,2,1,0:T(8,128)} %get-tuple-element.40.own_dn_ref, f32[10,2,8,128]{3,2,1,0:T(8,128)} %get-tuple-element.41.own_up_ref, f32[2,18,8,128]{3,2,1,0:T(8,128)} %copy-done.2, f32[2,18,8,128]{3,2,1,0:T(8,128)} %copy-done.2, ...), custom_call_target="tpu_custom_call" | custom-call | tf_op jit(solution)/shard_map/pallas_call | solution.py:448
  59.2 0.0 collective-permute-start.10
  59.2 5.1 %collective-permute-start.11 = (f32[10,2,8,128]{3,2,1,0:T(8,128)}, f32[10,2,8,128]{3,2,1,0:T(8,128)S(1)}, u32[]{:S(2)}, u32[]{:S(2)}) collective-permute-start(f32[10,2,8,128]{3,2,1,0:T(8,128)} %get-tuple-element.43), channel_id=1, source_target_pairs={{0,31},{1,0},{2,1},{3,2},{4,3},{5,4},{6,5},{7,6},{8,7},{9,8},{10,9... | collective-permute-start | bytes 245768 | tf_op jit(solution)/shard_map/ppermute | solution.py:429
  64.3 2.6 %collective-permute-done.10.d_ref = f32[10,2,8,128]{3,2,1,0:T(8,128)S(1)} collective-permute-done((f32[10,2,8,128]{3,2,1,0:T(8,128)}, f32[10,2,8,128]{3,2,1,0:T(8,128)S(1)}, u32[]{:S(2)}, u32[]{:S(2)}) %collective-permute-start.10) | collective-permute-done | bytes 81952 | tf_op jit(solution)/shard_map/ppermute | solution.py:429
  66.9 0.0 collective-permute-done.11.u_ref
  66.9 0.6 copy-done.10
  67.5 0.0 copy-done.11
  67.6 3.2 %shard_map.126 = (f32[512,256]{1,0:T(8,128)}, f32[512,256]{1,0:T(8,128)}, f32[32,128]{1,0:T(8,128)}) custom-call(f32[8,16,8,128]{3,2,1,0:T(8,128)} %get-tuple-element.25.src_ref, f32[8,128]{1,0:T(8,128)} %get-tuple-element.26.coef_ref, f32[10,18,8,128]{3,2,1,0:T(8,128)} %get-tuple-element.37.c_ref, f32[2,18,8,128]{3,2,1,0:T(8,128)} %copy-done.2, ...), custom_call_target="tpu_custom_call" | custom-call | tf_op jit(solution)/shard_map/pallas_call | solution.py:502
  70.7 20.6 %all_to_all.9 = f32[32,1,128]{2,1,0:T(1,128)S(1)} all-to-all(f32[32,1,128]{2,1,0:T(1,128)} %bitcast.21), channel_id=1, replica_groups=mesh['sx'=8,'sy'=32] {'sy'}, dimensions={0} | all-to-all | bytes 32768 | tf_op jit(solution)/shard_map/all_to_all | solution.py:507
  91.4 0.1 reduce_sum.9
  91.4 0.7 reshape.35
  (17 shorter events, 0.0 us)
Async XLA Ops:
  3.1 5.2 %collective-permute-start = (f32[17,8,128]{2,1,0:T(8,128)}, f32[17,8,128]{2,1,0:T(8,128)S(1)}, u32[]{:S(2)}, u32[]{:S(2)}) collective-permute-start(f32[17,8,128]{2,1,0:T(8,128)} %get-tuple-element.27), channel_id=1, source_target_pairs={{0,32},{32,64},{64,96},{96,128},{128,160},{160,192},{192,224},{224... | collective-permute-start | bytes 208904 | tf_op jit(solution)/shard_map/ppermute | solution.py:429
  3.1 6.0 %collective-permute-start.1 = (f32[17,8,128]{2,1,0:T(8,128)}, f32[17,8,128]{2,1,0:T(8,128)S(1)}, u32[]{:S(2)}, u32[]{:S(2)}) collective-permute-start(f32[17,8,128]{2,1,0:T(8,128)} %get-tuple-element.28), channel_id=1, source_target_pairs={{0,224},{32,0},{64,32},{96,64},{128,96},{160,128},{192,160},{224,1... | collective-permute-start | bytes 208904 | tf_op jit(solution)/shard_map/ppermute | solution.py:429
  8.3 0.8 copy-start.4
  9.1 11.6 %copy-start.5 = (f32[17,8,128]{2,1,0:T(8,128)}, f32[17,8,128]{2,1,0:T(8,128)S(1)}, u32[]{:S(2)}) copy-start(f32[17,8,128]{2,1,0:T(8,128)S(1)} %collective-permute-done.1.xr_ref) | copy-start | bytes 208900
  9.1 0.7 copy-start.12
  9.8 4.1 %collective-permute-start.3 = (f32[13,8,128]{2,1,0:T(8,128)S(1)}, f32[13,8,128]{2,1,0:T(8,128)S(1)}, u32[]{:S(2)}, u32[]{:S(2)}) collective-permute-start(f32[13,8,128]{2,1,0:T(8,128)S(1)} %get-tuple-element.49), channel_id=1, source_target_pairs={{0,31},{1,0},{2,1},{3,2},{4,3},{5,4},{6,5},{7,6},{8,7},{9,8},{10,9... | collective-permute-start | bytes 159752 | tf_op jit(solution)/shard_map/ppermute | solution.py:429
  12.0 8.7 %collective-permute-start.2 = (f32[13,8,128]{2,1,0:T(8,128)S(1)}, f32[13,8,128]{2,1,0:T(8,128)S(1)}, u32[]{:S(2)}, u32[]{:S(2)}) collective-permute-start(f32[13,8,128]{2,1,0:T(8,128)S(1)} %get-tuple-element.50), channel_id=1, source_target_pairs={{0,1},{1,2},{2,3},{3,4},{4,5},{5,6},{6,7},{7,8},{8,9},{9,10},{10,1... | collective-permute-start | bytes 159752 | tf_op jit(solution)/shard_map/ppermute | solution.py:429
  14.0 6.7 %copy-start.6 = (f32[13,8,128]{2,1,0:T(8,128)}, f32[13,8,128]{2,1,0:T(8,128)S(1)}, u32[]{:S(2)}) copy-start(f32[13,8,128]{2,1,0:T(8,128)S(1)} %collective-permute-done.3.yu_ref) | copy-start | bytes 159748
  20.7 0.6 copy-start.7
  26.0 6.8 %collective-permute-start.4 = (f32[3,18,8,128]{3,2,1,0:T(8,128)}, f32[3,18,8,128]{3,2,1,0:T(8,128)S(1)}, u32[]{:S(2)}, u32[]{:S(2)}) collective-permute-start(f32[3,18,8,128]{3,2,1,0:T(8,128)} %get-tuple-element.31), channel_id=1, source_target_pairs={{0,32},{32,64},{64,96},{96,128},{128,160},{160,192},{192,224},{224... | collective-permute-start | bytes 663560 | tf_op jit(solution)/shard_map/ppermute | solution.py:429
  26.0 6.8 %collective-permute-start.5 = (f32[3,18,8,128]{3,2,1,0:T(8,128)}, f32[3,18,8,128]{3,2,1,0:T(8,128)S(1)}, u32[]{:S(2)}, u32[]{:S(2)}) collective-permute-start(f32[3,18,8,128]{3,2,1,0:T(8,128)} %get-tuple-element.32), channel_id=1, source_target_pairs={{0,224},{32,0},{64,32},{96,64},{128,96},{160,128},{192,160},{224,1... | collective-permute-start | bytes 663560 | tf_op jit(solution)/shard_map/ppermute | solution.py:429
  32.8 0.7 copy-start
  32.8 0.8 copy-start.1
  35.3 9.1 %collective-permute-start.6 = (f32[12,3,8,128]{3,2,1,0:T(8,128)}, f32[12,3,8,128]{3,2,1,0:T(8,128)S(1)}, u32[]{:S(2)}, u32[]{:S(2)}) collective-permute-start(f32[12,3,8,128]{3,2,1,0:T(8,128)} %get-tuple-element.35), channel_id=1, source_target_pairs={{0,1},{1,2},{2,3},{3,4},{4,5},{5,6},{6,7},{7,8},{8,9},{9,10},{10,1... | collective-permute-start | bytes 442376 | tf_op jit(solution)/shard_map/ppermute | solution.py:429
  35.3 9.1 %collective-permute-start.7 = (f32[12,3,8,128]{3,2,1,0:T(8,128)}, f32[12,3,8,128]{3,2,1,0:T(8,128)S(1)}, u32[]{:S(2)}, u32[]{:S(2)}) collective-permute-start(f32[12,3,8,128]{3,2,1,0:T(8,128)} %get-tuple-element.36), channel_id=1, source_target_pairs={{0,31},{1,0},{2,1},{3,2},{4,3},{5,4},{6,5},{7,6},{8,7},{9,8},{10,9... | collective-permute-start | bytes 442376 | tf_op jit(solution)/shard_map/ppermute | solution.py:429
  44.4 0.7 copy-start.8
  44.4 0.7 copy-start.9
  50.9 6.0 %collective-permute-start.8 = (f32[2,18,8,128]{3,2,1,0:T(8,128)}, f32[2,18,8,128]{3,2,1,0:T(8,128)S(1)}, u32[]{:S(2)}, u32[]{:S(2)}) collective-permute-start(f32[2,18,8,128]{3,2,1,0:T(8,128)} %get-tuple-element.38), channel_id=1, source_target_pairs={{0,32},{32,64},{64,96},{96,128},{128,160},{160,192},{192,224},{224... | collective-permute-start | bytes 442376 | tf_op jit(solution)/shard_map/ppermute | solution.py:429
  50.9 6.0 %collective-permute-start.9 = (f32[2,18,8,128]{3,2,1,0:T(8,128)}, f32[2,18,8,128]{3,2,1,0:T(8,128)S(1)}, u32[]{:S(2)}, u32[]{:S(2)}) collective-permute-start(f32[2,18,8,128]{3,2,1,0:T(8,128)} %get-tuple-element.39), channel_id=1, source_target_pairs={{0,224},{32,0},{64,32},{96,64},{128,96},{160,128},{192,160},{224,1... | collective-permute-start | bytes 442376 | tf_op jit(solution)/shard_map/ppermute | solution.py:429
  56.9 0.7 copy-start.2
  56.9 0.7 copy-start.3
  59.2 7.7 %collective-permute-start.10 = (f32[10,2,8,128]{3,2,1,0:T(8,128)}, f32[10,2,8,128]{3,2,1,0:T(8,128)S(1)}, u32[]{:S(2)}, u32[]{:S(2)}) collective-permute-start(f32[10,2,8,128]{3,2,1,0:T(8,128)} %get-tuple-element.42), channel_id=1, source_target_pairs={{0,1},{1,2},{2,3},{3,4},{4,5},{5,6},{6,7},{7,8},{8,9},{9,10},{10,1... | collective-permute-start | bytes 245768 | tf_op jit(solution)/shard_map/ppermute | solution.py:429
  59.2 7.7 %collective-permute-start.11 = (f32[10,2,8,128]{3,2,1,0:T(8,128)}, f32[10,2,8,128]{3,2,1,0:T(8,128)S(1)}, u32[]{:S(2)}, u32[]{:S(2)}) collective-permute-start(f32[10,2,8,128]{3,2,1,0:T(8,128)} %get-tuple-element.43), channel_id=1, source_target_pairs={{0,31},{1,0},{2,1},{3,2},{4,3},{5,4},{6,5},{7,6},{8,7},{9,8},{10,9... | collective-permute-start | bytes 245768 | tf_op jit(solution)/shard_map/ppermute | solution.py:429
  66.9 0.6 copy-start.10
  66.9 0.6 copy-start.11
where the time goes:
time: 92.5 us; the launch traced here: 92.1 us
  waiting for transfers between devices  24.1 us (26%)
  starting transfers between devices  21.4 us (23%)
  blocking collectives  20.6 us (22%)
  Pallas kernels  19.5 us (21%)
  local copies, waits for them, and re-layouts  5.63 us (6%)
    ppermute x12, waiting for transfers between devices, ring(): return lax.ppermute(value, axis, [(i, (i + by) % n) for i in range(n)])  24.1 us
    ppermute x12, starting transfers between devices, ring(): return lax.ppermute(value, axis, [(i, (i + by) % n) for i in range(n)])  21.4 us
    all_to_all x1, blocking collectives, on_device(): lax.all_to_all(part, 'sy', split_axis=0, concat_axis=0, tiled=True)  20.6 us
    pallas_call x1, Pallas kernels, on_device(): call(second_kernel, [sd(10, 18, 8, LANES), slab, slab, side, side], [(12,...  5.8 us
    unnamed x31, local copies, waits for them, and re-layouts  4.95 us
    pallas_call x1, Pallas kernels, on_device(): call(first_kernel, [sd(1920, LANES), sd(10, 18, 8, LANES), slab, slab, si...  4.72 us
    pallas_call x2, Pallas kernels, edges(): pl.pallas_call(edge_kernel, grid=(1,), in_specs=[full, full, lo, hi, lo,...  3.33 us
    pallas_call x1, Pallas kernels, on_device(): call(last_kernel, [sd(512, 256), sd(512, 256), sd(ny, LANES)], [(10, 18,...  3.16 us
  transfers between devices with their start and end apart: 12, of which 7 were waited for; matrix products, arithmetic and copies ran while one was open for 1% of the time, Pallas kernels for 0%

commit v1 on v0

--- a/solution.py
+++ b/solution.py
@@ -247,17 +247,14 @@
         to_up_ref[p + 1] = line[15:18]
 
 
-def edge_kernel(own_dn_ref, own_up_ref, l_dn_ref, l_up_ref, r_dn_ref, r_up_ref, dn_ref, up_ref):
+def edge_kernel(own_dn_ref, own_up_ref, l_ref, r_ref, dn_ref, up_ref):
     left, right, _, _ = flags()
-    for own, l, r, out in (
-        (own_dn_ref, l_dn_ref, r_dn_ref, dn_ref),
-        (own_up_ref, l_up_ref, r_up_ref, up_ref),
-    ):
-        n = l.shape[0]
-        m = own.shape[0]
-        out[0:n] = own[0:n] + l[...] * left
+    n = l_ref.shape[0]
+    m = own_dn_ref.shape[0]
+    for own, y, out in ((own_dn_ref, 0, dn_ref), (own_up_ref, 18 - n, up_ref)):
+        out[0:n] = own[0:n] + l_ref[:, y : y + n] * left
         out[n : m - n] = own[n : m - n]
-        out[m - n :] = own[m - n :] + r[...] * right
+        out[m - n :] = own[m - n :] + r_ref[:, y : y + n] * right
 
 
 def neighbours_z(u):
@@ -424,34 +421,39 @@
     return jax.ShapeDtypeStruct(shape, F32)
 
 
+def vm(*shape):
+    return pltpu.VMEM(shape, F32)
+
+
 def ring(value, axis, by):
     n = lax.axis_size(axis)
     return lax.ppermute(value, axis, [(i, (i + by) % n) for i in range(n)])
 
 
+def mark(args):
+    return [a if isinstance(a, tuple) else (a, False) for a in args]
+
+
 def call(kernel, outs, scratch=(), **kw):
-    return pl.pallas_call(
-        kernel,
-        out_shape=outs,
-        scratch_shapes=[pltpu.VMEM(s, F32) for s in scratch],
-        **kw,
-    )
-
-
-def edges(own_dn, own_up, from_left, from_right, first, last, layers):
-    rows = own_dn.shape[0]
-    n = last - first
-    full = pl.BlockSpec((rows, layers, 8, LANES), lambda i: (0, 0, 0, 0))
-    top = 18 // layers - 1
-    lo = pl.BlockSpec((n, layers, 8, LANES), lambda i: (0, 0, 0, 0))
-    hi = pl.BlockSpec((n, layers, 8, LANES), lambda i: (0, top, 0, 0))
-    return pl.pallas_call(
-        edge_kernel,
-        grid=(1,),
-        in_specs=[full, full, lo, hi, lo, hi],
-        out_specs=[full, full],
-        out_shape=[sd(rows, layers, 8, LANES)] * 2,
-    )(own_dn, own_up, from_left, from_left, from_right, from_right)
+    vmem = pl.BlockSpec(memory_space=pltpu.VMEM)
+
+    def run(*args):
+        args = [a if at_home else pltpu.with_memory_space_constraint(a, pltpu.VMEM) for a, at_home in mark(args)]
+        return pl.pallas_call(
+            kernel,
+            out_shape=outs,
+            in_specs=[vmem] * len(args),
+            out_specs=[vmem] * len(outs),
+            scratch_shapes=[pltpu.VMEM(s, F32) for s in scratch],
+            compiler_params=pltpu.CompilerParams(vmem_limit_bytes=16 << 20),
+            **kw,
+        )(*args)
+
+    return run
+
+
+def edges(own_dn, own_up, from_left, from_right):
+    return call(edge_kernel, [vm(*own_dn.shape)] * 2)(own_dn, own_up, from_left, from_right)
 
 
 def on_device(right_side, stretch, mass_term, slot_position, coarse_group):
@@ -462,8 +464,8 @@
     wm = jnp.asarray(W_MOM, BF16)
     slot = slot_position.reshape(1, 256)
     src, coef, lo, hi = call(
-        place_kernel, [sd(8, 16, 8, LANES), sd(8, LANES), sd(17, 8, LANES), sd(17, 8, LANES)]
-    )(right_side.reshape(512, 256), stretch, mass_term.reshape(1, 256), slot)
+        place_kernel, [vm(8, 16, 8, LANES), vm(8, LANES), vm(17, 8, LANES), vm(17, 8, LANES)]
+    )((right_side.reshape(512, 256), True), (stretch, True), (mass_term.reshape(1, 256), True), (slot, True))
     xl = ring(hi, "sx", 1)
     xr = ring(lo, "sx", -1)
     c3 = coef[None]
@@ -472,38 +474,38 @@
     yd = ring(to_up, "sy", 1)
     yu = ring(to_dn, "sy", -1)
 
-    slab = sd(3, 18, 8, LANES)
-    side = sd(12, 3, 8, LANES)
+    slab = vm(3, 18, 8, LANES)
+    side = vm(12, 3, 8, LANES)
     rext, w, to_l, to_r, to_d, to_u = call(
         first_kernel,
-        [sd(1920, LANES), sd(10, 18, 8, LANES), slab, slab, side, side],
+        [vm(1920, LANES), vm(10, 18, 8, LANES), slab, slab, side, side],
         [(10, 104, 256), (1920, LANES)],
     )(src, coef, xl, xr, yd, yu, a1, a2, lj, lk)
     fl = ring(to_r, "sx", 1)
     fr = ring(to_l, "sx", -1)
-    to_d, to_u = edges(to_d, to_u, fl, fr, 0, 3, 3)
+    to_d, to_u = edges(to_d, to_u, fl, fr)
     fd = ring(to_u, "sy", 1)
     fu = ring(to_d, "sy", -1)
 
-    slab = sd(2, 18, 8, LANES)
-    side = sd(10, 2, 8, LANES)
+    slab = vm(2, 18, 8, LANES)
+    side = vm(10, 2, 8, LANES)
     c, to_l, to_r, to_d, to_u = call(
         second_kernel,
-        [sd(10, 18, 8, LANES), slab, slab, side, side],
+        [vm(10, 18, 8, LANES), slab, slab, side, side],
         [(12, 20, 8, LANES), (3, 4, 4, 8, LANES), (1920, LANES), (10, 104, 256), (1920, LANES)],
     )(rext, coef, xl, xr, yd, yu, w, fl, fr, fd, fu, a1, a2, lj, lk)
     fl = ring(to_r, "sx", 1)
     fr = ring(to_l, "sx", -1)
-    to_d, to_u = edges(to_d, to_u, fl, fr, 0, 2, 2)
+    to_d, to_u = edges(to_d, to_u, fl, fr)
     fd = ring(to_u, "sy", 1)
     fu = ring(to_d, "sy", -1)
 
     ny = lax.axis_size("sy")
     smooth, res, part = call(
         last_kernel,
-        [sd(512, 256), sd(512, 256), sd(ny, LANES)],
+        [sd(512, 256), sd(512, 256), vm(ny, LANES)],
         [(10, 18, 8, LANES), (512, 256), (512, 256)],
-    )(src, coef, c, fl, fr, fd, fu, slot, coarse_group.reshape(1, 256), wm)
+    )(src, coef, c, fl, fr, fd, fu, (slot, True), (coarse_group.reshape(1, 256), True), wm)
     arrived = lax.all_to_all(part, "sy", split_axis=0, concat_axis=0, tiled=True)
     coarse = arrived.sum(axis=0).reshape(8, GRP_DEV)
     return smooth.reshape(8, 8, 8, 256), res.reshape(8, 8, 8, 256), coarse

time: 92.5 us -> 78 us (0.84)
  Pallas kernels: 19.5 us -> 7.68 us
  local copies, waits for them, and re-layouts: 5.63 us -> 3.79 us
  waiting for transfers between devices: 24.1 us -> 23.1 us
    pallas_call x6, Pallas kernels: 19.5 us -> 7.68 us  [run(): pl.pallas_call(kernel, out_shape=outs, in_specs=[vmem] * len(args), out_s...]
    unnamed x31 -> x25, local copies, waits for them, and re-layouts: 4.95 us -> 3.11 us
    ppermute x12, waiting for transfers between devices: 24.1 us -> 23.1 us  [ring(): return lax.ppermute(value, axis, [(i, (i + by) % n) for i in range(n)])]
  transfers between devices with their start and end apart: 12 -> 12, of which waited for: 7 -> 7; matrix products, arithmetic and copies ran while one was open for 1% -> 0% of each run, Pallas kernels for 0% -> 0%
where the time goes in v1:
time: 78 us; the launch traced here: 77.8 us
  waiting for transfers between devices  23.1 us (30%)
  starting transfers between devices  21.8 us (28%)
  blocking collectives  20.5 us (26%)
  Pallas kernels  7.68 us (10%)
  local copies, waits for them, and re-layouts  3.79 us (5%)
  between operations  0.8 us (1%)
    ppermute x12, waiting for transfers between devices, ring(): return lax.ppermute(value, axis, [(i, (i + by) % n) for i in range(n)])  23.1 us
    ppermute x12, starting transfers between devices, ring(): return lax.ppermute(value, axis, [(i, (i + by) % n) for i in range(n)])  21.8 us
    all_to_all x1, blocking collectives, on_device(): lax.all_to_all(part, 'sy', split_axis=0, concat_axis=0, tiled=True)  20.5 us
    pallas_call x6, Pallas kernels, run(): pl.pallas_call(kernel, out_shape=outs, in_specs=[vmem] * len(args), out_s...  7.68 us
    unnamed x25, local copies, waits for them, and re-layouts  3.11 us
  transfers between devices with their start and end apart: 12, of which 7 were waited for; matrix products, arithmetic and copies ran while one was open for 0% of the time, Pallas kernels for 0%

profile of v1, /device:TPU:8, one launch (start us, length us, event | category | flops | bytes accessed | tf_op | source)
XLA Modules:
  0.0 77.8 jit_solution(9756719797489654657)
XLA Ops:
  0.6 0.0 copy-start.6
  0.6 0.0 copy-start.7
  0.7 0.7 copy-done.6
  1.3 0.0 copy-done.7
  1.3 0.0 copy-start
  1.3 1.0 %copy-done = f32[8,8,8,256]{3,2,1,0:T(8,128)S(1)} copy-done((f32[8,8,8,256]{3,2,1,0:T(8,128)S(1)}, f32[8,8,8,256]{3,2,1,0:T(8,128)}, u32[]{:S(2)}) %copy-start) | copy-done | bytes 524312
  2.4 0.0 copy-start.8
  2.4 0.7 copy-done.8
  3.0 0.0 copy-start.3
  3.1 0.0 copy-start.4
  3.1 0.6 shard_map.121
  3.7 0.0 copy-start.1
  3.7 0.0 collective-permute-start
  3.7 2.9 %collective-permute-start.1 = (f32[17,8,128]{2,1,0:T(8,128)S(1)}, f32[17,8,128]{2,1,0:T(8,128)S(1)}, u32[]{:S(2)}, u32[]{:S(2)}) collective-permute-start(f32[17,8,128]{2,1,0:T(8,128)S(1)} %get-tuple-element.28), channel_id=1, source_target_pairs={{0,224},{32,0},{64,32},{96,64},{128,96},{160,128},{192,160},{224,1... | collective-permute-start | bytes 208904 | tf_op jit(solution)/shard_map/ppermute | solution.py:430
  6.7 2.0 %collective-permute-done.xl_ref = f32[17,8,128]{2,1,0:T(8,128)S(1)} collective-permute-done((f32[17,8,128]{2,1,0:T(8,128)S(1)}, f32[17,8,128]{2,1,0:T(8,128)S(1)}, u32[]{:S(2)}, u32[]{:S(2)}) %collective-permute-start) | collective-permute-done | bytes 69664 | tf_op jit(solution)/shard_map/ppermute | solution.py:430
  8.7 0.0 collective-permute-done.1.xr_ref
  8.7 2.2 %collective-permute-start.3 = (f32[13,8,128]{2,1,0:T(8,128)S(1)}, f32[13,8,128]{2,1,0:T(8,128)S(1)}, u32[]{:S(2)}, u32[]{:S(2)}) collective-permute-start(f32[13,8,128]{2,1,0:T(8,128)S(1)} %get-tuple-element.49), channel_id=1, source_target_pairs={{0,31},{1,0},{2,1},{3,2},{4,3},{5,4},{6,5},{7,6},{8,7},{9,8},{10,9... | collective-permute-start | bytes 159752 | tf_op jit(solution)/shard_map/ppermute | solution.py:430
  10.9 0.0 collective-permute-start.2
  10.9 2.0 %collective-permute-done.3.yu_ref = f32[13,8,128]{2,1,0:T(8,128)S(1)} collective-permute-done((f32[13,8,128]{2,1,0:T(8,128)S(1)}, f32[13,8,128]{2,1,0:T(8,128)S(1)}, u32[]{:S(2)}, u32[]{:S(2)}) %collective-permute-start.3) | collective-permute-done | bytes 53280 | tf_op jit(solution)/shard_map/ppermute | solution.py:430
  12.9 6.7 %collective-permute-done.2.yd_ref = f32[13,8,128]{2,1,0:T(8,128)S(1)} collective-permute-done((f32[13,8,128]{2,1,0:T(8,128)S(1)}, f32[13,8,128]{2,1,0:T(8,128)S(1)}, u32[]{:S(2)}, u32[]{:S(2)}) %collective-permute-start.2) | collective-permute-done | bytes 53280 | tf_op jit(solution)/shard_map/ppermute | solution.py:430
  19.7 0.0 copy-done.3
  19.7 0.0 copy-done.4
  19.7 0.0 copy-done.1
  19.7 0.0 copy-done.2
  19.7 2.2 %shard_map.122 = (f32[1920,128]{1,0:T(8,128)S(1)}, f32[10,18,8,128]{3,2,1,0:T(8,128)S(1)}, f32[3,18,8,128]{3,2,1,0:T(8,128)S(1)}, f32[3,18,8,128]{3,2,1,0:T(8,12...) custom-call(f32[8,16,8,128]{3,2,1,0:T(8,128)S(1)} %get-tuple-element.25.src_ref, ...), custom_call_target="tpu_custom_call" | custom-call | tf_op jit(solution)/shard_map/pallas_call | solution.py:442
  21.9 0.0 collective-permute-start.4
  21.9 2.9 %collective-permute-start.5 = (f32[3,18,8,128]{3,2,1,0:T(8,128)S(1)}, f32[3,18,8,128]{3,2,1,0:T(8,128)S(1)}, u32[]{:S(2)}, u32[]{:S(2)}) collective-permute-start(f32[3,18,8,128]{3,2,1,0:T(8,128)S(1)} %get-tuple-element.32), channel_id=1, source_target_pairs={{0,224},{32,0},{64,32},{96,64},{128,96},{160,128},{192,160},{224,1... | collective-permute-start | bytes 663560 | tf_op jit(solution)/shard_map/ppermute | solution.py:430
  24.8 3.6 %collective-permute-done.4.l_ref = f32[3,18,8,128]{3,2,1,0:T(8,128)S(1)} collective-permute-done((f32[3,18,8,128]{3,2,1,0:T(8,128)S(1)}, f32[3,18,8,128]{3,2,1,0:T(8,128)S(1)}, u32[]{:S(2)}, u32[]{:S(2)}) %collective-permute-start.4) | collective-permute-done | bytes 221216 | tf_op jit(solution)/shard_map/ppermute | solution.py:430
  28.5 0.0 collective-permute-done.5.r_ref
  28.5 0.1 collective-permute-start.6
  28.6 5.4 %collective-permute-start.7 = (f32[12,3,8,128]{3,2,1,0:T(8,128)S(1)}, f32[12,3,8,128]{3,2,1,0:T(8,128)S(1)}, u32[]{:S(2)}, u32[]{:S(2)}) collective-permute-start(f32[12,3,8,128]{3,2,1,0:T(8,128)S(1)} %get-tuple-element.36), channel_id=1, source_target_pairs={{0,31},{1,0},{2,1},{3,2},{4,3},{5,4},{6,5},{7,6},{8,7},{9,8},{10,9... | collective-permute-start | bytes 442376 | tf_op jit(solution)/shard_map/ppermute | solution.py:430
  34.0 3.7 %collective-permute-done.6.d_ref = f32[12,3,8,128]{3,2,1,0:T(8,128)S(1)} collective-permute-done((f32[12,3,8,128]{3,2,1,0:T(8,128)S(1)}, f32[12,3,8,128]{3,2,1,0:T(8,128)S(1)}, u32[]{:S(2)}, u32[]{:S(2)}) %collective-permute-start.6) | collective-permute-done | bytes 147488 | tf_op jit(solution)/shard_map/ppermute | solution.py:430
  37.7 0.0 collective-permute-done.7.u_ref
  37.7 3.1 %shard_map.124 = (f32[10,18,8,128]{3,2,1,0:T(8,128)S(1)}, f32[2,18,8,128]{3,2,1,0:T(8,128)S(1)}, f32[2,18,8,128]{3,2,1,0:T(8,128)S(1)}, f32[10,2,8,128]{3,2,1,0:T(8,128)S(1)}, f32[10,2,8,128]{3,2,1,0:T(8,128)S(1)}) custom-call(f32[1920,128]{1,0:T(8,128)S(1)} %get-tuple-element.29.rext_ref, f32[8,128]{1,0:T(8,128)S(1)} %get-tuple-element.26.coef_ref, ...), custom_call_target="tpu_custom_call" | custom-call | tf_op jit(solution)/shard_map/pallas_call | solution.py:442
  40.7 0.0 collective-permute-start.8
  40.8 2.9 %collective-permute-start.9 = (f32[2,18,8,128]{3,2,1,0:T(8,128)S(1)}, f32[2,18,8,128]{3,2,1,0:T(8,128)S(1)}, u32[]{:S(2)}, u32[]{:S(2)}) collective-permute-start(f32[2,18,8,128]{3,2,1,0:T(8,128)S(1)} %get-tuple-element.39), channel_id=1, source_target_pairs={{0,224},{32,0},{64,32},{96,64},{128,96},{160,128},{192,160},{224,1... | collective-permute-start | bytes 442376 | tf_op jit(solution)/shard_map/ppermute | solution.py:430
  43.7 2.8 %collective-permute-done.8.l_ref = f32[2,18,8,128]{3,2,1,0:T(8,128)S(1)} collective-permute-done((f32[2,18,8,128]{3,2,1,0:T(8,128)S(1)}, f32[2,18,8,128]{3,2,1,0:T(8,128)S(1)}, u32[]{:S(2)}, u32[]{:S(2)}) %collective-permute-start.8) | collective-permute-done | bytes 147488 | tf_op jit(solution)/shard_map/ppermute | solution.py:430
  46.5 0.0 collective-permute-done.9.r_ref
  46.6 0.1 collective-permute-start.10
  46.6 5.1 %collective-permute-start.11 = (f32[10,2,8,128]{3,2,1,0:T(8,128)S(1)}, f32[10,2,8,128]{3,2,1,0:T(8,128)S(1)}, u32[]{:S(2)}, u32[]{:S(2)}) collective-permute-start(f32[10,2,8,128]{3,2,1,0:T(8,128)S(1)} %get-tuple-element.43), channel_id=1, source_target_pairs={{0,31},{1,0},{2,1},{3,2},{4,3},{5,4},{6,5},{7,6},{8,7},{9,8},{10,9... | collective-permute-start | bytes 245768 | tf_op jit(solution)/shard_map/ppermute | solution.py:430
  51.8 2.3 %collective-permute-done.10.d_ref = f32[10,2,8,128]{3,2,1,0:T(8,128)S(1)} collective-permute-done((f32[10,2,8,128]{3,2,1,0:T(8,128)S(1)}, f32[10,2,8,128]{3,2,1,0:T(8,128)S(1)}, u32[]{:S(2)}, u32[]{:S(2)}) %collective-permute-start.10) | collective-permute-done | bytes 81952 | tf_op jit(solution)/shard_map/ppermute | solution.py:430
  54.1 0.0 collective-permute-done.11.u_ref
  54.1 0.0 copy-done.5
  54.1 0.7 copy-done.9
  54.8 1.8 %shard_map.126 = (f32[512,256]{1,0:T(8,128)}, f32[512,256]{1,0:T(8,128)}, f32[32,128]{1,0:T(8,128)S(1)}) custom-call(f32[8,16,8,128]{3,2,1,0:T(8,128)S(1)} %get-tuple-element.25.src_ref, f32[8,128]{1,0:T(8,128)S(1)} %get-tuple-element.26.coef_ref, f32[10,18,8,128]{3,2,1,0:T(8,128)S(1)} %get-tuple-element.37.c_ref, ...), custom_call_target="tpu_custom_call" | custom-call | tf_op jit(solution)/shard_map/pallas_call | solution.py:442
  56.6 20.5 %all_to_all.9 = f32[32,1,128]{2,1,0:T(1,128)S(1)} all-to-all(f32[32,1,128]{2,1,0:T(1,128)S(1)} %bitcast.21), channel_id=1, replica_groups=mesh['sx'=8,'sy'=32] {'sy'}, dimensions={0} | all-to-all | bytes 32768 | tf_op jit(solution)/shard_map/all_to_all | solution.py:509
  77.0 0.1 reduce_sum.9
  77.1 0.7 reshape.35
  (11 shorter events, 0.1 us)
Async XLA Ops:
  0.6 0.7 copy-start.6
  0.6 0.7 copy-start.7
  1.3 1.0 %copy-start = (f32[8,8,8,256]{3,2,1,0:T(8,128)S(1)}, f32[8,8,8,256]{3,2,1,0:T(8,128)}, u32[]{:S(2)}) copy-start(f32[8,8,8,256]{3,2,1,0:T(8,128)} %param.10) | copy-start | bytes 1572868
  2.4 0.7 copy-start.8
  3.0 16.6 %copy-start.3 = (f32[104,128]{1,0:T(8,128)S(1)}, f32[104,128]{1,0:T(8,128)}, u32[]{:S(2)}) copy-start(f32[104,128]{1,0:T(8,128)} %constant.15.clone.lk_ref) | copy-start | bytes 159748
  3.1 16.6 %copy-start.4 = (f32[104,128]{1,0:T(8,128)S(1)}, f32[104,128]{1,0:T(8,128)}, u32[]{:S(2)}) copy-start(f32[104,128]{1,0:T(8,128)} %constant.14.clone.lj_ref) | copy-start | bytes 159748
  3.7 16.0 %copy-start.1 = (bf16[224,208]{1,0:T(8,128)(2,1)S(1)}, bf16[224,208]{1,0:T(8,128)(2,1)}, u32[]{:S(2)}) copy-start(bf16[224,208]{1,0:T(8,128)(2,1)} %constant.13.clone.a2_ref) | copy-start | bytes 279556
  3.7 5.0 %collective-permute-start = (f32[17,8,128]{2,1,0:T(8,128)S(1)}, f32[17,8,128]{2,1,0:T(8,128)S(1)}, u32[]{:S(2)}, u32[]{:S(2)}) collective-permute-start(f32[17,8,128]{2,1,0:T(8,128)S(1)} %get-tuple-element.27), channel_id=1, source_target_pairs={{0,32},{32,64},{64,96},{96,128},{128,160},{160,192},{192,224},{224... | collective-permute-start | bytes 208904 | tf_op jit(solution)/shard_map/ppermute | solution.py:430
  3.7 4.9 %collective-permute-start.1 = (f32[17,8,128]{2,1,0:T(8,128)S(1)}, f32[17,8,128]{2,1,0:T(8,128)S(1)}, u32[]{:S(2)}, u32[]{:S(2)}) collective-permute-start(f32[17,8,128]{2,1,0:T(8,128)S(1)} %get-tuple-element.28), channel_id=1, source_target_pairs={{0,224},{32,0},{64,32},{96,64},{128,96},{160,128},{192,160},{224,1... | collective-permute-start | bytes 208904 | tf_op jit(solution)/shard_map/ppermute | solution.py:430
  8.6 11.0 %copy-start.2 = (bf16[208,224]{1,0:T(8,128)(2,1)S(1)}, bf16[208,224]{1,0:T(8,128)(2,1)}, u32[]{:S(2)}) copy-start(bf16[208,224]{1,0:T(8,128)(2,1)} %constant.12.clone.a1_ref) | copy-start | bytes 279556
  8.7 4.2 %collective-permute-start.3 = (f32[13,8,128]{2,1,0:T(8,128)S(1)}, f32[13,8,128]{2,1,0:T(8,128)S(1)}, u32[]{:S(2)}, u32[]{:S(2)}) collective-permute-start(f32[13,8,128]{2,1,0:T(8,128)S(1)} %get-tuple-element.49), channel_id=1, source_target_pairs={{0,31},{1,0},{2,1},{3,2},{4,3},{5,4},{6,5},{7,6},{8,7},{9,8},{10,9... | collective-permute-start | bytes 159752 | tf_op jit(solution)/shard_map/ppermute | solution.py:430
  10.9 8.7 %collective-permute-start.2 = (f32[13,8,128]{2,1,0:T(8,128)S(1)}, f32[13,8,128]{2,1,0:T(8,128)S(1)}, u32[]{:S(2)}, u32[]{:S(2)}) collective-permute-start(f32[13,8,128]{2,1,0:T(8,128)S(1)} %get-tuple-element.50), channel_id=1, source_target_pairs={{0,1},{1,2},{2,3},{3,4},{4,5},{5,6},{6,7},{7,8},{8,9},{9,10},{10,1... | collective-permute-start | bytes 159752 | tf_op jit(solution)/shard_map/ppermute | solution.py:430
  21.9 6.6 %collective-permute-start.4 = (f32[3,18,8,128]{3,2,1,0:T(8,128)S(1)}, f32[3,18,8,128]{3,2,1,0:T(8,128)S(1)}, u32[]{:S(2)}, u32[]{:S(2)}) collective-permute-start(f32[3,18,8,128]{3,2,1,0:T(8,128)S(1)} %get-tuple-element.31), channel_id=1, source_target_pairs={{0,32},{32,64},{64,96},{96,128},{128,160},{160,192},{192,224},{224... | collective-permute-start | bytes 663560 | tf_op jit(solution)/shard_map/ppermute | solution.py:430
  21.9 6.6 %collective-permute-start.5 = (f32[3,18,8,128]{3,2,1,0:T(8,128)S(1)}, f32[3,18,8,128]{3,2,1,0:T(8,128)S(1)}, u32[]{:S(2)}, u32[]{:S(2)}) collective-permute-start(f32[3,18,8,128]{3,2,1,0:T(8,128)S(1)} %get-tuple-element.32), channel_id=1, source_target_pairs={{0,224},{32,0},{64,32},{96,64},{128,96},{160,128},{192,160},{224,1... | collective-permute-start | bytes 663560 | tf_op jit(solution)/shard_map/ppermute | solution.py:430
  28.5 9.2 %collective-permute-start.6 = (f32[12,3,8,128]{3,2,1,0:T(8,128)S(1)}, f32[12,3,8,128]{3,2,1,0:T(8,128)S(1)}, u32[]{:S(2)}, u32[]{:S(2)}) collective-permute-start(f32[12,3,8,128]{3,2,1,0:T(8,128)S(1)} %get-tuple-element.35), channel_id=1, source_target_pairs={{0,1},{1,2},{2,3},{3,4},{4,5},{5,6},{6,7},{7,8},{8,9},{9,10},{10,1... | collective-permute-start | bytes 442376 | tf_op jit(solution)/shard_map/ppermute | solution.py:430
  28.6 9.1 %collective-permute-start.7 = (f32[12,3,8,128]{3,2,1,0:T(8,128)S(1)}, f32[12,3,8,128]{3,2,1,0:T(8,128)S(1)}, u32[]{:S(2)}, u32[]{:S(2)}) collective-permute-start(f32[12,3,8,128]{3,2,1,0:T(8,128)S(1)} %get-tuple-element.36), channel_id=1, source_target_pairs={{0,31},{1,0},{2,1},{3,2},{4,3},{5,4},{6,5},{7,6},{8,7},{9,8},{10,9... | collective-permute-start | bytes 442376 | tf_op jit(solution)/shard_map/ppermute | solution.py:430
  40.7 5.8 %collective-permute-start.8 = (f32[2,18,8,128]{3,2,1,0:T(8,128)S(1)}, f32[2,18,8,128]{3,2,1,0:T(8,128)S(1)}, u32[]{:S(2)}, u32[]{:S(2)}) collective-permute-start(f32[2,18,8,128]{3,2,1,0:T(8,128)S(1)} %get-tuple-element.38), channel_id=1, source_target_pairs={{0,32},{32,64},{64,96},{96,128},{128,160},{160,192},{192,224},{224... | collective-permute-start | bytes 442376 | tf_op jit(solution)/shard_map/ppermute | solution.py:430
  40.8 5.8 %collective-permute-start.9 = (f32[2,18,8,128]{3,2,1,0:T(8,128)S(1)}, f32[2,18,8,128]{3,2,1,0:T(8,128)S(1)}, u32[]{:S(2)}, u32[]{:S(2)}) collective-permute-start(f32[2,18,8,128]{3,2,1,0:T(8,128)S(1)} %get-tuple-element.39), channel_id=1, source_target_pairs={{0,224},{32,0},{64,32},{96,64},{128,96},{160,128},{192,160},{224,1... | collective-permute-start | bytes 442376 | tf_op jit(solution)/shard_map/ppermute | solution.py:430
  46.5 7.6 %copy-start.5 = (bf16[16,512]{1,0:T(8,128)(2,1)S(1)}, bf16[16,512]{1,0:T(8,128)(2,1)}, u32[]{:S(2)}) copy-start(bf16[16,512]{1,0:T(8,128)(2,1)} %constant.16.clone.wm_ref) | copy-start | bytes 49156
  46.6 7.6 %collective-permute-start.10 = (f32[10,2,8,128]{3,2,1,0:T(8,128)S(1)}, f32[10,2,8,128]{3,2,1,0:T(8,128)S(1)}, u32[]{:S(2)}, u32[]{:S(2)}) collective-permute-start(f32[10,2,8,128]{3,2,1,0:T(8,128)S(1)} %get-tuple-element.42), channel_id=1, source_target_pairs={{0,1},{1,2},{2,3},{3,4},{4,5},{5,6},{6,7},{7,8},{8,9},{9,10},{10,1... | collective-permute-start | bytes 245768 | tf_op jit(solution)/shard_map/ppermute | solution.py:430
  46.6 7.5 %collective-permute-start.11 = (f32[10,2,8,128]{3,2,1,0:T(8,128)S(1)}, f32[10,2,8,128]{3,2,1,0:T(8,128)S(1)}, u32[]{:S(2)}, u32[]{:S(2)}) collective-permute-start(f32[10,2,8,128]{3,2,1,0:T(8,128)S(1)} %get-tuple-element.43), channel_id=1, source_target_pairs={{0,31},{1,0},{2,1},{3,2},{4,3},{5,4},{6,5},{7,6},{8,7},{9,8},{10,9... | collective-permute-start | bytes 245768 | tf_op jit(solution)/shard_map/ppermute | solution.py:430
  54.1 0.7 copy-start.9

commit v2 on v1

--- a/solution.py
+++ b/solution.py
@@ -90,19 +90,46 @@
     return jnp.where(p == slot_row, 1.0, 0.0).astype(BF16)
 
 
-def place_kernel(rhs_ref, stretch_ref, mass_ref, slot_ref, src_ref, coef_ref, lo_ref, hi_ref):
+def place_kernel(
+    rhs_hbm, stretch_hbm, mass_hbm, slot_hbm, group_hbm,
+    src_ref, coef_ref, to_down_ref, to_up_ref, slot_ref, group_ref,
+    rhs_ref, stretch_ref, mass_ref, sems,
+):
+    small = [
+        pltpu.make_async_copy(h, v, sems.at[8 + k])
+        for k, (h, v) in enumerate(
+            (
+                (slot_hbm, slot_ref),
+                (stretch_hbm, stretch_ref),
+                (mass_hbm, mass_ref),
+                (group_hbm, group_ref),
+            )
+        )
+    ]
+    big = [
+        pltpu.make_async_copy(
+            rhs_hbm.at[pl.ds(x * 64, 64), :], rhs_ref.at[pl.ds(x * 64, 64), :], sems.at[x]
+        )
+        for x in range(8)
+    ]
+    for c in small + big:
+        c.start()
+    small[0].wait()
     oh = onehot(slot_ref[...])
+    small[1].wait()
+    small[2].wait()
     c = jnp.concatenate([stretch_ref[...], mass_ref[...], jnp.zeros((4, 256), F32)], 0)
-    c1, rest = split(c)
+    c1 = c.astype(BF16)
     r1 = c - c1.astype(F32)
     c2 = r1.astype(BF16)
     c3 = (r1 - c2.astype(F32)).astype(BF16)
     cg = dot_t(c1, oh) + dot_t(c2, oh) + dot_t(c3, oh)
     coef = jnp.concatenate([cg[0:4, :LANES], cg[0:4, LANES:]], 0)
     coef_ref[...] = coef
-    lo_ref[16] = coef
-    hi_ref[16] = coef
+    to_down_ref[8] = coef
+    to_up_ref[8] = coef
     for x in range(8):
+        big[x].wait()
         a = rhs_ref[x * 64 : (x + 1) * 64, :]
         a1 = a.astype(BF16)
         e = a - a1.astype(F32)
@@ -113,10 +140,21 @@
         for b in range(2):
             block = g[:, b * LANES : (b + 1) * LANES].reshape(8, 8, LANES)
             src_ref[x, b * 8 : b * 8 + 8] = block
-            if x == 0:
-                lo_ref[b * 8 : b * 8 + 8] = block
-            if x == 7:
-                hi_ref[b * 8 : b * 8 + 8] = block
+            if b == 0:
+                to_down_ref[x] = block[0]
+            else:
+                to_up_ref[x] = block[7]
+    small[3].wait()
+
+
+def rim_kernel(src_ref, coef_ref, yd_ref, yu_ref, to_left_ref, to_right_ref):
+    coef_y = jnp.concatenate([yd_ref[8, 4:8, :], yu_ref[8, 0:4, :]], 0)
+    for x, out in ((0, to_left_ref), (7, to_right_ref)):
+        out[0] = yd_ref[x]
+        out[1:17] = src_ref[x]
+        out[17] = yu_ref[x]
+        out[18] = coef_ref[...]
+        out[19] = coef_y
 
 
 def block_solves(rext, coef_ref, a1_ref, a2_ref, lj_ref, lk_ref, spec, wout):
@@ -207,54 +245,49 @@
     return ref[at : at + n * 8, :].reshape(n, 8, LANES)
 
 
+def with_rows(line, n, d, u, down, up):
+    rows_d = d * down
+    rows_u = u * up
+    low = rows_d[n - 2 : n] + jnp.concatenate([line[0:1] * down, line[1:2]], 0)
+    high = rows_u[0:2] + jnp.concatenate([line[16:17], line[17:18] * up], 0)
+    parts = [low, line[2:16], high]
+    if n > 2:
+        parts = [rows_d[0 : n - 2]] + parts + [rows_u[2:n]]
+    return jnp.concatenate(parts, 0)
+
+
 def first_kernel(
     src_ref, coef_ref, xl_ref, xr_ref, yd_ref, yu_ref, a1_ref, a2_ref, lj_ref, lk_ref,
-    rext_ref, w_ref, to_left_ref, to_right_ref, to_down_ref, to_up_ref, spec, wout,
+    rext_ref, w_ref, to_down_ref, to_up_ref, spec, wout,
 ):
     left, right, down, up = flags()
     zero = jnp.zeros((6, 8, LANES), F32)
     for p in range(10):
-        side = {0: left, 9: right}.get(p)
-        if p == 0:
-            line = xl_ref[0:16] * left
-        elif p == 9:
-            line = xr_ref[0:16] * right
+        if p in (0, 9):
+            x_ref, side = (xl_ref, left) if p == 0 else (xr_ref, right)
+            put(rext_ref, p, 0, x_ref[0:1] * (side * down))
+            put(rext_ref, p, 1, x_ref[1:17] * side)
+            put(rext_ref, p, 17, x_ref[17:18] * (side * up))
         else:
-            line = src_ref[p - 1]
-        fd = down if side is None else down * side
-        fu = up if side is None else up * side
-        put(rext_ref, p, 0, yd_ref[p : p + 1] * fd)
-        put(rext_ref, p, 1, line)
-        put(rext_ref, p, 17, yu_ref[p : p + 1] * fu)
+            put(rext_ref, p, 0, yd_ref[p - 1 : p] * down)
+            put(rext_ref, p, 1, src_ref[p - 1])
+            put(rext_ref, p, 17, yu_ref[p - 1 : p] * up)
         put(rext_ref, p, 18, zero)
     block_solves(rext_ref, coef_ref, a1_ref, a2_ref, lj_ref, lk_ref, spec, wout)
-    empty = jnp.zeros((3, 8, LANES), F32)
-    to_up_ref[0] = empty
-    to_up_ref[11] = empty
-    to_down_ref[0] = empty
-    to_down_ref[11] = empty
     for p in range(10):
         line = get(wout, p, 0, 18)
         w_ref[p] = line
-        if p < 3:
-            to_left_ref[p] = line
-        if p > 6:
-            to_right_ref[p - 7] = line
-        side = {0: left, 9: right}.get(p)
-        if side is not None:
-            line = line * side
-        to_down_ref[p + 1] = line[0:3]
-        to_up_ref[p + 1] = line[15:18]
-
-
-def edge_kernel(own_dn_ref, own_up_ref, l_ref, r_ref, dn_ref, up_ref):
-    left, right, _, _ = flags()
-    n = l_ref.shape[0]
-    m = own_dn_ref.shape[0]
-    for own, y, out in ((own_dn_ref, 0, dn_ref), (own_up_ref, 18 - n, up_ref)):
-        out[0:n] = own[0:n] + l_ref[:, y : y + n] * left
-        out[n : m - n] = own[n : m - n]
-        out[m - n :] = own[m - n :] + r_ref[:, y : y + n] * right
+        to_down_ref[p] = line[0:3]
+        to_up_ref[p] = line[15:18]
+
+
+def edge_kernel(w_ref, d_ref, u_ref, to_left_ref, to_right_ref):
+    _, _, down, up = flags()
+    n = d_ref.shape[1]
+    for k in range(n):
+        for p, out in ((k, to_left_ref), (10 - n + k, to_right_ref)):
+            at = p if w_ref.shape[0] == 10 or p < n else p - 10 + 2 * n
+            out[k] = with_rows(w_ref[at], n, d_ref[p], u_ref[p], down, up)
 
 
 def neighbours_z(u):
@@ -269,43 +302,38 @@
 def second_kernel(
     rext_ref, coef_ref, xl_ref, xr_ref, yd_ref, yu_ref, w_ref, l_ref, r_ref, d_ref, u_ref,
     a1_ref, a2_ref, lj_ref, lk_ref,
-    c_ref, to_left_ref, to_right_ref, to_down_ref, to_up_ref, h, cb, r1, spec, wout,
+    c_ref, edge_ref, to_down_ref, to_up_ref, h, cb, r1, spec, wout,
 ):
     left, right, down, up = flags()
     for x in range(12):
         if x == 0:
             g = l_ref[0] * left
-        elif x == 1:
-            g = (l_ref[1] + w_ref[0]) * left
-        elif x == 2:
-            g = l_ref[2] * left + w_ref[1]
-        elif x == 9:
-            g = w_ref[8] + r_ref[0] * right
-        elif x == 10:
-            g = (w_ref[9] + r_ref[1]) * right
         elif x == 11:
             g = r_ref[2] * right
         else:
-            g = w_ref[x - 1]
-        d = d_ref[x] * down
-        u = u_ref[x] * up
-        h[x, 0] = d[0]
-        h[x, 1] = g[0] * down + d[1]
-        h[x, 2] = g[1] + d[2]
-        h[x, 3:17] = g[2:16]
-        h[x, 17] = g[16] + u[0]
-        h[x, 18] = g[17] * up + u[1]
-        h[x, 19] = u[2]
-    for a, own in ((0, xl_ref), (1, None), (2, xr_ref)):
+            g = with_rows(w_ref[x - 1], 3, d_ref[x - 1], u_ref[x - 1], down, up)
+            if x == 1:
+                g = (g + l_ref[1]) * left
+            elif x == 2:
+                g = g + l_ref[2] * left
+            elif x == 9:
+                g = g + r_ref[0] * right
+            elif x == 10:
+                g = (g + r_ref[1]) * right
+        h[x] = g
+    for a, x_ref in ((0, xl_ref), (1, None), (2, xr_ref)):
         for b in range(4):
             for k in range(4):
-                if b == 0:
-                    row = yd_ref[10 + a, 4 + k : 5 + k, :]
-                elif b == 3:
-                    row = yu_ref[10 + a, k : k + 1, :]
+                if b == 1 or b == 2:
+                    at = (b - 1) * 4 + k
+                    row = coef_ref[at : at + 1, :] if x_ref is None else x_ref[18, at : at + 1, :]
+                elif x_ref is not None:
+                    at = k if b == 0 else 4 + k
+                    row = x_ref[19, at : at + 1, :]
+                elif b == 0:
+                    row = yd_ref[8, 4 + k : 5 + k, :]
                 else:
-                    at = (b - 1) * 4 + k
-                    row = coef_ref[at : at + 1, :] if own is None else own[16, at : at + 1, :]
+                    row = yu_ref[8, k : k + 1, :]
                 cb[a, b, k] = jnp.broadcast_to(row, (8, LANES))
     zero = jnp.zeros((6, 8, LANES), F32)
     for p in range(10):
@@ -335,23 +363,20 @@
         line = get(wout, p, 0, 18)
         c_ref[p] = h[p + 1, 1:19] + line
         if p < 2:
-            to_left_ref[p] = line
+            edge_ref[p] = line
         if p > 7:
-            to_right_ref[p - 8] = line
-        side = {0: left, 9: right}.get(p)
-        if side is not None:
-            line = line * side
+            edge_ref[p - 6] = line
         to_down_ref[p] = line[0:2]
         to_up_ref[p] = line[16:18]
 
 
 def last_kernel(
     src_ref, coef_ref, c_ref, l_ref, r_ref, d_ref, u_ref, slot_ref, group_ref, wm_ref,
-    smooth_ref, res_ref, part_ref, h, mu, mr,
+    smooth_hbm, res_hbm, part_ref, h, mu, mr, smooth_ref, res_ref, sems,
 ):
     left, right, down, up = flags()
     for p in range(10):
-        g = c_ref[p]
+        g = with_rows(c_ref[p], 2, d_ref[p], u_ref[p], down, up)
         if p == 0:
             g = (g + l_ref[0]) * left
         elif p == 1:
@@ -360,13 +385,7 @@
             g = g + r_ref[0] * right
         elif p == 9:
             g = (g + r_ref[1]) * right
-        d = d_ref[p] * down
-        u = u_ref[p] * up
-        h[p, 0] = g[0] * down + d[0]
-        h[p, 1] = g[1] + d[1]
-        h[p, 2:16] = g[2:16]
-        h[p, 16] = g[16] + u[0]
-        h[p, 17] = g[17] * up + u[1]
+        h[p] = g
     for b in range(2):
         lanes = slice(b * LANES, (b + 1) * LANES)
         cf = [
@@ -390,6 +409,7 @@
                 mr[at : at + 32, lanes] = res.reshape(32, LANES)
     oh = onehot(slot_ref[...])
     mom = jnp.zeros((16, 256), F32)
+    copies = []
     for x in range(8):
         at = slice(x * 64, x * 64 + 64)
         uh, ul = split(mu[at, :])
@@ -397,6 +417,10 @@
         o = dot(jnp.concatenate([uh, ul, rh, rl], 0), oh)
         smooth_ref[at, :] = o[0:64] + o[64:128]
         res_ref[at, :] = o[128:192] + o[192:256]
+        for k, (v, hbm) in enumerate(((smooth_ref, smooth_hbm), (res_ref, res_hbm))):
+            at = pl.ds(x * 64, 64)
+            copies.append(pltpu.make_async_copy(v.at[at, :], hbm.at[at, :], sems.at[2 * x + k]))
+            copies[-1].start()
     for x in range(4):
         at = slice(x * 128, x * 128 + 128)
         rh, rl = split(mr[at, :])
@@ -415,6 +439,8 @@
     )
     sh, sl = split(spread)
     part_ref[...] = dot_t(pick, sh) + dot_t(pick, sl)
+    for c in copies:
+        c.wait()
 
 
 def sd(*shape):
@@ -430,30 +456,24 @@
     return lax.ppermute(value, axis, [(i, (i + by) % n) for i in range(n)])
 
 
-def mark(args):
-    return [a if isinstance(a, tuple) else (a, False) for a in args]
-
-
-def call(kernel, outs, scratch=(), **kw):
+def call(kernel, outs, args, scratch=(), hbm_in=0, hbm_out=0, sems=0):
     vmem = pl.BlockSpec(memory_space=pltpu.VMEM)
-
-    def run(*args):
-        args = [a if at_home else pltpu.with_memory_space_constraint(a, pltpu.VMEM) for a, at_home in mark(args)]
-        return pl.pallas_call(
-            kernel,
-            out_shape=outs,
-            in_specs=[vmem] * len(args),
-            out_specs=[vmem] * len(outs),
-            scratch_shapes=[pltpu.VMEM(s, F32) for s in scratch],
-            compiler_params=pltpu.CompilerParams(vmem_limit_bytes=16 << 20),
-            **kw,
-        )(*args)
-
-    return run
-
-
-def edges(own_dn, own_up, from_left, from_right):
-    return call(edge_kernel, [vm(*own_dn.shape)] * 2)(own_dn, own_up, from_left, from_right)
+    hbm = pl.BlockSpec(memory_space=pl.ANY)
+    args = [
+        a if k < hbm_in else pltpu.with_memory_space_constraint(a, pltpu.VMEM)
+        for k, a in enumerate(args)
+    ]
+    scratch = [pltpu.VMEM(s, F32) for s in scratch]
+    if sems:
+        scratch.append(pltpu.SemaphoreType.DMA((sems,)))
+    return pl.pallas_call(
+        kernel,
+        out_shape=outs,
+        in_specs=[hbm if k < hbm_in else vmem for k in range(len(args))],
+        out_specs=[hbm if k < hbm_out else vmem for k in range(len(outs))],
+        scratch_shapes=scratch,
+        compiler_params=pltpu.CompilerParams(vmem_limit_bytes=16 << 20),
+    )(*args)
 
 
 def on_device(right_side, stretch, mass_term, slot_position, coarse_group):
@@ -462,50 +482,62 @@
     lj = jnp.asarray(LAM_J, F32)
     lk = jnp.asarray(LAM_K, F32)
     wm = jnp.asarray(W_MOM, BF16)
-    slot = slot_position.reshape(1, 256)
-    src, coef, lo, hi = call(
-        place_kernel, [vm(8, 16, 8, LANES), vm(8, LANES), vm(17, 8, LANES), vm(17, 8, LANES)]
-    )((right_side.reshape(512, 256), True), (stretch, True), (mass_term.reshape(1, 256), True), (slot, True))
-    xl = ring(hi, "sx", 1)
-    xr = ring(lo, "sx", -1)
-    c3 = coef[None]
-    to_up = jnp.concatenate([xl[15:16], src[:, 15], xr[15:16], xl[16:17], c3, xr[16:17]], 0)
-    to_dn = jnp.concatenate([xl[0:1], src[:, 0], xr[0:1], xl[16:17], c3, xr[16:17]], 0)
-    yd = ring(to_up, "sy", 1)
-    yu = ring(to_dn, "sy", -1)
-
-    slab = vm(3, 18, 8, LANES)
-    side = vm(12, 3, 8, LANES)
-    rext, w, to_l, to_r, to_d, to_u = call(
+    row = pltpu.VMEM((1, 256), jnp.int32)
+    src, coef, to_d, to_u, slot, group = call(
+        place_kernel,
+        [vm(8, 16, 8, LANES), vm(8, LANES), vm(9, 8, LANES), vm(9, 8, LANES), row, row],
+        (
+            right_side.reshape(512, 256),
+            stretch,
+            mass_term.reshape(1, 256),
+            slot_position.reshape(1, 256),
+            coarse_group.reshape(1, 256),
+        ),
+        [(512, 256), (3, 256), (1, 256)],
+        hbm_in=5,
+        sems=12,
+    )
+    yd = ring(to_u, "sy", 1)
+    yu = ring(to_d, "sy", -1)
+    to_l, to_r = call(rim_kernel, [vm(20, 8, LANES)] * 2, (src, coef, yd, yu))
+    xl = ring(to_r, "sx", 1)
+    xr = ring(to_l, "sx", -1)
+
+    side = vm(10, 3, 8, LANES)
+    rext, w, to_d, to_u = call(
         first_kernel,
-        [vm(1920, LANES), vm(10, 18, 8, LANES), slab, slab, side, side],
+        [vm(1920, LANES), vm(10, 18, 8, LANES), side, side],
+        (src, coef, xl, xr, yd, yu, a1, a2, lj, lk),
         [(10, 104, 256), (1920, LANES)],
-    )(src, coef, xl, xr, yd, yu, a1, a2, lj, lk)
-    fl = ring(to_r, "sx", 1)
-    fr = ring(to_l, "sx", -1)
-    to_d, to_u = edges(to_d, to_u, fl, fr)
-    fd = ring(to_u, "sy", 1)
-    fu = ring(to_d, "sy", -1)
-
-    slab = vm(2, 18, 8, LANES)
+    )
+    d = ring(to_u, "sy", 1)
+    u = ring(to_d, "sy", -1)
+    to_l, to_r = call(edge_kernel, [vm(3, 20, 8, LANES)] * 2, (w, d, u))
+    l = ring(to_r, "sx", 1)
+    r = ring(to_l, "sx", -1)
+
     side = vm(10, 2, 8, LANES)
-    c, to_l, to_r, to_d, to_u = call(
+    c, w, to_d, to_u = call(
         second_kernel,
-        [vm(10, 18, 8, LANES), slab, slab, side, side],
+        [vm(10, 18, 8, LANES), vm(4, 18, 8, LANES), side, side],
+        (rext, coef, xl, xr, yd, yu, w, l, r, d, u, a1, a2, lj, lk),
         [(12, 20, 8, LANES), (3, 4, 4, 8, LANES), (1920, LANES), (10, 104, 256), (1920, LANES)],
-    )(rext, coef, xl, xr, yd, yu, w, fl, fr, fd, fu, a1, a2, lj, lk)
-    fl = ring(to_r, "sx", 1)
-    fr = ring(to_l, "sx", -1)
-    to_d, to_u = edges(to_d, to_u, fl, fr)
-    fd = ring(to_u, "sy", 1)
-    fu = ring(to_d, "sy", -1)
+    )
+    d = ring(to_u, "sy", 1)
+    u = ring(to_d, "sy", -1)
+    to_l, to_r = call(edge_kernel, [vm(2, 18, 8, LANES)] * 2, (w, d, u))
+    l = ring(to_r, "sx", 1)
+    r = ring(to_l, "sx", -1)
 
     ny = lax.axis_size("sy")
     smooth, res, part = call(
         last_kernel,
         [sd(512, 256), sd(512, 256), vm(ny, LANES)],
-        [(10, 18, 8, LANES), (512, 256), (512, 256)],
-    )(src, coef, c, fl, fr, fd, fu, (slot, True), (coarse_group.reshape(1, 256), True), wm)
+        (src, coef, c, l, r, d, u, slot, group, wm),
+        [(10, 18, 8, LANES)] + [(512, 256)] * 4,
+        hbm_out=2,
+        sems=16,
+    )
     arrived = lax.all_to_all(part, "sy", split_axis=0, concat_axis=0, tiled=True)
     coarse = arrived.sum(axis=0).reshape(8, GRP_DEV)
     return smooth.reshape(8, 8, 8, 256), res.reshape(8, 8, 8, 256), coarse

time: 78 us -> 75.9 us (0.973)
  waiting for transfers between devices: 23.1 us -> 18.2 us
  Pallas kernels: 7.68 us -> 9.88 us
  blocking collectives: 20.5 us -> 21.9 us
  local copies, waits for them, and re-layouts: 3.79 us -> 2.43 us
    ppermute x12, waiting for transfers between devices: 23.1 us -> 18.2 us  [ring(): return lax.ppermute(value, axis, [(i, (i + by) % n) for i in range(n)])]
    pallas_call x6 -> x7, Pallas kernels: 7.68 us -> 9.88 us  [call(): pl.pallas_call(kernel, out_shape=outs, in_specs=[hbm if k < hbm_in else v...]
    all_to_all x1, blocking collectives: 20.5 us -> 21.9 us  [on_device(): lax.all_to_all(part, 'sy', split_axis=0, concat_axis=0, tiled=True)]
    unnamed x25 -> x20, local copies, waits for them, and re-layouts: 3.11 us -> 1.75 us
where the time goes in v2:
time: 75.9 us; the launch traced here: 75.4 us
  starting transfers between devices  22.1 us (29%)
  blocking collectives  21.9 us (29%)
  waiting for transfers between devices  18.2 us (24%)
  Pallas kernels  9.88 us (13%)
  local copies, waits for them, and re-layouts  2.43 us (3%)
  between operations  0.77 us (1%)
    ppermute x12, starting transfers between devices, ring(): return lax.ppermute(value, axis, [(i, (i + by) % n) for i in range(n)])  22.1 us
    all_to_all x1, blocking collectives, on_device(): lax.all_to_all(part, 'sy', split_axis=0, concat_axis=0, tiled=True)  21.9 us
    ppermute x12, waiting for transfers between devices, ring(): return lax.ppermute(value, axis, [(i, (i + by) % n) for i in range(n)])  18.2 us
    pallas_call x7, Pallas kernels, call(): pl.pallas_call(kernel, out_shape=outs, in_specs=[hbm if k < hbm_in else v...  9.88 us
    unnamed x20, local copies, waits for them, and re-layouts  1.75 us
  transfers between devices with their start and end apart: 12, of which 7 were waited for; matrix products, arithmetic and copies ran while one was open for 0% of the time, Pallas kernels for 0%

profile of v2, /device:TPU:8, one launch (start us, length us, event | category | flops | bytes accessed | tf_op | source)
XLA Modules:
  0.0 75.4 jit_solution(5033010760644033379)
XLA Ops:
  0.6 0.0 copy-start.6
  0.6 0.0 copy-start.8
  0.7 0.0 copy-start.9
  0.7 0.0 copy-start.7
  0.7 0.6 copy-done.6
  1.3 0.0 copy-done.8
  1.3 0.0 copy-done.9
  1.3 0.0 copy-done.7
  1.4 0.0 copy-start
  1.4 1.0 %copy-done = f32[8,8,8,256]{3,2,1,0:T(8,128)S(1)} copy-done((f32[8,8,8,256]{3,2,1,0:T(8,128)S(1)}, f32[8,8,8,256]{3,2,1,0:T(8,128)}, u32[]{:S(2)}) %copy-start) | copy-done | bytes 524312
  2.4 3.0 %shard_map.121 = (f32[8,16,8,128]{3,2,1,0:T(8,128)S(1)}, f32[8,128]{1,0:T(8,128)S(1)}, f32[9,8,128]{2,1,0:T(8,128)S(1)}, f32[9,8,128]{2,1,0:T(8,128)S(1)}, s32[1,256]{1,0:T(1,128)S(1)}, /*index=5*/s32[1,256]{1,0:T(1,128)S(1)}) custom-call(f32[512,256]{1,0:T(8,128)S(1)} %bitcast.9, f32[3,256]{1,0:T(4,128)S(1)} %copy-done.6, f32[1,256]{1,0:T(1,128)S(1)} %bitcast.11, ...), custom_call_target="tpu_custom_call" | custom-call | tf_op jit(solution)/shard_map/pallas_call | solution.py:469
  5.4 1.7 %collective-permute-start = (f32[9,8,128]{2,1,0:T(8,128)S(1)}, f32[9,8,128]{2,1,0:T(8,128)S(1)}, u32[]{:S(2)}, u32[]{:S(2)}) collective-permute-start(f32[9,8,128]{2,1,0:T(8,128)S(1)} %get-tuple-element.28), channel_id=1, source_target_pairs={{0,1},{1,2},{2,3},{3,4},{4,5},{5,6},{6,7},{7,8},{8,9},{9,10},{10,1... | collective-permute-start | bytes 110600 | tf_op jit(solution)/shard_map/ppermute | solution.py:456
  7.0 0.7 collective-permute-start.1
  7.7 1.8 %collective-permute-done.yd_ref = f32[9,8,128]{2,1,0:T(8,128)S(1)} collective-permute-done((f32[9,8,128]{2,1,0:T(8,128)S(1)}, f32[9,8,128]{2,1,0:T(8,128)S(1)}, u32[]{:S(2)}, u32[]{:S(2)}) %collective-permute-start) | collective-permute-done | bytes 36896 | tf_op jit(solution)/shard_map/ppermute | solution.py:456
  9.6 1.4 %collective-permute-done.1.yu_ref = f32[9,8,128]{2,1,0:T(8,128)S(1)} collective-permute-done((f32[9,8,128]{2,1,0:T(8,128)S(1)}, f32[9,8,128]{2,1,0:T(8,128)S(1)}, u32[]{:S(2)}, u32[]{:S(2)}) %collective-permute-start.1) | collective-permute-done | bytes 36896 | tf_op jit(solution)/shard_map/ppermute | solution.py:456
  11.0 0.0 copy-start.1
  11.0 0.0 copy-start.2
  11.0 0.0 collective-permute-start.2
  11.0 2.9 %collective-permute-start.3 = (f32[20,8,128]{2,1,0:T(8,128)S(1)}, f32[20,8,128]{2,1,0:T(8,128)S(1)}, u32[]{:S(2)}, u32[]{:S(2)}) collective-permute-start(f32[20,8,128]{2,1,0:T(8,128)S(1)} %get-tuple-element.31), channel_id=1, source_target_pairs={{0,224},{32,0},{64,32},{96,64},{128,96},{160,128},{192,160},{224,1... | collective-permute-start | bytes 245768 | tf_op jit(solution)/shard_map/ppermute | solution.py:456
  14.0 2.1 %collective-permute-done.2.xl_ref = f32[20,8,128]{2,1,0:T(8,128)S(1)} collective-permute-done((f32[20,8,128]{2,1,0:T(8,128)S(1)}, f32[20,8,128]{2,1,0:T(8,128)S(1)}, u32[]{:S(2)}, u32[]{:S(2)}) %collective-permute-start.2) | collective-permute-done | bytes 81952 | tf_op jit(solution)/shard_map/ppermute | solution.py:456
  16.1 0.0 collective-permute-done.3.xr_ref
  16.1 0.0 copy-done.1
  16.1 0.0 copy-done.2
  16.1 0.0 copy-done.3
  16.1 0.0 copy-done.4
  16.1 2.2 %shard_map.123 = (f32[1920,128]{1,0:T(8,128)S(1)}, f32[10,18,8,128]{3,2,1,0:T(8,128)S(1)}, f32[10,3,8,128]{3,2,1,0:T(8,128)S(1)}, f32[10,3,8,128]{3,2,1,0:T(8,128)S(1)}) custom-call(f32[8,16,8,128]{3,2,1,0:T(8,128)S(1)} %get-tuple-element.26.src_ref, f32[8,128]{1,0:T(8,128)S(1)} %get-tuple-element.27.coef_ref, ...), custom_call_target="tpu_custom_call" | custom-call | tf_op jit(solution)/shard_map/pallas_call | solution.py:469
  18.3 1.4 %collective-permute-start.4 = (f32[10,3,8,128]{3,2,1,0:T(8,128)S(1)}, f32[10,3,8,128]{3,2,1,0:T(8,128)S(1)}, u32[]{:S(2)}, u32[]{:S(2)}) collective-permute-start(f32[10,3,8,128]{3,2,1,0:T(8,128)S(1)} %get-tuple-element.34), channel_id=1, source_target_pairs={{0,1},{1,2},{2,3},{3,4},{4,5},{5,6},{6,7},{7,8},{8,9},{9,10},{10,1... | collective-permute-start | bytes 368648 | tf_op jit(solution)/shard_map/ppermute | solution.py:456
  19.7 4.0 %collective-permute-start.5 = (f32[10,3,8,128]{3,2,1,0:T(8,128)S(1)}, f32[10,3,8,128]{3,2,1,0:T(8,128)S(1)}, u32[]{:S(2)}, u32[]{:S(2)}) collective-permute-start(f32[10,3,8,128]{3,2,1,0:T(8,128)S(1)} %get-tuple-element.35), channel_id=1, source_target_pairs={{0,31},{1,0},{2,1},{3,2},{4,3},{5,4},{6,5},{7,6},{8,7},{9,8},{10,9... | collective-permute-start | bytes 368648 | tf_op jit(solution)/shard_map/ppermute | solution.py:456
  23.7 3.8 %collective-permute-done.4.d_ref = f32[10,3,8,128]{3,2,1,0:T(8,128)S(1)} collective-permute-done((f32[10,3,8,128]{3,2,1,0:T(8,128)S(1)}, f32[10,3,8,128]{3,2,1,0:T(8,128)S(1)}, u32[]{:S(2)}, u32[]{:S(2)}) %collective-permute-start.4) | collective-permute-done | bytes 122912 | tf_op jit(solution)/shard_map/ppermute | solution.py:456
  27.4 0.0 collective-permute-done.5.u_ref
  27.5 0.0 collective-permute-start.6
  27.5 2.9 %collective-permute-start.7 = (f32[3,20,8,128]{3,2,1,0:T(8,128)S(1)}, f32[3,20,8,128]{3,2,1,0:T(8,128)S(1)}, u32[]{:S(2)}, u32[]{:S(2)}) collective-permute-start(f32[3,20,8,128]{3,2,1,0:T(8,128)S(1)} %get-tuple-element.37), channel_id=1, source_target_pairs={{0,224},{32,0},{64,32},{96,64},{128,96},{160,128},{192,160},{224,1... | collective-permute-start | bytes 737288 | tf_op jit(solution)/shard_map/ppermute | solution.py:456
  30.5 3.9 %collective-permute-done.6.l_ref = f32[3,20,8,128]{3,2,1,0:T(8,128)S(1)} collective-permute-done((f32[3,20,8,128]{3,2,1,0:T(8,128)S(1)}, f32[3,20,8,128]{3,2,1,0:T(8,128)S(1)}, u32[]{:S(2)}, u32[]{:S(2)}) %collective-permute-start.6) | collective-permute-done | bytes 245792 | tf_op jit(solution)/shard_map/ppermute | solution.py:456
  34.3 0.0 collective-permute-done.7.r_ref
  34.3 3.0 %shard_map.125 = (f32[10,18,8,128]{3,2,1,0:T(8,128)S(1)}, f32[4,18,8,128]{3,2,1,0:T(8,128)S(1)}, f32[10,2,8,128]{3,2,1,0:T(8,128)S(1)}, f32[10,2,8,128]{3,2,1,0:T(8,128)S(1)}) custom-call(f32[1920,128]{1,0:T(8,128)S(1)} %get-tuple-element.32.rext_ref, f32[8,128]{1,0:T(8,128)S(1)} %get-tuple-element.27.coef_ref, ...), custom_call_target="tpu_custom_call" | custom-call | tf_op jit(solution)/shard_map/pallas_call | solution.py:469
  37.4 1.3 %collective-permute-start.8 = (f32[10,2,8,128]{3,2,1,0:T(8,128)S(1)}, f32[10,2,8,128]{3,2,1,0:T(8,128)S(1)}, u32[]{:S(2)}, u32[]{:S(2)}) collective-permute-start(f32[10,2,8,128]{3,2,1,0:T(8,128)S(1)} %get-tuple-element.40), channel_id=1, source_target_pairs={{0,1},{1,2},{2,3},{3,4},{4,5},{5,6},{6,7},{7,8},{8,9},{9,10},{10,1... | collective-permute-start | bytes 245768 | tf_op jit(solution)/shard_map/ppermute | solution.py:456
  38.7 4.2 %collective-permute-start.9 = (f32[10,2,8,128]{3,2,1,0:T(8,128)S(1)}, f32[10,2,8,128]{3,2,1,0:T(8,128)S(1)}, u32[]{:S(2)}, u32[]{:S(2)}) collective-permute-start(f32[10,2,8,128]{3,2,1,0:T(8,128)S(1)} %get-tuple-element.41), channel_id=1, source_target_pairs={{0,31},{1,0},{2,1},{3,2},{4,3},{5,4},{6,5},{7,6},{8,7},{9,8},{10,9... | collective-permute-start | bytes 245768 | tf_op jit(solution)/shard_map/ppermute | solution.py:456
  43.0 2.3 %collective-permute-done.8.d_ref = f32[10,2,8,128]{3,2,1,0:T(8,128)S(1)} collective-permute-done((f32[10,2,8,128]{3,2,1,0:T(8,128)S(1)}, f32[10,2,8,128]{3,2,1,0:T(8,128)S(1)}, u32[]{:S(2)}, u32[]{:S(2)}) %collective-permute-start.8) | collective-permute-done | bytes 81952 | tf_op jit(solution)/shard_map/ppermute | solution.py:456
  45.3 0.0 collective-permute-done.9.u_ref
  45.3 0.0 collective-permute-start.10
  45.4 2.9 %collective-permute-start.11 = (f32[2,18,8,128]{3,2,1,0:T(8,128)S(1)}, f32[2,18,8,128]{3,2,1,0:T(8,128)S(1)}, u32[]{:S(2)}, u32[]{:S(2)}) collective-permute-start(f32[2,18,8,128]{3,2,1,0:T(8,128)S(1)} %get-tuple-element.43), channel_id=1, source_target_pairs={{0,224},{32,0},{64,32},{96,64},{128,96},{160,128},{192,160},{224,1... | collective-permute-start | bytes 442376 | tf_op jit(solution)/shard_map/ppermute | solution.py:456
  48.3 2.8 %collective-permute-done.10.l_ref = f32[2,18,8,128]{3,2,1,0:T(8,128)S(1)} collective-permute-done((f32[2,18,8,128]{3,2,1,0:T(8,128)S(1)}, f32[2,18,8,128]{3,2,1,0:T(8,128)S(1)}, u32[]{:S(2)}, u32[]{:S(2)}) %collective-permute-start.10) | collective-permute-done | bytes 147488 | tf_op jit(solution)/shard_map/ppermute | solution.py:456
  51.1 0.0 collective-permute-done.11.r_ref
  51.1 0.0 copy-done.5
  51.1 1.6 %shard_map.127 = (f32[512,256]{1,0:T(8,128)}, f32[512,256]{1,0:T(8,128)}, f32[32,128]{1,0:T(8,128)S(1)}) custom-call(f32[8,16,8,128]{3,2,1,0:T(8,128)S(1)} %get-tuple-element.26.src_ref, f32[8,128]{1,0:T(8,128)S(1)} %get-tuple-element.27.coef_ref, f32[10,18,8,128]{3,2,1,0:T(8,128)S(1)} %get-tuple-element.38.c_ref, ...), custom_call_target="tpu_custom_call" | custom-call | tf_op jit(solution)/shard_map/pallas_call | solution.py:469
  52.8 21.9 %all_to_all.9 = f32[32,1,128]{2,1,0:T(1,128)S(1)} all-to-all(f32[32,1,128]{2,1,0:T(1,128)S(1)} %bitcast.10), channel_id=1, replica_groups=mesh['sx'=8,'sy'=32] {'sy'}, dimensions={0} | all-to-all | bytes 32768 | tf_op jit(solution)/shard_map/all_to_all | solution.py:541
  74.7 0.1 reduce_sum.9
  74.7 0.7 reshape.35
  (6 shorter events, 0.1 us)
Async XLA Ops:
  0.6 0.7 copy-start.6
  0.6 0.7 copy-start.8
  0.7 0.7 copy-start.9
  0.7 0.7 copy-start.7
  1.4 1.0 %copy-start = (f32[8,8,8,256]{3,2,1,0:T(8,128)S(1)}, f32[8,8,8,256]{3,2,1,0:T(8,128)}, u32[]{:S(2)}) copy-start(f32[8,8,8,256]{3,2,1,0:T(8,128)} %param.10) | copy-start | bytes 1572868
  5.4 4.2 %collective-permute-start = (f32[9,8,128]{2,1,0:T(8,128)S(1)}, f32[9,8,128]{2,1,0:T(8,128)S(1)}, u32[]{:S(2)}, u32[]{:S(2)}) collective-permute-start(f32[9,8,128]{2,1,0:T(8,128)S(1)} %get-tuple-element.28), channel_id=1, source_target_pairs={{0,1},{1,2},{2,3},{3,4},{4,5},{5,6},{6,7},{7,8},{8,9},{9,10},{10,1... | collective-permute-start | bytes 110600 | tf_op jit(solution)/shard_map/ppermute | solution.py:456
  7.0 4.0 %collective-permute-start.1 = (f32[9,8,128]{2,1,0:T(8,128)S(1)}, f32[9,8,128]{2,1,0:T(8,128)S(1)}, u32[]{:S(2)}, u32[]{:S(2)}) collective-permute-start(f32[9,8,128]{2,1,0:T(8,128)S(1)} %get-tuple-element.29), channel_id=1, source_target_pairs={{0,31},{1,0},{2,1},{3,2},{4,3},{5,4},{6,5},{7,6},{8,7},{9,8},{10,9... | collective-permute-start | bytes 110600 | tf_op jit(solution)/shard_map/ppermute | solution.py:456
  11.0 5.1 %copy-start.1 = (bf16[224,208]{1,0:T(8,128)(2,1)S(1)}, bf16[224,208]{1,0:T(8,128)(2,1)}, u32[]{:S(2)}) copy-start(bf16[224,208]{1,0:T(8,128)(2,1)} %constant.13.clone.a2_ref) | copy-start | bytes 279556
  11.0 5.1 %copy-start.2 = (bf16[208,224]{1,0:T(8,128)(2,1)S(1)}, bf16[208,224]{1,0:T(8,128)(2,1)}, u32[]{:S(2)}) copy-start(bf16[208,224]{1,0:T(8,128)(2,1)} %constant.12.clone.a1_ref) | copy-start | bytes 279556
  11.0 5.1 %copy-start.3 = (f32[104,128]{1,0:T(8,128)S(1)}, f32[104,128]{1,0:T(8,128)}, u32[]{:S(2)}) copy-start(f32[104,128]{1,0:T(8,128)} %constant.15.clone.lk_ref) | copy-start | bytes 159748
  11.0 5.1 %copy-start.4 = (f32[104,128]{1,0:T(8,128)S(1)}, f32[104,128]{1,0:T(8,128)}, u32[]{:S(2)}) copy-start(f32[104,128]{1,0:T(8,128)} %constant.14.clone.lj_ref) | copy-start | bytes 159748
  11.0 5.1 %collective-permute-start.2 = (f32[20,8,128]{2,1,0:T(8,128)S(1)}, f32[20,8,128]{2,1,0:T(8,128)S(1)}, u32[]{:S(2)}, u32[]{:S(2)}) collective-permute-start(f32[20,8,128]{2,1,0:T(8,128)S(1)} %get-tuple-element.30), channel_id=1, source_target_pairs={{0,32},{32,64},{64,96},{96,128},{128,160},{160,192},{192,224},{224... | collective-permute-start | bytes 245768 | tf_op jit(solution)/shard_map/ppermute | solution.py:456
  11.0 5.1 %collective-permute-start.3 = (f32[20,8,128]{2,1,0:T(8,128)S(1)}, f32[20,8,128]{2,1,0:T(8,128)S(1)}, u32[]{:S(2)}, u32[]{:S(2)}) collective-permute-start(f32[20,8,128]{2,1,0:T(8,128)S(1)} %get-tuple-element.31), channel_id=1, source_target_pairs={{0,224},{32,0},{64,32},{96,64},{128,96},{160,128},{192,160},{224,1... | collective-permute-start | bytes 245768 | tf_op jit(solution)/shard_map/ppermute | solution.py:456
  18.3 9.1 %collective-permute-start.4 = (f32[10,3,8,128]{3,2,1,0:T(8,128)S(1)}, f32[10,3,8,128]{3,2,1,0:T(8,128)S(1)}, u32[]{:S(2)}, u32[]{:S(2)}) collective-permute-start(f32[10,3,8,128]{3,2,1,0:T(8,128)S(1)} %get-tuple-element.34), channel_id=1, source_target_pairs={{0,1},{1,2},{2,3},{3,4},{4,5},{5,6},{6,7},{7,8},{8,9},{9,10},{10,1... | collective-permute-start | bytes 368648 | tf_op jit(solution)/shard_map/ppermute | solution.py:456
  19.7 7.8 %collective-permute-start.5 = (f32[10,3,8,128]{3,2,1,0:T(8,128)S(1)}, f32[10,3,8,128]{3,2,1,0:T(8,128)S(1)}, u32[]{:S(2)}, u32[]{:S(2)}) collective-permute-start(f32[10,3,8,128]{3,2,1,0:T(8,128)S(1)} %get-tuple-element.35), channel_id=1, source_target_pairs={{0,31},{1,0},{2,1},{3,2},{4,3},{5,4},{6,5},{7,6},{8,7},{9,8},{10,9... | collective-permute-start | bytes 368648 | tf_op jit(solution)/shard_map/ppermute | solution.py:456
  27.5 6.8 %collective-permute-start.6 = (f32[3,20,8,128]{3,2,1,0:T(8,128)S(1)}, f32[3,20,8,128]{3,2,1,0:T(8,128)S(1)}, u32[]{:S(2)}, u32[]{:S(2)}) collective-permute-start(f32[3,20,8,128]{3,2,1,0:T(8,128)S(1)} %get-tuple-element.36), channel_id=1, source_target_pairs={{0,32},{32,64},{64,96},{96,128},{128,160},{160,192},{192,224},{224... | collective-permute-start | bytes 737288 | tf_op jit(solution)/shard_map/ppermute | solution.py:456
  27.5 6.8 %collective-permute-start.7 = (f32[3,20,8,128]{3,2,1,0:T(8,128)S(1)}, f32[3,20,8,128]{3,2,1,0:T(8,128)S(1)}, u32[]{:S(2)}, u32[]{:S(2)}) collective-permute-start(f32[3,20,8,128]{3,2,1,0:T(8,128)S(1)} %get-tuple-element.37), channel_id=1, source_target_pairs={{0,224},{32,0},{64,32},{96,64},{128,96},{160,128},{192,160},{224,1... | collective-permute-start | bytes 737288 | tf_op jit(solution)/shard_map/ppermute | solution.py:456
  37.4 7.9 %collective-permute-start.8 = (f32[10,2,8,128]{3,2,1,0:T(8,128)S(1)}, f32[10,2,8,128]{3,2,1,0:T(8,128)S(1)}, u32[]{:S(2)}, u32[]{:S(2)}) collective-permute-start(f32[10,2,8,128]{3,2,1,0:T(8,128)S(1)} %get-tuple-element.40), channel_id=1, source_target_pairs={{0,1},{1,2},{2,3},{3,4},{4,5},{5,6},{6,7},{7,8},{8,9},{9,10},{10,1... | collective-permute-start | bytes 245768 | tf_op jit(solution)/shard_map/ppermute | solution.py:456
  38.7 6.6 %collective-permute-start.9 = (f32[10,2,8,128]{3,2,1,0:T(8,128)S(1)}, f32[10,2,8,128]{3,2,1,0:T(8,128)S(1)}, u32[]{:S(2)}, u32[]{:S(2)}) collective-permute-start(f32[10,2,8,128]{3,2,1,0:T(8,128)S(1)} %get-tuple-element.41), channel_id=1, source_target_pairs={{0,31},{1,0},{2,1},{3,2},{4,3},{5,4},{6,5},{7,6},{8,7},{9,8},{10,9... | collective-permute-start | bytes 245768 | tf_op jit(solution)/shard_map/ppermute | solution.py:456
  45.3 5.8 %copy-start.5 = (bf16[16,512]{1,0:T(8,128)(2,1)S(1)}, bf16[16,512]{1,0:T(8,128)(2,1)}, u32[]{:S(2)}) copy-start(bf16[16,512]{1,0:T(8,128)(2,1)} %constant.16.clone.wm_ref) | copy-start | bytes 49156
  45.3 5.8 %collective-permute-start.10 = (f32[2,18,8,128]{3,2,1,0:T(8,128)S(1)}, f32[2,18,8,128]{3,2,1,0:T(8,128)S(1)}, u32[]{:S(2)}, u32[]{:S(2)}) collective-permute-start(f32[2,18,8,128]{3,2,1,0:T(8,128)S(1)} %get-tuple-element.42), channel_id=1, source_target_pairs={{0,32},{32,64},{64,96},{96,128},{128,160},{160,192},{192,224},{224... | collective-permute-start | bytes 442376 | tf_op jit(solution)/shard_map/ppermute | solution.py:456
  45.4 5.8 %collective-permute-start.11 = (f32[2,18,8,128]{3,2,1,0:T(8,128)S(1)}, f32[2,18,8,128]{3,2,1,0:T(8,128)S(1)}, u32[]{:S(2)}, u32[]{:S(2)}) collective-permute-start(f32[2,18,8,128]{3,2,1,0:T(8,128)S(1)} %get-tuple-element.43), channel_id=1, source_target_pairs={{0,224},{32,0},{64,32},{96,64},{128,96},{160,128},{192,160},{224,1... | collective-permute-start | bytes 442376 | tf_op jit(solution)/shard_map/ppermute | solution.py:456

commit v3 on v2

--- a/solution.py
+++ b/solution.py
@@ -47,10 +47,11 @@
     wm = np.einsum("ax,by,cz->abcxyz", w, w, w).reshape(8, 512)
     wh, wl = split_np(wm)
     wm = np.concatenate([wh, wl], 0)
-    return s, lam, a1, a2, lam_j, lam_k, wm
-
-
-SINES, LAM, A_FWD, A_BWD, LAM_J, LAM_K, W_MOM = constants()
+    rim = wm.reshape(16, 8, 8, 8)[:, :, [0, 1, 6, 7]].reshape(16, 256)
+    return s, lam, a1, a2, lam_j, lam_k, wm, rim
+
+
+SINES, LAM, A_FWD, A_BWD, LAM_J, LAM_K, W_MOM, W_RIM = constants()
 
 
 def split(x):
@@ -92,8 +93,8 @@
 
 def place_kernel(
     rhs_hbm, stretch_hbm, mass_hbm, slot_hbm, group_hbm,
-    src_ref, coef_ref, to_down_ref, to_up_ref, slot_ref, group_ref,
-    rhs_ref, stretch_ref, mass_ref, sems,
+    src_ref, coef_ref, to_down_ref, to_up_ref, slot_ref,
+    rhs_ref, stretch_ref, mass_ref, group_ref, sems,
 ):
     small = [
         pltpu.make_async_copy(h, v, sems.at[8 + k])
@@ -116,18 +117,29 @@
         c.start()
     small[0].wait()
     oh = onehot(slot_ref[...])
-    small[1].wait()
-    small[2].wait()
-    c = jnp.concatenate([stretch_ref[...], mass_ref[...], jnp.zeros((4, 256), F32)], 0)
+    for c in small[1:]:
+        c.wait()
+    c = jnp.concatenate(
+        [
+            stretch_ref[...],
+            mass_ref[...],
+            group_ref[...].astype(F32),
+            jnp.zeros((3, 256), F32),
+        ],
+        0,
+    )
     c1 = c.astype(BF16)
     r1 = c - c1.astype(F32)
     c2 = r1.astype(BF16)
     c3 = (r1 - c2.astype(F32)).astype(BF16)
     cg = dot_t(c1, oh) + dot_t(c2, oh) + dot_t(c3, oh)
     coef = jnp.concatenate([cg[0:4, :LANES], cg[0:4, LANES:]], 0)
-    coef_ref[...] = coef
-    to_down_ref[8] = coef
-    to_up_ref[8] = coef
+    gr = jnp.concatenate([cg[4:5, :LANES], cg[4:5, LANES:], jnp.zeros((6, LANES), F32)], 0)
+    coef_ref[0] = coef
+    coef_ref[1] = gr
+    for out in (to_down_ref, to_up_ref):
+        out[8] = coef
+        out[9] = gr
     for x in range(8):
         big[x].wait()
         a = rhs_ref[x * 64 : (x + 1) * 64, :]
@@ -144,7 +156,6 @@
                 to_down_ref[x] = block[0]
             else:
                 to_up_ref[x] = block[7]
-    small[3].wait()
 
 
 def rim_kernel(src_ref, coef_ref, yd_ref, yu_ref, to_left_ref, to_right_ref):
@@ -153,7 +164,7 @@
         out[0] = yd_ref[x]
         out[1:17] = src_ref[x]
         out[17] = yu_ref[x]
-        out[18] = coef_ref[...]
+        out[18] = coef_ref[0]
         out[19] = coef_y
 
 
@@ -183,7 +194,7 @@
     for b in range(2):
         lanes = slice(b * LANES, (b + 1) * LANES)
         cx, cy, cz, m = [
-            jnp.broadcast_to(coef_ref[b * 4 + k : b * 4 + k + 1, :], (8, LANES)) for k in range(4)
+            jnp.broadcast_to(coef_ref[0, b * 4 + k : b * 4 + k + 1, :], (8, LANES)) for k in range(4)
         ]
 
         def chunk(t, carry):
@@ -283,11 +294,9 @@
 
 def edge_kernel(w_ref, d_ref, u_ref, to_left_ref, to_right_ref):
     _, _, down, up = flags()
-    n = d_ref.shape[1]
-    for k in range(n):
-        for p, out in ((k, to_left_ref), (10 - n + k, to_right_ref)):
-            at = p if w_ref.shape[0] == 10 or p < n else p - 10 + 2 * n
-            out[k] = with_rows(w_ref[at], n, d_ref[p], u_ref[p], down, up)
+    for k in range(3):
+        for p, out in ((k, to_left_ref), (7 + k, to_right_ref)):
+            out[k] = with_rows(w_ref[p], 3, d_ref[p], u_ref[p], down, up)
 
 
 def neighbours_z(u):
@@ -302,7 +311,7 @@
 def second_kernel(
     rext_ref, coef_ref, xl_ref, xr_ref, yd_ref, yu_ref, w_ref, l_ref, r_ref, d_ref, u_ref,
     a1_ref, a2_ref, lj_ref, lk_ref,
-    c_ref, edge_ref, to_down_ref, to_up_ref, h, cb, r1, spec, wout,
+    c_ref, to_left_ref, to_right_ref, own_down_ref, own_up_ref, h, cb, r1, spec, wout,
 ):
     left, right, down, up = flags()
     for x in range(12):
@@ -326,7 +335,7 @@
             for k in range(4):
                 if b == 1 or b == 2:
                     at = (b - 1) * 4 + k
-                    row = coef_ref[at : at + 1, :] if x_ref is None else x_ref[18, at : at + 1, :]
+                    row = coef_ref[0, at : at + 1, :] if x_ref is None else x_ref[18, at : at + 1, :]
                 elif x_ref is not None:
                     at = k if b == 0 else 4 + k
                     row = x_ref[19, at : at + 1, :]
@@ -363,82 +372,158 @@
         line = get(wout, p, 0, 18)
         c_ref[p] = h[p + 1, 1:19] + line
         if p < 2:
-            edge_ref[p] = line
+            to_left_ref[p] = line
         if p > 7:
-            edge_ref[p - 6] = line
-        to_down_ref[p] = line[0:2]
-        to_up_ref[p] = line[16:18]
-
-
-def last_kernel(
-    src_ref, coef_ref, c_ref, l_ref, r_ref, d_ref, u_ref, slot_ref, group_ref, wm_ref,
-    smooth_hbm, res_hbm, part_ref, h, mu, mr, smooth_ref, res_ref, sems,
+            to_right_ref[p - 8] = line
+        own_down_ref[p] = line[0:2]
+        own_up_ref[p] = line[16:18]
+
+
+def add_x(g, p, l, r, left, right):
+    if p == 0:
+        return (g + l[0]) * left
+    if p == 1:
+        return g + l[1] * left
+    if p == 8:
+        return g + r[0] * right
+    if p == 9:
+        return (g + r[1]) * right
+    return g
+
+
+def rows_of(tile, at):
+    return [jnp.broadcast_to(tile[at + k : at + k + 1, :], (8, LANES)) for k in range(4)]
+
+
+def stencil(cf, v, x_sum, y_sum):
+    above, below = neighbours_z(v)
+    two = v + v
+    return (
+        cf[0] * (two - x_sum) + cf[1] * (two - y_sum) + cf[2] * (two - above - below) + cf[3] * v
+    )
+
+
+def middle_kernel(
+    src_ref, coef_ref, yd_ref, yu_ref, c_ref, l_ref, r_ref, own_down_ref, own_up_ref,
+    wm_ref, wr_ref,
+    mu_ref, mr_ref, to_down_ref, to_up_ref, part_ref, h, rim,
 ):
     left, right, down, up = flags()
     for p in range(10):
-        g = with_rows(c_ref[p], 2, d_ref[p], u_ref[p], down, up)
-        if p == 0:
-            g = (g + l_ref[0]) * left
-        elif p == 1:
-            g = g + l_ref[1] * left
-        elif p == 8:
-            g = g + r_ref[0] * right
-        elif p == 9:
-            g = (g + r_ref[1]) * right
-        h[p] = g
+        h[p] = add_x(c_ref[p], p, l_ref, r_ref, left, right)
+        e = add_x(own_down_ref[p], p, l_ref[:, 0:2], r_ref[:, 0:2], left, right)
+        to_down_ref[p] = jnp.concatenate([e[0:1] * down, e[1:2]], 0)
+        e = add_x(own_up_ref[p], p, l_ref[:, 16:18], r_ref[:, 16:18], left, right)
+        to_up_ref[p] = jnp.concatenate([e[0:1], e[1:2] * up], 0)
+        h[p, 0] = h[p, 0] * down
+        h[p, 17] = h[p, 17] * up
     for b in range(2):
         lanes = slice(b * LANES, (b + 1) * LANES)
-        cf = [
-            jnp.broadcast_to(coef_ref[b * 4 + k : b * 4 + k + 1, :], (8, LANES)) for k in range(4)
-        ]
+        cf = rows_of(coef_ref[0], b * 4)
         for x in range(8):
             p = x + 1
             for y in (0, 4):
                 yy = b * 8 + y + 1
                 v = h[p, yy : yy + 4]
-                above, below = neighbours_z(v)
-                two = v + v
-                res = src_ref[x, yy - 1 : yy + 3] - (
-                    cf[0] * (two - h[p + 1, yy : yy + 4] - h[p - 1, yy : yy + 4])
-                    + cf[1] * (two - h[p, yy + 1 : yy + 5] - h[p, yy - 1 : yy + 3])
-                    + cf[2] * (two - above - below)
-                    + cf[3] * v
+                res = src_ref[x, yy - 1 : yy + 3] - stencil(
+                    cf,
+                    v,
+                    h[p + 1, yy : yy + 4] + h[p - 1, yy : yy + 4],
+                    h[p, yy + 1 : yy + 5] + h[p, yy - 1 : yy + 3],
                 )
                 at = (x * 8 + y) * 8
-                mu[at : at + 32, lanes] = v.reshape(32, LANES)
-                mr[at : at + 32, lanes] = res.reshape(32, LANES)
+                mu_ref[at : at + 32, lanes] = v.reshape(32, LANES)
+                mr_ref[at : at + 32, lanes] = res.reshape(32, LANES)
+    rim[...] = jnp.zeros((256, 256), F32)
+    for slab, far, near, tile, b, lanes, y_far, y_near in (
+        (to_down_ref, 0, 1, yd_ref, 1, slice(0, LANES), 2, 3),
+        (to_up_ref, 1, 0, yu_ref, 0, slice(LANES, 256), 1, 0),
+    ):
+        cf = rows_of(tile[8], b * 4)
+        for x in range(8):
+            p = x + 1
+            v = slab[p, far : far + 1]
+            res = stencil(
+                cf,
+                v,
+                slab[p + 1, far : far + 1] + slab[p - 1, far : far + 1],
+                slab[p, near : near + 1],
+            )
+            at = (x * 4 + y_near) * 8
+            rim[at : at + 8, lanes] = -res[0]
+            at = (x * 4 + y_far) * 8
+            rim[at : at + 8, lanes] = cf[1] * v[0]
+    mom = jnp.zeros((16, 256), F32)
+    for x in range(4):
+        at = slice(x * 128, x * 128 + 128)
+        rh, rl = split(mr_ref[at, :])
+        mom = mom + dot(wm_ref[:, at], rh) + dot(wm_ref[:, at], rl)
+    rh, rl = split(rim[...])
+    mom_y = dot(wr_ref[...], rh) + dot(wr_ref[...], rl)
+    mom_y = mom_y[0:8] + mom_y[8:16]
+    mom = jnp.concatenate(
+        [mom[0:8] + mom[8:16], mom_y[:, :LANES] * down, mom_y[:, LANES:] * up], 1
+    )
+    gr = coef_ref[1]
+    group = jnp.concatenate([gr[0:1], gr[1:2], yd_ref[9, 1:2, :], yu_ref[9, 0:1, :]], 1)
+    ny = part_ref.shape[0]
+    col = (group + 0.5).astype(jnp.int32) - lax.axis_index("sx") * (ny * GRP_DEV)
+    owner = lax.shift_right_logical(col, 4)
+    member = jnp.bitwise_and(col, 15)
+    sel = lax.broadcasted_iota(jnp.int32, (ny, 512), 0)
+    pick = jnp.where(sel == owner, 1.0, 0.0).astype(BF16)
+    m16 = lax.broadcasted_iota(jnp.int32, (16, 512), 0) == member
+    spread = jnp.concatenate(
+        [jnp.where(m16, jnp.broadcast_to(mom[v : v + 1], (16, 512)), 0.0) for v in range(8)], 0
+    )
+    sh, sl = split(spread)
+    part_ref[...] = dot_t(pick, sh) + dot_t(pick, sl)
+
+
+def last_kernel(
+    mu_ref, mr_ref, coef_ref, d_ref, u_ref, slot_ref, arrived_ref,
+    smooth_hbm, res_hbm, coarse_hbm, smooth_ref, res_ref, coarse_ref, sems,
+):
+    _, _, down, up = flags()
+    total = jnp.sum(arrived_ref[...], axis=0, keepdims=True)
+    for v in range(8):
+        coarse_ref[v : v + 1, :] = total[:, v * GRP_DEV : (v + 1) * GRP_DEV]
+    copies = [pltpu.make_async_copy(coarse_ref, coarse_hbm, sems.at[16])]
+    copies[0].start()
     oh = onehot(slot_ref[...])
-    mom = jnp.zeros((16, 256), F32)
-    copies = []
+    sides = (
+        (d_ref, down, 0, 1, rows_of(coef_ref[0], 0), 0, 1),
+        (u_ref, up, 1, 0, rows_of(coef_ref[0], 4), 7, 6),
+    )
     for x in range(8):
         at = slice(x * 64, x * 64 + 64)
-        uh, ul = split(mu[at, :])
-        rh, rl = split(mr[at, :])
+        mu = mu_ref[at, :]
+        mr = mr_ref[at, :]
+        add_u, add_r = [], []
+        for slab, on, far, near, cf, y0, y1 in sides:
+            p = x + 1
+            v = slab[p, near : near + 1] * on
+            x_sum = (slab[p + 1, near : near + 1] + slab[p - 1, near : near + 1]) * on
+            res = stencil(cf, v, x_sum, slab[p, far : far + 1] * on)
+            zero = jnp.zeros((8, LANES), F32)
+            ru = [zero] * 8
+            rr = [zero] * 8
+            ru[y0] = v[0]
+            rr[y0] = -res[0]
+            rr[y1] = cf[1] * v[0]
+            add_u.append(jnp.concatenate(ru, 0))
+            add_r.append(jnp.concatenate(rr, 0))
+        uh, ul = split(mu + jnp.concatenate(add_u, 1))
+        rh, rl = split(mr + jnp.concatenate(add_r, 1))
         o = dot(jnp.concatenate([uh, ul, rh, rl], 0), oh)
         smooth_ref[at, :] = o[0:64] + o[64:128]
         res_ref[at, :] = o[128:192] + o[192:256]
         for k, (v, hbm) in enumerate(((smooth_ref, smooth_hbm), (res_ref, res_hbm))):
-            at = pl.ds(x * 64, 64)
-            copies.append(pltpu.make_async_copy(v.at[at, :], hbm.at[at, :], sems.at[2 * x + k]))
+            rows = pl.ds(x * 64, 64)
+            copies.append(
+                pltpu.make_async_copy(v.at[rows, :], hbm.at[rows, :], sems.at[2 * x + k])
+            )
             copies[-1].start()
-    for x in range(4):
-        at = slice(x * 128, x * 128 + 128)
-        rh, rl = split(mr[at, :])
-        mom = mom + dot(wm_ref[:, at], rh) + dot(wm_ref[:, at], rl)
-    mh, ml = split(mom[0:8] + mom[8:16])
-    mom = dot(mh, oh) + dot(ml, oh)
-    ny = part_ref.shape[0]
-    col = group_ref[...] - lax.axis_index("sx") * (ny * GRP_DEV)
-    owner = lax.shift_right_logical(col, 4)
-    member = jnp.bitwise_and(col, 15)
-    sel = lax.broadcasted_iota(jnp.int32, (ny, 256), 0)
-    pick = jnp.where(sel == owner, 1.0, 0.0).astype(BF16)
-    m16 = lax.broadcasted_iota(jnp.int32, (16, 256), 0) == member
-    spread = jnp.concatenate(
-        [jnp.where(m16, jnp.broadcast_to(mom[v : v + 1], (16, 256)), 0.0) for v in range(8)], 0
-    )
-    sh, sl = split(spread)
-    part_ref[...] = dot_t(pick, sh) + dot_t(pick, sl)
     for c in copies:
         c.wait()
 
@@ -458,12 +543,12 @@
 
 def call(kernel, outs, args, scratch=(), hbm_in=0, hbm_out=0, sems=0):
     vmem = pl.BlockSpec(memory_space=pltpu.VMEM)
-    hbm = pl.BlockSpec(memory_space=pl.ANY)
+    hbm = pl.BlockSpec(memory_space=pltpu.HBM)
     args = [
-        a if k < hbm_in else pltpu.with_memory_space_constraint(a, pltpu.VMEM)
+        pltpu.with_memory_space_constraint(a, pltpu.HBM if k < hbm_in else pltpu.VMEM)
         for k, a in enumerate(args)
     ]
-    scratch = [pltpu.VMEM(s, F32) for s in scratch]
+    scratch = [pltpu.VMEM(s, F32) if isinstance(s, tuple) else s for s in scratch]
     if sems:
         scratch.append(pltpu.SemaphoreType.DMA((sems,)))
     return pl.pallas_call(
@@ -482,10 +567,11 @@
     lj = jnp.asarray(LAM_J, F32)
     lk = jnp.asarray(LAM_K, F32)
     wm = jnp.asarray(W_MOM, BF16)
+    wr = jnp.asarray(W_RIM, BF16)
     row = pltpu.VMEM((1, 256), jnp.int32)
-    src, coef, to_d, to_u, slot, group = call(
+    src, coef, to_d, to_u, slot = call(
         place_kernel,
-        [vm(8, 16, 8, LANES), vm(8, LANES), vm(9, 8, LANES), vm(9, 8, LANES), row, row],
+        [vm(8, 16, 8, LANES), vm(2, 8, LANES), vm(10, 8, LANES), vm(10, 8, LANES), row],
         (
             right_side.reshape(512, 256),
             stretch,
@@ -493,7 +579,7 @@
             slot_position.reshape(1, 256),
             coarse_group.reshape(1, 256),
         ),
-        [(512, 256), (3, 256), (1, 256)],
+        [(512, 256), (3, 256), (1, 256), row],
         hbm_in=5,
         sems=12,
     )
@@ -516,30 +602,34 @@
     l = ring(to_r, "sx", 1)
     r = ring(to_l, "sx", -1)
 
+    slab = vm(2, 18, 8, LANES)
     side = vm(10, 2, 8, LANES)
-    c, w, to_d, to_u = call(
+    c, to_l, to_r, own_d, own_u = call(
         second_kernel,
-        [vm(10, 18, 8, LANES), vm(4, 18, 8, LANES), side, side],
+        [vm(10, 18, 8, LANES), slab, slab, side, side],
         (rext, coef, xl, xr, yd, yu, w, l, r, d, u, a1, a2, lj, lk),
         [(12, 20, 8, LANES), (3, 4, 4, 8, LANES), (1920, LANES), (10, 104, 256), (1920, LANES)],
     )
+    l = ring(to_r, "sx", 1)
+    r = ring(to_l, "sx", -1)
+    ny = lax.axis_size("sy")
+    mu, mr, to_d, to_u, part = call(
+        middle_kernel,
+        [vm(512, 256), vm(512, 256), side, side, vm(ny, LANES)],
+        (src, coef, yd, yu, c, l, r, own_d, own_u, wm, wr),
+        [(10, 18, 8, LANES), (256, 256)],
+    )
     d = ring(to_u, "sy", 1)
     u = ring(to_d, "sy", -1)
-    to_l, to_r = call(edge_kernel, [vm(2, 18, 8, LANES)] * 2, (w, d, u))
-    l = ring(to_r, "sx", 1)
-    r = ring(to_l, "sx", -1)
-
-    ny = lax.axis_size("sy")
-    smooth, res, part = call(
+    arrived = lax.all_to_all(part, "sy", split_axis=0, concat_axis=0, tiled=True)
+    smooth, res, coarse = call(
         last_kernel,
-        [sd(512, 256), sd(512, 256), vm(ny, LANES)],
-        (src, coef, c, l, r, d, u, slot, group, wm),
-        [(10, 18, 8, LANES)] + [(512, 256)] * 4,
-        hbm_out=2,
-        sems=16,
-    )
-    arrived = lax.all_to_all(part, "sy", split_axis=0, concat_axis=0, tiled=True)
-    coarse = arrived.sum(axis=0).reshape(8, GRP_DEV)
+        [sd(512, 256), sd(512, 256), sd(8, GRP_DEV)],
+        (mu, mr, coef, d, u, slot, arrived),
+        [(512, 256), (512, 256), (8, GRP_DEV)],
+        hbm_out=3,
+        sems=17,
+    )
     return smooth.reshape(8, 8, 8, 256), res.reshape(8, 8, 8, 256), coarse
 
 

time: 75.9 us -> 68.6 us (0.904)
  blocking collectives: 21.9 us -> 19.2 us
  local copies, waits for them, and re-layouts: 2.43 us -> 0.03 us
  waiting for transfers between devices: 18.2 us -> 15.9 us
    all_to_all x1, blocking collectives: 21.9 us -> 19.2 us  [on_device(): lax.all_to_all(part, 'sy', split_axis=0, concat_axis=0, tiled=True)]
    ppermute x12, waiting for transfers between devices: 18.2 us -> 15.9 us  [ring(): return lax.ppermute(value, axis, [(i, (i + by) % n) for i in range(n)])]
    unnamed x20 -> x12, local copies, waits for them, and re-layouts: 1.75 us -> 0.03 us
  transfers between devices with their start and end apart: 12 -> 12, of which waited for: 7 -> 6; matrix products, arithmetic and copies ran while one was open for 0% -> 0% of each run, Pallas kernels for 0% -> 0%
where the time goes in v3:
time: 68.6 us; the launch traced here: 68.5 us
  starting transfers between devices  22.1 us (32%)
  blocking collectives  19.2 us (28%)
  waiting for transfers between devices  15.9 us (23%)
  Pallas kernels  10.5 us (15%)
  between operations  0.74 us (1%)
    ppermute x12, starting transfers between devices, ring(): return lax.ppermute(value, axis, [(i, (i + by) % n) for i in range(n)])  22.1 us
    all_to_all x1, blocking collectives, on_device(): lax.all_to_all(part, 'sy', split_axis=0, concat_axis=0, tiled=True)  19.2 us
    ppermute x12, waiting for transfers between devices, ring(): return lax.ppermute(value, axis, [(i, (i + by) % n) for i in range(n)])  15.9 us
    pallas_call x7, Pallas kernels, call(): pl.pallas_call(kernel, out_shape=outs, in_specs=[hbm if k < hbm_in else v...  10.5 us
  transfers between devices with their start and end apart: 12, of which 6 were waited for; matrix products, arithmetic and copies ran while one was open for 0% of the time, Pallas kernels for 0%

profile of v3, /device:TPU:8, one launch (start us, length us, event | category | flops | bytes accessed | tf_op | source)
XLA Modules:
  0.0 68.5 jit_solution(7235555968685041484)
XLA Ops:
  0.6 3.0 %shard_map.130 = (f32[8,16,8,128]{3,2,1,0:T(8,128)S(1)}, f32[2,8,128]{2,1,0:T(8,128)S(1)}, f32[10,8,128]{2,1,0:T(8,128)S(1)}, f32[10,8,128]{2,1,0:T(8,128)S(1)}, s32[1,256]{1,0:T(1,128)S(1)}) custom-call(f32[512,256]{1,0:T(8,128)} %bitcast.12, f32[3,256]{1,0:T(4,128)} %stretch_hbm.1, f32[1,256]{1,0:T(1,128)} %bitcast.13, s32[1,256]{1,0:T(1,128)} %bitcast.14, ...), custom_call_target="tpu_custom_call" | custom-call | tf_op jit(solution)/shard_map/pallas_call | solution.py:554
  3.6 1.7 %collective-permute-start = (f32[10,8,128]{2,1,0:T(8,128)S(1)}, f32[10,8,128]{2,1,0:T(8,128)S(1)}, u32[]{:S(2)}, u32[]{:S(2)}) collective-permute-start(f32[10,8,128]{2,1,0:T(8,128)S(1)} %get-tuple-element.31), channel_id=1, source_target_pairs={{0,1},{1,2},{2,3},{3,4},{4,5},{5,6},{6,7},{7,8},{8,9},{9,10},{10,1... | collective-permute-start | bytes 122888 | tf_op jit(solution)/shard_map/ppermute | solution.py:541
  5.3 0.7 collective-permute-start.1
  5.9 1.9 %collective-permute-done.yd_ref = f32[10,8,128]{2,1,0:T(8,128)S(1)} collective-permute-done((f32[10,8,128]{2,1,0:T(8,128)S(1)}, f32[10,8,128]{2,1,0:T(8,128)S(1)}, u32[]{:S(2)}, u32[]{:S(2)}) %collective-permute-start) | collective-permute-done | bytes 40992 | tf_op jit(solution)/shard_map/ppermute | solution.py:541
  7.8 1.4 %collective-permute-done.1.yu_ref = f32[10,8,128]{2,1,0:T(8,128)S(1)} collective-permute-done((f32[10,8,128]{2,1,0:T(8,128)S(1)}, f32[10,8,128]{2,1,0:T(8,128)S(1)}, u32[]{:S(2)}, u32[]{:S(2)}) %collective-permute-start.1) | collective-permute-done | bytes 40992 | tf_op jit(solution)/shard_map/ppermute | solution.py:541
  9.3 0.0 copy-start
  9.3 0.0 copy-start.1
  9.3 0.0 copy-start.2
  9.3 0.0 copy-start.3
  9.3 0.0 collective-permute-start.2
  9.3 2.9 %collective-permute-start.3 = (f32[20,8,128]{2,1,0:T(8,128)S(1)}, f32[20,8,128]{2,1,0:T(8,128)S(1)}, u32[]{:S(2)}, u32[]{:S(2)}) collective-permute-start(f32[20,8,128]{2,1,0:T(8,128)S(1)} %get-tuple-element.34), channel_id=1, source_target_pairs={{0,224},{32,0},{64,32},{96,64},{128,96},{160,128},{192,160},{224,1... | collective-permute-start | bytes 245768 | tf_op jit(solution)/shard_map/ppermute | solution.py:541
  12.3 2.1 %collective-permute-done.2.xl_ref = f32[20,8,128]{2,1,0:T(8,128)S(1)} collective-permute-done((f32[20,8,128]{2,1,0:T(8,128)S(1)}, f32[20,8,128]{2,1,0:T(8,128)S(1)}, u32[]{:S(2)}, u32[]{:S(2)}) %collective-permute-start.2) | collective-permute-done | bytes 81952 | tf_op jit(solution)/shard_map/ppermute | solution.py:541
  14.4 0.0 collective-permute-done.3.xr_ref
  14.4 0.0 copy-done
  14.4 0.0 copy-done.1
  14.4 0.0 copy-done.2
  14.4 0.0 copy-done.3
  14.4 2.2 %shard_map.132 = (f32[1920,128]{1,0:T(8,128)S(1)}, f32[10,18,8,128]{3,2,1,0:T(8,128)S(1)}, f32[10,3,8,128]{3,2,1,0:T(8,128)S(1)}, f32[10,3,8,128]{3,2,1,0:T(8,128)S(1)}) custom-call(f32[8,16,8,128]{3,2,1,0:T(8,128)S(1)} %get-tuple-element.29.src_ref, f32[2,8,128]{2,1,0:T(8,128)S(1)} %get-tuple-element.30.coef_ref, ...), custom_call_target="tpu_custom_call" | custom-call | tf_op jit(solution)/shard_map/pallas_call | solution.py:554
  16.6 1.4 %collective-permute-start.4 = (f32[10,3,8,128]{3,2,1,0:T(8,128)S(1)}, f32[10,3,8,128]{3,2,1,0:T(8,128)S(1)}, u32[]{:S(2)}, u32[]{:S(2)}) collective-permute-start(f32[10,3,8,128]{3,2,1,0:T(8,128)S(1)} %get-tuple-element.37), channel_id=1, source_target_pairs={{0,1},{1,2},{2,3},{3,4},{4,5},{5,6},{6,7},{7,8},{8,9},{9,10},{10,1... | collective-permute-start | bytes 368648 | tf_op jit(solution)/shard_map/ppermute | solution.py:541
  18.0 4.0 %collective-permute-start.5 = (f32[10,3,8,128]{3,2,1,0:T(8,128)S(1)}, f32[10,3,8,128]{3,2,1,0:T(8,128)S(1)}, u32[]{:S(2)}, u32[]{:S(2)}) collective-permute-start(f32[10,3,8,128]{3,2,1,0:T(8,128)S(1)} %get-tuple-element.38), channel_id=1, source_target_pairs={{0,31},{1,0},{2,1},{3,2},{4,3},{5,4},{6,5},{7,6},{8,7},{9,8},{10,9... | collective-permute-start | bytes 368648 | tf_op jit(solution)/shard_map/ppermute | solution.py:541
  21.9 3.8 %collective-permute-done.4.d_ref = f32[10,3,8,128]{3,2,1,0:T(8,128)S(1)} collective-permute-done((f32[10,3,8,128]{3,2,1,0:T(8,128)S(1)}, f32[10,3,8,128]{3,2,1,0:T(8,128)S(1)}, u32[]{:S(2)}, u32[]{:S(2)}) %collective-permute-start.4) | collective-permute-done | bytes 122912 | tf_op jit(solution)/shard_map/ppermute | solution.py:541
  25.7 0.0 collective-permute-done.5.u_ref
  25.8 0.0 collective-permute-start.6
  25.8 2.9 %collective-permute-start.7 = (f32[3,20,8,128]{3,2,1,0:T(8,128)S(1)}, f32[3,20,8,128]{3,2,1,0:T(8,128)S(1)}, u32[]{:S(2)}, u32[]{:S(2)}) collective-permute-start(f32[3,20,8,128]{3,2,1,0:T(8,128)S(1)} %get-tuple-element.40), channel_id=1, source_target_pairs={{0,224},{32,0},{64,32},{96,64},{128,96},{160,128},{192,160},{224,1... | collective-permute-start | bytes 737288 | tf_op jit(solution)/shard_map/ppermute | solution.py:541
  28.7 3.9 %collective-permute-done.6.l_ref = f32[3,20,8,128]{3,2,1,0:T(8,128)S(1)} collective-permute-done((f32[3,20,8,128]{3,2,1,0:T(8,128)S(1)}, f32[3,20,8,128]{3,2,1,0:T(8,128)S(1)}, u32[]{:S(2)}, u32[]{:S(2)}) %collective-permute-start.6) | collective-permute-done | bytes 245792 | tf_op jit(solution)/shard_map/ppermute | solution.py:541
  32.6 0.0 collective-permute-done.7.r_ref
  32.6 0.0 copy-start.4
  32.6 3.0 %shard_map.134 = (f32[10,18,8,128]{3,2,1,0:T(8,128)S(1)}, f32[2,18,8,128]{3,2,1,0:T(8,128)S(1)}, f32[2,18,8,128]{3,2,1,0:T(8,128)S(1)}, f32[10,2,8,128]{3,2,1,0:T(8,128)S(1)}, f32[10,2,8,128]{3,2,1,0:T(8,128)S(1)}) custom-call(f32[1920,128]{1,0:T(8,128)S(1)} %get-tuple-element.35.rext_ref, f32[2,8,128]{2,1,0:T(8,128)S(1)} %get-tuple-element.30.coef_ref, ...), custom_call_target="tpu_custom_call" | custom-call | tf_op jit(solution)/shard_map/pallas_call | solution.py:554
  35.7 0.0 copy-start.5
  35.7 0.0 collective-permute-start.8
  35.7 3.0 %collective-permute-start.9 = (f32[2,18,8,128]{3,2,1,0:T(8,128)S(1)}, f32[2,18,8,128]{3,2,1,0:T(8,128)S(1)}, u32[]{:S(2)}, u32[]{:S(2)}) collective-permute-start(f32[2,18,8,128]{3,2,1,0:T(8,128)S(1)} %get-tuple-element.43), channel_id=1, source_target_pairs={{0,224},{32,0},{64,32},{96,64},{128,96},{160,128},{192,160},{224,1... | collective-permute-start | bytes 442376 | tf_op jit(solution)/shard_map/ppermute | solution.py:541
  38.7 2.8 %collective-permute-done.8.l_ref = f32[2,18,8,128]{3,2,1,0:T(8,128)S(1)} collective-permute-done((f32[2,18,8,128]{3,2,1,0:T(8,128)S(1)}, f32[2,18,8,128]{3,2,1,0:T(8,128)S(1)}, u32[]{:S(2)}, u32[]{:S(2)}) %collective-permute-start.8) | collective-permute-done | bytes 147488 | tf_op jit(solution)/shard_map/ppermute | solution.py:541
  41.5 0.0 collective-permute-done.9.r_ref
  41.5 0.0 copy-done.4
  41.5 0.0 copy-done.5
  41.5 0.9 %shard_map.135 = (f32[512,256]{1,0:T(8,128)S(1)}, f32[512,256]{1,0:T(8,128)S(1)}, f32[10,2,8,128]{3,2,1,0:T(8,128)S(1)}, f32[10,2,8,128]{3,2,1,0:T(8,128)S(1)}, f32[32,128]{1,0:T(8,128)S(1)}) custom-call(f32[8,16,8,128]{3,2,1,0:T(8,128)S(1)} %get-tuple-element.29.src_ref, f32[2,8,128]{2,1,0:T(8,128)S(1)} %get-tuple-element.30.coef_ref, ...), custom_call_target="tpu_custom_call" | custom-call | tf_op jit(solution)/shard_map/pallas_call | solution.py:554
  42.4 1.3 %collective-permute-start.10 = (f32[10,2,8,128]{3,2,1,0:T(8,128)S(1)}, f32[10,2,8,128]{3,2,1,0:T(8,128)S(1)}, u32[]{:S(2)}, u32[]{:S(2)}) collective-permute-start(f32[10,2,8,128]{3,2,1,0:T(8,128)S(1)} %get-tuple-element.48), channel_id=1, source_target_pairs={{0,1},{1,2},{2,3},{3,4},{4,5},{5,6},{6,7},{7,8},{8,9},{9,10},{10,1... | collective-permute-start | bytes 245768 | tf_op jit(solution)/shard_map/ppermute | solution.py:541
  43.7 4.2 %collective-permute-start.11 = (f32[10,2,8,128]{3,2,1,0:T(8,128)S(1)}, f32[10,2,8,128]{3,2,1,0:T(8,128)S(1)}, u32[]{:S(2)}, u32[]{:S(2)}) collective-permute-start(f32[10,2,8,128]{3,2,1,0:T(8,128)S(1)} %get-tuple-element.49), channel_id=1, source_target_pairs={{0,31},{1,0},{2,1},{3,2},{4,3},{5,4},{6,5},{7,6},{8,7},{9,8},{10,9... | collective-permute-start | bytes 245768 | tf_op jit(solution)/shard_map/ppermute | solution.py:541
  47.9 19.2 %all_to_all.11 = f32[32,1,128]{2,1,0:T(1,128)S(1)} all-to-all(f32[32,1,128]{2,1,0:T(1,128)S(1)} %bitcast.11), channel_id=1, replica_groups=mesh['sx'=8,'sy'=32] {'sy'}, dimensions={0} | all-to-all | bytes 32768 | tf_op jit(solution)/shard_map/all_to_all | solution.py:624
  67.1 0.0 collective-permute-done.10.d_ref
  67.1 0.0 collective-permute-done.11.u_ref
  67.1 1.4 %shard_map.136 = (f32[512,256]{1,0:T(8,128)}, f32[512,256]{1,0:T(8,128)}, f32[8,16]{1,0:T(8,128)}) custom-call(f32[512,256]{1,0:T(8,128)S(1)} %get-tuple-element.46.mu_ref, f32[512,256]{1,0:T(8,128)S(1)} %get-tuple-element.47.mr_ref, f32[2,8,128]{2,1,0:T(8,128)S(1)} %get-tuple-element.30.coef_ref, f32[10,2,8,128]{3,2,1,0:T(8,128)S(1)} %collective-permute-done.10.d_ref, ...), custom_call_target="tpu_custom_call" | custom-call | tf_op jit(solution)/shard_map/pallas_call | solution.py:554
  (2 shorter events, 0.1 us)
Async XLA Ops:
  3.6 4.2 %collective-permute-start = (f32[10,8,128]{2,1,0:T(8,128)S(1)}, f32[10,8,128]{2,1,0:T(8,128)S(1)}, u32[]{:S(2)}, u32[]{:S(2)}) collective-permute-start(f32[10,8,128]{2,1,0:T(8,128)S(1)} %get-tuple-element.31), channel_id=1, source_target_pairs={{0,1},{1,2},{2,3},{3,4},{4,5},{5,6},{6,7},{7,8},{8,9},{9,10},{10,1... | collective-permute-start | bytes 122888 | tf_op jit(solution)/shard_map/ppermute | solution.py:541
  5.3 4.0 %collective-permute-start.1 = (f32[10,8,128]{2,1,0:T(8,128)S(1)}, f32[10,8,128]{2,1,0:T(8,128)S(1)}, u32[]{:S(2)}, u32[]{:S(2)}) collective-permute-start(f32[10,8,128]{2,1,0:T(8,128)S(1)} %get-tuple-element.32), channel_id=1, source_target_pairs={{0,31},{1,0},{2,1},{3,2},{4,3},{5,4},{6,5},{7,6},{8,7},{9,8},{10,9... | collective-permute-start | bytes 122888 | tf_op jit(solution)/shard_map/ppermute | solution.py:541
  9.3 5.1 %copy-start = (bf16[224,208]{1,0:T(8,128)(2,1)S(1)}, bf16[224,208]{1,0:T(8,128)(2,1)}, u32[]{:S(2)}) copy-start(bf16[224,208]{1,0:T(8,128)(2,1)} %constant.13.clone.a2_ref) | copy-start | bytes 279556
  9.3 5.1 %copy-start.1 = (bf16[208,224]{1,0:T(8,128)(2,1)S(1)}, bf16[208,224]{1,0:T(8,128)(2,1)}, u32[]{:S(2)}) copy-start(bf16[208,224]{1,0:T(8,128)(2,1)} %constant.12.clone.a1_ref) | copy-start | bytes 279556
  9.3 5.1 %copy-start.2 = (f32[104,128]{1,0:T(8,128)S(1)}, f32[104,128]{1,0:T(8,128)}, u32[]{:S(2)}) copy-start(f32[104,128]{1,0:T(8,128)} %constant.15.clone.lk_ref) | copy-start | bytes 159748
  9.3 5.1 %copy-start.3 = (f32[104,128]{1,0:T(8,128)S(1)}, f32[104,128]{1,0:T(8,128)}, u32[]{:S(2)}) copy-start(f32[104,128]{1,0:T(8,128)} %constant.14.clone.lj_ref) | copy-start | bytes 159748
  9.3 5.1 %collective-permute-start.2 = (f32[20,8,128]{2,1,0:T(8,128)S(1)}, f32[20,8,128]{2,1,0:T(8,128)S(1)}, u32[]{:S(2)}, u32[]{:S(2)}) collective-permute-start(f32[20,8,128]{2,1,0:T(8,128)S(1)} %get-tuple-element.33), channel_id=1, source_target_pairs={{0,32},{32,64},{64,96},{96,128},{128,160},{160,192},{192,224},{224... | collective-permute-start | bytes 245768 | tf_op jit(solution)/shard_map/ppermute | solution.py:541
  9.3 5.1 %collective-permute-start.3 = (f32[20,8,128]{2,1,0:T(8,128)S(1)}, f32[20,8,128]{2,1,0:T(8,128)S(1)}, u32[]{:S(2)}, u32[]{:S(2)}) collective-permute-start(f32[20,8,128]{2,1,0:T(8,128)S(1)} %get-tuple-element.34), channel_id=1, source_target_pairs={{0,224},{32,0},{64,32},{96,64},{128,96},{160,128},{192,160},{224,1... | collective-permute-start | bytes 245768 | tf_op jit(solution)/shard_map/ppermute | solution.py:541
  16.6 9.1 %collective-permute-start.4 = (f32[10,3,8,128]{3,2,1,0:T(8,128)S(1)}, f32[10,3,8,128]{3,2,1,0:T(8,128)S(1)}, u32[]{:S(2)}, u32[]{:S(2)}) collective-permute-start(f32[10,3,8,128]{3,2,1,0:T(8,128)S(1)} %get-tuple-element.37), channel_id=1, source_target_pairs={{0,1},{1,2},{2,3},{3,4},{4,5},{5,6},{6,7},{7,8},{8,9},{9,10},{10,1... | collective-permute-start | bytes 368648 | tf_op jit(solution)/shard_map/ppermute | solution.py:541
  18.0 7.8 %collective-permute-start.5 = (f32[10,3,8,128]{3,2,1,0:T(8,128)S(1)}, f32[10,3,8,128]{3,2,1,0:T(8,128)S(1)}, u32[]{:S(2)}, u32[]{:S(2)}) collective-permute-start(f32[10,3,8,128]{3,2,1,0:T(8,128)S(1)} %get-tuple-element.38), channel_id=1, source_target_pairs={{0,31},{1,0},{2,1},{3,2},{4,3},{5,4},{6,5},{7,6},{8,7},{9,8},{10,9... | collective-permute-start | bytes 368648 | tf_op jit(solution)/shard_map/ppermute | solution.py:541
  25.8 6.8 %collective-permute-start.6 = (f32[3,20,8,128]{3,2,1,0:T(8,128)S(1)}, f32[3,20,8,128]{3,2,1,0:T(8,128)S(1)}, u32[]{:S(2)}, u32[]{:S(2)}) collective-permute-start(f32[3,20,8,128]{3,2,1,0:T(8,128)S(1)} %get-tuple-element.39), channel_id=1, source_target_pairs={{0,32},{32,64},{64,96},{96,128},{128,160},{160,192},{192,224},{224... | collective-permute-start | bytes 737288 | tf_op jit(solution)/shard_map/ppermute | solution.py:541
  25.8 6.8 %collective-permute-start.7 = (f32[3,20,8,128]{3,2,1,0:T(8,128)S(1)}, f32[3,20,8,128]{3,2,1,0:T(8,128)S(1)}, u32[]{:S(2)}, u32[]{:S(2)}) collective-permute-start(f32[3,20,8,128]{3,2,1,0:T(8,128)S(1)} %get-tuple-element.40), channel_id=1, source_target_pairs={{0,224},{32,0},{64,32},{96,64},{128,96},{160,128},{192,160},{224,1... | collective-permute-start | bytes 737288 | tf_op jit(solution)/shard_map/ppermute | solution.py:541
  32.6 8.9 %copy-start.4 = (bf16[16,512]{1,0:T(8,128)(2,1)S(1)}, bf16[16,512]{1,0:T(8,128)(2,1)}, u32[]{:S(2)}) copy-start(bf16[16,512]{1,0:T(8,128)(2,1)} %constant.16.clone.wm_ref) | copy-start | bytes 49156
  35.7 5.8 %copy-start.5 = (bf16[16,256]{1,0:T(8,128)(2,1)S(1)}, bf16[16,256]{1,0:T(8,128)(2,1)}, u32[]{:S(2)}) copy-start(bf16[16,256]{1,0:T(8,128)(2,1)} %constant.17.clone.wr_ref) | copy-start | bytes 24580
  35.7 5.8 %collective-permute-start.8 = (f32[2,18,8,128]{3,2,1,0:T(8,128)S(1)}, f32[2,18,8,128]{3,2,1,0:T(8,128)S(1)}, u32[]{:S(2)}, u32[]{:S(2)}) collective-permute-start(f32[2,18,8,128]{3,2,1,0:T(8,128)S(1)} %get-tuple-element.42), channel_id=1, source_target_pairs={{0,32},{32,64},{64,96},{96,128},{128,160},{160,192},{192,224},{224... | collective-permute-start | bytes 442376 | tf_op jit(solution)/shard_map/ppermute | solution.py:541
  35.7 5.8 %collective-permute-start.9 = (f32[2,18,8,128]{3,2,1,0:T(8,128)S(1)}, f32[2,18,8,128]{3,2,1,0:T(8,128)S(1)}, u32[]{:S(2)}, u32[]{:S(2)}) collective-permute-start(f32[2,18,8,128]{3,2,1,0:T(8,128)S(1)} %get-tuple-element.43), channel_id=1, source_target_pairs={{0,224},{32,0},{64,32},{96,64},{128,96},{160,128},{192,160},{224,1... | collective-permute-start | bytes 442376 | tf_op jit(solution)/shard_map/ppermute | solution.py:541
  42.4 24.7 %collective-permute-start.10 = (f32[10,2,8,128]{3,2,1,0:T(8,128)S(1)}, f32[10,2,8,128]{3,2,1,0:T(8,128)S(1)}, u32[]{:S(2)}, u32[]{:S(2)}) collective-permute-start(f32[10,2,8,128]{3,2,1,0:T(8,128)S(1)} %get-tuple-element.48), channel_id=1, source_target_pairs={{0,1},{1,2},{2,3},{3,4},{4,5},{5,6},{6,7},{7,8},{8,9},{9,10},{10,1... | collective-permute-start | bytes 245768 | tf_op jit(solution)/shard_map/ppermute | solution.py:541
  43.7 23.4 %collective-permute-start.11 = (f32[10,2,8,128]{3,2,1,0:T(8,128)S(1)}, f32[10,2,8,128]{3,2,1,0:T(8,128)S(1)}, u32[]{:S(2)}, u32[]{:S(2)}) collective-permute-start(f32[10,2,8,128]{3,2,1,0:T(8,128)S(1)} %get-tuple-element.49), channel_id=1, source_target_pairs={{0,31},{1,0},{2,1},{3,2},{4,3},{5,4},{6,5},{7,6},{8,7},{9,8},{10,9... | collective-permute-start | bytes 245768 | tf_op jit(solution)/shard_map/ppermute | solution.py:541

commit v4 on v3

--- a/solution.py
+++ b/solution.py
@@ -91,33 +91,37 @@
     return jnp.where(p == slot_row, 1.0, 0.0).astype(BF16)
 
 
-def place_kernel(
+def split3(a):
+    a1 = a.astype(BF16)
+    e = a - a1.astype(F32)
+    a2 = e.astype(BF16)
+    return a1, a2, (e - a2.astype(F32)).astype(BF16)
+
+
+def start_kernel(
     rhs_hbm, stretch_hbm, mass_hbm, slot_hbm, group_hbm,
-    src_ref, coef_ref, to_down_ref, to_up_ref, slot_ref,
-    rhs_ref, stretch_ref, mass_ref, group_ref, sems,
+    coef_ref, to_down_ref, to_up_ref, slot_ref,
+    face_ref, stretch_ref, mass_ref, group_ref, sems,
 ):
-    small = [
-        pltpu.make_async_copy(h, v, sems.at[8 + k])
-        for k, (h, v) in enumerate(
-            (
-                (slot_hbm, slot_ref),
-                (stretch_hbm, stretch_ref),
-                (mass_hbm, mass_ref),
-                (group_hbm, group_ref),
-            )
-        )
-    ]
-    big = [
-        pltpu.make_async_copy(
-            rhs_hbm.at[pl.ds(x * 64, 64), :], rhs_ref.at[pl.ds(x * 64, 64), :], sems.at[x]
-        )
-        for x in range(8)
-    ]
-    for c in small + big:
+    pairs = (
+        (slot_hbm, slot_ref),
+        (rhs_hbm.at[:, pl.ds(0, 8), :], face_ref.at[0]),
+        (rhs_hbm.at[:, pl.ds(56, 8), :], face_ref.at[1]),
+        (stretch_hbm, stretch_ref),
+        (mass_hbm, mass_ref),
+        (group_hbm, group_ref),
+    )
+    copies = [pltpu.make_async_copy(h, v, sems.at[k]) for k, (h, v) in enumerate(pairs)]
+    for c in copies:
         c.start()
-    small[0].wait()
+    copies[0].wait()
     oh = onehot(slot_ref[...])
-    for c in small[1:]:
+    for k, out, b in ((1, to_down_ref, 0), (2, to_up_ref, 1)):
+        copies[k].wait()
+        g = dot_t(jnp.concatenate(split3(face_ref[k - 1].reshape(64, 256)), 0), oh)
+        g = g[0:64] + g[64:128] + g[128:192]
+        out[0:8] = g[:, b * LANES : (b + 1) * LANES].reshape(8, 8, LANES)
+    for c in copies[3:]:
         c.wait()
     c = jnp.concatenate(
         [
@@ -128,10 +132,7 @@
         ],
         0,
     )
-    c1 = c.astype(BF16)
-    r1 = c - c1.astype(F32)
-    c2 = r1.astype(BF16)
-    c3 = (r1 - c2.astype(F32)).astype(BF16)
+    c1, c2, c3 = split3(c)
     cg = dot_t(c1, oh) + dot_t(c2, oh) + dot_t(c3, oh)
     coef = jnp.concatenate([cg[0:4, :LANES], cg[0:4, LANES:]], 0)
     gr = jnp.concatenate([cg[4:5, :LANES], cg[4:5, LANES:], jnp.zeros((6, LANES), F32)], 0)
@@ -140,22 +141,21 @@
     for out in (to_down_ref, to_up_ref):
         out[8] = coef
         out[9] = gr
+
+
+def place_kernel(rhs_hbm, slot_ref, src_ref, rhs_ref, sems):
+    copies = [
+        pltpu.make_async_copy(rhs_hbm.at[x], rhs_ref.at[x], sems.at[x]) for x in range(8)
+    ]
+    for c in copies:
+        c.start()
+    oh = onehot(slot_ref[...])
     for x in range(8):
-        big[x].wait()
-        a = rhs_ref[x * 64 : (x + 1) * 64, :]
-        a1 = a.astype(BF16)
-        e = a - a1.astype(F32)
-        a2 = e.astype(BF16)
-        a3 = (e - a2.astype(F32)).astype(BF16)
-        g = dot_t(jnp.concatenate([a1, a2, a3], 0), oh)
+        copies[x].wait()
+        g = dot_t(jnp.concatenate(split3(rhs_ref[x]), 0), oh)
         g = g[0:64] + g[64:128] + g[128:192]
         for b in range(2):
-            block = g[:, b * LANES : (b + 1) * LANES].reshape(8, 8, LANES)
-            src_ref[x, b * 8 : b * 8 + 8] = block
-            if b == 0:
-                to_down_ref[x] = block[0]
-            else:
-                to_up_ref[x] = block[7]
+            src_ref[x, b * 8 : b * 8 + 8] = g[:, b * LANES : (b + 1) * LANES].reshape(8, 8, LANES)
 
 
 def rim_kernel(src_ref, coef_ref, yd_ref, yu_ref, to_left_ref, to_right_ref):
@@ -168,38 +168,32 @@
         out[19] = coef_y
 
 
-def block_solves(rext, coef_ref, a1_ref, a2_ref, lj_ref, lk_ref, spec, wout):
-    for p in range(10):
-        base = p * 192
-        ends = []
-        for z, shift in ((7, lane_down), (0, lane_up)):
-            rows = [shift(rext[pl.ds(base + 64 * t + z, 8, stride=8), :]) for t in range(3)]
-            ends.append(rows)
-        halves = []
-        for b in range(2):
-            halves.append(
-                jnp.concatenate(
-                    [rext[base + 64 * b : base + 64 * b + 80, :]]
-                    + ends[0][b : b + 2]
-                    + ends[1][b : b + 2],
-                    0,
-                )
-            )
-        hi, lo = split(jnp.concatenate(halves, 1))
-        r = dot(a1_ref[...], jnp.concatenate([hi, lo], 0))
-        spec[p] = r[:104] + r[104:]
-
+def forward(res, base, a1_ref):
+    ends = []
+    for z, shift in ((7, lane_down), (0, lane_up)):
+        ends.append([shift(res[pl.ds(base + 64 * t + z, 8, stride=8), :]) for t in range(3)])
+    halves = [
+        jnp.concatenate(
+            [res[base + 64 * b : base + 64 * b + 80, :]] + ends[0][b : b + 2] + ends[1][b : b + 2],
+            0,
+        )
+        for b in range(2)
+    ]
+    hi, lo = split(jnp.concatenate(halves, 1))
+    r = dot(a1_ref[...], jnp.concatenate([hi, lo], 0))
+    return r[:104] + r[104:]
+
+
+def finish_solves(layers, coef_ref, a2_ref, lj_ref, lk_ref, spec, wout):
     even = [i for i in range(0, 10, 2)]
     odd = [i for i in range(1, 10, 2)]
     for b in range(2):
         lanes = slice(b * LANES, (b + 1) * LANES)
-        cx, cy, cz, m = [
-            jnp.broadcast_to(coef_ref[0, b * 4 + k : b * 4 + k + 1, :], (8, LANES)) for k in range(4)
-        ]
+        cx, cy, cz, m = rows_of(coef_ref[0], b * 4)
 
         def chunk(t, carry):
             row = pl.ds(pl.multiple_of(t * 8, 8), 8)
-            v = [spec[p, row, lanes] for p in range(10)]
+            v = [ref[at, row, lanes] for ref, at in layers]
             d0 = cy * lj_ref[row, :] + cz * lk_ref[row, :] + m
             s = [v[p] + v[9 - p] for p in range(5)]
             d = [v[p] - v[9 - p] for p in range(5)]
@@ -267,24 +261,36 @@
     return jnp.concatenate(parts, 0)
 
 
+def put_layer(ref, at, below, line, above):
+    put(ref, at, 0, below)
+    put(ref, at, 1, line)
+    put(ref, at, 17, above)
+    put(ref, at, 18, jnp.zeros((6, 8, LANES), F32))
+
+
+def first_inner_kernel(src_ref, yd_ref, yu_ref, a1_ref, rin_ref, sin_ref):
+    _, _, down, up = flags()
+    for x in range(8):
+        put_layer(rin_ref, x, yd_ref[x : x + 1] * down, src_ref[x], yu_ref[x : x + 1] * up)
+        sin_ref[x] = forward(rin_ref, x * 192, a1_ref)
+
+
 def first_kernel(
-    src_ref, coef_ref, xl_ref, xr_ref, yd_ref, yu_ref, a1_ref, a2_ref, lj_ref, lk_ref,
-    rext_ref, w_ref, to_down_ref, to_up_ref, spec, wout,
+    coef_ref, xl_ref, xr_ref, sin_ref, a1_ref, a2_ref, lj_ref, lk_ref,
+    rout_ref, w_ref, to_down_ref, to_up_ref, sout, spec, wout,
 ):
     left, right, down, up = flags()
-    zero = jnp.zeros((6, 8, LANES), F32)
-    for p in range(10):
-        if p in (0, 9):
-            x_ref, side = (xl_ref, left) if p == 0 else (xr_ref, right)
-            put(rext_ref, p, 0, x_ref[0:1] * (side * down))
-            put(rext_ref, p, 1, x_ref[1:17] * side)
-            put(rext_ref, p, 17, x_ref[17:18] * (side * up))
-        else:
-            put(rext_ref, p, 0, yd_ref[p - 1 : p] * down)
-            put(rext_ref, p, 1, src_ref[p - 1])
-            put(rext_ref, p, 17, yu_ref[p - 1 : p] * up)
-        put(rext_ref, p, 18, zero)
-    block_solves(rext_ref, coef_ref, a1_ref, a2_ref, lj_ref, lk_ref, spec, wout)
+    for k, (x_ref, side) in enumerate(((xl_ref, left), (xr_ref, right))):
+        put_layer(
+            rout_ref,
+            k,
+            x_ref[0:1] * (side * down),
+            x_ref[1:17] * side,
+            x_ref[17:18] * (side * up),
+        )
+        sout[k] = forward(rout_ref, k * 192, a1_ref)
+    layers = [(sout, 0)] + [(sin_ref, x) for x in range(8)] + [(sout, 1)]
+    finish_solves(layers, coef_ref, a2_ref, lj_ref, lk_ref, spec, wout)
     for p in range(10):
         line = get(wout, p, 0, 18)
         w_ref[p] = line
@@ -308,13 +314,70 @@
     return above, below
 
 
-def second_kernel(
-    rext_ref, coef_ref, xl_ref, xr_ref, yd_ref, yu_ref, w_ref, l_ref, r_ref, d_ref, u_ref,
-    a1_ref, a2_ref, lj_ref, lk_ref,
-    c_ref, to_left_ref, to_right_ref, own_down_ref, own_up_ref, h, cb, r1, spec, wout,
+ROWS = ((0, 1, 0), (1, 4, 1), (5, 4, 1), (9, 4, 2), (13, 4, 2), (17, 1, 3))
+
+
+def second_residual(get_h, get_r, cb, p, at, res_ref, left, right, down, up):
+    for y, n, b in ROWS:
+        v = get_h(p + 1, y + 1, n)
+        res = get_r(y, n) - stencil(
+            cb[b],
+            v,
+            get_h(p + 2, y + 1, n) + get_h(p, y + 1, n),
+            get_h(p + 1, y + 2, n) + get_h(p + 1, y, n),
+        )
+        if p == 0:
+            res = res * left
+        if p == 9:
+            res = res * right
+        if y == 0:
+            res = res * down
+        if y == 17:
+            res = res * up
+        put(res_ref, at, y, res)
+    put(res_ref, at, 18, jnp.zeros((6, 8, LANES), F32))
+
+
+def spread_coefs(cb, rows):
+    for b, (tile, at) in enumerate(rows):
+        for k, v in enumerate(rows_of(tile, at)):
+            cb[b, k] = v
+    return [[cb.at[b, k] for k in range(4)] for b in range(4)]
+
+
+class Loaded:
+    def __init__(self, refs):
+        self.refs = refs
+
+    def __getitem__(self, k):
+        return self.refs[k][...]
+
+
+def second_inner_kernel(
+    rin_ref, coef_ref, yd_ref, yu_ref, w_ref, d_ref, u_ref, a1_ref, h_ref, sin_ref, cb, r1,
 ):
     left, right, down, up = flags()
-    for x in range(12):
+    for x in range(3, 9):
+        h_ref[x - 3] = with_rows(w_ref[x - 1], 3, d_ref[x - 1], u_ref[x - 1], down, up)
+    tiles = spread_coefs(
+        cb, ((yd_ref[8], 4), (coef_ref[0], 0), (coef_ref[0], 4), (yu_ref[8], 0))
+    )
+    coefs = [Loaded(t) for t in tiles]
+    get_h = lambda x, y, n: h_ref[x - 3, y : y + n]
+    for k in range(4):
+        p = 3 + k
+        get_r = lambda y, n: get(rin_ref, p - 1, y, n)
+        second_residual(get_h, get_r, coefs, p, k, r1, left, right, down, up)
+        sin_ref[k] = forward(r1, k * 192, a1_ref)
+
+
+def second_kernel(
+    rin_ref, rout_ref, coef_ref, xl_ref, xr_ref, yd_ref, yu_ref, w_ref, l_ref, r_ref, d_ref, u_ref,
+    hin_ref, sin_ref, a1_ref, a2_ref, lj_ref, lk_ref,
+    c_ref, to_left_ref, to_right_ref, own_down_ref, own_up_ref, h, cb, r1, sout, spec, wout,
+):
+    left, right, down, up = flags()
+    for x in (0, 1, 2, 9, 10, 11):
         if x == 0:
             g = l_ref[0] * left
         elif x == 11:
@@ -329,48 +392,34 @@
                 g = g + r_ref[0] * right
             elif x == 10:
                 g = (g + r_ref[1]) * right
-        h[x] = g
+        h[x if x < 3 else x - 6] = g
+
+    def get_h(x, y, n):
+        if 3 <= x <= 8:
+            return hin_ref[x - 3, y : y + n]
+        return h[x if x < 3 else x - 6, y : y + n]
+
+    coefs = []
     for a, x_ref in ((0, xl_ref), (1, None), (2, xr_ref)):
-        for b in range(4):
-            for k in range(4):
-                if b == 1 or b == 2:
-                    at = (b - 1) * 4 + k
-                    row = coef_ref[0, at : at + 1, :] if x_ref is None else x_ref[18, at : at + 1, :]
-                elif x_ref is not None:
-                    at = k if b == 0 else 4 + k
-                    row = x_ref[19, at : at + 1, :]
-                elif b == 0:
-                    row = yd_ref[8, 4 + k : 5 + k, :]
-                else:
-                    row = yu_ref[8, k : k + 1, :]
-                cb[a, b, k] = jnp.broadcast_to(row, (8, LANES))
-    zero = jnp.zeros((6, 8, LANES), F32)
-    for p in range(10):
-        a = 0 if p == 0 else 2 if p == 9 else 1
-        for y, n, b in ((0, 1, 0), (1, 4, 1), (5, 4, 1), (9, 4, 2), (13, 4, 2), (17, 1, 3)):
-            v = h[p + 1, y + 1 : y + 1 + n]
-            above, below = neighbours_z(v)
-            two = v + v
-            res = get(rext_ref, p, y, n) - (
-                cb[a, b, 0] * (two - h[p + 2, y + 1 : y + 1 + n] - h[p, y + 1 : y + 1 + n])
-                + cb[a, b, 1] * (two - h[p + 1, y + 2 : y + 2 + n] - h[p + 1, y : y + n])
-                + cb[a, b, 2] * (two - above - below)
-                + cb[a, b, 3] * v
-            )
-            if p == 0:
-                res = res * left
-            if p == 9:
-                res = res * right
-            if y == 0:
-                res = res * down
-            if y == 17:
-                res = res * up
-            put(r1, p, y, res)
-        put(r1, p, 18, zero)
-    block_solves(r1, coef_ref, a1_ref, a2_ref, lj_ref, lk_ref, spec, wout)
+        if x_ref is None:
+            rows = ((yd_ref[8], 4), (coef_ref[0], 0), (coef_ref[0], 4), (yu_ref[8], 0))
+        else:
+            rows = ((x_ref[19], 0), (x_ref[18], 0), (x_ref[18], 4), (x_ref[19], 4))
+        coefs.append([Loaded(t) for t in spread_coefs(cb.at[a], rows)])
+    layers = [None] * 3 + [(sin_ref, k) for k in range(4)] + [None] * 3
+    for k, p in enumerate((0, 1, 2, 7, 8, 9)):
+        if p in (0, 9):
+            get_r = lambda y, n: get(rout_ref, 0 if p == 0 else 1, y, n)
+        else:
+            get_r = lambda y, n: get(rin_ref, p - 1, y, n)
+        cb_p = coefs[0 if p == 0 else 2 if p == 9 else 1]
+        second_residual(get_h, get_r, cb_p, p, k, r1, left, right, down, up)
+        sout[k] = forward(r1, k * 192, a1_ref)
+        layers[p] = (sout, k)
+    finish_solves(layers, coef_ref, a2_ref, lj_ref, lk_ref, spec, wout)
     for p in range(10):
         line = get(wout, p, 0, 18)
-        c_ref[p] = h[p + 1, 1:19] + line
+        c_ref[p] = get_h(p + 1, 1, 18) + line
         if p < 2:
             to_left_ref[p] = line
         if p > 7:
@@ -569,46 +618,66 @@
     wm = jnp.asarray(W_MOM, BF16)
     wr = jnp.asarray(W_RIM, BF16)
     row = pltpu.VMEM((1, 256), jnp.int32)
-    src, coef, to_d, to_u, slot = call(
-        place_kernel,
-        [vm(8, 16, 8, LANES), vm(2, 8, LANES), vm(10, 8, LANES), vm(10, 8, LANES), row],
+    rhs = right_side.reshape(8, 64, 256)
+    coef, to_d, to_u, slot = call(
+        start_kernel,
+        [vm(2, 8, LANES), vm(10, 8, LANES), vm(10, 8, LANES), row],
         (
-            right_side.reshape(512, 256),
+            rhs,
             stretch,
             mass_term.reshape(1, 256),
             slot_position.reshape(1, 256),
             coarse_group.reshape(1, 256),
         ),
-        [(512, 256), (3, 256), (1, 256), row],
+        [(2, 8, 8, 256), (3, 256), (1, 256), row],
         hbm_in=5,
-        sems=12,
+        sems=6,
     )
     yd = ring(to_u, "sy", 1)
     yu = ring(to_d, "sy", -1)
+    src = call(
+        place_kernel, [vm(8, 16, 8, LANES)], (rhs, slot), [(8, 64, 256)], hbm_in=1, sems=8
+    )[0]
     to_l, to_r = call(rim_kernel, [vm(20, 8, LANES)] * 2, (src, coef, yd, yu))
     xl = ring(to_r, "sx", 1)
     xr = ring(to_l, "sx", -1)
+    rin, sin = call(
+        first_inner_kernel, [vm(8 * 192, LANES), vm(8, 104, 256)], (src, yd, yu, a1)
+    )
 
     side = vm(10, 3, 8, LANES)
-    rext, w, to_d, to_u = call(
+    rout, w, to_d, to_u = call(
         first_kernel,
-        [vm(1920, LANES), vm(10, 18, 8, LANES), side, side],
-        (src, coef, xl, xr, yd, yu, a1, a2, lj, lk),
-        [(10, 104, 256), (1920, LANES)],
+        [vm(2 * 192, LANES), vm(10, 18, 8, LANES), side, side],
+        (coef, xl, xr, sin, a1, a2, lj, lk),
+        [(2, 104, 256), (10, 104, 256), (1920, LANES)],
     )
     d = ring(to_u, "sy", 1)
     u = ring(to_d, "sy", -1)
     to_l, to_r = call(edge_kernel, [vm(3, 20, 8, LANES)] * 2, (w, d, u))
     l = ring(to_r, "sx", 1)
     r = ring(to_l, "sx", -1)
+    hin, sin = call(
+        second_inner_kernel,
+        [vm(6, 20, 8, LANES), vm(4, 104, 256)],
+        (rin, coef, yd, yu, w, d, u, a1),
+        [(4, 4, 8, LANES), (4 * 192, LANES)],
+    )
 
     slab = vm(2, 18, 8, LANES)
     side = vm(10, 2, 8, LANES)
     c, to_l, to_r, own_d, own_u = call(
         second_kernel,
         [vm(10, 18, 8, LANES), slab, slab, side, side],
-        (rext, coef, xl, xr, yd, yu, w, l, r, d, u, a1, a2, lj, lk),
-        [(12, 20, 8, LANES), (3, 4, 4, 8, LANES), (1920, LANES), (10, 104, 256), (1920, LANES)],
+        (rin, rout, coef, xl, xr, yd, yu, w, l, r, d, u, hin, sin, a1, a2, lj, lk),
+        [
+            (6, 20, 8, LANES),
+            (3, 4, 4, 8, LANES),
+            (6 * 192, LANES),
+            (6, 104, 256),
+            (10, 104, 256),
+            (1920, LANES),
+        ],
     )
     l = ring(to_r, "sx", 1)
     r = ring(to_l, "sx", -1)

time: 68.6 us -> 67.1 us (0.978)
  waiting for transfers between devices: 15.9 us -> 11.9 us
  Pallas kernels: 10.5 us -> 12.4 us
    ppermute x12, waiting for transfers between devices: 15.9 us -> 11.9 us  [ring(): return lax.ppermute(value, axis, [(i, (i + by) % n) for i in range(n)])]
    pallas_call x7 -> x10, Pallas kernels: 10.5 us -> 12.4 us  [call(): pl.pallas_call(kernel, out_shape=outs, in_specs=[hbm if k < hbm_in else v...]
  transfers between devices with their start and end apart: 12 -> 12, of which waited for: 6 -> 5; matrix products, arithmetic and copies ran while one was open for 0% -> 0% of each run, Pallas kernels for 0% -> 6%
where the time goes in v4:
time: 67.1 us; the launch traced here: 66.9 us
  starting transfers between devices  22.6 us (34%)
  blocking collectives  19.2 us (29%)
  Pallas kernels  12.4 us (18%)
  waiting for transfers between devices  11.9 us (18%)
  between operations  0.78 us (1%)
    ppermute x12, starting transfers between devices, ring(): return lax.ppermute(value, axis, [(i, (i + by) % n) for i in range(n)])  22.6 us
    all_to_all x1, blocking collectives, on_device(): lax.all_to_all(part, 'sy', split_axis=0, concat_axis=0, tiled=True)  19.2 us
    pallas_call x10, Pallas kernels, call(): pl.pallas_call(kernel, out_shape=outs, in_specs=[hbm if k < hbm_in else v...  12.4 us
    ppermute x12, waiting for transfers between devices, ring(): return lax.ppermute(value, axis, [(i, (i + by) % n) for i in range(n)])  11.9 us
  transfers between devices with their start and end apart: 12, of which 5 were waited for; matrix products, arithmetic and copies ran while one was open for 0% of the time, Pallas kernels for 6%

profile of v4, /device:TPU:8, one launch (start us, length us, event | category | flops | bytes accessed | tf_op | source)
XLA Modules:
  0.0 66.9 jit_solution(13164418902620459934)
XLA Ops:
  0.6 1.7 %shard_map.130 = (f32[2,8,128]{2,1,0:T(8,128)S(1)}, f32[10,8,128]{2,1,0:T(8,128)S(1)}, f32[10,8,128]{2,1,0:T(8,128)S(1)}, s32[1,256]{1,0:T(1,128)S(1)}) custom-call(f32[8,64,256]{2,1,0:T(8,128)} %bitcast.12, f32[3,256]{1,0:T(4,128)} %stretch_hbm.1, f32[1,256]{1,0:T(1,128)} %bitcast.14, s32[1,256]{1,0:T(1,128)} %bitcast.15, s32[1,256]{1,0:T(1,128)} %bitcast.16), custom_call_target="tpu_custom_call" | custom-call | tf_op jit(solution)/shard_map/pallas_call | solution.py:603
  2.3 1.7 %collective-permute-start = (f32[10,8,128]{2,1,0:T(8,128)S(1)}, f32[10,8,128]{2,1,0:T(8,128)S(1)}, u32[]{:S(2)}, u32[]{:S(2)}) collective-permute-start(f32[10,8,128]{2,1,0:T(8,128)S(1)} %get-tuple-element.34), channel_id=1, source_target_pairs={{0,1},{1,2},{2,3},{3,4},{4,5},{5,6},{6,7},{7,8},{8,9},{9,10},{10,1... | collective-permute-start | bytes 122888 | tf_op jit(solution)/shard_map/ppermute | solution.py:590
  4.0 0.7 %collective-permute-start.1 = (f32[10,8,128]{2,1,0:T(8,128)S(1)}, f32[10,8,128]{2,1,0:T(8,128)S(1)}, u32[]{:S(2)}, u32[]{:S(2)}) collective-permute-start(f32[10,8,128]{2,1,0:T(8,128)S(1)} %get-tuple-element.35), channel_id=1, source_target_pairs={{0,31},{1,0},{2,1},{3,2},{4,3},{5,4},{6,5},{7,6},{8,7},{9,8},{10,9... | collective-permute-start | bytes 122888 | tf_op jit(solution)/shard_map/ppermute | solution.py:590
  4.6 2.8 %shard_map.131.src_ref = f32[8,16,8,128]{3,2,1,0:T(8,128)S(1)} custom-call(f32[8,64,256]{2,1,0:T(8,128)} %bitcast.13, s32[1,256]{1,0:T(1,128)S(1)} %get-tuple-element.32.slot_ref), custom_call_target="tpu_custom_call" | custom-call | tf_op jit(solution)/shard_map/pallas_call | solution.py:603
  7.4 0.0 collective-permute-done.yd_ref
  7.4 0.6 collective-permute-done.1.yu_ref
  8.0 0.0 copy-start
  8.0 0.0 collective-permute-start.2
  8.0 0.0 copy-start.1
  8.0 0.0 copy-start.2
  8.0 0.0 copy-start.3
  8.1 2.9 %collective-permute-start.3 = (f32[20,8,128]{2,1,0:T(8,128)S(1)}, f32[20,8,128]{2,1,0:T(8,128)S(1)}, u32[]{:S(2)}, u32[]{:S(2)}) collective-permute-start(f32[20,8,128]{2,1,0:T(8,128)S(1)} %get-tuple-element.38), channel_id=1, source_target_pairs={{0,224},{32,0},{64,32},{96,64},{128,96},{160,128},{192,160},{224,1... | collective-permute-start | bytes 245768 | tf_op jit(solution)/shard_map/ppermute | solution.py:590
  11.0 0.0 copy-done
  11.0 0.5 shard_map.132
  11.5 1.6 %collective-permute-done.2.xl_ref = f32[20,8,128]{2,1,0:T(8,128)S(1)} collective-permute-done((f32[20,8,128]{2,1,0:T(8,128)S(1)}, f32[20,8,128]{2,1,0:T(8,128)S(1)}, u32[]{:S(2)}, u32[]{:S(2)}) %collective-permute-start.2) | collective-permute-done | bytes 81952 | tf_op jit(solution)/shard_map/ppermute | solution.py:590
  13.1 0.0 collective-permute-done.3.xr_ref
  13.1 0.0 copy-done.1
  13.1 0.0 copy-done.2
  13.1 0.0 copy-done.3
  13.1 1.9 %shard_map.134 = (f32[384,128]{1,0:T(8,128)S(1)}, f32[10,18,8,128]{3,2,1,0:T(8,128)S(1)}, f32[10,3,8,128]{3,2,1,0:T(8,128)S(1)}, f32[10,3,8,128]{3,2,1,0:T(8,128)S(1)}) custom-call(f32[2,8,128]{2,1,0:T(8,128)S(1)} %get-tuple-element.33.coef_ref, f32[20,8,128]{2,1,0:T(8,128)S(1)} %collective-permute-done.2.xl_ref, ...), custom_call_target="tpu_custom_call" | custom-call | tf_op jit(solution)/shard_map/pallas_call | solution.py:603
  15.0 1.4 %collective-permute-start.4 = (f32[10,3,8,128]{3,2,1,0:T(8,128)S(1)}, f32[10,3,8,128]{3,2,1,0:T(8,128)S(1)}, u32[]{:S(2)}, u32[]{:S(2)}) collective-permute-start(f32[10,3,8,128]{3,2,1,0:T(8,128)S(1)} %get-tuple-element.42), channel_id=1, source_target_pairs={{0,1},{1,2},{2,3},{3,4},{4,5},{5,6},{6,7},{7,8},{8,9},{9,10},{10,1... | collective-permute-start | bytes 368648 | tf_op jit(solution)/shard_map/ppermute | solution.py:590
  16.3 4.9 %collective-permute-start.5 = (f32[10,3,8,128]{3,2,1,0:T(8,128)S(1)}, f32[10,3,8,128]{3,2,1,0:T(8,128)S(1)}, u32[]{:S(2)}, u32[]{:S(2)}) collective-permute-start(f32[10,3,8,128]{3,2,1,0:T(8,128)S(1)} %get-tuple-element.43), channel_id=1, source_target_pairs={{0,31},{1,0},{2,1},{3,2},{4,3},{5,4},{6,5},{7,6},{8,7},{9,8},{10,9... | collective-permute-start | bytes 368648 | tf_op jit(solution)/shard_map/ppermute | solution.py:590
  21.2 3.8 %collective-permute-done.4.d_ref = f32[10,3,8,128]{3,2,1,0:T(8,128)S(1)} collective-permute-done((f32[10,3,8,128]{3,2,1,0:T(8,128)S(1)}, f32[10,3,8,128]{3,2,1,0:T(8,128)S(1)}, u32[]{:S(2)}, u32[]{:S(2)}) %collective-permute-start.4) | collective-permute-done | bytes 122912 | tf_op jit(solution)/shard_map/ppermute | solution.py:590
  25.0 0.0 collective-permute-done.5.u_ref
  25.0 0.0 collective-permute-start.6
  25.1 2.9 %collective-permute-start.7 = (f32[3,20,8,128]{3,2,1,0:T(8,128)S(1)}, f32[3,20,8,128]{3,2,1,0:T(8,128)S(1)}, u32[]{:S(2)}, u32[]{:S(2)}) collective-permute-start(f32[3,20,8,128]{3,2,1,0:T(8,128)S(1)} %get-tuple-element.45), channel_id=1, source_target_pairs={{0,224},{32,0},{64,32},{96,64},{128,96},{160,128},{192,160},{224,1... | collective-permute-start | bytes 737288 | tf_op jit(solution)/shard_map/ppermute | solution.py:590
  28.0 0.7 %shard_map.136 = (f32[6,20,8,128]{3,2,1,0:T(8,128)S(1)}, f32[4,104,256]{2,1,0:T(8,128)S(1)}) custom-call(f32[1536,128]{1,0:T(8,128)S(1)} %get-tuple-element.36.rin_ref, f32[2,8,128]{2,1,0:T(8,128)S(1)} %get-tuple-element.33.coef_ref, f32[10,8,128]{2,1,0:T(8,128)S(1)} %collective-permute-done.yd_ref, f32[10,8,128]{2,1,0:T(8,128)S(1)} %collective-permute-done.1.yu_ref, ...), custom_call_target="tpu_custom_call" | custom-call | tf_op jit(solution)/shard_map/pallas_call | solution.py:603
  28.7 3.2 %collective-permute-done.6.l_ref = f32[3,20,8,128]{3,2,1,0:T(8,128)S(1)} collective-permute-done((f32[3,20,8,128]{3,2,1,0:T(8,128)S(1)}, f32[3,20,8,128]{3,2,1,0:T(8,128)S(1)}, u32[]{:S(2)}, u32[]{:S(2)}) %collective-permute-start.6) | collective-permute-done | bytes 245792 | tf_op jit(solution)/shard_map/ppermute | solution.py:590
  31.9 0.0 collective-permute-done.7.r_ref
  31.9 0.0 copy-start.4
  31.9 2.5 %shard_map.137 = (f32[10,18,8,128]{3,2,1,0:T(8,128)S(1)}, f32[2,18,8,128]{3,2,1,0:T(8,128)S(1)}, f32[2,18,8,128]{3,2,1,0:T(8,128)S(1)}, f32[10,2,8,128]{3,2,1,0:T(8,128)S(1)}, f32[10,2,8,128]{3,2,1,0:T(8,128)S(1)}) custom-call(f32[1536,128]{1,0:T(8,128)S(1)} %get-tuple-element.36.rin_ref, f32[384,128]{1,0:T(8,128)S(1)} %get-tuple-element.40.rout_ref, ...), custom_call_target="tpu_custom_call" | custom-call | tf_op jit(solution)/shard_map/pallas_call | solution.py:603
  34.4 0.0 copy-start.5
  34.4 0.0 collective-permute-start.8
  34.4 3.0 %collective-permute-start.9 = (f32[2,18,8,128]{3,2,1,0:T(8,128)S(1)}, f32[2,18,8,128]{3,2,1,0:T(8,128)S(1)}, u32[]{:S(2)}, u32[]{:S(2)}) collective-permute-start(f32[2,18,8,128]{3,2,1,0:T(8,128)S(1)} %get-tuple-element.50), channel_id=1, source_target_pairs={{0,224},{32,0},{64,32},{96,64},{128,96},{160,128},{192,160},{224,1... | collective-permute-start | bytes 442376 | tf_op jit(solution)/shard_map/ppermute | solution.py:590
  37.4 2.8 %collective-permute-done.8.l_ref = f32[2,18,8,128]{3,2,1,0:T(8,128)S(1)} collective-permute-done((f32[2,18,8,128]{3,2,1,0:T(8,128)S(1)}, f32[2,18,8,128]{3,2,1,0:T(8,128)S(1)}, u32[]{:S(2)}, u32[]{:S(2)}) %collective-permute-start.8) | collective-permute-done | bytes 147488 | tf_op jit(solution)/shard_map/ppermute | solution.py:590
  40.2 0.0 collective-permute-done.9.r_ref
  40.2 0.0 copy-done.4
  40.2 0.0 copy-done.5
  40.2 0.9 %shard_map.138 = (f32[512,256]{1,0:T(8,128)S(1)}, f32[512,256]{1,0:T(8,128)S(1)}, f32[10,2,8,128]{3,2,1,0:T(8,128)S(1)}, f32[10,2,8,128]{3,2,1,0:T(8,128)S(1)}, f32[32,128]{1,0:T(8,128)S(1)}) custom-call(f32[8,16,8,128]{3,2,1,0:T(8,128)S(1)} %shard_map.131.src_ref, f32[2,8,128]{2,1,0:T(8,128)S(1)} %get-tuple-element.33.coef_ref, ...), custom_call_target="tpu_custom_call" | custom-call | tf_op jit(solution)/shard_map/pallas_call | solution.py:603
  41.2 0.4 collective-permute-start.10
  41.6 4.7 %collective-permute-start.11 = (f32[10,2,8,128]{3,2,1,0:T(8,128)S(1)}, f32[10,2,8,128]{3,2,1,0:T(8,128)S(1)}, u32[]{:S(2)}, u32[]{:S(2)}) collective-permute-start(f32[10,2,8,128]{3,2,1,0:T(8,128)S(1)} %get-tuple-element.56), channel_id=1, source_target_pairs={{0,31},{1,0},{2,1},{3,2},{4,3},{5,4},{6,5},{7,6},{8,7},{9,8},{10,9... | collective-permute-start | bytes 245768 | tf_op jit(solution)/shard_map/ppermute | solution.py:590
  46.3 19.2 %all_to_all.11 = f32[32,1,128]{2,1,0:T(1,128)S(1)} all-to-all(f32[32,1,128]{2,1,0:T(1,128)S(1)} %bitcast.11), channel_id=1, replica_groups=mesh['sx'=8,'sy'=32] {'sy'}, dimensions={0} | all-to-all | bytes 32768 | tf_op jit(solution)/shard_map/all_to_all | solution.py:693
  65.5 0.0 collective-permute-done.10.d_ref
  65.5 0.0 collective-permute-done.11.u_ref
  65.5 1.3 %shard_map.139 = (f32[512,256]{1,0:T(8,128)}, f32[512,256]{1,0:T(8,128)}, f32[8,16]{1,0:T(8,128)}) custom-call(f32[512,256]{1,0:T(8,128)S(1)} %get-tuple-element.53.mu_ref, f32[512,256]{1,0:T(8,128)S(1)} %get-tuple-element.54.mr_ref, f32[2,8,128]{2,1,0:T(8,128)S(1)} %get-tuple-element.33.coef_ref, f32[10,2,8,128]{3,2,1,0:T(8,128)S(1)} %collective-permute-done.10.d_ref, ...), custom_call_target="tpu_custom_call" | custom-call | tf_op jit(solution)/shard_map/pallas_call | solution.py:603
  (2 shorter events, 0.1 us)
Async XLA Ops:
  2.3 5.1 %collective-permute-start = (f32[10,8,128]{2,1,0:T(8,128)S(1)}, f32[10,8,128]{2,1,0:T(8,128)S(1)}, u32[]{:S(2)}, u32[]{:S(2)}) collective-permute-start(f32[10,8,128]{2,1,0:T(8,128)S(1)} %get-tuple-element.34), channel_id=1, source_target_pairs={{0,1},{1,2},{2,3},{3,4},{4,5},{5,6},{6,7},{7,8},{8,9},{9,10},{10,1... | collective-permute-start | bytes 122888 | tf_op jit(solution)/shard_map/ppermute | solution.py:590
  4.0 4.0 %collective-permute-start.1 = (f32[10,8,128]{2,1,0:T(8,128)S(1)}, f32[10,8,128]{2,1,0:T(8,128)S(1)}, u32[]{:S(2)}, u32[]{:S(2)}) collective-permute-start(f32[10,8,128]{2,1,0:T(8,128)S(1)} %get-tuple-element.35), channel_id=1, source_target_pairs={{0,31},{1,0},{2,1},{3,2},{4,3},{5,4},{6,5},{7,6},{8,7},{9,8},{10,9... | collective-permute-start | bytes 122888 | tf_op jit(solution)/shard_map/ppermute | solution.py:590
  8.0 3.0 %copy-start = (bf16[208,224]{1,0:T(8,128)(2,1)S(1)}, bf16[208,224]{1,0:T(8,128)(2,1)}, u32[]{:S(2)}) copy-start(bf16[208,224]{1,0:T(8,128)(2,1)} %constant.12.clone.a1_ref) | copy-start | bytes 279556
  8.0 5.1 %collective-permute-start.2 = (f32[20,8,128]{2,1,0:T(8,128)S(1)}, f32[20,8,128]{2,1,0:T(8,128)S(1)}, u32[]{:S(2)}, u32[]{:S(2)}) collective-permute-start(f32[20,8,128]{2,1,0:T(8,128)S(1)} %get-tuple-element.37), channel_id=1, source_target_pairs={{0,32},{32,64},{64,96},{96,128},{128,160},{160,192},{192,224},{224... | collective-permute-start | bytes 245768 | tf_op jit(solution)/shard_map/ppermute | solution.py:590
  8.0 5.1 %copy-start.1 = (bf16[224,208]{1,0:T(8,128)(2,1)S(1)}, bf16[224,208]{1,0:T(8,128)(2,1)}, u32[]{:S(2)}) copy-start(bf16[224,208]{1,0:T(8,128)(2,1)} %constant.13.clone.a2_ref) | copy-start | bytes 279556
  8.0 5.1 %copy-start.2 = (f32[104,128]{1,0:T(8,128)S(1)}, f32[104,128]{1,0:T(8,128)}, u32[]{:S(2)}) copy-start(f32[104,128]{1,0:T(8,128)} %constant.15.clone.lk_ref) | copy-start | bytes 159748
  8.0 5.1 %copy-start.3 = (f32[104,128]{1,0:T(8,128)S(1)}, f32[104,128]{1,0:T(8,128)}, u32[]{:S(2)}) copy-start(f32[104,128]{1,0:T(8,128)} %constant.14.clone.lj_ref) | copy-start | bytes 159748
  8.1 5.0 %collective-permute-start.3 = (f32[20,8,128]{2,1,0:T(8,128)S(1)}, f32[20,8,128]{2,1,0:T(8,128)S(1)}, u32[]{:S(2)}, u32[]{:S(2)}) collective-permute-start(f32[20,8,128]{2,1,0:T(8,128)S(1)} %get-tuple-element.38), channel_id=1, source_target_pairs={{0,224},{32,0},{64,32},{96,64},{128,96},{160,128},{192,160},{224,1... | collective-permute-start | bytes 245768 | tf_op jit(solution)/shard_map/ppermute | solution.py:590
  15.0 10.0 %collective-permute-start.4 = (f32[10,3,8,128]{3,2,1,0:T(8,128)S(1)}, f32[10,3,8,128]{3,2,1,0:T(8,128)S(1)}, u32[]{:S(2)}, u32[]{:S(2)}) collective-permute-start(f32[10,3,8,128]{3,2,1,0:T(8,128)S(1)} %get-tuple-element.42), channel_id=1, source_target_pairs={{0,1},{1,2},{2,3},{3,4},{4,5},{5,6},{6,7},{7,8},{8,9},{9,10},{10,1... | collective-permute-start | bytes 368648 | tf_op jit(solution)/shard_map/ppermute | solution.py:590
  16.3 8.7 %collective-permute-start.5 = (f32[10,3,8,128]{3,2,1,0:T(8,128)S(1)}, f32[10,3,8,128]{3,2,1,0:T(8,128)S(1)}, u32[]{:S(2)}, u32[]{:S(2)}) collective-permute-start(f32[10,3,8,128]{3,2,1,0:T(8,128)S(1)} %get-tuple-element.43), channel_id=1, source_target_pairs={{0,31},{1,0},{2,1},{3,2},{4,3},{5,4},{6,5},{7,6},{8,7},{9,8},{10,9... | collective-permute-start | bytes 368648 | tf_op jit(solution)/shard_map/ppermute | solution.py:590
  25.0 6.8 %collective-permute-start.6 = (f32[3,20,8,128]{3,2,1,0:T(8,128)S(1)}, f32[3,20,8,128]{3,2,1,0:T(8,128)S(1)}, u32[]{:S(2)}, u32[]{:S(2)}) collective-permute-start(f32[3,20,8,128]{3,2,1,0:T(8,128)S(1)} %get-tuple-element.44), channel_id=1, source_target_pairs={{0,32},{32,64},{64,96},{96,128},{128,160},{160,192},{192,224},{224... | collective-permute-start | bytes 737288 | tf_op jit(solution)/shard_map/ppermute | solution.py:590
  25.1 6.8 %collective-permute-start.7 = (f32[3,20,8,128]{3,2,1,0:T(8,128)S(1)}, f32[3,20,8,128]{3,2,1,0:T(8,128)S(1)}, u32[]{:S(2)}, u32[]{:S(2)}) collective-permute-start(f32[3,20,8,128]{3,2,1,0:T(8,128)S(1)} %get-tuple-element.45), channel_id=1, source_target_pairs={{0,224},{32,0},{64,32},{96,64},{128,96},{160,128},{192,160},{224,1... | collective-permute-start | bytes 737288 | tf_op jit(solution)/shard_map/ppermute | solution.py:590
  31.9 8.3 %copy-start.4 = (bf16[16,512]{1,0:T(8,128)(2,1)S(1)}, bf16[16,512]{1,0:T(8,128)(2,1)}, u32[]{:S(2)}) copy-start(bf16[16,512]{1,0:T(8,128)(2,1)} %constant.16.clone.wm_ref) | copy-start | bytes 49156
  34.4 5.8 %copy-start.5 = (bf16[16,256]{1,0:T(8,128)(2,1)S(1)}, bf16[16,256]{1,0:T(8,128)(2,1)}, u32[]{:S(2)}) copy-start(bf16[16,256]{1,0:T(8,128)(2,1)} %constant.17.clone.wr_ref) | copy-start | bytes 24580
  34.4 5.8 %collective-permute-start.8 = (f32[2,18,8,128]{3,2,1,0:T(8,128)S(1)}, f32[2,18,8,128]{3,2,1,0:T(8,128)S(1)}, u32[]{:S(2)}, u32[]{:S(2)}) collective-permute-start(f32[2,18,8,128]{3,2,1,0:T(8,128)S(1)} %get-tuple-element.49), channel_id=1, source_target_pairs={{0,32},{32,64},{64,96},{96,128},{128,160},{160,192},{192,224},{224... | collective-permute-start | bytes 442376 | tf_op jit(solution)/shard_map/ppermute | solution.py:590
  34.4 5.8 %collective-permute-start.9 = (f32[2,18,8,128]{3,2,1,0:T(8,128)S(1)}, f32[2,18,8,128]{3,2,1,0:T(8,128)S(1)}, u32[]{:S(2)}, u32[]{:S(2)}) collective-permute-start(f32[2,18,8,128]{3,2,1,0:T(8,128)S(1)} %get-tuple-element.50), channel_id=1, source_target_pairs={{0,224},{32,0},{64,32},{96,64},{128,96},{160,128},{192,160},{224,1... | collective-permute-start | bytes 442376 | tf_op jit(solution)/shard_map/ppermute | solution.py:590
  41.2 24.4 %collective-permute-start.10 = (f32[10,2,8,128]{3,2,1,0:T(8,128)S(1)}, f32[10,2,8,128]{3,2,1,0:T(8,128)S(1)}, u32[]{:S(2)}, u32[]{:S(2)}) collective-permute-start(f32[10,2,8,128]{3,2,1,0:T(8,128)S(1)} %get-tuple-element.55), channel_id=1, source_target_pairs={{0,1},{1,2},{2,3},{3,4},{4,5},{5,6},{6,7},{7,8},{8,9},{9,10},{10,1... | collective-permute-start | bytes 245768 | tf_op jit(solution)/shard_map/ppermute | solution.py:590
  41.6 24.0 %collective-permute-start.11 = (f32[10,2,8,128]{3,2,1,0:T(8,128)S(1)}, f32[10,2,8,128]{3,2,1,0:T(8,128)S(1)}, u32[]{:S(2)}, u32[]{:S(2)}) collective-permute-start(f32[10,2,8,128]{3,2,1,0:T(8,128)S(1)} %get-tuple-element.56), channel_id=1, source_target_pairs={{0,31},{1,0},{2,1},{3,2},{4,3},{5,4},{6,5},{7,6},{8,7},{9,8},{10,9... | collective-permute-start | bytes 245768 | tf_op jit(solution)/shard_map/ppermute | solution.py:590

commit v5 on v4

--- a/solution.py
+++ b/solution.py
@@ -452,37 +452,104 @@
     )
 
 
+def column_residual(get_h, src_ref, cf, x, b, mr_ref, at):
+    lanes = slice(b * LANES, (b + 1) * LANES)
+    for y in (0, 4):
+        yy = b * 8 + y + 1
+        p = x + 1
+        v = get_h(p, yy, 4)
+        res = src_ref[x, yy - 1 : yy + 3] - stencil(
+            cf,
+            v,
+            get_h(p + 1, yy, 4) + get_h(p - 1, yy, 4),
+            get_h(p, yy + 1, 4) + get_h(p, yy - 1, 4),
+        )
+        mr_ref[at, y * 8 : y * 8 + 32, lanes] = res.reshape(32, LANES)
+
+
+def moments(wm_ref, x, rows):
+    rh, rl = split(rows)
+    w = wm_ref[:, x * 64 : x * 64 + rows.shape[0]]
+    return dot(w, rh) + dot(w, rl)
+
+
+def to_slots(uv, oh):
+    hi, lo = split(uv)
+    n = uv.shape[0]
+    o = dot(jnp.concatenate([hi, lo], 0), oh)
+    return o[:n] + o[n:]
+
+
+def middle_inner_kernel(
+    src_ref, coef_ref, yd_ref, yu_ref, c_ref, slot_ref, wm_ref,
+    smooth_hbm, res_hbm, mr_ref, mom_ref, pick_ref, member_ref, h, smooth_ref, res_ref, sems,
+):
+    _, _, down, up = flags()
+    oh = onehot(slot_ref[...])
+    copies = []
+    for x in range(1, 7):
+        both = [c_ref[x + 1, 8 * b + 2 : 8 * b + 8].reshape(48, LANES) for b in range(2)]
+        smooth_ref[x - 1] = to_slots(jnp.concatenate(both, 1), oh)
+    copies.append(
+        pltpu.make_async_copy(smooth_ref, smooth_hbm.at[pl.ds(1, 6), pl.ds(8, 48), :], sems.at[0])
+    )
+    copies[0].start()
+    for k in range(6):
+        h[k] = c_ref[k + 2]
+        h[k, 0] = c_ref[k + 2, 0] * down
+        h[k, 17] = c_ref[k + 2, 17] * up
+    get_h = lambda p, y, n: h[p - 2, y : y + n]
+    coefs = [rows_of(coef_ref[0], 0), rows_of(coef_ref[0], 4)]
+    for k in range(4):
+        for b in range(2):
+            column_residual(get_h, src_ref, coefs[b], 2 + k, b, mr_ref, k)
+        res_ref[k] = to_slots(mr_ref[k, 16:48, :], oh)
+    copies.append(
+        pltpu.make_async_copy(res_ref, res_hbm.at[pl.ds(2, 4), pl.ds(16, 32), :], sems.at[1])
+    )
+    copies[1].start()
+    mom = jnp.zeros((16, 256), F32)
+    for k in (0, 2):
+        mom = mom + moments(wm_ref, 2 + k, mr_ref[k : k + 2].reshape(128, 256))
+    mom_ref[...] = mom
+    gr = coef_ref[1]
+    group = jnp.concatenate([gr[0:1], gr[1:2], yd_ref[9, 1:2, :], yu_ref[9, 0:1, :]], 1)
+    ny = pick_ref.shape[0]
+    col = (group + 0.5).astype(jnp.int32) - lax.axis_index("sx") * (ny * GRP_DEV)
+    owner = lax.shift_right_logical(col, 4)
+    member = jnp.bitwise_and(col, 15)
+    sel = lax.broadcasted_iota(jnp.int32, (ny, 512), 0)
+    pick_ref[...] = jnp.where(sel == owner, 1.0, 0.0)
+    sel = lax.broadcasted_iota(jnp.int32, (16, 512), 0)
+    member_ref[...] = jnp.where(sel == member, 1.0, 0.0)
+    for c in copies:
+        c.wait()
+
+
 def middle_kernel(
     src_ref, coef_ref, yd_ref, yu_ref, c_ref, l_ref, r_ref, own_down_ref, own_up_ref,
-    wm_ref, wr_ref,
-    mu_ref, mr_ref, to_down_ref, to_up_ref, part_ref, h, rim,
+    mom_ref, pick_ref, member_ref, wm_ref, wr_ref,
+    u_ref, mr_ref, to_down_ref, to_up_ref, part_ref, h, rim,
 ):
     left, right, down, up = flags()
     for p in range(10):
-        h[p] = add_x(c_ref[p], p, l_ref, r_ref, left, right)
         e = add_x(own_down_ref[p], p, l_ref[:, 0:2], r_ref[:, 0:2], left, right)
         to_down_ref[p] = jnp.concatenate([e[0:1] * down, e[1:2]], 0)
         e = add_x(own_up_ref[p], p, l_ref[:, 16:18], r_ref[:, 16:18], left, right)
         to_up_ref[p] = jnp.concatenate([e[0:1], e[1:2] * up], 0)
-        h[p, 0] = h[p, 0] * down
-        h[p, 17] = h[p, 17] * up
-    for b in range(2):
-        lanes = slice(b * LANES, (b + 1) * LANES)
-        cf = rows_of(coef_ref[0], b * 4)
-        for x in range(8):
-            p = x + 1
-            for y in (0, 4):
-                yy = b * 8 + y + 1
-                v = h[p, yy : yy + 4]
-                res = src_ref[x, yy - 1 : yy + 3] - stencil(
-                    cf,
-                    v,
-                    h[p + 1, yy : yy + 4] + h[p - 1, yy : yy + 4],
-                    h[p, yy + 1 : yy + 5] + h[p, yy - 1 : yy + 3],
-                )
-                at = (x * 8 + y) * 8
-                mu_ref[at : at + 32, lanes] = v.reshape(32, LANES)
-                mr_ref[at : at + 32, lanes] = res.reshape(32, LANES)
+        if 3 < p < 6:
+            continue
+        g = add_x(c_ref[p], p, l_ref, r_ref, left, right)
+        h[p] = g
+        h[p, 0] = g[0] * down
+        h[p, 17] = g[17] * up
+    u_ref[0] = h[1, 1:17]
+    u_ref[1] = h[8, 1:17]
+    get_h = lambda p, y, n: h[p, y : y + n]
+    coefs = [rows_of(coef_ref[0], 0), rows_of(coef_ref[0], 4)]
+    for k, x in enumerate((0, 1, 6, 7)):
+        for b in range(2):
+            column_residual(get_h, src_ref, coefs[b], x, b, mr_ref, k)
     rim[...] = jnp.zeros((256, 256), F32)
     for slab, far, near, tile, b, lanes, y_far, y_near in (
         (to_down_ref, 0, 1, yd_ref, 1, slice(0, LANES), 2, 3),
@@ -502,77 +569,102 @@
             rim[at : at + 8, lanes] = -res[0]
             at = (x * 4 + y_far) * 8
             rim[at : at + 8, lanes] = cf[1] * v[0]
-    mom = jnp.zeros((16, 256), F32)
-    for x in range(4):
-        at = slice(x * 128, x * 128 + 128)
-        rh, rl = split(mr_ref[at, :])
-        mom = mom + dot(wm_ref[:, at], rh) + dot(wm_ref[:, at], rl)
+    mom = mom_ref[...]
+    mom = mom + moments(wm_ref, 0, mr_ref[0:2].reshape(128, 256))
+    mom = mom + moments(wm_ref, 6, mr_ref[2:4].reshape(128, 256))
     rh, rl = split(rim[...])
     mom_y = dot(wr_ref[...], rh) + dot(wr_ref[...], rl)
     mom_y = mom_y[0:8] + mom_y[8:16]
     mom = jnp.concatenate(
         [mom[0:8] + mom[8:16], mom_y[:, :LANES] * down, mom_y[:, LANES:] * up], 1
     )
-    gr = coef_ref[1]
-    group = jnp.concatenate([gr[0:1], gr[1:2], yd_ref[9, 1:2, :], yu_ref[9, 0:1, :]], 1)
-    ny = part_ref.shape[0]
-    col = (group + 0.5).astype(jnp.int32) - lax.axis_index("sx") * (ny * GRP_DEV)
-    owner = lax.shift_right_logical(col, 4)
-    member = jnp.bitwise_and(col, 15)
-    sel = lax.broadcasted_iota(jnp.int32, (ny, 512), 0)
-    pick = jnp.where(sel == owner, 1.0, 0.0).astype(BF16)
-    m16 = lax.broadcasted_iota(jnp.int32, (16, 512), 0) == member
-    spread = jnp.concatenate(
-        [jnp.where(m16, jnp.broadcast_to(mom[v : v + 1], (16, 512)), 0.0) for v in range(8)], 0
-    )
+    member = member_ref[...]
+    spread = jnp.concatenate([member * mom[v : v + 1] for v in range(8)], 0)
     sh, sl = split(spread)
+    pick = pick_ref[...].astype(BF16)
     part_ref[...] = dot_t(pick, sh) + dot_t(pick, sl)
 
 
 def last_kernel(
-    mu_ref, mr_ref, coef_ref, d_ref, u_ref, slot_ref, arrived_ref,
+    smooth_in, res_in, c_ref, uout_ref, rin_ref, rout_ref, coef_ref, d_ref, u_ref, slot_ref,
+    arrived_ref,
     smooth_hbm, res_hbm, coarse_hbm, smooth_ref, res_ref, coarse_ref, sems,
 ):
     _, _, down, up = flags()
     total = jnp.sum(arrived_ref[...], axis=0, keepdims=True)
     for v in range(8):
         coarse_ref[v : v + 1, :] = total[:, v * GRP_DEV : (v + 1) * GRP_DEV]
-    copies = [pltpu.make_async_copy(coarse_ref, coarse_hbm, sems.at[16])]
+    copies = [pltpu.make_async_copy(coarse_ref, coarse_hbm, sems.at[8])]
     copies[0].start()
+
+    def send(ref, hbm, x, nx, row, rows):
+        at = (pl.ds(x, nx), pl.ds(row, rows), slice(None))
+        k = len(copies) - 1
+        copies.append(pltpu.make_async_copy(ref.at[at], hbm.at[at], sems.at[k]))
+        copies[-1].start()
+
     oh = onehot(slot_ref[...])
     sides = (
-        (d_ref, down, 0, 1, rows_of(coef_ref[0], 0), 0, 1),
-        (u_ref, up, 1, 0, rows_of(coef_ref[0], 4), 7, 6),
-    )
-    for x in range(8):
-        at = slice(x * 64, x * 64 + 64)
-        mu = mu_ref[at, :]
-        mr = mr_ref[at, :]
-        add_u, add_r = [], []
-        for slab, on, far, near, cf, y0, y1 in sides:
+        (d_ref, down, 0, 1, rows_of(coef_ref[0], 0)),
+        (u_ref, up, 1, 0, rows_of(coef_ref[0], 4)),
+    )
+
+    def added(x):
+        out = []
+        for slab, on, far, near, cf in sides:
             p = x + 1
             v = slab[p, near : near + 1] * on
             x_sum = (slab[p + 1, near : near + 1] + slab[p - 1, near : near + 1]) * on
             res = stencil(cf, v, x_sum, slab[p, far : far + 1] * on)
-            zero = jnp.zeros((8, LANES), F32)
-            ru = [zero] * 8
-            rr = [zero] * 8
-            ru[y0] = v[0]
-            rr[y0] = -res[0]
-            rr[y1] = cf[1] * v[0]
-            add_u.append(jnp.concatenate(ru, 0))
-            add_r.append(jnp.concatenate(rr, 0))
-        uh, ul = split(mu + jnp.concatenate(add_u, 1))
-        rh, rl = split(mr + jnp.concatenate(add_r, 1))
-        o = dot(jnp.concatenate([uh, ul, rh, rl], 0), oh)
-        smooth_ref[at, :] = o[0:64] + o[64:128]
-        res_ref[at, :] = o[128:192] + o[192:256]
-        for k, (v, hbm) in enumerate(((smooth_ref, smooth_hbm), (res_ref, res_hbm))):
-            rows = pl.ds(x * 64, 64)
-            copies.append(
-                pltpu.make_async_copy(v.at[rows, :], hbm.at[rows, :], sems.at[2 * x + k])
-            )
-            copies[-1].start()
+            out.append((v[0], -res[0], cf[1] * v[0]))
+        return out
+
+    zero = jnp.zeros((8, LANES), F32)
+    pairs = [added(x) for x in range(8)]
+    for k, x in enumerate((0, 1, 6, 7)):
+        (_, d0, d1), (_, e0, e1) = pairs[x]
+        add = jnp.concatenate(
+            [
+                jnp.concatenate([d0, d1] + [zero] * 6, 0),
+                jnp.concatenate([zero] * 6 + [e1, e0], 0),
+            ],
+            1,
+        )
+        res_ref[x] = to_slots(rout_ref[k] + add, oh)
+        if k == 1:
+            send(res_ref, res_hbm, 0, 2, 0, 64)
+    send(res_ref, res_hbm, 6, 2, 0, 64)
+    low, high = [], []
+    for k in range(4):
+        (_, d0, d1), (_, e0, e1) = pairs[2 + k]
+        z2 = jnp.zeros((16, LANES), F32)
+        low.append(
+            rin_ref[k, 0:16, :] + jnp.concatenate([jnp.concatenate([d0, d1], 0), z2], 1)
+        )
+        high.append(
+            rin_ref[k, 48:64, :] + jnp.concatenate([z2, jnp.concatenate([e1, e0], 0)], 1)
+        )
+    res_ref[2:6, 0:16, :] = to_slots(jnp.concatenate(low, 0), oh).reshape(4, 16, 256)
+    send(res_ref, res_hbm, 2, 4, 0, 16)
+    res_ref[2:6, 48:64, :] = to_slots(jnp.concatenate(high, 0), oh).reshape(4, 16, 256)
+    send(res_ref, res_hbm, 2, 4, 48, 16)
+    for k, x in enumerate((0, 7)):
+        (d0, _, _), (e0, _, _) = pairs[x]
+        both = [uout_ref[k, 0:8].reshape(64, LANES), uout_ref[k, 8:16].reshape(64, LANES)]
+        both[0] = both[0] + jnp.concatenate([d0] + [zero] * 7, 0)
+        both[1] = both[1] + jnp.concatenate([zero] * 7 + [e0], 0)
+        smooth_ref[x] = to_slots(jnp.concatenate(both, 1), oh)
+        send(smooth_ref, smooth_hbm, x, 1, 0, 64)
+    low, high = [], []
+    for x in range(1, 7):
+        (d0, _, _), (e0, _, _) = pairs[x]
+        c = [c_ref[x + 1, y] for y in (1, 9, 8, 16)]
+        low.append(jnp.concatenate([c[0] + d0, c[1]], 1))
+        high.append(jnp.concatenate([c[2], c[3] + e0], 1))
+    smooth_ref[1:7, 0:8, :] = to_slots(jnp.concatenate(low, 0), oh).reshape(6, 8, 256)
+    send(smooth_ref, smooth_hbm, 1, 6, 0, 8)
+    smooth_ref[1:7, 56:64, :] = to_slots(jnp.concatenate(high, 0), oh).reshape(6, 8, 256)
+    send(smooth_ref, smooth_hbm, 1, 6, 56, 8)
     for c in copies:
         c.wait()
 
@@ -590,7 +682,7 @@
     return lax.ppermute(value, axis, [(i, (i + by) % n) for i in range(n)])
 
 
-def call(kernel, outs, args, scratch=(), hbm_in=0, hbm_out=0, sems=0):
+def call(kernel, outs, args, scratch=(), hbm_in=0, hbm_out=0, sems=0, alias=0):
     vmem = pl.BlockSpec(memory_space=pltpu.VMEM)
     hbm = pl.BlockSpec(memory_space=pltpu.HBM)
     args = [
@@ -606,6 +698,7 @@
         in_specs=[hbm if k < hbm_in else vmem for k in range(len(args))],
         out_specs=[hbm if k < hbm_out else vmem for k in range(len(outs))],
         scratch_shapes=scratch,
+        input_output_aliases={k: k for k in range(alias)},
         compiler_params=pltpu.CompilerParams(vmem_limit_bytes=16 << 20),
     )(*args)
 
@@ -682,10 +775,18 @@
     l = ring(to_r, "sx", 1)
     r = ring(to_l, "sx", -1)
     ny = lax.axis_size("sy")
-    mu, mr, to_d, to_u, part = call(
+    smooth, res, rin, mom, pick, member = call(
+        middle_inner_kernel,
+        [sd(8, 64, 256), sd(8, 64, 256), vm(4, 64, 256), vm(16, 256), vm(ny, 512), vm(16, 512)],
+        (src, coef, yd, yu, c, slot, wm),
+        [(6, 18, 8, LANES), (6, 48, 256), (4, 32, 256)],
+        hbm_out=2,
+        sems=2,
+    )
+    uout, rout, to_d, to_u, part = call(
         middle_kernel,
-        [vm(512, 256), vm(512, 256), side, side, vm(ny, LANES)],
-        (src, coef, yd, yu, c, l, r, own_d, own_u, wm, wr),
+        [vm(2, 16, 8, LANES), vm(4, 64, 256), side, side, vm(ny, LANES)],
+        (src, coef, yd, yu, c, l, r, own_d, own_u, mom, pick, member, wm, wr),
         [(10, 18, 8, LANES), (256, 256)],
     )
     d = ring(to_u, "sy", 1)
@@ -693,11 +794,13 @@
     arrived = lax.all_to_all(part, "sy", split_axis=0, concat_axis=0, tiled=True)
     smooth, res, coarse = call(
         last_kernel,
-        [sd(512, 256), sd(512, 256), sd(8, GRP_DEV)],
-        (mu, mr, coef, d, u, slot, arrived),
-        [(512, 256), (512, 256), (8, GRP_DEV)],
+        [sd(8, 64, 256), sd(8, 64, 256), sd(8, GRP_DEV)],
+        (smooth, res, c, uout, rin, rout, coef, d, u, slot, arrived),
+        [(8, 64, 256), (8, 64, 256), (8, GRP_DEV)],
+        hbm_in=2,
         hbm_out=3,
-        sems=17,
+        sems=9,
+        alias=2,
     )
     return smooth.reshape(8, 8, 8, 256), res.reshape(8, 8, 8, 256), coarse
 

time: 67.1 us -> 66.6 us (level)
  waiting for transfers between devices: 11.9 us -> 10.7 us
  Pallas kernels: 12.4 us -> 13.1 us
    ppermute x12, waiting for transfers between devices: 11.9 us -> 10.7 us  [ring(): return lax.ppermute(value, axis, [(i, (i + by) % n) for i in range(n)])]
    pallas_call x10 -> x11, Pallas kernels: 12.4 us -> 13.1 us  [call(): pl.pallas_call(kernel, out_shape=outs, in_specs=[hbm if k < hbm_in else v...]
  transfers between devices with their start and end apart: 12 -> 12, of which waited for: 5 -> 5; matrix products, arithmetic and copies ran while one was open for 0% -> 0% of each run, Pallas kernels for 6% -> 8%
where the time goes in v5:
time: 66.6 us; the launch traced here: 66.4 us
  starting transfers between devices  22.6 us (34%)
  blocking collectives  19.2 us (29%)
  Pallas kernels  13.1 us (20%)
  waiting for transfers between devices  10.7 us (16%)
  between operations  0.78 us (1%)
    ppermute x12, starting transfers between devices, ring(): return lax.ppermute(value, axis, [(i, (i + by) % n) for i in range(n)])  22.6 us
    all_to_all x1, blocking collectives, on_device(): lax.all_to_all(part, 'sy', split_axis=0, concat_axis=0, tiled=True)  19.2 us
    pallas_call x11, Pallas kernels, call(): pl.pallas_call(kernel, out_shape=outs, in_specs=[hbm if k < hbm_in else v...  13.1 us
    ppermute x12, waiting for transfers between devices, ring(): return lax.ppermute(value, axis, [(i, (i + by) % n) for i in range(n)])  10.7 us
  transfers between devices with their start and end apart: 12, of which 5 were waited for; matrix products, arithmetic and copies ran while one was open for 0% of the time, Pallas kernels for 8%

profile of v5, /device:TPU:8, one launch (start us, length us, event | category | flops | bytes accessed | tf_op | source)
XLA Modules:
  0.0 66.4 jit_solution(12317531232268690359)
XLA Ops:
  0.6 1.7 %shard_map.130 = (f32[2,8,128]{2,1,0:T(8,128)S(1)}, f32[10,8,128]{2,1,0:T(8,128)S(1)}, f32[10,8,128]{2,1,0:T(8,128)S(1)}, s32[1,256]{1,0:T(1,128)S(1)}) custom-call(f32[8,64,256]{2,1,0:T(8,128)} %bitcast.12, f32[3,256]{1,0:T(4,128)} %stretch_hbm.1, f32[1,256]{1,0:T(1,128)} %bitcast.16, s32[1,256]{1,0:T(1,128)} %bitcast.17, s32[1,256]{1,0:T(1,128)} %bitcast.18), custom_call_target="tpu_custom_call" | custom-call | tf_op jit(solution)/shard_map/pallas_call | solution.py:695
  2.3 1.7 %collective-permute-start = (f32[10,8,128]{2,1,0:T(8,128)S(1)}, f32[10,8,128]{2,1,0:T(8,128)S(1)}, u32[]{:S(2)}, u32[]{:S(2)}) collective-permute-start(f32[10,8,128]{2,1,0:T(8,128)S(1)} %get-tuple-element.40), channel_id=1, source_target_pairs={{0,1},{1,2},{2,3},{3,4},{4,5},{5,6},{6,7},{7,8},{8,9},{9,10},{10,1... | collective-permute-start | bytes 122888 | tf_op jit(solution)/shard_map/ppermute | solution.py:682
  4.0 0.7 %collective-permute-start.1 = (f32[10,8,128]{2,1,0:T(8,128)S(1)}, f32[10,8,128]{2,1,0:T(8,128)S(1)}, u32[]{:S(2)}, u32[]{:S(2)}) collective-permute-start(f32[10,8,128]{2,1,0:T(8,128)S(1)} %get-tuple-element.41), channel_id=1, source_target_pairs={{0,31},{1,0},{2,1},{3,2},{4,3},{5,4},{6,5},{7,6},{8,7},{9,8},{10,9... | collective-permute-start | bytes 122888 | tf_op jit(solution)/shard_map/ppermute | solution.py:682
  4.6 2.8 %shard_map.131.src_ref = f32[8,16,8,128]{3,2,1,0:T(8,128)S(1)} custom-call(f32[8,64,256]{2,1,0:T(8,128)} %bitcast.13, s32[1,256]{1,0:T(1,128)S(1)} %get-tuple-element.38.slot_ref), custom_call_target="tpu_custom_call" | custom-call | tf_op jit(solution)/shard_map/pallas_call | solution.py:695
  7.4 0.0 collective-permute-done.yd_ref
  7.4 0.6 collective-permute-done.1.yu_ref
  8.0 0.0 copy-start
  8.0 0.0 collective-permute-start.2
  8.0 0.0 copy-start.1
  8.0 0.0 copy-start.2
  8.0 0.0 copy-start.3
  8.1 2.9 %collective-permute-start.3 = (f32[20,8,128]{2,1,0:T(8,128)S(1)}, f32[20,8,128]{2,1,0:T(8,128)S(1)}, u32[]{:S(2)}, u32[]{:S(2)}) collective-permute-start(f32[20,8,128]{2,1,0:T(8,128)S(1)} %get-tuple-element.44), channel_id=1, source_target_pairs={{0,224},{32,0},{64,32},{96,64},{128,96},{160,128},{192,160},{224,1... | collective-permute-start | bytes 245768 | tf_op jit(solution)/shard_map/ppermute | solution.py:682
  11.0 0.0 copy-done
  11.0 0.5 shard_map.132
  11.5 1.6 %collective-permute-done.2.xl_ref = f32[20,8,128]{2,1,0:T(8,128)S(1)} collective-permute-done((f32[20,8,128]{2,1,0:T(8,128)S(1)}, f32[20,8,128]{2,1,0:T(8,128)S(1)}, u32[]{:S(2)}, u32[]{:S(2)}) %collective-permute-start.2) | collective-permute-done | bytes 81952 | tf_op jit(solution)/shard_map/ppermute | solution.py:682
  13.1 0.0 collective-permute-done.3.xr_ref
  13.1 0.0 copy-done.1
  13.1 0.0 copy-done.2
  13.1 0.0 copy-done.3
  13.1 1.9 %shard_map.134 = (f32[384,128]{1,0:T(8,128)S(1)}, f32[10,18,8,128]{3,2,1,0:T(8,128)S(1)}, f32[10,3,8,128]{3,2,1,0:T(8,128)S(1)}, f32[10,3,8,128]{3,2,1,0:T(8,128)S(1)}) custom-call(f32[2,8,128]{2,1,0:T(8,128)S(1)} %get-tuple-element.39.coef_ref, f32[20,8,128]{2,1,0:T(8,128)S(1)} %collective-permute-done.2.xl_ref, ...), custom_call_target="tpu_custom_call" | custom-call | tf_op jit(solution)/shard_map/pallas_call | solution.py:695
  15.0 1.4 %collective-permute-start.4 = (f32[10,3,8,128]{3,2,1,0:T(8,128)S(1)}, f32[10,3,8,128]{3,2,1,0:T(8,128)S(1)}, u32[]{:S(2)}, u32[]{:S(2)}) collective-permute-start(f32[10,3,8,128]{3,2,1,0:T(8,128)S(1)} %get-tuple-element.48), channel_id=1, source_target_pairs={{0,1},{1,2},{2,3},{3,4},{4,5},{5,6},{6,7},{7,8},{8,9},{9,10},{10,1... | collective-permute-start | bytes 368648 | tf_op jit(solution)/shard_map/ppermute | solution.py:682
  16.4 4.9 %collective-permute-start.5 = (f32[10,3,8,128]{3,2,1,0:T(8,128)S(1)}, f32[10,3,8,128]{3,2,1,0:T(8,128)S(1)}, u32[]{:S(2)}, u32[]{:S(2)}) collective-permute-start(f32[10,3,8,128]{3,2,1,0:T(8,128)S(1)} %get-tuple-element.49), channel_id=1, source_target_pairs={{0,31},{1,0},{2,1},{3,2},{4,3},{5,4},{6,5},{7,6},{8,7},{9,8},{10,9... | collective-permute-start | bytes 368648 | tf_op jit(solution)/shard_map/ppermute | solution.py:682
  21.2 3.8 %collective-permute-done.4.d_ref = f32[10,3,8,128]{3,2,1,0:T(8,128)S(1)} collective-permute-done((f32[10,3,8,128]{3,2,1,0:T(8,128)S(1)}, f32[10,3,8,128]{3,2,1,0:T(8,128)S(1)}, u32[]{:S(2)}, u32[]{:S(2)}) %collective-permute-start.4) | collective-permute-done | bytes 122912 | tf_op jit(solution)/shard_map/ppermute | solution.py:682
  25.0 0.0 collective-permute-done.5.u_ref
  25.1 0.0 collective-permute-start.6
  25.1 2.9 %collective-permute-start.7 = (f32[3,20,8,128]{3,2,1,0:T(8,128)S(1)}, f32[3,20,8,128]{3,2,1,0:T(8,128)S(1)}, u32[]{:S(2)}, u32[]{:S(2)}) collective-permute-start(f32[3,20,8,128]{3,2,1,0:T(8,128)S(1)} %get-tuple-element.51), channel_id=1, source_target_pairs={{0,224},{32,0},{64,32},{96,64},{128,96},{160,128},{192,160},{224,1... | collective-permute-start | bytes 737288 | tf_op jit(solution)/shard_map/ppermute | solution.py:682
  28.0 0.7 %shard_map.136 = (f32[6,20,8,128]{3,2,1,0:T(8,128)S(1)}, f32[4,104,256]{2,1,0:T(8,128)S(1)}) custom-call(f32[1536,128]{1,0:T(8,128)S(1)} %get-tuple-element.42.rin_ref, f32[2,8,128]{2,1,0:T(8,128)S(1)} %get-tuple-element.39.coef_ref, f32[10,8,128]{2,1,0:T(8,128)S(1)} %collective-permute-done.yd_ref, f32[10,8,128]{2,1,0:T(8,128)S(1)} %collective-permute-done.1.yu_ref, ...), custom_call_target="tpu_custom_call" | custom-call | tf_op jit(solution)/shard_map/pallas_call | solution.py:695
  28.8 3.2 %collective-permute-done.6.l_ref = f32[3,20,8,128]{3,2,1,0:T(8,128)S(1)} collective-permute-done((f32[3,20,8,128]{3,2,1,0:T(8,128)S(1)}, f32[3,20,8,128]{3,2,1,0:T(8,128)S(1)}, u32[]{:S(2)}, u32[]{:S(2)}) %collective-permute-start.6) | collective-permute-done | bytes 245792 | tf_op jit(solution)/shard_map/ppermute | solution.py:682
  31.9 0.0 collective-permute-done.7.r_ref
  31.9 0.0 copy-start.4
  31.9 2.5 %shard_map.137 = (f32[10,18,8,128]{3,2,1,0:T(8,128)S(1)}, f32[2,18,8,128]{3,2,1,0:T(8,128)S(1)}, f32[2,18,8,128]{3,2,1,0:T(8,128)S(1)}, f32[10,2,8,128]{3,2,1,0:T(8,128)S(1)}, f32[10,2,8,128]{3,2,1,0:T(8,128)S(1)}) custom-call(f32[1536,128]{1,0:T(8,128)S(1)} %get-tuple-element.42.rin_ref, f32[384,128]{1,0:T(8,128)S(1)} %get-tuple-element.46.rout_ref, ...), custom_call_target="tpu_custom_call" | custom-call | tf_op jit(solution)/shard_map/pallas_call | solution.py:695
  34.4 0.0 collective-permute-start.8
  34.5 3.0 %collective-permute-start.9 = (f32[2,18,8,128]{3,2,1,0:T(8,128)S(1)}, f32[2,18,8,128]{3,2,1,0:T(8,128)S(1)}, u32[]{:S(2)}, u32[]{:S(2)}) collective-permute-start(f32[2,18,8,128]{3,2,1,0:T(8,128)S(1)} %get-tuple-element.58), channel_id=1, source_target_pairs={{0,224},{32,0},{64,32},{96,64},{128,96},{160,128},{192,160},{224,1... | collective-permute-start | bytes 442376 | tf_op jit(solution)/shard_map/ppermute | solution.py:682
  37.4 0.0 copy-done.4
  37.4 1.2 %shard_map.138 = (f32[8,64,256]{2,1,0:T(8,128)}, f32[8,64,256]{2,1,0:T(8,128)}, f32[4,64,256]{2,1,0:T(8,128)S(1)}, f32[16,256]{1,0:T(8,128)S(1)}, f32[32,512]{1,0:T(8,128)S(1)}, /*index=5*/f32[16,512]{1,0:T(8,128)S(1)}) custom-call(f32[8,16,8,128]{3,2,1,0:T(8,128)S(1)} %shard_map.131.src_ref, f32[2,8,128]{2,1,0:T(8,128)S(1)} %get-tuple-element.39.coef_ref, ...), custom_call_target="tpu_custom_call" | custom-call | tf_op jit(solution)/shard_map/pallas_call | solution.py:695
  38.6 0.0 copy-start.5
  38.6 1.6 %collective-permute-done.8.l_ref = f32[2,18,8,128]{3,2,1,0:T(8,128)S(1)} collective-permute-done((f32[2,18,8,128]{3,2,1,0:T(8,128)S(1)}, f32[2,18,8,128]{3,2,1,0:T(8,128)S(1)}, u32[]{:S(2)}, u32[]{:S(2)}) %collective-permute-start.8) | collective-permute-done | bytes 147488 | tf_op jit(solution)/shard_map/ppermute | solution.py:682
  40.2 0.0 collective-permute-done.9.r_ref
  40.2 0.0 copy-done.5
  40.2 0.7 %shard_map.139 = (f32[2,16,8,128]{3,2,1,0:T(8,128)S(1)}, f32[4,64,256]{2,1,0:T(8,128)S(1)}, f32[10,2,8,128]{3,2,1,0:T(8,128)S(1)}, f32[10,2,8,128]{3,2,1,0:T(8,128)S(1)}, f32[32,128]{1,0:T(8,128)S(1)}) custom-call(f32[8,16,8,128]{3,2,1,0:T(8,128)S(1)} %shard_map.131.src_ref, f32[2,8,128]{2,1,0:T(8,128)S(1)} %get-tuple-element.39.coef_ref, ...), custom_call_target="tpu_custom_call" | custom-call | tf_op jit(solution)/shard_map/pallas_call | solution.py:695
  40.9 0.4 collective-permute-start.10
  41.3 4.8 %collective-permute-start.11 = (f32[10,2,8,128]{3,2,1,0:T(8,128)S(1)}, f32[10,2,8,128]{3,2,1,0:T(8,128)S(1)}, u32[]{:S(2)}, u32[]{:S(2)}) collective-permute-start(f32[10,2,8,128]{3,2,1,0:T(8,128)S(1)} %get-tuple-element.68), channel_id=1, source_target_pairs={{0,31},{1,0},{2,1},{3,2},{4,3},{5,4},{6,5},{7,6},{8,7},{9,8},{10,9... | collective-permute-start | bytes 245768 | tf_op jit(solution)/shard_map/ppermute | solution.py:682
  46.1 19.2 %all_to_all.11 = f32[32,1,128]{2,1,0:T(1,128)S(1)} all-to-all(f32[32,1,128]{2,1,0:T(1,128)S(1)} %bitcast.11), channel_id=1, replica_groups=mesh['sx'=8,'sy'=32] {'sy'}, dimensions={0} | all-to-all | bytes 32768 | tf_op jit(solution)/shard_map/all_to_all | solution.py:794
  65.3 0.0 collective-permute-done.10.d_ref
  65.3 0.0 collective-permute-done.11.u_ref
  65.3 1.2 %shard_map.140 = (f32[8,64,256]{2,1,0:T(8,128)}, f32[8,64,256]{2,1,0:T(8,128)}, f32[8,16]{1,0:T(8,128)}) custom-call(f32[8,64,256]{2,1,0:T(8,128)} %get-tuple-element.55.smooth_in, f32[8,64,256]{2,1,0:T(8,128)} %get-tuple-element.56.res_in, f32[10,18,8,128]{3,2,1,0:T(8,128)S(1)} %get-tuple-element.54.c_ref, ...), custom_call_target="tpu_custom_call", output_to_operand_aliasing={{0}: (0, {}), {1}: (1, {})} | custom-call | tf_op jit(solution)/shard_map/pallas_call | solution.py:695
  (2 shorter events, 0.1 us)
Async XLA Ops:
  2.3 5.1 %collective-permute-start = (f32[10,8,128]{2,1,0:T(8,128)S(1)}, f32[10,8,128]{2,1,0:T(8,128)S(1)}, u32[]{:S(2)}, u32[]{:S(2)}) collective-permute-start(f32[10,8,128]{2,1,0:T(8,128)S(1)} %get-tuple-element.40), channel_id=1, source_target_pairs={{0,1},{1,2},{2,3},{3,4},{4,5},{5,6},{6,7},{7,8},{8,9},{9,10},{10,1... | collective-permute-start | bytes 122888 | tf_op jit(solution)/shard_map/ppermute | solution.py:682
  4.0 4.0 %collective-permute-start.1 = (f32[10,8,128]{2,1,0:T(8,128)S(1)}, f32[10,8,128]{2,1,0:T(8,128)S(1)}, u32[]{:S(2)}, u32[]{:S(2)}) collective-permute-start(f32[10,8,128]{2,1,0:T(8,128)S(1)} %get-tuple-element.41), channel_id=1, source_target_pairs={{0,31},{1,0},{2,1},{3,2},{4,3},{5,4},{6,5},{7,6},{8,7},{9,8},{10,9... | collective-permute-start | bytes 122888 | tf_op jit(solution)/shard_map/ppermute | solution.py:682
  8.0 3.0 %copy-start = (bf16[208,224]{1,0:T(8,128)(2,1)S(1)}, bf16[208,224]{1,0:T(8,128)(2,1)}, u32[]{:S(2)}) copy-start(bf16[208,224]{1,0:T(8,128)(2,1)} %constant.12.clone.a1_ref) | copy-start | bytes 279556
  8.0 5.1 %collective-permute-start.2 = (f32[20,8,128]{2,1,0:T(8,128)S(1)}, f32[20,8,128]{2,1,0:T(8,128)S(1)}, u32[]{:S(2)}, u32[]{:S(2)}) collective-permute-start(f32[20,8,128]{2,1,0:T(8,128)S(1)} %get-tuple-element.43), channel_id=1, source_target_pairs={{0,32},{32,64},{64,96},{96,128},{128,160},{160,192},{192,224},{224... | collective-permute-start | bytes 245768 | tf_op jit(solution)/shard_map/ppermute | solution.py:682
  8.0 5.1 %copy-start.1 = (bf16[224,208]{1,0:T(8,128)(2,1)S(1)}, bf16[224,208]{1,0:T(8,128)(2,1)}, u32[]{:S(2)}) copy-start(bf16[224,208]{1,0:T(8,128)(2,1)} %constant.13.clone.a2_ref) | copy-start | bytes 279556
  8.0 5.1 %copy-start.2 = (f32[104,128]{1,0:T(8,128)S(1)}, f32[104,128]{1,0:T(8,128)}, u32[]{:S(2)}) copy-start(f32[104,128]{1,0:T(8,128)} %constant.15.clone.lk_ref) | copy-start | bytes 159748
  8.0 5.1 %copy-start.3 = (f32[104,128]{1,0:T(8,128)S(1)}, f32[104,128]{1,0:T(8,128)}, u32[]{:S(2)}) copy-start(f32[104,128]{1,0:T(8,128)} %constant.14.clone.lj_ref) | copy-start | bytes 159748
  8.1 5.0 %collective-permute-start.3 = (f32[20,8,128]{2,1,0:T(8,128)S(1)}, f32[20,8,128]{2,1,0:T(8,128)S(1)}, u32[]{:S(2)}, u32[]{:S(2)}) collective-permute-start(f32[20,8,128]{2,1,0:T(8,128)S(1)} %get-tuple-element.44), channel_id=1, source_target_pairs={{0,224},{32,0},{64,32},{96,64},{128,96},{160,128},{192,160},{224,1... | collective-permute-start | bytes 245768 | tf_op jit(solution)/shard_map/ppermute | solution.py:682
  15.0 10.0 %collective-permute-start.4 = (f32[10,3,8,128]{3,2,1,0:T(8,128)S(1)}, f32[10,3,8,128]{3,2,1,0:T(8,128)S(1)}, u32[]{:S(2)}, u32[]{:S(2)}) collective-permute-start(f32[10,3,8,128]{3,2,1,0:T(8,128)S(1)} %get-tuple-element.48), channel_id=1, source_target_pairs={{0,1},{1,2},{2,3},{3,4},{4,5},{5,6},{6,7},{7,8},{8,9},{9,10},{10,1... | collective-permute-start | bytes 368648 | tf_op jit(solution)/shard_map/ppermute | solution.py:682
  16.4 8.7 %collective-permute-start.5 = (f32[10,3,8,128]{3,2,1,0:T(8,128)S(1)}, f32[10,3,8,128]{3,2,1,0:T(8,128)S(1)}, u32[]{:S(2)}, u32[]{:S(2)}) collective-permute-start(f32[10,3,8,128]{3,2,1,0:T(8,128)S(1)} %get-tuple-element.49), channel_id=1, source_target_pairs={{0,31},{1,0},{2,1},{3,2},{4,3},{5,4},{6,5},{7,6},{8,7},{9,8},{10,9... | collective-permute-start | bytes 368648 | tf_op jit(solution)/shard_map/ppermute | solution.py:682
  25.1 6.8 %collective-permute-start.6 = (f32[3,20,8,128]{3,2,1,0:T(8,128)S(1)}, f32[3,20,8,128]{3,2,1,0:T(8,128)S(1)}, u32[]{:S(2)}, u32[]{:S(2)}) collective-permute-start(f32[3,20,8,128]{3,2,1,0:T(8,128)S(1)} %get-tuple-element.50), channel_id=1, source_target_pairs={{0,32},{32,64},{64,96},{96,128},{128,160},{160,192},{192,224},{224... | collective-permute-start | bytes 737288 | tf_op jit(solution)/shard_map/ppermute | solution.py:682
  25.1 6.8 %collective-permute-start.7 = (f32[3,20,8,128]{3,2,1,0:T(8,128)S(1)}, f32[3,20,8,128]{3,2,1,0:T(8,128)S(1)}, u32[]{:S(2)}, u32[]{:S(2)}) collective-permute-start(f32[3,20,8,128]{3,2,1,0:T(8,128)S(1)} %get-tuple-element.51), channel_id=1, source_target_pairs={{0,224},{32,0},{64,32},{96,64},{128,96},{160,128},{192,160},{224,1... | collective-permute-start | bytes 737288 | tf_op jit(solution)/shard_map/ppermute | solution.py:682
  31.9 5.5 %copy-start.4 = (bf16[16,512]{1,0:T(8,128)(2,1)S(1)}, bf16[16,512]{1,0:T(8,128)(2,1)}, u32[]{:S(2)}) copy-start(bf16[16,512]{1,0:T(8,128)(2,1)} %constant.16.clone.wm_ref) | copy-start | bytes 49156
  34.4 5.8 %collective-permute-start.8 = (f32[2,18,8,128]{3,2,1,0:T(8,128)S(1)}, f32[2,18,8,128]{3,2,1,0:T(8,128)S(1)}, u32[]{:S(2)}, u32[]{:S(2)}) collective-permute-start(f32[2,18,8,128]{3,2,1,0:T(8,128)S(1)} %get-tuple-element.57), channel_id=1, source_target_pairs={{0,32},{32,64},{64,96},{96,128},{128,160},{160,192},{192,224},{224... | collective-permute-start | bytes 442376 | tf_op jit(solution)/shard_map/ppermute | solution.py:682
  34.5 5.8 %collective-permute-start.9 = (f32[2,18,8,128]{3,2,1,0:T(8,128)S(1)}, f32[2,18,8,128]{3,2,1,0:T(8,128)S(1)}, u32[]{:S(2)}, u32[]{:S(2)}) collective-permute-start(f32[2,18,8,128]{3,2,1,0:T(8,128)S(1)} %get-tuple-element.58), channel_id=1, source_target_pairs={{0,224},{32,0},{64,32},{96,64},{128,96},{160,128},{192,160},{224,1... | collective-permute-start | bytes 442376 | tf_op jit(solution)/shard_map/ppermute | solution.py:682
  38.6 1.6 %copy-start.5 = (bf16[16,256]{1,0:T(8,128)(2,1)S(1)}, bf16[16,256]{1,0:T(8,128)(2,1)}, u32[]{:S(2)}) copy-start(bf16[16,256]{1,0:T(8,128)(2,1)} %constant.17.clone.wr_ref) | copy-start | bytes 24580
  40.9 24.3 %collective-permute-start.10 = (f32[10,2,8,128]{3,2,1,0:T(8,128)S(1)}, f32[10,2,8,128]{3,2,1,0:T(8,128)S(1)}, u32[]{:S(2)}, u32[]{:S(2)}) collective-permute-start(f32[10,2,8,128]{3,2,1,0:T(8,128)S(1)} %get-tuple-element.67), channel_id=1, source_target_pairs={{0,1},{1,2},{2,3},{3,4},{4,5},{5,6},{6,7},{7,8},{8,9},{9,10},{10,1... | collective-permute-start | bytes 245768 | tf_op jit(solution)/shard_map/ppermute | solution.py:682
  41.3 24.0 %collective-permute-start.11 = (f32[10,2,8,128]{3,2,1,0:T(8,128)S(1)}, f32[10,2,8,128]{3,2,1,0:T(8,128)S(1)}, u32[]{:S(2)}, u32[]{:S(2)}) collective-permute-start(f32[10,2,8,128]{3,2,1,0:T(8,128)S(1)} %get-tuple-element.68), channel_id=1, source_target_pairs={{0,31},{1,0},{2,1},{3,2},{4,3},{5,4},{6,5},{7,6},{8,7},{9,8},{10,9... | collective-permute-start | bytes 245768 | tf_op jit(solution)/shard_map/ppermute | solution.py:682

commit v6 on v5

--- a/solution.py
+++ b/solution.py
@@ -143,13 +143,27 @@
         out[9] = gr
 
 
-def place_kernel(rhs_hbm, slot_ref, src_ref, rhs_ref, sems):
+def place_kernel(
+    rhs_hbm, lam_hbm, slot_ref, coef_ref, src_ref, dinv_ref, rhs_ref, lam_ref, sems
+):
     copies = [
         pltpu.make_async_copy(rhs_hbm.at[x], rhs_ref.at[x], sems.at[x]) for x in range(8)
     ]
+    lam = pltpu.make_async_copy(lam_hbm, lam_ref, sems.at[8])
+    lam.start()
     for c in copies:
         c.start()
     oh = onehot(slot_ref[...])
+    lam.wait()
+    for b in range(2):
+        lanes = slice(b * LANES, (b + 1) * LANES)
+        cx, cy, cz, m = rows_of(coef_ref[0], b * 4)
+        cxl = [cx * float(v) for v in LAM]
+        for t in range(13):
+            row = slice(t * 8, t * 8 + 8)
+            d0 = cy * lam_ref[0, row, :] + cz * lam_ref[1, row, :] + m
+            for i in range(10):
+                dinv_ref[i, row, lanes] = 1.0 / (d0 + cxl[i])
     for x in range(8):
         copies[x].wait()
         g = dot_t(jnp.concatenate(split3(rhs_ref[x]), 0), oh)
@@ -184,33 +198,45 @@
     return r[:104] + r[104:]
 
 
-def finish_solves(layers, coef_ref, a2_ref, lj_ref, lk_ref, spec, wout):
-    even = [i for i in range(0, 10, 2)]
-    odd = [i for i in range(1, 10, 2)]
+def along_x(layers, partial, row, lanes):
+    acc = [None if partial is None else partial[i, row, lanes] for i in range(10)]
+    for p, (low, high) in layers.items():
+        v = low[0][low[1], row, lanes]
+        w = high[0][high[1], row, lanes]
+        h = (v + w, v - w)
+        for i in range(10):
+            term = h[i % 2] * float(SINES[i, p])
+            acc[i] = term if acc[i] is None else acc[i] + term
+    return acc
+
+
+def partial_x(layers, out_ref):
     for b in range(2):
         lanes = slice(b * LANES, (b + 1) * LANES)
-        cx, cy, cz, m = rows_of(coef_ref[0], b * 4)
 
         def chunk(t, carry):
             row = pl.ds(pl.multiple_of(t * 8, 8), 8)
-            v = [ref[at, row, lanes] for ref, at in layers]
-            d0 = cy * lj_ref[row, :] + cz * lk_ref[row, :] + m
-            s = [v[p] + v[9 - p] for p in range(5)]
-            d = [v[p] - v[9 - p] for p in range(5)]
-            z = [None] * 10
-            for i in range(10):
-                h = s if i % 2 == 0 else d
-                acc = h[0] * float(SINES[i, 0])
-                for p in range(1, 5):
-                    acc = acc + h[p] * float(SINES[i, p])
-                z[i] = acc / (d0 + cx * float(LAM[i]))
+            for i, v in enumerate(along_x(layers, None, row, lanes)):
+                out_ref[i, row, lanes] = v
+            return carry
+
+        lax.fori_loop(0, 13, chunk, 0)
+
+
+def finish_solves(layers, partial, dinv_ref, a2_ref, spec, wout):
+    for b in range(2):
+        lanes = slice(b * LANES, (b + 1) * LANES)
+
+        def chunk(t, carry):
+            row = pl.ds(pl.multiple_of(t * 8, 8), 8)
+            z = along_x(layers, partial, row, lanes)
+            z = [z[i] * dinv_ref[i, row, lanes] for i in range(10)]
             for p in range(5):
                 e = z[0] * float(SINES[0, p])
                 o = z[1] * float(SINES[1, p])
-                for i in even[1:]:
+                for i in range(2, 10, 2):
                     e = e + z[i] * float(SINES[i, p])
-                for i in odd[1:]:
-                    o = o + z[i] * float(SINES[i, p])
+                    o = o + z[i + 1] * float(SINES[i + 1, p])
                 spec[p, row, lanes] = e + o
                 spec[9 - p, row, lanes] = e - o
             return carry
@@ -268,15 +294,16 @@
     put(ref, at, 18, jnp.zeros((6, 8, LANES), F32))
 
 
-def first_inner_kernel(src_ref, yd_ref, yu_ref, a1_ref, rin_ref, sin_ref):
+def first_inner_kernel(src_ref, yd_ref, yu_ref, a1_ref, rin_ref, sin_ref, sout):
     _, _, down, up = flags()
     for x in range(8):
         put_layer(rin_ref, x, yd_ref[x : x + 1] * down, src_ref[x], yu_ref[x : x + 1] * up)
-        sin_ref[x] = forward(rin_ref, x * 192, a1_ref)
+        sout[x] = forward(rin_ref, x * 192, a1_ref)
+    partial_x({p: ((sout, p - 1), (sout, 8 - p)) for p in range(1, 5)}, sin_ref)
 
 
 def first_kernel(
-    coef_ref, xl_ref, xr_ref, sin_ref, a1_ref, a2_ref, lj_ref, lk_ref,
+    xl_ref, xr_ref, sin_ref, dinv_ref, a1_ref, a2_ref,
     rout_ref, w_ref, to_down_ref, to_up_ref, sout, spec, wout,
 ):
     left, right, down, up = flags()
@@ -289,8 +316,7 @@
             x_ref[17:18] * (side * up),
         )
         sout[k] = forward(rout_ref, k * 192, a1_ref)
-    layers = [(sout, 0)] + [(sin_ref, x) for x in range(8)] + [(sout, 1)]
-    finish_solves(layers, coef_ref, a2_ref, lj_ref, lk_ref, spec, wout)
+    finish_solves({0: ((sout, 0), (sout, 1))}, sin_ref, dinv_ref, a2_ref, spec, wout)
     for p in range(10):
         line = get(wout, p, 0, 18)
         w_ref[p] = line
@@ -354,7 +380,7 @@
 
 
 def second_inner_kernel(
-    rin_ref, coef_ref, yd_ref, yu_ref, w_ref, d_ref, u_ref, a1_ref, h_ref, sin_ref, cb, r1,
+    rin_ref, coef_ref, yd_ref, yu_ref, w_ref, d_ref, u_ref, a1_ref, h_ref, sin_ref, cb, r1, sout,
 ):
     left, right, down, up = flags()
     for x in range(3, 9):
@@ -368,12 +394,13 @@
         p = 3 + k
         get_r = lambda y, n: get(rin_ref, p - 1, y, n)
         second_residual(get_h, get_r, coefs, p, k, r1, left, right, down, up)
-        sin_ref[k] = forward(r1, k * 192, a1_ref)
+        sout[k] = forward(r1, k * 192, a1_ref)
+    partial_x({p: ((sout, p - 3), (sout, 6 - p)) for p in (3, 4)}, sin_ref)
 
 
 def second_kernel(
     rin_ref, rout_ref, coef_ref, xl_ref, xr_ref, yd_ref, yu_ref, w_ref, l_ref, r_ref, d_ref, u_ref,
-    hin_ref, sin_ref, a1_ref, a2_ref, lj_ref, lk_ref,
+    hin_ref, sin_ref, dinv_ref, a1_ref, a2_ref,
     c_ref, to_left_ref, to_right_ref, own_down_ref, own_up_ref, h, cb, r1, sout, spec, wout,
 ):
     left, right, down, up = flags()
@@ -406,7 +433,6 @@
         else:
             rows = ((x_ref[19], 0), (x_ref[18], 0), (x_ref[18], 4), (x_ref[19], 4))
         coefs.append([Loaded(t) for t in spread_coefs(cb.at[a], rows)])
-    layers = [None] * 3 + [(sin_ref, k) for k in range(4)] + [None] * 3
     for k, p in enumerate((0, 1, 2, 7, 8, 9)):
         if p in (0, 9):
             get_r = lambda y, n: get(rout_ref, 0 if p == 0 else 1, y, n)
@@ -415,8 +441,8 @@
         cb_p = coefs[0 if p == 0 else 2 if p == 9 else 1]
         second_residual(get_h, get_r, cb_p, p, k, r1, left, right, down, up)
         sout[k] = forward(r1, k * 192, a1_ref)
-        layers[p] = (sout, k)
-    finish_solves(layers, coef_ref, a2_ref, lj_ref, lk_ref, spec, wout)
+    layers = {p: ((sout, p), (sout, 5 - p)) for p in range(3)}
+    finish_solves(layers, sin_ref, dinv_ref, a2_ref, spec, wout)
     for p in range(10):
         line = get(wout, p, 0, 18)
         c_ref[p] = get_h(p + 1, 1, 18) + line
@@ -529,14 +555,14 @@
 def middle_kernel(
     src_ref, coef_ref, yd_ref, yu_ref, c_ref, l_ref, r_ref, own_down_ref, own_up_ref,
     mom_ref, pick_ref, member_ref, wm_ref, wr_ref,
-    u_ref, mr_ref, to_down_ref, to_up_ref, part_ref, h, rim,
+    u_ref, mr_ref, to_down_ref, to_up_ref, part_ref, h, rim, edge,
 ):
     left, right, down, up = flags()
     for p in range(10):
         e = add_x(own_down_ref[p], p, l_ref[:, 0:2], r_ref[:, 0:2], left, right)
-        to_down_ref[p] = jnp.concatenate([e[0:1] * down, e[1:2]], 0)
+        edge[0, p] = jnp.concatenate([e[0:1] * down, e[1:2]], 0)
         e = add_x(own_up_ref[p], p, l_ref[:, 16:18], r_ref[:, 16:18], left, right)
-        to_up_ref[p] = jnp.concatenate([e[0:1], e[1:2] * up], 0)
+        edge[1, p] = jnp.concatenate([e[0:1], e[1:2] * up], 0)
         if 3 < p < 6:
             continue
         g = add_x(c_ref[p], p, l_ref, r_ref, left, right)
@@ -551,10 +577,11 @@
         for b in range(2):
             column_residual(get_h, src_ref, coefs[b], x, b, mr_ref, k)
     rim[...] = jnp.zeros((256, 256), F32)
-    for slab, far, near, tile, b, lanes, y_far, y_near in (
-        (to_down_ref, 0, 1, yd_ref, 1, slice(0, LANES), 2, 3),
-        (to_up_ref, 1, 0, yu_ref, 0, slice(LANES, 256), 1, 0),
+    for k, out, far, near, tile, b, lanes, y_far, y_near in (
+        (0, to_down_ref, 0, 1, yd_ref, 1, slice(0, LANES), 2, 3),
+        (1, to_up_ref, 1, 0, yu_ref, 0, slice(LANES, 256), 1, 0),
     ):
+        slab = edge.at[k]
         cf = rows_of(tile[8], b * 4)
         for x in range(8):
             p = x + 1
@@ -565,6 +592,8 @@
                 slab[p + 1, far : far + 1] + slab[p - 1, far : far + 1],
                 slab[p, near : near + 1],
             )
+            out[0, x] = v[0]
+            out[1, x] = -res[0]
             at = (x * 4 + y_near) * 8
             rim[at : at + 8, lanes] = -res[0]
             at = (x * 4 + y_far) * 8
@@ -605,18 +634,15 @@
 
     oh = onehot(slot_ref[...])
     sides = (
-        (d_ref, down, 0, 1, rows_of(coef_ref[0], 0)),
-        (u_ref, up, 1, 0, rows_of(coef_ref[0], 4)),
+        (d_ref, down, jnp.broadcast_to(coef_ref[0, 1:2, :], (8, LANES))),
+        (u_ref, up, jnp.broadcast_to(coef_ref[0, 5:6, :], (8, LANES))),
     )
 
     def added(x):
         out = []
-        for slab, on, far, near, cf in sides:
-            p = x + 1
-            v = slab[p, near : near + 1] * on
-            x_sum = (slab[p + 1, near : near + 1] + slab[p - 1, near : near + 1]) * on
-            res = stencil(cf, v, x_sum, slab[p, far : far + 1] * on)
-            out.append((v[0], -res[0], cf[1] * v[0]))
+        for slab, on, cy in sides:
+            v = slab[0, x] * on
+            out.append((v, slab[1, x] * on, cy * v))
         return out
 
     zero = jnp.zeros((8, LANES), F32)
@@ -706,8 +732,7 @@
 def on_device(right_side, stretch, mass_term, slot_position, coarse_group):
     a1 = jnp.asarray(A_FWD, BF16)
     a2 = jnp.asarray(A_BWD, BF16)
-    lj = jnp.asarray(LAM_J, F32)
-    lk = jnp.asarray(LAM_K, F32)
+    lam = jnp.asarray(np.stack([LAM_J, LAM_K]), F32)
     wm = jnp.asarray(W_MOM, BF16)
     wr = jnp.asarray(W_RIM, BF16)
     row = pltpu.VMEM((1, 256), jnp.int32)
@@ -728,21 +753,29 @@
     )
     yd = ring(to_u, "sy", 1)
     yu = ring(to_d, "sy", -1)
-    src = call(
-        place_kernel, [vm(8, 16, 8, LANES)], (rhs, slot), [(8, 64, 256)], hbm_in=1, sems=8
-    )[0]
+    src, dinv = call(
+        place_kernel,
+        [vm(8, 16, 8, LANES), vm(10, 104, 256)],
+        (rhs, lam, slot, coef),
+        [(8, 64, 256), (2, 104, LANES)],
+        hbm_in=2,
+        sems=9,
+    )
     to_l, to_r = call(rim_kernel, [vm(20, 8, LANES)] * 2, (src, coef, yd, yu))
     xl = ring(to_r, "sx", 1)
     xr = ring(to_l, "sx", -1)
     rin, sin = call(
-        first_inner_kernel, [vm(8 * 192, LANES), vm(8, 104, 256)], (src, yd, yu, a1)
+        first_inner_kernel,
+        [vm(8 * 192, LANES), vm(10, 104, 256)],
+        (src, yd, yu, a1),
+        [(8, 104, 256)],
     )
 
     side = vm(10, 3, 8, LANES)
     rout, w, to_d, to_u = call(
         first_kernel,
         [vm(2 * 192, LANES), vm(10, 18, 8, LANES), side, side],
-        (coef, xl, xr, sin, a1, a2, lj, lk),
+        (xl, xr, sin, dinv, a1, a2),
         [(2, 104, 256), (10, 104, 256), (1920, LANES)],
     )
     d = ring(to_u, "sy", 1)
@@ -752,9 +785,9 @@
     r = ring(to_l, "sx", -1)
     hin, sin = call(
         second_inner_kernel,
-        [vm(6, 20, 8, LANES), vm(4, 104, 256)],
+        [vm(6, 20, 8, LANES), vm(10, 104, 256)],
         (rin, coef, yd, yu, w, d, u, a1),
-        [(4, 4, 8, LANES), (4 * 192, LANES)],
+        [(4, 4, 8, LANES), (4 * 192, LANES), (4, 104, 256)],
     )
 
     slab = vm(2, 18, 8, LANES)
@@ -762,7 +795,7 @@
     c, to_l, to_r, own_d, own_u = call(
         second_kernel,
         [vm(10, 18, 8, LANES), slab, slab, side, side],
-        (rin, rout, coef, xl, xr, yd, yu, w, l, r, d, u, hin, sin, a1, a2, lj, lk),
+        (rin, rout, coef, xl, xr, yd, yu, w, l, r, d, u, hin, sin, dinv, a1, a2),
         [
             (6, 20, 8, LANES),
             (3, 4, 4, 8, LANES),
@@ -774,6 +807,7 @@
     )
     l = ring(to_r, "sx", 1)
     r = ring(to_l, "sx", -1)
+    edge = vm(2, 8, 8, LANES)
     ny = lax.axis_size("sy")
     smooth, res, rin, mom, pick, member = call(
         middle_inner_kernel,
@@ -785,9 +819,9 @@
     )
     uout, rout, to_d, to_u, part = call(
         middle_kernel,
-        [vm(2, 16, 8, LANES), vm(4, 64, 256), side, side, vm(ny, LANES)],
+        [vm(2, 16, 8, LANES), vm(4, 64, 256), edge, edge, vm(ny, LANES)],
         (src, coef, yd, yu, c, l, r, own_d, own_u, mom, pick, member, wm, wr),
-        [(10, 18, 8, LANES), (256, 256)],
+        [(10, 18, 8, LANES), (256, 256), (2, 10, 2, 8, LANES)],
     )
     d = ring(to_u, "sy", 1)
     u = ring(to_d, "sy", -1)

time: 66.6 us -> 66.3 us (level)
  waiting for transfers between devices: 10.7 us -> 9.81 us
    ppermute x12, waiting for transfers between devices: 10.7 us -> 9.81 us  [ring(): return lax.ppermute(value, axis, [(i, (i + by) % n) for i in range(n)])]
  transfers between devices with their start and end apart: 12 -> 12, of which waited for: 5 -> 5; matrix products, arithmetic and copies ran while one was open for 0% -> 0% of each run, Pallas kernels for 8% -> 9%
where the time goes in v6:
time: 66.3 us; the launch traced here: 66.1 us
  starting transfers between devices  22.8 us (34%)
  blocking collectives  19.2 us (29%)
  Pallas kernels  13.5 us (20%)
  waiting for transfers between devices  9.81 us (15%)
  between operations  0.76 us (1%)
    ppermute x12, starting transfers between devices, ring(): return lax.ppermute(value, axis, [(i, (i + by) % n) for i in range(n)])  22.8 us
    all_to_all x1, blocking collectives, on_device(): lax.all_to_all(part, 'sy', split_axis=0, concat_axis=0, tiled=True)  19.2 us
    pallas_call x11, Pallas kernels, call(): pl.pallas_call(kernel, out_shape=outs, in_specs=[hbm if k < hbm_in else v...  13.5 us
    ppermute x12, waiting for transfers between devices, ring(): return lax.ppermute(value, axis, [(i, (i + by) % n) for i in range(n)])  9.81 us
  transfers between devices with their start and end apart: 12, of which 5 were waited for; matrix products, arithmetic and copies ran while one was open for 0% of the time, Pallas kernels for 9%

profile of v6, /device:TPU:8, one launch (start us, length us, event | category | flops | bytes accessed | tf_op | source)
XLA Modules:
  0.0 66.1 jit_solution(17560704990415456274)
XLA Ops:
  0.6 0.0 copy-start
  0.6 1.7 %shard_map.121 = (f32[2,8,128]{2,1,0:T(8,128)S(1)}, f32[10,8,128]{2,1,0:T(8,128)S(1)}, f32[10,8,128]{2,1,0:T(8,128)S(1)}, s32[1,256]{1,0:T(1,128)S(1)}) custom-call(f32[8,64,256]{2,1,0:T(8,128)} %bitcast.12, f32[3,256]{1,0:T(4,128)} %stretch_hbm.1, f32[1,256]{1,0:T(1,128)} %bitcast.16, s32[1,256]{1,0:T(1,128)} %bitcast.17, s32[1,256]{1,0:T(1,128)} %bitcast.18), custom_call_target="tpu_custom_call" | custom-call | tf_op jit(solution)/shard_map/pallas_call | solution.py:721
  2.4 0.0 copy-start.1
  2.4 1.7 %collective-permute-start = (f32[10,8,128]{2,1,0:T(8,128)S(1)}, f32[10,8,128]{2,1,0:T(8,128)S(1)}, u32[]{:S(2)}, u32[]{:S(2)}) collective-permute-start(f32[10,8,128]{2,1,0:T(8,128)S(1)} %get-tuple-element.43), channel_id=1, source_target_pairs={{0,1},{1,2},{2,3},{3,4},{4,5},{5,6},{6,7},{7,8},{8,9},{9,10},{10,1... | collective-permute-start | bytes 122888 | tf_op jit(solution)/shard_map/ppermute | solution.py:708
  4.0 0.7 %collective-permute-start.1 = (f32[10,8,128]{2,1,0:T(8,128)S(1)}, f32[10,8,128]{2,1,0:T(8,128)S(1)}, u32[]{:S(2)}, u32[]{:S(2)}) collective-permute-start(f32[10,8,128]{2,1,0:T(8,128)S(1)} %get-tuple-element.44), channel_id=1, source_target_pairs={{0,31},{1,0},{2,1},{3,2},{4,3},{5,4},{6,5},{7,6},{8,7},{9,8},{10,9... | collective-permute-start | bytes 122888 | tf_op jit(solution)/shard_map/ppermute | solution.py:708
  4.7 3.0 %shard_map.122 = (f32[8,16,8,128]{3,2,1,0:T(8,128)S(1)}, f32[10,104,256]{2,1,0:T(8,128)S(1)}) custom-call(f32[8,64,256]{2,1,0:T(8,128)} %bitcast.13, f32[2,104,128]{2,1,0:T(8,128)} %constant.12.clone.lam_hbm, s32[1,256]{1,0:T(1,128)S(1)} %get-tuple-element.40.slot_ref, f32[2,8,128]{2,1,0:T(8,128)S(1)} %get-tuple-element.41.coef_ref), custom_call_target="tpu_custom_call" | custom-call | tf_op jit(solution)/shard_map/pallas_call | solution.py:721
  7.7 0.0 collective-permute-done.yd_ref
  7.7 0.3 collective-permute-done.1.yu_ref
  8.1 0.0 collective-permute-start.2
  8.1 2.9 %collective-permute-start.3 = (f32[20,8,128]{2,1,0:T(8,128)S(1)}, f32[20,8,128]{2,1,0:T(8,128)S(1)}, u32[]{:S(2)}, u32[]{:S(2)}) collective-permute-start(f32[20,8,128]{2,1,0:T(8,128)S(1)} %get-tuple-element.47), channel_id=1, source_target_pairs={{0,224},{32,0},{64,32},{96,64},{128,96},{160,128},{192,160},{224,1... | collective-permute-start | bytes 245768 | tf_op jit(solution)/shard_map/ppermute | solution.py:708
  11.0 0.0 copy-done
  11.0 0.9 %shard_map.123 = (f32[1536,128]{1,0:T(8,128)S(1)}, f32[10,104,256]{2,1,0:T(8,128)S(1)}) custom-call(f32[8,16,8,128]{3,2,1,0:T(8,128)S(1)} %get-tuple-element.42.src_ref, f32[10,8,128]{2,1,0:T(8,128)S(1)} %collective-permute-done.yd_ref, f32[10,8,128]{2,1,0:T(8,128)S(1)} %collective-permute-done.1.yu_ref, bf16[208,224]{1,0:T(8,128)(2,1)S(1)} %copy-done), custom_call_target="tpu_custom_call" | custom-call | tf_op jit(solution)/shard_map/pallas_call | solution.py:721
  12.0 1.2 %collective-permute-done.2.xl_ref = f32[20,8,128]{2,1,0:T(8,128)S(1)} collective-permute-done((f32[20,8,128]{2,1,0:T(8,128)S(1)}, f32[20,8,128]{2,1,0:T(8,128)S(1)}, u32[]{:S(2)}, u32[]{:S(2)}) %collective-permute-start.2) | collective-permute-done | bytes 81952 | tf_op jit(solution)/shard_map/ppermute | solution.py:708
  13.1 0.0 collective-permute-done.3.xr_ref
  13.1 0.0 copy-done.1
  13.1 1.5 %shard_map.125 = (f32[384,128]{1,0:T(8,128)S(1)}, f32[10,18,8,128]{3,2,1,0:T(8,128)S(1)}, f32[10,3,8,128]{3,2,1,0:T(8,128)S(1)}, f32[10,3,8,128]{3,2,1,0:T(8,128)S(1)}) custom-call(f32[20,8,128]{2,1,0:T(8,128)S(1)} %collective-permute-done.2.xl_ref, f32[20,8,128]{2,1,0:T(8,128)S(1)} %collective-permute-done.3.xr_ref, ...), custom_call_target="tpu_custom_call" | custom-call | tf_op jit(solution)/shard_map/pallas_call | solution.py:721
  14.7 1.4 %collective-permute-start.4 = (f32[10,3,8,128]{3,2,1,0:T(8,128)S(1)}, f32[10,3,8,128]{3,2,1,0:T(8,128)S(1)}, u32[]{:S(2)}, u32[]{:S(2)}) collective-permute-start(f32[10,3,8,128]{3,2,1,0:T(8,128)S(1)} %get-tuple-element.52), channel_id=1, source_target_pairs={{0,1},{1,2},{2,3},{3,4},{4,5},{5,6},{6,7},{7,8},{8,9},{9,10},{10,1... | collective-permute-start | bytes 368648 | tf_op jit(solution)/shard_map/ppermute | solution.py:708
  16.1 5.1 %collective-permute-start.5 = (f32[10,3,8,128]{3,2,1,0:T(8,128)S(1)}, f32[10,3,8,128]{3,2,1,0:T(8,128)S(1)}, u32[]{:S(2)}, u32[]{:S(2)}) collective-permute-start(f32[10,3,8,128]{3,2,1,0:T(8,128)S(1)} %get-tuple-element.53), channel_id=1, source_target_pairs={{0,31},{1,0},{2,1},{3,2},{4,3},{5,4},{6,5},{7,6},{8,7},{9,8},{10,9... | collective-permute-start | bytes 368648 | tf_op jit(solution)/shard_map/ppermute | solution.py:708
  21.1 3.8 %collective-permute-done.4.d_ref = f32[10,3,8,128]{3,2,1,0:T(8,128)S(1)} collective-permute-done((f32[10,3,8,128]{3,2,1,0:T(8,128)S(1)}, f32[10,3,8,128]{3,2,1,0:T(8,128)S(1)}, u32[]{:S(2)}, u32[]{:S(2)}) %collective-permute-start.4) | collective-permute-done | bytes 122912 | tf_op jit(solution)/shard_map/ppermute | solution.py:708
  24.9 0.0 collective-permute-done.5.u_ref
  25.0 0.0 collective-permute-start.6
  25.0 2.9 %collective-permute-start.7 = (f32[3,20,8,128]{3,2,1,0:T(8,128)S(1)}, f32[3,20,8,128]{3,2,1,0:T(8,128)S(1)}, u32[]{:S(2)}, u32[]{:S(2)}) collective-permute-start(f32[3,20,8,128]{3,2,1,0:T(8,128)S(1)} %get-tuple-element.55), channel_id=1, source_target_pairs={{0,224},{32,0},{64,32},{96,64},{128,96},{160,128},{192,160},{224,1... | collective-permute-start | bytes 737288 | tf_op jit(solution)/shard_map/ppermute | solution.py:708
  27.9 1.0 %shard_map.127 = (f32[6,20,8,128]{3,2,1,0:T(8,128)S(1)}, f32[10,104,256]{2,1,0:T(8,128)S(1)}) custom-call(f32[1536,128]{1,0:T(8,128)S(1)} %get-tuple-element.45.rin_ref, f32[2,8,128]{2,1,0:T(8,128)S(1)} %get-tuple-element.41.coef_ref, f32[10,8,128]{2,1,0:T(8,128)S(1)} %collective-permute-done.yd_ref, f32[10,8,128]{2,1,0:T(8,128)S(1)} %collective-permute-done.1.yu_ref, ...), custom_call_target="tpu_custom_call" | custom-call | tf_op jit(solution)/shard_map/pallas_call | solution.py:721
  29.0 2.9 %collective-permute-done.6.l_ref = f32[3,20,8,128]{3,2,1,0:T(8,128)S(1)} collective-permute-done((f32[3,20,8,128]{3,2,1,0:T(8,128)S(1)}, f32[3,20,8,128]{3,2,1,0:T(8,128)S(1)}, u32[]{:S(2)}, u32[]{:S(2)}) %collective-permute-start.6) | collective-permute-done | bytes 245792 | tf_op jit(solution)/shard_map/ppermute | solution.py:708
  31.8 0.0 collective-permute-done.7.r_ref
  31.8 0.0 copy-start.2
  31.8 2.3 %shard_map.128 = (f32[10,18,8,128]{3,2,1,0:T(8,128)S(1)}, f32[2,18,8,128]{3,2,1,0:T(8,128)S(1)}, f32[2,18,8,128]{3,2,1,0:T(8,128)S(1)}, f32[10,2,8,128]{3,2,1,0:T(8,128)S(1)}, f32[10,2,8,128]{3,2,1,0:T(8,128)S(1)}) custom-call(f32[1536,128]{1,0:T(8,128)S(1)} %get-tuple-element.45.rin_ref, f32[384,128]{1,0:T(8,128)S(1)} %get-tuple-element.50.rout_ref, ...), custom_call_target="tpu_custom_call" | custom-call | tf_op jit(solution)/shard_map/pallas_call | solution.py:721
  34.2 0.0 copy-start.3
  34.2 0.0 collective-permute-start.8
  34.2 3.0 %collective-permute-start.9 = (f32[2,18,8,128]{3,2,1,0:T(8,128)S(1)}, f32[2,18,8,128]{3,2,1,0:T(8,128)S(1)}, u32[]{:S(2)}, u32[]{:S(2)}) collective-permute-start(f32[2,18,8,128]{3,2,1,0:T(8,128)S(1)} %get-tuple-element.62), channel_id=1, source_target_pairs={{0,224},{32,0},{64,32},{96,64},{128,96},{160,128},{192,160},{224,1... | collective-permute-start | bytes 442376 | tf_op jit(solution)/shard_map/ppermute | solution.py:708
  37.2 0.0 copy-done.2
  37.2 1.2 %shard_map.129 = (f32[8,64,256]{2,1,0:T(8,128)}, f32[8,64,256]{2,1,0:T(8,128)}, f32[4,64,256]{2,1,0:T(8,128)S(1)}, f32[16,256]{1,0:T(8,128)S(1)}, f32[32,512]{1,0:T(8,128)S(1)}, /*index=5*/f32[16,512]{1,0:T(8,128)S(1)}) custom-call(f32[8,16,8,128]{3,2,1,0:T(8,128)S(1)} %get-tuple-element.42.src_ref, f32[2,8,128]{2,1,0:T(8,128)S(1)} %get-tuple-element.41.coef_ref, ...), custom_call_target="tpu_custom_call" | custom-call | tf_op jit(solution)/shard_map/pallas_call | solution.py:721
  38.3 1.6 %collective-permute-done.8.l_ref = f32[2,18,8,128]{3,2,1,0:T(8,128)S(1)} collective-permute-done((f32[2,18,8,128]{3,2,1,0:T(8,128)S(1)}, f32[2,18,8,128]{3,2,1,0:T(8,128)S(1)}, u32[]{:S(2)}, u32[]{:S(2)}) %collective-permute-start.8) | collective-permute-done | bytes 147488 | tf_op jit(solution)/shard_map/ppermute | solution.py:708
  40.0 0.0 collective-permute-done.9.r_ref
  40.0 0.0 copy-done.3
  40.0 0.7 shard_map.130
  40.6 0.2 collective-permute-start.10
  40.8 5.0 %collective-permute-start.11 = (f32[2,8,8,128]{3,2,1,0:T(8,128)S(1)}, f32[2,8,8,128]{3,2,1,0:T(8,128)S(1)}, u32[]{:S(2)}, u32[]{:S(2)}) collective-permute-start(f32[2,8,8,128]{3,2,1,0:T(8,128)S(1)} %get-tuple-element.72), channel_id=1, source_target_pairs={{0,31},{1,0},{2,1},{3,2},{4,3},{5,4},{6,5},{7,6},{8,7},{9,8},{10,9... | collective-permute-start | bytes 196616 | tf_op jit(solution)/shard_map/ppermute | solution.py:708
  45.8 19.2 %all_to_all.11 = f32[32,1,128]{2,1,0:T(1,128)S(1)} all-to-all(f32[32,1,128]{2,1,0:T(1,128)S(1)} %bitcast.11), channel_id=1, replica_groups=mesh['sx'=8,'sy'=32] {'sy'}, dimensions={0} | all-to-all | bytes 32768 | tf_op jit(solution)/shard_map/all_to_all | solution.py:828
  65.0 0.0 collective-permute-done.10.d_ref
  65.0 0.0 collective-permute-done.11.u_ref
  65.0 1.1 %shard_map.131 = (f32[8,64,256]{2,1,0:T(8,128)}, f32[8,64,256]{2,1,0:T(8,128)}, f32[8,16]{1,0:T(8,128)}) custom-call(f32[8,64,256]{2,1,0:T(8,128)} %get-tuple-element.59.smooth_in, f32[8,64,256]{2,1,0:T(8,128)} %get-tuple-element.60.res_in, f32[10,18,8,128]{3,2,1,0:T(8,128)S(1)} %get-tuple-element.58.c_ref, ...), custom_call_target="tpu_custom_call", output_to_operand_aliasing={{0}: (0, {}), {1}: (1, {})} | custom-call | tf_op jit(solution)/shard_map/pallas_call | solution.py:721
  (2 shorter events, 0.1 us)
Async XLA Ops:
  0.6 10.4 %copy-start = (bf16[208,224]{1,0:T(8,128)(2,1)S(1)}, bf16[208,224]{1,0:T(8,128)(2,1)}, u32[]{:S(2)}) copy-start(bf16[208,224]{1,0:T(8,128)(2,1)} %constant.10.clone.a1_ref) | copy-start | bytes 279556
  2.4 10.8 %copy-start.1 = (bf16[224,208]{1,0:T(8,128)(2,1)S(1)}, bf16[224,208]{1,0:T(8,128)(2,1)}, u32[]{:S(2)}) copy-start(bf16[224,208]{1,0:T(8,128)(2,1)} %constant.11.clone.a2_ref) | copy-start | bytes 279556
  2.4 5.3 %collective-permute-start = (f32[10,8,128]{2,1,0:T(8,128)S(1)}, f32[10,8,128]{2,1,0:T(8,128)S(1)}, u32[]{:S(2)}, u32[]{:S(2)}) collective-permute-start(f32[10,8,128]{2,1,0:T(8,128)S(1)} %get-tuple-element.43), channel_id=1, source_target_pairs={{0,1},{1,2},{2,3},{3,4},{4,5},{5,6},{6,7},{7,8},{8,9},{9,10},{10,1... | collective-permute-start | bytes 122888 | tf_op jit(solution)/shard_map/ppermute | solution.py:708
  4.0 4.0 %collective-permute-start.1 = (f32[10,8,128]{2,1,0:T(8,128)S(1)}, f32[10,8,128]{2,1,0:T(8,128)S(1)}, u32[]{:S(2)}, u32[]{:S(2)}) collective-permute-start(f32[10,8,128]{2,1,0:T(8,128)S(1)} %get-tuple-element.44), channel_id=1, source_target_pairs={{0,31},{1,0},{2,1},{3,2},{4,3},{5,4},{6,5},{7,6},{8,7},{9,8},{10,9... | collective-permute-start | bytes 122888 | tf_op jit(solution)/shard_map/ppermute | solution.py:708
  8.1 5.1 %collective-permute-start.2 = (f32[20,8,128]{2,1,0:T(8,128)S(1)}, f32[20,8,128]{2,1,0:T(8,128)S(1)}, u32[]{:S(2)}, u32[]{:S(2)}) collective-permute-start(f32[20,8,128]{2,1,0:T(8,128)S(1)} %get-tuple-element.46), channel_id=1, source_target_pairs={{0,32},{32,64},{64,96},{96,128},{128,160},{160,192},{192,224},{224... | collective-permute-start | bytes 245768 | tf_op jit(solution)/shard_map/ppermute | solution.py:708
  8.1 5.1 %collective-permute-start.3 = (f32[20,8,128]{2,1,0:T(8,128)S(1)}, f32[20,8,128]{2,1,0:T(8,128)S(1)}, u32[]{:S(2)}, u32[]{:S(2)}) collective-permute-start(f32[20,8,128]{2,1,0:T(8,128)S(1)} %get-tuple-element.47), channel_id=1, source_target_pairs={{0,224},{32,0},{64,32},{96,64},{128,96},{160,128},{192,160},{224,1... | collective-permute-start | bytes 245768 | tf_op jit(solution)/shard_map/ppermute | solution.py:708
  14.7 10.2 %collective-permute-start.4 = (f32[10,3,8,128]{3,2,1,0:T(8,128)S(1)}, f32[10,3,8,128]{3,2,1,0:T(8,128)S(1)}, u32[]{:S(2)}, u32[]{:S(2)}) collective-permute-start(f32[10,3,8,128]{3,2,1,0:T(8,128)S(1)} %get-tuple-element.52), channel_id=1, source_target_pairs={{0,1},{1,2},{2,3},{3,4},{4,5},{5,6},{6,7},{7,8},{8,9},{9,10},{10,1... | collective-permute-start | bytes 368648 | tf_op jit(solution)/shard_map/ppermute | solution.py:708
  16.1 8.9 %collective-permute-start.5 = (f32[10,3,8,128]{3,2,1,0:T(8,128)S(1)}, f32[10,3,8,128]{3,2,1,0:T(8,128)S(1)}, u32[]{:S(2)}, u32[]{:S(2)}) collective-permute-start(f32[10,3,8,128]{3,2,1,0:T(8,128)S(1)} %get-tuple-element.53), channel_id=1, source_target_pairs={{0,31},{1,0},{2,1},{3,2},{4,3},{5,4},{6,5},{7,6},{8,7},{9,8},{10,9... | collective-permute-start | bytes 368648 | tf_op jit(solution)/shard_map/ppermute | solution.py:708
  25.0 6.8 %collective-permute-start.6 = (f32[3,20,8,128]{3,2,1,0:T(8,128)S(1)}, f32[3,20,8,128]{3,2,1,0:T(8,128)S(1)}, u32[]{:S(2)}, u32[]{:S(2)}) collective-permute-start(f32[3,20,8,128]{3,2,1,0:T(8,128)S(1)} %get-tuple-element.54), channel_id=1, source_target_pairs={{0,32},{32,64},{64,96},{96,128},{128,160},{160,192},{192,224},{224... | collective-permute-start | bytes 737288 | tf_op jit(solution)/shard_map/ppermute | solution.py:708
  25.0 6.8 %collective-permute-start.7 = (f32[3,20,8,128]{3,2,1,0:T(8,128)S(1)}, f32[3,20,8,128]{3,2,1,0:T(8,128)S(1)}, u32[]{:S(2)}, u32[]{:S(2)}) collective-permute-start(f32[3,20,8,128]{3,2,1,0:T(8,128)S(1)} %get-tuple-element.55), channel_id=1, source_target_pairs={{0,224},{32,0},{64,32},{96,64},{128,96},{160,128},{192,160},{224,1... | collective-permute-start | bytes 737288 | tf_op jit(solution)/shard_map/ppermute | solution.py:708
  31.8 5.3 %copy-start.2 = (bf16[16,512]{1,0:T(8,128)(2,1)S(1)}, bf16[16,512]{1,0:T(8,128)(2,1)}, u32[]{:S(2)}) copy-start(bf16[16,512]{1,0:T(8,128)(2,1)} %constant.13.clone.wm_ref) | copy-start | bytes 49156
  34.2 5.8 %copy-start.3 = (bf16[16,256]{1,0:T(8,128)(2,1)S(1)}, bf16[16,256]{1,0:T(8,128)(2,1)}, u32[]{:S(2)}) copy-start(bf16[16,256]{1,0:T(8,128)(2,1)} %constant.14.clone.wr_ref) | copy-start | bytes 24580
  34.2 5.8 %collective-permute-start.8 = (f32[2,18,8,128]{3,2,1,0:T(8,128)S(1)}, f32[2,18,8,128]{3,2,1,0:T(8,128)S(1)}, u32[]{:S(2)}, u32[]{:S(2)}) collective-permute-start(f32[2,18,8,128]{3,2,1,0:T(8,128)S(1)} %get-tuple-element.61), channel_id=1, source_target_pairs={{0,32},{32,64},{64,96},{96,128},{128,160},{160,192},{192,224},{224... | collective-permute-start | bytes 442376 | tf_op jit(solution)/shard_map/ppermute | solution.py:708
  34.2 5.8 %collective-permute-start.9 = (f32[2,18,8,128]{3,2,1,0:T(8,128)S(1)}, f32[2,18,8,128]{3,2,1,0:T(8,128)S(1)}, u32[]{:S(2)}, u32[]{:S(2)}) collective-permute-start(f32[2,18,8,128]{3,2,1,0:T(8,128)S(1)} %get-tuple-element.62), channel_id=1, source_target_pairs={{0,224},{32,0},{64,32},{96,64},{128,96},{160,128},{192,160},{224,1... | collective-permute-start | bytes 442376 | tf_op jit(solution)/shard_map/ppermute | solution.py:708
  40.6 24.3 %collective-permute-start.10 = (f32[2,8,8,128]{3,2,1,0:T(8,128)S(1)}, f32[2,8,8,128]{3,2,1,0:T(8,128)S(1)}, u32[]{:S(2)}, u32[]{:S(2)}) collective-permute-start(f32[2,8,8,128]{3,2,1,0:T(8,128)S(1)} %get-tuple-element.71), channel_id=1, source_target_pairs={{0,1},{1,2},{2,3},{3,4},{4,5},{5,6},{6,7},{7,8},{8,9},{9,10},{10,1... | collective-permute-start | bytes 196616 | tf_op jit(solution)/shard_map/ppermute | solution.py:708
  40.8 24.2 %collective-permute-start.11 = (f32[2,8,8,128]{3,2,1,0:T(8,128)S(1)}, f32[2,8,8,128]{3,2,1,0:T(8,128)S(1)}, u32[]{:S(2)}, u32[]{:S(2)}) collective-permute-start(f32[2,8,8,128]{3,2,1,0:T(8,128)S(1)} %get-tuple-element.72), channel_id=1, source_target_pairs={{0,31},{1,0},{2,1},{3,2},{4,3},{5,4},{6,5},{7,6},{8,7},{9,8},{10,9... | collective-permute-start | bytes 196616 | tf_op jit(solution)/shard_map/ppermute | solution.py:708

commit v7 on v6

--- a/solution.py
+++ b/solution.py
@@ -138,9 +138,9 @@
     gr = jnp.concatenate([cg[4:5, :LANES], cg[4:5, LANES:], jnp.zeros((6, LANES), F32)], 0)
     coef_ref[0] = coef
     coef_ref[1] = gr
-    for out in (to_down_ref, to_up_ref):
-        out[8] = coef
-        out[9] = gr
+    pad = jnp.zeros((3, LANES), F32)
+    to_down_ref[8] = jnp.concatenate([coef[0:4], gr[0:1], pad], 0)
+    to_up_ref[8] = jnp.concatenate([coef[4:8], gr[1:2], pad], 0)
 
 
 def place_kernel(
@@ -157,7 +157,7 @@
     lam.wait()
     for b in range(2):
         lanes = slice(b * LANES, (b + 1) * LANES)
-        cx, cy, cz, m = rows_of(coef_ref[0], b * 4)
+        cx, cy, cz, m, _ = rows_of(coef_ref[0], b * 4)
         cxl = [cx * float(v) for v in LAM]
         for t in range(13):
             row = slice(t * 8, t * 8 + 8)
@@ -173,7 +173,7 @@
 
 
 def rim_kernel(src_ref, coef_ref, yd_ref, yu_ref, to_left_ref, to_right_ref):
-    coef_y = jnp.concatenate([yd_ref[8, 4:8, :], yu_ref[8, 0:4, :]], 0)
+    coef_y = jnp.concatenate([yd_ref[8, 0:4, :], yu_ref[8, 0:4, :]], 0)
     for x, out in ((0, to_left_ref), (7, to_right_ref)):
         out[0] = yd_ref[x]
         out[1:17] = src_ref[x]
@@ -304,7 +304,7 @@
 
 def first_kernel(
     xl_ref, xr_ref, sin_ref, dinv_ref, a1_ref, a2_ref,
-    rout_ref, w_ref, to_down_ref, to_up_ref, sout, spec, wout,
+    rout_ref, wout, to_down_ref, to_up_ref, sout, spec,
 ):
     left, right, down, up = flags()
     for k, (x_ref, side) in enumerate(((xl_ref, left), (xr_ref, right))):
@@ -318,17 +318,31 @@
         sout[k] = forward(rout_ref, k * 192, a1_ref)
     finish_solves({0: ((sout, 0), (sout, 1))}, sin_ref, dinv_ref, a2_ref, spec, wout)
     for p in range(10):
-        line = get(wout, p, 0, 18)
-        w_ref[p] = line
-        to_down_ref[p] = line[0:3]
-        to_up_ref[p] = line[15:18]
-
-
-def edge_kernel(w_ref, d_ref, u_ref, to_left_ref, to_right_ref):
+        to_down_ref[p] = get(wout, p, 0, 3)
+        to_up_ref[p] = get(wout, p, 15, 3)
+
+
+def even_row():
+    return lax.rem(lax.axis_index("sy"), 2) == 0
+
+
+class Picked:
+    def __init__(self, first, second):
+        self.refs = (first, second)
+
+    def __getitem__(self, at):
+        return jnp.where(even_row(), self.refs[0][at], self.refs[1][at])
+
+
+def edge_kernel(w_ref, d_ref, u_ref, a_ref, b_ref):
     _, _, down, up = flags()
+    even = even_row()
     for k in range(3):
-        for p, out in ((k, to_left_ref), (7 + k, to_right_ref)):
-            out[k] = with_rows(w_ref[p], 3, d_ref[p], u_ref[p], down, up)
+        to_l, to_r = [
+            with_rows(get(w_ref, p, 0, 18), 3, d_ref[p], u_ref[p], down, up) for p in (k, 7 + k)
+        ]
+        a_ref[k] = jnp.where(even, to_r, to_l)
+        b_ref[k] = jnp.where(even, to_l, to_r)
 
 
 def neighbours_z(u):
@@ -368,7 +382,7 @@
     for b, (tile, at) in enumerate(rows):
         for k, v in enumerate(rows_of(tile, at)):
             cb[b, k] = v
-    return [[cb.at[b, k] for k in range(4)] for b in range(4)]
+    return [[cb.at[b, k] for k in range(5)] for b in range(4)]
 
 
 class Loaded:
@@ -384,9 +398,9 @@
 ):
     left, right, down, up = flags()
     for x in range(3, 9):
-        h_ref[x - 3] = with_rows(w_ref[x - 1], 3, d_ref[x - 1], u_ref[x - 1], down, up)
+        h_ref[x - 3] = with_rows(get(w_ref, x - 1, 0, 18), 3, d_ref[x - 1], u_ref[x - 1], down, up)
     tiles = spread_coefs(
-        cb, ((yd_ref[8], 4), (coef_ref[0], 0), (coef_ref[0], 4), (yu_ref[8], 0))
+        cb, ((yd_ref[8], 0), (coef_ref[0], 0), (coef_ref[0], 4), (yu_ref[8], 0))
     )
     coefs = [Loaded(t) for t in tiles]
     get_h = lambda x, y, n: h_ref[x - 3, y : y + n]
@@ -399,18 +413,19 @@
 
 
 def second_kernel(
-    rin_ref, rout_ref, coef_ref, xl_ref, xr_ref, yd_ref, yu_ref, w_ref, l_ref, r_ref, d_ref, u_ref,
+    rin_ref, rout_ref, coef_ref, xl_ref, xr_ref, yd_ref, yu_ref, w_ref, a_ref, b_ref, d_ref, u_ref,
     hin_ref, sin_ref, dinv_ref, a1_ref, a2_ref,
-    c_ref, to_left_ref, to_right_ref, own_down_ref, own_up_ref, h, cb, r1, sout, spec, wout,
+    c_ref, to_a_ref, to_b_ref, own_down_ref, own_up_ref, h, cb, r1, sout, spec, wout,
 ):
     left, right, down, up = flags()
+    l_ref, r_ref = Picked(a_ref, b_ref), Picked(b_ref, a_ref)
     for x in (0, 1, 2, 9, 10, 11):
         if x == 0:
             g = l_ref[0] * left
         elif x == 11:
             g = r_ref[2] * right
         else:
-            g = with_rows(w_ref[x - 1], 3, d_ref[x - 1], u_ref[x - 1], down, up)
+            g = with_rows(get(w_ref, x - 1, 0, 18), 3, d_ref[x - 1], u_ref[x - 1], down, up)
             if x == 1:
                 g = (g + l_ref[1]) * left
             elif x == 2:
@@ -429,7 +444,7 @@
     coefs = []
     for a, x_ref in ((0, xl_ref), (1, None), (2, xr_ref)):
         if x_ref is None:
-            rows = ((yd_ref[8], 4), (coef_ref[0], 0), (coef_ref[0], 4), (yu_ref[8], 0))
+            rows = ((yd_ref[8], 0), (coef_ref[0], 0), (coef_ref[0], 4), (yu_ref[8], 0))
         else:
             rows = ((x_ref[19], 0), (x_ref[18], 0), (x_ref[18], 4), (x_ref[19], 4))
         coefs.append([Loaded(t) for t in spread_coefs(cb.at[a], rows)])
@@ -446,36 +461,35 @@
     for p in range(10):
         line = get(wout, p, 0, 18)
         c_ref[p] = get_h(p + 1, 1, 18) + line
-        if p < 2:
-            to_left_ref[p] = line
-        if p > 7:
-            to_right_ref[p - 8] = line
         own_down_ref[p] = line[0:2]
         own_up_ref[p] = line[16:18]
-
-
-def add_x(g, p, l, r, left, right):
+    even = even_row()
+    for k in range(2):
+        to_l, to_r = get(wout, k, 0, 18), get(wout, 8 + k, 0, 18)
+        to_a_ref[k] = jnp.where(even, to_r, to_l)
+        to_b_ref[k] = jnp.where(even, to_l, to_r)
+
+
+def add_x(g, p, l, r, left, right, y=slice(0, 18)):
     if p == 0:
-        return (g + l[0]) * left
+        return (g + l[0, y]) * left
     if p == 1:
-        return g + l[1] * left
+        return g + l[1, y] * left
     if p == 8:
-        return g + r[0] * right
+        return g + r[0, y] * right
     if p == 9:
-        return (g + r[1]) * right
+        return (g + r[1, y]) * right
     return g
 
 
 def rows_of(tile, at):
-    return [jnp.broadcast_to(tile[at + k : at + k + 1, :], (8, LANES)) for k in range(4)]
+    c = [jnp.broadcast_to(tile[at + k : at + k + 1, :], (8, LANES)) for k in range(4)]
+    return c + [2.0 * (c[0] + c[1] + c[2]) + c[3]]
 
 
 def stencil(cf, v, x_sum, y_sum):
     above, below = neighbours_z(v)
-    two = v + v
-    return (
-        cf[0] * (two - x_sum) + cf[1] * (two - y_sum) + cf[2] * (two - above - below) + cf[3] * v
-    )
+    return cf[4] * v - cf[0] * x_sum - cf[1] * y_sum - cf[2] * (above + below)
 
 
 def column_residual(get_h, src_ref, cf, x, b, mr_ref, at):
@@ -539,7 +553,7 @@
         mom = mom + moments(wm_ref, 2 + k, mr_ref[k : k + 2].reshape(128, 256))
     mom_ref[...] = mom
     gr = coef_ref[1]
-    group = jnp.concatenate([gr[0:1], gr[1:2], yd_ref[9, 1:2, :], yu_ref[9, 0:1, :]], 1)
+    group = jnp.concatenate([gr[0:1], gr[1:2], yd_ref[8, 4:5, :], yu_ref[8, 4:5, :]], 1)
     ny = pick_ref.shape[0]
     col = (group + 0.5).astype(jnp.int32) - lax.axis_index("sx") * (ny * GRP_DEV)
     owner = lax.shift_right_logical(col, 4)
@@ -553,15 +567,16 @@
 
 
 def middle_kernel(
-    src_ref, coef_ref, yd_ref, yu_ref, c_ref, l_ref, r_ref, own_down_ref, own_up_ref,
+    src_ref, coef_ref, yd_ref, yu_ref, c_ref, a_ref, b_ref, own_down_ref, own_up_ref,
     mom_ref, pick_ref, member_ref, wm_ref, wr_ref,
     u_ref, mr_ref, to_down_ref, to_up_ref, part_ref, h, rim, edge,
 ):
     left, right, down, up = flags()
+    l_ref, r_ref = Picked(a_ref, b_ref), Picked(b_ref, a_ref)
     for p in range(10):
-        e = add_x(own_down_ref[p], p, l_ref[:, 0:2], r_ref[:, 0:2], left, right)
+        e = add_x(own_down_ref[p], p, l_ref, r_ref, left, right, slice(0, 2))
         edge[0, p] = jnp.concatenate([e[0:1] * down, e[1:2]], 0)
-        e = add_x(own_up_ref[p], p, l_ref[:, 16:18], r_ref[:, 16:18], left, right)
+        e = add_x(own_up_ref[p], p, l_ref, r_ref, left, right, slice(16, 18))
         edge[1, p] = jnp.concatenate([e[0:1], e[1:2] * up], 0)
         if 3 < p < 6:
             continue
@@ -577,12 +592,12 @@
         for b in range(2):
             column_residual(get_h, src_ref, coefs[b], x, b, mr_ref, k)
     rim[...] = jnp.zeros((256, 256), F32)
-    for k, out, far, near, tile, b, lanes, y_far, y_near in (
-        (0, to_down_ref, 0, 1, yd_ref, 1, slice(0, LANES), 2, 3),
-        (1, to_up_ref, 1, 0, yu_ref, 0, slice(LANES, 256), 1, 0),
+    for k, out, far, near, tile, lanes, y_far, y_near in (
+        (0, to_down_ref, 0, 1, yd_ref, slice(0, LANES), 2, 3),
+        (1, to_up_ref, 1, 0, yu_ref, slice(LANES, 256), 1, 0),
     ):
         slab = edge.at[k]
-        cf = rows_of(tile[8], b * 4)
+        cf = rows_of(tile[8], 0)
         for x in range(8):
             p = x + 1
             v = slab[p, far : far + 1]
@@ -708,6 +723,18 @@
     return lax.ppermute(value, axis, [(i, (i + by) % n) for i in range(n)])
 
 
+def snake(value, by):
+    nx = lax.axis_size("sx")
+    ny = lax.axis_size("sy")
+    pairs = []
+    for i in range(nx):
+        for j in range(ny):
+            to = i + (by if j % 2 == 0 else -by)
+            target = to * ny + j if 0 <= to < nx else i * ny + (j ^ 1)
+            pairs.append((i * ny + j, target))
+    return lax.ppermute(value, ("sx", "sy"), pairs)
+
+
 def call(kernel, outs, args, scratch=(), hbm_in=0, hbm_out=0, sems=0, alias=0):
     vmem = pl.BlockSpec(memory_space=pltpu.VMEM)
     hbm = pl.BlockSpec(memory_space=pltpu.HBM)
@@ -739,7 +766,7 @@
     rhs = right_side.reshape(8, 64, 256)
     coef, to_d, to_u, slot = call(
         start_kernel,
-        [vm(2, 8, LANES), vm(10, 8, LANES), vm(10, 8, LANES), row],
+        [vm(2, 8, LANES), vm(9, 8, LANES), vm(9, 8, LANES), row],
         (
             rhs,
             stretch,
@@ -774,39 +801,39 @@
     side = vm(10, 3, 8, LANES)
     rout, w, to_d, to_u = call(
         first_kernel,
-        [vm(2 * 192, LANES), vm(10, 18, 8, LANES), side, side],
+        [vm(2 * 192, LANES), vm(1920, LANES), side, side],
         (xl, xr, sin, dinv, a1, a2),
-        [(2, 104, 256), (10, 104, 256), (1920, LANES)],
+        [(2, 104, 256), (10, 104, 256)],
     )
     d = ring(to_u, "sy", 1)
     u = ring(to_d, "sy", -1)
-    to_l, to_r = call(edge_kernel, [vm(3, 20, 8, LANES)] * 2, (w, d, u))
-    l = ring(to_r, "sx", 1)
-    r = ring(to_l, "sx", -1)
+    to_a, to_b = call(edge_kernel, [vm(3, 20, 8, LANES)] * 2, (w, d, u))
+    a = snake(to_a, 1)
+    b = snake(to_b, -1)
     hin, sin = call(
         second_inner_kernel,
         [vm(6, 20, 8, LANES), vm(10, 104, 256)],
         (rin, coef, yd, yu, w, d, u, a1),
-        [(4, 4, 8, LANES), (4 * 192, LANES), (4, 104, 256)],
+        [(4, 5, 8, LANES), (4 * 192, LANES), (4, 104, 256)],
     )
 
     slab = vm(2, 18, 8, LANES)
     side = vm(10, 2, 8, LANES)
-    c, to_l, to_r, own_d, own_u = call(
+    c, to_a, to_b, own_d, own_u = call(
         second_kernel,
         [vm(10, 18, 8, LANES), slab, slab, side, side],
-        (rin, rout, coef, xl, xr, yd, yu, w, l, r, d, u, hin, sin, dinv, a1, a2),
+        (rin, rout, coef, xl, xr, yd, yu, w, a, b, d, u, hin, sin, dinv, a1, a2),
         [
             (6, 20, 8, LANES),
-            (3, 4, 4, 8, LANES),
+            (3, 4, 5, 8, LANES),
             (6 * 192, LANES),
             (6, 104, 256),
             (10, 104, 256),
             (1920, LANES),
         ],
     )
-    l = ring(to_r, "sx", 1)
-    r = ring(to_l, "sx", -1)
+    a = snake(to_a, 1)
+    b = snake(to_b, -1)
     edge = vm(2, 8, 8, LANES)
     ny = lax.axis_size("sy")
     smooth, res, rin, mom, pick, member = call(
@@ -820,7 +847,7 @@
     uout, rout, to_d, to_u, part = call(
         middle_kernel,
         [vm(2, 16, 8, LANES), vm(4, 64, 256), edge, edge, vm(ny, LANES)],
-        (src, coef, yd, yu, c, l, r, own_d, own_u, mom, pick, member, wm, wr),
+        (src, coef, yd, yu, c, a, b, own_d, own_u, mom, pick, member, wm, wr),
         [(10, 18, 8, LANES), (256, 256), (2, 10, 2, 8, LANES)],
     )
     d = ring(to_u, "sy", 1)

time: 66.3 us -> 65.1 us (0.982)
  waiting for transfers between devices: 9.81 us -> 14 us
  starting transfers between devices: 22.8 us -> 19.5 us
  blocking collectives: 19.2 us -> 17.1 us
    ppermute x12 -> x8, starting transfers between devices: 22.8 us -> 13.8 us  [ring(): return lax.ppermute(value, axis, [(i, (i + by) % n) for i in range(n)])]
    ppermute x0 -> x4, waiting for transfers between devices: none -> 8.78 us  [snake(): return lax.ppermute(value, ('sx', 'sy'), pairs)]
    ppermute x0 -> x4, starting transfers between devices: none -> 5.73 us  [snake(): return lax.ppermute(value, ('sx', 'sy'), pairs)]
    ppermute x12 -> x8, waiting for transfers between devices: 9.81 us -> 5.26 us  [ring(): return lax.ppermute(value, axis, [(i, (i + by) % n) for i in range(n)])]
    all_to_all x1, blocking collectives: 19.2 us -> 17.1 us  [on_device(): lax.all_to_all(part, 'sy', split_axis=0, concat_axis=0, tiled=True)]
  transfers between devices with their start and end apart: 12 -> 12, of which waited for: 5 -> 7; matrix products, arithmetic and copies ran while one was open for 0% -> 0% of each run, Pallas kernels for 9% -> 9%
where the time goes in v7:
time: 65.1 us; the launch traced here: 64.9 us
  starting transfers between devices  19.5 us (30%)
  blocking collectives  17.1 us (26%)
  waiting for transfers between devices  14 us (22%)
  Pallas kernels  13.4 us (21%)
  between operations  0.76 us (1%)
    all_to_all x1, blocking collectives, on_device(): lax.all_to_all(part, 'sy', split_axis=0, concat_axis=0, tiled=True)  17.1 us
    ppermute x8, starting transfers between devices, ring(): return lax.ppermute(value, axis, [(i, (i + by) % n) for i in range(n)])  13.8 us
    pallas_call x11, Pallas kernels, call(): pl.pallas_call(kernel, out_shape=outs, in_specs=[hbm if k < hbm_in else v...  13.4 us
    ppermute x4, waiting for transfers between devices, snake(): return lax.ppermute(value, ('sx', 'sy'), pairs)  8.78 us
    ppermute x4, starting transfers between devices, snake(): return lax.ppermute(value, ('sx', 'sy'), pairs)  5.73 us
    ppermute x8, waiting for transfers between devices, ring(): return lax.ppermute(value, axis, [(i, (i + by) % n) for i in range(n)])  5.26 us
  transfers between devices with their start and end apart: 12, of which 7 were waited for; matrix products, arithmetic and copies ran while one was open for 0% of the time, Pallas kernels for 9%

profile of v7, /device:TPU:8, one launch (start us, length us, event | category | flops | bytes accessed | tf_op | source)
XLA Modules:
  0.0 64.9 jit_solution(3444861937089871144)
XLA Ops:
  0.6 0.0 copy-start
  0.6 1.7 %shard_map.121 = (f32[2,8,128]{2,1,0:T(8,128)S(1)}, f32[9,8,128]{2,1,0:T(8,128)S(1)}, f32[9,8,128]{2,1,0:T(8,128)S(1)}, s32[1,256]{1,0:T(1,128)S(1)}) custom-call(f32[8,64,256]{2,1,0:T(8,128)} %bitcast.12, f32[3,256]{1,0:T(4,128)} %stretch_hbm.1, f32[1,256]{1,0:T(1,128)} %bitcast.16, s32[1,256]{1,0:T(1,128)} %bitcast.17, s32[1,256]{1,0:T(1,128)} %bitcast.18), custom_call_target="tpu_custom_call" | custom-call | tf_op jit(solution)/shard_map/pallas_call | solution.py:748
  2.4 0.0 copy-start.1
  2.4 1.7 %collective-permute-start = (f32[9,8,128]{2,1,0:T(8,128)S(1)}, f32[9,8,128]{2,1,0:T(8,128)S(1)}, u32[]{:S(2)}, u32[]{:S(2)}) collective-permute-start(f32[9,8,128]{2,1,0:T(8,128)S(1)} %get-tuple-element.43), channel_id=1, source_target_pairs={{0,1},{1,2},{2,3},{3,4},{4,5},{5,6},{6,7},{7,8},{8,9},{9,10},{10,1... | collective-permute-start | bytes 110600 | tf_op jit(solution)/shard_map/ppermute | solution.py:723
  4.0 0.7 %collective-permute-start.1 = (f32[9,8,128]{2,1,0:T(8,128)S(1)}, f32[9,8,128]{2,1,0:T(8,128)S(1)}, u32[]{:S(2)}, u32[]{:S(2)}) collective-permute-start(f32[9,8,128]{2,1,0:T(8,128)S(1)} %get-tuple-element.44), channel_id=1, source_target_pairs={{0,31},{1,0},{2,1},{3,2},{4,3},{5,4},{6,5},{7,6},{8,7},{9,8},{10,9... | collective-permute-start | bytes 110600 | tf_op jit(solution)/shard_map/ppermute | solution.py:723
  4.7 3.0 %shard_map.122 = (f32[8,16,8,128]{3,2,1,0:T(8,128)S(1)}, f32[10,104,256]{2,1,0:T(8,128)S(1)}) custom-call(f32[8,64,256]{2,1,0:T(8,128)} %bitcast.13, f32[2,104,128]{2,1,0:T(8,128)} %constant.12.clone.lam_hbm, s32[1,256]{1,0:T(1,128)S(1)} %get-tuple-element.40.slot_ref, f32[2,8,128]{2,1,0:T(8,128)S(1)} %get-tuple-element.41.coef_ref), custom_call_target="tpu_custom_call" | custom-call | tf_op jit(solution)/shard_map/pallas_call | solution.py:748
  7.7 0.0 collective-permute-done.yd_ref
  7.7 0.3 collective-permute-done.1.yu_ref
  8.0 0.0 collective-permute-start.2
  8.0 2.9 %collective-permute-start.3 = (f32[20,8,128]{2,1,0:T(8,128)S(1)}, f32[20,8,128]{2,1,0:T(8,128)S(1)}, u32[]{:S(2)}, u32[]{:S(2)}) collective-permute-start(f32[20,8,128]{2,1,0:T(8,128)S(1)} %get-tuple-element.47), channel_id=1, source_target_pairs={{0,224},{32,0},{64,32},{96,64},{128,96},{160,128},{192,160},{224,1... | collective-permute-start | bytes 245768 | tf_op jit(solution)/shard_map/ppermute | solution.py:723
  11.0 0.0 copy-done
  11.0 0.9 %shard_map.123 = (f32[1536,128]{1,0:T(8,128)S(1)}, f32[10,104,256]{2,1,0:T(8,128)S(1)}) custom-call(f32[8,16,8,128]{3,2,1,0:T(8,128)S(1)} %get-tuple-element.42.src_ref, f32[9,8,128]{2,1,0:T(8,128)S(1)} %collective-permute-done.yd_ref, f32[9,8,128]{2,1,0:T(8,128)S(1)} %collective-permute-done.1.yu_ref, bf16[208,224]{1,0:T(8,128)(2,1)S(1)} %copy-done), custom_call_target="tpu_custom_call" | custom-call | tf_op jit(solution)/shard_map/pallas_call | solution.py:748
  11.9 1.2 %collective-permute-done.2.xl_ref = f32[20,8,128]{2,1,0:T(8,128)S(1)} collective-permute-done((f32[20,8,128]{2,1,0:T(8,128)S(1)}, f32[20,8,128]{2,1,0:T(8,128)S(1)}, u32[]{:S(2)}, u32[]{:S(2)}) %collective-permute-start.2) | collective-permute-done | bytes 81952 | tf_op jit(solution)/shard_map/ppermute | solution.py:723
  13.1 0.0 collective-permute-done.3.xr_ref
  13.1 0.0 copy-done.1
  13.1 1.5 %shard_map.125 = (f32[384,128]{1,0:T(8,128)S(1)}, f32[1920,128]{1,0:T(8,128)S(1)}, f32[10,3,8,128]{3,2,1,0:T(8,128)S(1)}, f32[10,3,8,128]{3,2,1,0:T(8,128)S(1)}) custom-call(f32[20,8,128]{2,1,0:T(8,128)S(1)} %collective-permute-done.2.xl_ref, f32[20,8,128]{2,1,0:T(8,128)S(1)} %collective-permute-done.3.xr_ref, ...), custom_call_target="tpu_custom_call" | custom-call | tf_op jit(solution)/shard_map/pallas_call | solution.py:748
  14.6 1.4 %collective-permute-start.4 = (f32[10,3,8,128]{3,2,1,0:T(8,128)S(1)}, f32[10,3,8,128]{3,2,1,0:T(8,128)S(1)}, u32[]{:S(2)}, u32[]{:S(2)}) collective-permute-start(f32[10,3,8,128]{3,2,1,0:T(8,128)S(1)} %get-tuple-element.52), channel_id=1, source_target_pairs={{0,1},{1,2},{2,3},{3,4},{4,5},{5,6},{6,7},{7,8},{8,9},{9,10},{10,1... | collective-permute-start | bytes 368648 | tf_op jit(solution)/shard_map/ppermute | solution.py:723
  16.0 5.1 %collective-permute-start.5 = (f32[10,3,8,128]{3,2,1,0:T(8,128)S(1)}, f32[10,3,8,128]{3,2,1,0:T(8,128)S(1)}, u32[]{:S(2)}, u32[]{:S(2)}) collective-permute-start(f32[10,3,8,128]{3,2,1,0:T(8,128)S(1)} %get-tuple-element.53), channel_id=1, source_target_pairs={{0,31},{1,0},{2,1},{3,2},{4,3},{5,4},{6,5},{7,6},{8,7},{9,8},{10,9... | collective-permute-start | bytes 368648 | tf_op jit(solution)/shard_map/ppermute | solution.py:723
  21.1 3.8 %collective-permute-done.4.d_ref = f32[10,3,8,128]{3,2,1,0:T(8,128)S(1)} collective-permute-done((f32[10,3,8,128]{3,2,1,0:T(8,128)S(1)}, f32[10,3,8,128]{3,2,1,0:T(8,128)S(1)}, u32[]{:S(2)}, u32[]{:S(2)}) %collective-permute-start.4) | collective-permute-done | bytes 122912 | tf_op jit(solution)/shard_map/ppermute | solution.py:723
  24.9 0.0 collective-permute-done.5.u_ref
  25.0 5.1 %collective-permute-start.6 = (f32[3,20,8,128]{3,2,1,0:T(8,128)S(1)}, f32[3,20,8,128]{3,2,1,0:T(8,128)S(1)}, u32[]{:S(2)}, u32[]{:S(2)}) collective-permute-start(f32[3,20,8,128]{3,2,1,0:T(8,128)S(1)} %get-tuple-element.54), channel_id=1, source_target_pairs={{0,32},{1,0},{2,34},{3,2},{4,36},{5,4},{6,38},{7,6},{8,40},{9,8},{... | collective-permute-start | bytes 737288 | tf_op jit(solution)/shard_map/ppermute | solution.py:735
  30.1 0.0 collective-permute-start.7
  30.1 1.0 %shard_map.127 = (f32[6,20,8,128]{3,2,1,0:T(8,128)S(1)}, f32[10,104,256]{2,1,0:T(8,128)S(1)}) custom-call(f32[1536,128]{1,0:T(8,128)S(1)} %get-tuple-element.45.rin_ref, f32[2,8,128]{2,1,0:T(8,128)S(1)} %get-tuple-element.41.coef_ref, f32[9,8,128]{2,1,0:T(8,128)S(1)} %collective-permute-done.yd_ref, f32[9,8,128]{2,1,0:T(8,128)S(1)} %collective-permute-done.1.yu_ref, ...), custom_call_target="tpu_custom_call" | custom-call | tf_op jit(solution)/shard_map/pallas_call | solution.py:748
  31.1 2.7 %collective-permute-done.6.a_ref = f32[3,20,8,128]{3,2,1,0:T(8,128)S(1)} collective-permute-done((f32[3,20,8,128]{3,2,1,0:T(8,128)S(1)}, f32[3,20,8,128]{3,2,1,0:T(8,128)S(1)}, u32[]{:S(2)}, u32[]{:S(2)}) %collective-permute-start.6) | collective-permute-done | bytes 245792 | tf_op jit(solution)/shard_map/ppermute | solution.py:735
  33.8 2.5 %collective-permute-done.7.b_ref = f32[3,20,8,128]{3,2,1,0:T(8,128)S(1)} collective-permute-done((f32[3,20,8,128]{3,2,1,0:T(8,128)S(1)}, f32[3,20,8,128]{3,2,1,0:T(8,128)S(1)}, u32[]{:S(2)}, u32[]{:S(2)}) %collective-permute-start.7) | collective-permute-done | bytes 245792 | tf_op jit(solution)/shard_map/ppermute | solution.py:735
  36.3 0.0 copy-start.2
  36.3 2.3 %shard_map.128 = (f32[10,18,8,128]{3,2,1,0:T(8,128)S(1)}, f32[2,18,8,128]{3,2,1,0:T(8,128)S(1)}, f32[2,18,8,128]{3,2,1,0:T(8,128)S(1)}, f32[10,2,8,128]{3,2,1,0:T(8,128)S(1)}, f32[10,2,8,128]{3,2,1,0:T(8,128)S(1)}) custom-call(f32[1536,128]{1,0:T(8,128)S(1)} %get-tuple-element.45.rin_ref, f32[384,128]{1,0:T(8,128)S(1)} %get-tuple-element.50.rout_ref, ...), custom_call_target="tpu_custom_call" | custom-call | tf_op jit(solution)/shard_map/pallas_call | solution.py:748
  38.6 0.0 copy-start.3
  38.6 0.1 collective-permute-start.8
  38.7 0.5 collective-permute-start.9
  39.2 0.0 copy-done.2
  39.2 1.2 %shard_map.129 = (f32[8,64,256]{2,1,0:T(8,128)}, f32[8,64,256]{2,1,0:T(8,128)}, f32[4,64,256]{2,1,0:T(8,128)S(1)}, f32[16,256]{1,0:T(8,128)S(1)}, f32[32,512]{1,0:T(8,128)S(1)}, /*index=5*/f32[16,512]{1,0:T(8,128)S(1)}) custom-call(f32[8,16,8,128]{3,2,1,0:T(8,128)S(1)} %get-tuple-element.42.src_ref, f32[2,8,128]{2,1,0:T(8,128)S(1)} %get-tuple-element.41.coef_ref, ...), custom_call_target="tpu_custom_call" | custom-call | tf_op jit(solution)/shard_map/pallas_call | solution.py:748
  40.4 1.0 %collective-permute-done.8.a_ref = f32[2,18,8,128]{3,2,1,0:T(8,128)S(1)} collective-permute-done((f32[2,18,8,128]{3,2,1,0:T(8,128)S(1)}, f32[2,18,8,128]{3,2,1,0:T(8,128)S(1)}, u32[]{:S(2)}, u32[]{:S(2)}) %collective-permute-start.8) | collective-permute-done | bytes 147488 | tf_op jit(solution)/shard_map/ppermute | solution.py:735
  41.4 2.6 %collective-permute-done.9.b_ref = f32[2,18,8,128]{3,2,1,0:T(8,128)S(1)} collective-permute-done((f32[2,18,8,128]{3,2,1,0:T(8,128)S(1)}, f32[2,18,8,128]{3,2,1,0:T(8,128)S(1)}, u32[]{:S(2)}, u32[]{:S(2)}) %collective-permute-start.9) | collective-permute-done | bytes 147488 | tf_op jit(solution)/shard_map/ppermute | solution.py:735
  43.9 0.0 copy-done.3
  43.9 0.6 shard_map.130
  44.6 0.0 collective-permute-start.10
  44.6 2.0 %collective-permute-start.11 = (f32[2,8,8,128]{3,2,1,0:T(8,128)S(1)}, f32[2,8,8,128]{3,2,1,0:T(8,128)S(1)}, u32[]{:S(2)}, u32[]{:S(2)}) collective-permute-start(f32[2,8,8,128]{3,2,1,0:T(8,128)S(1)} %get-tuple-element.72), channel_id=1, source_target_pairs={{0,31},{1,0},{2,1},{3,2},{4,3},{5,4},{6,5},{7,6},{8,7},{9,8},{10,9... | collective-permute-start | bytes 196616 | tf_op jit(solution)/shard_map/ppermute | solution.py:723
  46.6 17.1 %all_to_all.11 = f32[32,1,128]{2,1,0:T(1,128)S(1)} all-to-all(f32[32,1,128]{2,1,0:T(1,128)S(1)} %bitcast.11), channel_id=1, replica_groups=mesh['sx'=8,'sy'=32] {'sy'}, dimensions={0} | all-to-all | bytes 32768 | tf_op jit(solution)/shard_map/all_to_all | solution.py:855
  63.8 0.0 collective-permute-done.10.d_ref
  63.8 0.0 collective-permute-done.11.u_ref
  63.8 1.1 %shard_map.131 = (f32[8,64,256]{2,1,0:T(8,128)}, f32[8,64,256]{2,1,0:T(8,128)}, f32[8,16]{1,0:T(8,128)}) custom-call(f32[8,64,256]{2,1,0:T(8,128)} %get-tuple-element.59.smooth_in, f32[8,64,256]{2,1,0:T(8,128)} %get-tuple-element.60.res_in, f32[10,18,8,128]{3,2,1,0:T(8,128)S(1)} %get-tuple-element.58.c_ref, ...), custom_call_target="tpu_custom_call", output_to_operand_aliasing={{0}: (0, {}), {1}: (1, {})} | custom-call | tf_op jit(solution)/shard_map/pallas_call | solution.py:748
  (2 shorter events, 0.1 us)
Async XLA Ops:
  0.6 10.3 %copy-start = (bf16[208,224]{1,0:T(8,128)(2,1)S(1)}, bf16[208,224]{1,0:T(8,128)(2,1)}, u32[]{:S(2)}) copy-start(bf16[208,224]{1,0:T(8,128)(2,1)} %constant.10.clone.a1_ref) | copy-start | bytes 279556
  2.4 10.7 %copy-start.1 = (bf16[224,208]{1,0:T(8,128)(2,1)S(1)}, bf16[224,208]{1,0:T(8,128)(2,1)}, u32[]{:S(2)}) copy-start(bf16[224,208]{1,0:T(8,128)(2,1)} %constant.11.clone.a2_ref) | copy-start | bytes 279556
  2.4 5.3 %collective-permute-start = (f32[9,8,128]{2,1,0:T(8,128)S(1)}, f32[9,8,128]{2,1,0:T(8,128)S(1)}, u32[]{:S(2)}, u32[]{:S(2)}) collective-permute-start(f32[9,8,128]{2,1,0:T(8,128)S(1)} %get-tuple-element.43), channel_id=1, source_target_pairs={{0,1},{1,2},{2,3},{3,4},{4,5},{5,6},{6,7},{7,8},{8,9},{9,10},{10,1... | collective-permute-start | bytes 110600 | tf_op jit(solution)/shard_map/ppermute | solution.py:723
  4.0 4.0 %collective-permute-start.1 = (f32[9,8,128]{2,1,0:T(8,128)S(1)}, f32[9,8,128]{2,1,0:T(8,128)S(1)}, u32[]{:S(2)}, u32[]{:S(2)}) collective-permute-start(f32[9,8,128]{2,1,0:T(8,128)S(1)} %get-tuple-element.44), channel_id=1, source_target_pairs={{0,31},{1,0},{2,1},{3,2},{4,3},{5,4},{6,5},{7,6},{8,7},{9,8},{10,9... | collective-permute-start | bytes 110600 | tf_op jit(solution)/shard_map/ppermute | solution.py:723
  8.0 5.1 %collective-permute-start.2 = (f32[20,8,128]{2,1,0:T(8,128)S(1)}, f32[20,8,128]{2,1,0:T(8,128)S(1)}, u32[]{:S(2)}, u32[]{:S(2)}) collective-permute-start(f32[20,8,128]{2,1,0:T(8,128)S(1)} %get-tuple-element.46), channel_id=1, source_target_pairs={{0,32},{32,64},{64,96},{96,128},{128,160},{160,192},{192,224},{224... | collective-permute-start | bytes 245768 | tf_op jit(solution)/shard_map/ppermute | solution.py:723
  8.0 5.1 %collective-permute-start.3 = (f32[20,8,128]{2,1,0:T(8,128)S(1)}, f32[20,8,128]{2,1,0:T(8,128)S(1)}, u32[]{:S(2)}, u32[]{:S(2)}) collective-permute-start(f32[20,8,128]{2,1,0:T(8,128)S(1)} %get-tuple-element.47), channel_id=1, source_target_pairs={{0,224},{32,0},{64,32},{96,64},{128,96},{160,128},{192,160},{224,1... | collective-permute-start | bytes 245768 | tf_op jit(solution)/shard_map/ppermute | solution.py:723
  14.6 10.3 %collective-permute-start.4 = (f32[10,3,8,128]{3,2,1,0:T(8,128)S(1)}, f32[10,3,8,128]{3,2,1,0:T(8,128)S(1)}, u32[]{:S(2)}, u32[]{:S(2)}) collective-permute-start(f32[10,3,8,128]{3,2,1,0:T(8,128)S(1)} %get-tuple-element.52), channel_id=1, source_target_pairs={{0,1},{1,2},{2,3},{3,4},{4,5},{5,6},{6,7},{7,8},{8,9},{9,10},{10,1... | collective-permute-start | bytes 368648 | tf_op jit(solution)/shard_map/ppermute | solution.py:723
  16.0 8.9 %collective-permute-start.5 = (f32[10,3,8,128]{3,2,1,0:T(8,128)S(1)}, f32[10,3,8,128]{3,2,1,0:T(8,128)S(1)}, u32[]{:S(2)}, u32[]{:S(2)}) collective-permute-start(f32[10,3,8,128]{3,2,1,0:T(8,128)S(1)} %get-tuple-element.53), channel_id=1, source_target_pairs={{0,31},{1,0},{2,1},{3,2},{4,3},{5,4},{6,5},{7,6},{8,7},{9,8},{10,9... | collective-permute-start | bytes 368648 | tf_op jit(solution)/shard_map/ppermute | solution.py:723
  25.0 8.9 %collective-permute-start.6 = (f32[3,20,8,128]{3,2,1,0:T(8,128)S(1)}, f32[3,20,8,128]{3,2,1,0:T(8,128)S(1)}, u32[]{:S(2)}, u32[]{:S(2)}) collective-permute-start(f32[3,20,8,128]{3,2,1,0:T(8,128)S(1)} %get-tuple-element.54), channel_id=1, source_target_pairs={{0,32},{1,0},{2,34},{3,2},{4,36},{5,4},{6,38},{7,6},{8,40},{9,8},{... | collective-permute-start | bytes 737288 | tf_op jit(solution)/shard_map/ppermute | solution.py:735
  30.1 6.2 %collective-permute-start.7 = (f32[3,20,8,128]{3,2,1,0:T(8,128)S(1)}, f32[3,20,8,128]{3,2,1,0:T(8,128)S(1)}, u32[]{:S(2)}, u32[]{:S(2)}) collective-permute-start(f32[3,20,8,128]{3,2,1,0:T(8,128)S(1)} %get-tuple-element.55), channel_id=1, source_target_pairs={{0,1},{1,33},{2,3},{3,35},{4,5},{5,37},{6,7},{7,39},{8,9},{9,41},{... | collective-permute-start | bytes 737288 | tf_op jit(solution)/shard_map/ppermute | solution.py:735
  36.3 2.9 %copy-start.2 = (bf16[16,512]{1,0:T(8,128)(2,1)S(1)}, bf16[16,512]{1,0:T(8,128)(2,1)}, u32[]{:S(2)}) copy-start(bf16[16,512]{1,0:T(8,128)(2,1)} %constant.13.clone.wm_ref) | copy-start | bytes 49156
  38.6 5.3 %copy-start.3 = (bf16[16,256]{1,0:T(8,128)(2,1)S(1)}, bf16[16,256]{1,0:T(8,128)(2,1)}, u32[]{:S(2)}) copy-start(bf16[16,256]{1,0:T(8,128)(2,1)} %constant.14.clone.wr_ref) | copy-start | bytes 24580
  38.6 2.8 %collective-permute-start.8 = (f32[2,18,8,128]{3,2,1,0:T(8,128)S(1)}, f32[2,18,8,128]{3,2,1,0:T(8,128)S(1)}, u32[]{:S(2)}, u32[]{:S(2)}) collective-permute-start(f32[2,18,8,128]{3,2,1,0:T(8,128)S(1)} %get-tuple-element.61), channel_id=1, source_target_pairs={{0,32},{1,0},{2,34},{3,2},{4,36},{5,4},{6,38},{7,6},{8,40},{9,8},{... | collective-permute-start | bytes 442376 | tf_op jit(solution)/shard_map/ppermute | solution.py:735
  38.7 5.2 %collective-permute-start.9 = (f32[2,18,8,128]{3,2,1,0:T(8,128)S(1)}, f32[2,18,8,128]{3,2,1,0:T(8,128)S(1)}, u32[]{:S(2)}, u32[]{:S(2)}) collective-permute-start(f32[2,18,8,128]{3,2,1,0:T(8,128)S(1)} %get-tuple-element.62), channel_id=1, source_target_pairs={{0,1},{1,33},{2,3},{3,35},{4,5},{5,37},{6,7},{7,39},{8,9},{9,41},{... | collective-permute-start | bytes 442376 | tf_op jit(solution)/shard_map/ppermute | solution.py:735
  44.6 19.2 %collective-permute-start.10 = (f32[2,8,8,128]{3,2,1,0:T(8,128)S(1)}, f32[2,8,8,128]{3,2,1,0:T(8,128)S(1)}, u32[]{:S(2)}, u32[]{:S(2)}) collective-permute-start(f32[2,8,8,128]{3,2,1,0:T(8,128)S(1)} %get-tuple-element.71), channel_id=1, source_target_pairs={{0,1},{1,2},{2,3},{3,4},{4,5},{5,6},{6,7},{7,8},{8,9},{9,10},{10,1... | collective-permute-start | bytes 196616 | tf_op jit(solution)/shard_map/ppermute | solution.py:723
  44.6 19.2 %collective-permute-start.11 = (f32[2,8,8,128]{3,2,1,0:T(8,128)S(1)}, f32[2,8,8,128]{3,2,1,0:T(8,128)S(1)}, u32[]{:S(2)}, u32[]{:S(2)}) collective-permute-start(f32[2,8,8,128]{3,2,1,0:T(8,128)S(1)} %get-tuple-element.72), channel_id=1, source_target_pairs={{0,31},{1,0},{2,1},{3,2},{4,3},{5,4},{6,5},{7,6},{8,7},{9,8},{10,9... | collective-permute-start | bytes 196616 | tf_op jit(solution)/shard_map/ppermute | solution.py:723

commit v8 on v7

--- a/solution.py
+++ b/solution.py
@@ -76,6 +76,18 @@
     return one(i > 0), one(i < nx - 1), one(j > 0), one(j < ny - 1)
 
 
+def even_row():
+    return lax.rem(lax.axis_index("sy"), 2) == 0
+
+
+class Picked:
+    def __init__(self, first, second):
+        self.refs = (first, second)
+
+    def __getitem__(self, at):
+        return jnp.where(even_row(), self.refs[0][at], self.refs[1][at])
+
+
 def lane_up(x):
     lane = lax.broadcasted_iota(jnp.int32, x.shape, x.ndim - 1)
     return jnp.where(lane == LANES - 1, 0.0, pltpu.roll(x, LANES - 1, x.ndim - 1))
@@ -143,17 +155,15 @@
     to_up_ref[8] = jnp.concatenate([coef[4:8], gr[1:2], pad], 0)
 
 
-def place_kernel(
-    rhs_hbm, lam_hbm, slot_ref, coef_ref, src_ref, dinv_ref, rhs_ref, lam_ref, sems
-):
-    copies = [
-        pltpu.make_async_copy(rhs_hbm.at[x], rhs_ref.at[x], sems.at[x]) for x in range(8)
-    ]
-    lam = pltpu.make_async_copy(lam_hbm, lam_ref, sems.at[8])
+def place_kernel(lam_hbm, rhs_ref, slot_ref, coef_ref, src_ref, dinv_ref, lam_ref, sems):
+    lam = pltpu.make_async_copy(lam_hbm, lam_ref, sems.at[0])
     lam.start()
-    for c in copies:
-        c.start()
     oh = onehot(slot_ref[...])
+    for x in range(8):
+        g = dot_t(jnp.concatenate(split3(rhs_ref[x]), 0), oh)
+        g = g[0:64] + g[64:128] + g[128:192]
+        for b in range(2):
+            src_ref[x, b * 8 : b * 8 + 8] = g[:, b * LANES : (b + 1) * LANES].reshape(8, 8, LANES)
     lam.wait()
     for b in range(2):
         lanes = slice(b * LANES, (b + 1) * LANES)
@@ -164,21 +174,18 @@
             d0 = cy * lam_ref[0, row, :] + cz * lam_ref[1, row, :] + m
             for i in range(10):
                 dinv_ref[i, row, lanes] = 1.0 / (d0 + cxl[i])
-    for x in range(8):
-        copies[x].wait()
-        g = dot_t(jnp.concatenate(split3(rhs_ref[x]), 0), oh)
-        g = g[0:64] + g[64:128] + g[128:192]
-        for b in range(2):
-            src_ref[x, b * 8 : b * 8 + 8] = g[:, b * LANES : (b + 1) * LANES].reshape(8, 8, LANES)
-
-
-def rim_kernel(src_ref, coef_ref, yd_ref, yu_ref, to_left_ref, to_right_ref):
+
+
+def rim_kernel(src_ref, coef_ref, yd_ref, yu_ref, to_a_ref, to_b_ref):
     coef_y = jnp.concatenate([yd_ref[8, 0:4, :], yu_ref[8, 0:4, :]], 0)
-    for x, out in ((0, to_left_ref), (7, to_right_ref)):
-        out[0] = yd_ref[x]
-        out[1:17] = src_ref[x]
-        out[17] = yu_ref[x]
-        out[18] = coef_ref[0]
+    even = even_row()
+    coef = coef_ref[0]
+    for out, x_even, x_odd in ((to_a_ref, 7, 0), (to_b_ref, 0, 7)):
+        pick = lambda ref: jnp.where(even, ref[x_even], ref[x_odd])
+        out[0] = pick(yd_ref)
+        out[1:17] = pick(src_ref)
+        out[17] = pick(yu_ref)
+        out[18] = coef
         out[19] = coef_y
 
 
@@ -303,11 +310,12 @@
 
 
 def first_kernel(
-    xl_ref, xr_ref, sin_ref, dinv_ref, a1_ref, a2_ref,
+    xa_ref, xb_ref, sin_ref, dinv_ref, a1_ref, a2_ref,
     rout_ref, wout, to_down_ref, to_up_ref, sout, spec,
 ):
     left, right, down, up = flags()
-    for k, (x_ref, side) in enumerate(((xl_ref, left), (xr_ref, right))):
+    x_refs = Picked(xa_ref, xb_ref), Picked(xb_ref, xa_ref)
+    for k, (x_ref, side) in enumerate(zip(x_refs, (left, right))):
         put_layer(
             rout_ref,
             k,
@@ -320,18 +328,6 @@
     for p in range(10):
         to_down_ref[p] = get(wout, p, 0, 3)
         to_up_ref[p] = get(wout, p, 15, 3)
-
-
-def even_row():
-    return lax.rem(lax.axis_index("sy"), 2) == 0
-
-
-class Picked:
-    def __init__(self, first, second):
-        self.refs = (first, second)
-
-    def __getitem__(self, at):
-        return jnp.where(even_row(), self.refs[0][at], self.refs[1][at])
 
 
 def edge_kernel(w_ref, d_ref, u_ref, a_ref, b_ref):
@@ -413,7 +409,7 @@
 
 
 def second_kernel(
-    rin_ref, rout_ref, coef_ref, xl_ref, xr_ref, yd_ref, yu_ref, w_ref, a_ref, b_ref, d_ref, u_ref,
+    rin_ref, rout_ref, coef_ref, xa_ref, xb_ref, yd_ref, yu_ref, w_ref, a_ref, b_ref, d_ref, u_ref,
     hin_ref, sin_ref, dinv_ref, a1_ref, a2_ref,
     c_ref, to_a_ref, to_b_ref, own_down_ref, own_up_ref, h, cb, r1, sout, spec, wout,
 ):
@@ -442,11 +438,12 @@
         return h[x if x < 3 else x - 6, y : y + n]
 
     coefs = []
-    for a, x_ref in ((0, xl_ref), (1, None), (2, xr_ref)):
+    for a, x_ref in ((0, Picked(xa_ref, xb_ref)), (1, None), (2, Picked(xb_ref, xa_ref))):
         if x_ref is None:
             rows = ((yd_ref[8], 0), (coef_ref[0], 0), (coef_ref[0], 4), (yu_ref[8], 0))
         else:
-            rows = ((x_ref[19], 0), (x_ref[18], 0), (x_ref[18], 4), (x_ref[19], 4))
+            own, beside = x_ref[18], x_ref[19]
+            rows = ((beside, 0), (own, 0), (own, 4), (beside, 4))
         coefs.append([Loaded(t) for t in spread_coefs(cb.at[a], rows)])
     for k, p in enumerate((0, 1, 2, 7, 8, 9)):
         if p in (0, 9):
@@ -783,14 +780,14 @@
     src, dinv = call(
         place_kernel,
         [vm(8, 16, 8, LANES), vm(10, 104, 256)],
-        (rhs, lam, slot, coef),
-        [(8, 64, 256), (2, 104, LANES)],
-        hbm_in=2,
-        sems=9,
-    )
-    to_l, to_r = call(rim_kernel, [vm(20, 8, LANES)] * 2, (src, coef, yd, yu))
-    xl = ring(to_r, "sx", 1)
-    xr = ring(to_l, "sx", -1)
+        (lam, rhs, slot, coef),
+        [(2, 104, LANES)],
+        hbm_in=1,
+        sems=1,
+    )
+    to_a, to_b = call(rim_kernel, [vm(20, 8, LANES)] * 2, (src, coef, yd, yu))
+    xa = snake(to_a, 1)
+    xb = snake(to_b, -1)
     rin, sin = call(
         first_inner_kernel,
         [vm(8 * 192, LANES), vm(10, 104, 256)],
@@ -802,7 +799,7 @@
     rout, w, to_d, to_u = call(
         first_kernel,
         [vm(2 * 192, LANES), vm(1920, LANES), side, side],
-        (xl, xr, sin, dinv, a1, a2),
+        (xa, xb, sin, dinv, a1, a2),
         [(2, 104, 256), (10, 104, 256)],
     )
     d = ring(to_u, "sy", 1)
@@ -822,7 +819,7 @@
     c, to_a, to_b, own_d, own_u = call(
         second_kernel,
         [vm(10, 18, 8, LANES), slab, slab, side, side],
-        (rin, rout, coef, xl, xr, yd, yu, w, a, b, d, u, hin, sin, dinv, a1, a2),
+        (rin, rout, coef, xa, xb, yd, yu, w, a, b, d, u, hin, sin, dinv, a1, a2),
         [
             (6, 20, 8, LANES),
             (3, 4, 5, 8, LANES),

time: 65.1 us -> 64.6 us (level)
  waiting for transfers between devices: 14 us -> 16.6 us
  starting transfers between devices: 19.5 us -> 17.2 us
  Pallas kernels: 13.4 us -> 11.5 us
  local copies, waits for them, and re-layouts: 0.02 us -> 1.07 us
    ppermute x8 -> x6, starting transfers between devices: 13.8 us -> 6.46 us  [ring(): return lax.ppermute(value, axis, [(i, (i + by) % n) for i in range(n)])]
    ppermute x4 -> x6, starting transfers between devices: 5.73 us -> 10.7 us  [snake(): return lax.ppermute(value, ('sx', 'sy'), pairs)]
    ppermute x4 -> x6, waiting for transfers between devices: 8.78 us -> 12.4 us  [snake(): return lax.ppermute(value, ('sx', 'sy'), pairs)]
    pallas_call x11, Pallas kernels: 13.4 us -> 11.5 us  [call(): pl.pallas_call(kernel, out_shape=outs, in_specs=[hbm if k < hbm_in else v...]
    ppermute x8 -> x6, waiting for transfers between devices: 5.26 us -> 4.12 us  [ring(): return lax.ppermute(value, axis, [(i, (i + by) % n) for i in range(n)])]
    unnamed x8 -> x10, local copies, waits for them, and re-layouts: 0.02 us -> 1.07 us
  transfers between devices with their start and end apart: 12 -> 12, of which waited for: 7 -> 9; matrix products, arithmetic and copies ran while one was open for 0% -> 0% of each run, Pallas kernels for 9% -> 6%
where the time goes in v8:
time: 64.6 us; the launch traced here: 64.4 us
  starting transfers between devices  17.2 us (27%)
  blocking collectives  17.2 us (27%)
  waiting for transfers between devices  16.6 us (26%)
  Pallas kernels  11.5 us (18%)
  local copies, waits for them, and re-layouts  1.07 us (2%)
  between operations  0.92 us (1%)
    all_to_all x1, blocking collectives, on_device(): lax.all_to_all(part, 'sy', split_axis=0, concat_axis=0, tiled=True)  17.2 us
    ppermute x6, waiting for transfers between devices, snake(): return lax.ppermute(value, ('sx', 'sy'), pairs)  12.4 us
    pallas_call x11, Pallas kernels, call(): pl.pallas_call(kernel, out_shape=outs, in_specs=[hbm if k < hbm_in else v...  11.5 us
    ppermute x6, starting transfers between devices, snake(): return lax.ppermute(value, ('sx', 'sy'), pairs)  10.7 us
    ppermute x6, starting transfers between devices, ring(): return lax.ppermute(value, axis, [(i, (i + by) % n) for i in range(n)])  6.46 us
    ppermute x6, waiting for transfers between devices, ring(): return lax.ppermute(value, axis, [(i, (i + by) % n) for i in range(n)])  4.12 us
  transfers between devices with their start and end apart: 12, of which 9 were waited for; matrix products, arithmetic and copies ran while one was open for 0% of the time, Pallas kernels for 6%

profile of v8, /device:TPU:8, one launch (start us, length us, event | category | flops | bytes accessed | tf_op | source)
XLA Modules:
  0.0 64.4 jit_solution(8087018102974103444)
XLA Ops:
  0.6 0.0 copy-start.1
  0.6 0.0 copy-start.2
  0.7 1.7 %shard_map.121 = (f32[2,8,128]{2,1,0:T(8,128)S(1)}, f32[9,8,128]{2,1,0:T(8,128)S(1)}, f32[9,8,128]{2,1,0:T(8,128)S(1)}, s32[1,256]{1,0:T(1,128)S(1)}) custom-call(f32[8,64,256]{2,1,0:T(8,128)} %bitcast.10, f32[3,256]{1,0:T(4,128)} %stretch_hbm.1, f32[1,256]{1,0:T(1,128)} %bitcast.16, s32[1,256]{1,0:T(1,128)} %bitcast.17, s32[1,256]{1,0:T(1,128)} %bitcast.18), custom_call_target="tpu_custom_call" | custom-call | tf_op jit(solution)/shard_map/pallas_call | solution.py:745
  2.4 1.7 %collective-permute-start = (f32[9,8,128]{2,1,0:T(8,128)S(1)}, f32[9,8,128]{2,1,0:T(8,128)S(1)}, u32[]{:S(2)}, u32[]{:S(2)}) collective-permute-start(f32[9,8,128]{2,1,0:T(8,128)S(1)} %get-tuple-element.43), channel_id=1, source_target_pairs={{0,1},{1,2},{2,3},{3,4},{4,5},{5,6},{6,7},{7,8},{8,9},{9,10},{10,1... | collective-permute-start | bytes 110600 | tf_op jit(solution)/shard_map/ppermute | solution.py:720
  4.0 0.7 %collective-permute-start.1 = (f32[9,8,128]{2,1,0:T(8,128)S(1)}, f32[9,8,128]{2,1,0:T(8,128)S(1)}, u32[]{:S(2)}, u32[]{:S(2)}) collective-permute-start(f32[9,8,128]{2,1,0:T(8,128)S(1)} %get-tuple-element.44), channel_id=1, source_target_pairs={{0,31},{1,0},{2,1},{3,2},{4,3},{5,4},{6,5},{7,6},{8,7},{9,8},{10,9... | collective-permute-start | bytes 110600 | tf_op jit(solution)/shard_map/ppermute | solution.py:720
  4.7 0.0 copy-start
  4.7 1.0 %copy-done = f32[8,8,8,256]{3,2,1,0:T(8,128)S(1)} copy-done((f32[8,8,8,256]{3,2,1,0:T(8,128)S(1)}, f32[8,8,8,256]{3,2,1,0:T(8,128)}, u32[]{:S(2)}) %copy-start) | copy-done | bytes 524312
  5.8 1.1 %shard_map.122 = (f32[8,16,8,128]{3,2,1,0:T(8,128)S(1)}, f32[10,104,256]{2,1,0:T(8,128)S(1)}) custom-call(f32[2,104,128]{2,1,0:T(8,128)} %constant.12.clone.lam_hbm, f32[8,64,256]{2,1,0:T(8,128)S(1)} %bitcast.11, s32[1,256]{1,0:T(1,128)S(1)} %get-tuple-element.40.slot_ref, f32[2,8,128]{2,1,0:T(8,128)S(1)} %get-tuple-element.41.coef_ref), custom_call_target="tpu_custom_call" | custom-call | tf_op jit(solution)/shard_map/pallas_call | solution.py:745
  6.8 0.0 collective-permute-done.yd_ref
  6.8 1.2 %collective-permute-done.1.yu_ref = f32[9,8,128]{2,1,0:T(8,128)S(1)} collective-permute-done((f32[9,8,128]{2,1,0:T(8,128)S(1)}, f32[9,8,128]{2,1,0:T(8,128)S(1)}, u32[]{:S(2)}, u32[]{:S(2)}) %collective-permute-start.1) | collective-permute-done | bytes 36896 | tf_op jit(solution)/shard_map/ppermute | solution.py:720
  8.0 5.5 %collective-permute-start.2 = (f32[20,8,128]{2,1,0:T(8,128)S(1)}, f32[20,8,128]{2,1,0:T(8,128)S(1)}, u32[]{:S(2)}, u32[]{:S(2)}) collective-permute-start(f32[20,8,128]{2,1,0:T(8,128)S(1)} %get-tuple-element.46), channel_id=1, source_target_pairs={{0,32},{1,0},{2,34},{3,2},{4,36},{5,4},{6,38},{7,6},{8,40},{9,8},{... | collective-permute-start | bytes 245768 | tf_op jit(solution)/shard_map/ppermute | solution.py:732
  13.6 0.0 collective-permute-start.3
  13.6 0.0 copy-done.1
  13.6 0.9 %shard_map.123 = (f32[1536,128]{1,0:T(8,128)S(1)}, f32[10,104,256]{2,1,0:T(8,128)S(1)}) custom-call(f32[8,16,8,128]{3,2,1,0:T(8,128)S(1)} %get-tuple-element.42.src_ref, f32[9,8,128]{2,1,0:T(8,128)S(1)} %collective-permute-done.yd_ref, f32[9,8,128]{2,1,0:T(8,128)S(1)} %collective-permute-done.1.yu_ref, bf16[208,224]{1,0:T(8,128)(2,1)S(1)} %copy-done.1), custom_call_target="tpu_custom_call" | custom-call | tf_op jit(solution)/shard_map/pallas_call | solution.py:745
  14.5 1.1 %collective-permute-done.2.xa_ref = f32[20,8,128]{2,1,0:T(8,128)S(1)} collective-permute-done((f32[20,8,128]{2,1,0:T(8,128)S(1)}, f32[20,8,128]{2,1,0:T(8,128)S(1)}, u32[]{:S(2)}, u32[]{:S(2)}) %collective-permute-start.2) | collective-permute-done | bytes 81952 | tf_op jit(solution)/shard_map/ppermute | solution.py:732
  15.6 2.4 %collective-permute-done.3.xb_ref = f32[20,8,128]{2,1,0:T(8,128)S(1)} collective-permute-done((f32[20,8,128]{2,1,0:T(8,128)S(1)}, f32[20,8,128]{2,1,0:T(8,128)S(1)}, u32[]{:S(2)}, u32[]{:S(2)}) %collective-permute-start.3) | collective-permute-done | bytes 81952 | tf_op jit(solution)/shard_map/ppermute | solution.py:732
  18.0 0.0 copy-done.2
  18.0 1.5 %shard_map.125 = (f32[384,128]{1,0:T(8,128)S(1)}, f32[1920,128]{1,0:T(8,128)S(1)}, f32[10,3,8,128]{3,2,1,0:T(8,128)S(1)}, f32[10,3,8,128]{3,2,1,0:T(8,128)S(1)}) custom-call(f32[20,8,128]{2,1,0:T(8,128)S(1)} %collective-permute-done.2.xa_ref, f32[20,8,128]{2,1,0:T(8,128)S(1)} %collective-permute-done.3.xb_ref, ...), custom_call_target="tpu_custom_call" | custom-call | tf_op jit(solution)/shard_map/pallas_call | solution.py:745
  19.5 0.1 collective-permute-start.4
  19.6 2.0 %collective-permute-start.5 = (f32[10,3,8,128]{3,2,1,0:T(8,128)S(1)}, f32[10,3,8,128]{3,2,1,0:T(8,128)S(1)}, u32[]{:S(2)}, u32[]{:S(2)}) collective-permute-start(f32[10,3,8,128]{3,2,1,0:T(8,128)S(1)} %get-tuple-element.53), channel_id=1, source_target_pairs={{0,31},{1,0},{2,1},{3,2},{4,3},{5,4},{6,5},{7,6},{8,7},{9,8},{10,9... | collective-permute-start | bytes 368648 | tf_op jit(solution)/shard_map/ppermute | solution.py:720
  21.6 2.9 %collective-permute-done.4.d_ref = f32[10,3,8,128]{3,2,1,0:T(8,128)S(1)} collective-permute-done((f32[10,3,8,128]{3,2,1,0:T(8,128)S(1)}, f32[10,3,8,128]{3,2,1,0:T(8,128)S(1)}, u32[]{:S(2)}, u32[]{:S(2)}) %collective-permute-start.4) | collective-permute-done | bytes 122912 | tf_op jit(solution)/shard_map/ppermute | solution.py:720
  24.5 0.1 collective-permute-done.5.u_ref
  24.6 4.6 %collective-permute-start.6 = (f32[3,20,8,128]{3,2,1,0:T(8,128)S(1)}, f32[3,20,8,128]{3,2,1,0:T(8,128)S(1)}, u32[]{:S(2)}, u32[]{:S(2)}) collective-permute-start(f32[3,20,8,128]{3,2,1,0:T(8,128)S(1)} %get-tuple-element.54), channel_id=1, source_target_pairs={{0,32},{1,0},{2,34},{3,2},{4,36},{5,4},{6,38},{7,6},{8,40},{9,8},{... | collective-permute-start | bytes 737288 | tf_op jit(solution)/shard_map/ppermute | solution.py:732
  29.2 0.0 collective-permute-start.7
  29.2 1.0 %shard_map.127 = (f32[6,20,8,128]{3,2,1,0:T(8,128)S(1)}, f32[10,104,256]{2,1,0:T(8,128)S(1)}) custom-call(f32[1536,128]{1,0:T(8,128)S(1)} %get-tuple-element.45.rin_ref, f32[2,8,128]{2,1,0:T(8,128)S(1)} %get-tuple-element.41.coef_ref, f32[9,8,128]{2,1,0:T(8,128)S(1)} %collective-permute-done.yd_ref, f32[9,8,128]{2,1,0:T(8,128)S(1)} %collective-permute-done.1.yu_ref, ...), custom_call_target="tpu_custom_call" | custom-call | tf_op jit(solution)/shard_map/pallas_call | solution.py:745
  30.2 2.7 %collective-permute-done.6.a_ref = f32[3,20,8,128]{3,2,1,0:T(8,128)S(1)} collective-permute-done((f32[3,20,8,128]{3,2,1,0:T(8,128)S(1)}, f32[3,20,8,128]{3,2,1,0:T(8,128)S(1)}, u32[]{:S(2)}, u32[]{:S(2)}) %collective-permute-start.6) | collective-permute-done | bytes 245792 | tf_op jit(solution)/shard_map/ppermute | solution.py:732
  32.9 2.5 %collective-permute-done.7.b_ref = f32[3,20,8,128]{3,2,1,0:T(8,128)S(1)} collective-permute-done((f32[3,20,8,128]{3,2,1,0:T(8,128)S(1)}, f32[3,20,8,128]{3,2,1,0:T(8,128)S(1)}, u32[]{:S(2)}, u32[]{:S(2)}) %collective-permute-start.7) | collective-permute-done | bytes 245792 | tf_op jit(solution)/shard_map/ppermute | solution.py:732
  35.4 0.0 copy-start.3
  35.4 2.3 %shard_map.128 = (f32[10,18,8,128]{3,2,1,0:T(8,128)S(1)}, f32[2,18,8,128]{3,2,1,0:T(8,128)S(1)}, f32[2,18,8,128]{3,2,1,0:T(8,128)S(1)}, f32[10,2,8,128]{3,2,1,0:T(8,128)S(1)}, f32[10,2,8,128]{3,2,1,0:T(8,128)S(1)}) custom-call(f32[1536,128]{1,0:T(8,128)S(1)} %get-tuple-element.45.rin_ref, f32[384,128]{1,0:T(8,128)S(1)} %get-tuple-element.50.rout_ref, ...), custom_call_target="tpu_custom_call" | custom-call | tf_op jit(solution)/shard_map/pallas_call | solution.py:745
  37.7 0.0 copy-start.4
  37.7 0.1 collective-permute-start.8
  37.8 0.5 collective-permute-start.9
  38.3 0.0 copy-done.3
  38.3 1.2 %shard_map.129 = (f32[8,64,256]{2,1,0:T(8,128)}, f32[8,64,256]{2,1,0:T(8,128)}, f32[4,64,256]{2,1,0:T(8,128)S(1)}, f32[16,256]{1,0:T(8,128)S(1)}, f32[32,512]{1,0:T(8,128)S(1)}, /*index=5*/f32[16,512]{1,0:T(8,128)S(1)}) custom-call(f32[8,16,8,128]{3,2,1,0:T(8,128)S(1)} %get-tuple-element.42.src_ref, f32[2,8,128]{2,1,0:T(8,128)S(1)} %get-tuple-element.41.coef_ref, ...), custom_call_target="tpu_custom_call" | custom-call | tf_op jit(solution)/shard_map/pallas_call | solution.py:745
  39.5 1.0 %collective-permute-done.8.a_ref = f32[2,18,8,128]{3,2,1,0:T(8,128)S(1)} collective-permute-done((f32[2,18,8,128]{3,2,1,0:T(8,128)S(1)}, f32[2,18,8,128]{3,2,1,0:T(8,128)S(1)}, u32[]{:S(2)}, u32[]{:S(2)}) %collective-permute-start.8) | collective-permute-done | bytes 147488 | tf_op jit(solution)/shard_map/ppermute | solution.py:732
  40.5 2.7 %collective-permute-done.9.b_ref = f32[2,18,8,128]{3,2,1,0:T(8,128)S(1)} collective-permute-done((f32[2,18,8,128]{3,2,1,0:T(8,128)S(1)}, f32[2,18,8,128]{3,2,1,0:T(8,128)S(1)}, u32[]{:S(2)}, u32[]{:S(2)}) %collective-permute-start.9) | collective-permute-done | bytes 147488 | tf_op jit(solution)/shard_map/ppermute | solution.py:732
  43.2 0.0 copy-done.4
  43.2 0.6 shard_map.130
  43.8 0.0 collective-permute-start.10
  43.9 2.0 %collective-permute-start.11 = (f32[2,8,8,128]{3,2,1,0:T(8,128)S(1)}, f32[2,8,8,128]{3,2,1,0:T(8,128)S(1)}, u32[]{:S(2)}, u32[]{:S(2)}) collective-permute-start(f32[2,8,8,128]{3,2,1,0:T(8,128)S(1)} %get-tuple-element.72), channel_id=1, source_target_pairs={{0,31},{1,0},{2,1},{3,2},{4,3},{5,4},{6,5},{7,6},{8,7},{9,8},{10,9... | collective-permute-start | bytes 196616 | tf_op jit(solution)/shard_map/ppermute | solution.py:720
  45.9 17.2 %all_to_all.11 = f32[32,1,128]{2,1,0:T(1,128)S(1)} all-to-all(f32[32,1,128]{2,1,0:T(1,128)S(1)} %bitcast.13), channel_id=1, replica_groups=mesh['sx'=8,'sy'=32] {'sy'}, dimensions={0} | all-to-all | bytes 32768 | tf_op jit(solution)/shard_map/all_to_all | solution.py:852
  63.1 0.0 collective-permute-done.10.d_ref
  63.1 0.0 collective-permute-done.11.u_ref
  63.1 1.1 %shard_map.131 = (f32[8,64,256]{2,1,0:T(8,128)}, f32[8,64,256]{2,1,0:T(8,128)}, f32[8,16]{1,0:T(8,128)}) custom-call(f32[8,64,256]{2,1,0:T(8,128)} %get-tuple-element.59.smooth_in, f32[8,64,256]{2,1,0:T(8,128)} %get-tuple-element.60.res_in, f32[10,18,8,128]{3,2,1,0:T(8,128)S(1)} %get-tuple-element.58.c_ref, ...), custom_call_target="tpu_custom_call", output_to_operand_aliasing={{0}: (0, {}), {1}: (1, {})} | custom-call | tf_op jit(solution)/shard_map/pallas_call | solution.py:745
  (2 shorter events, 0.1 us)
Async XLA Ops:
  0.6 12.9 %copy-start.1 = (bf16[208,224]{1,0:T(8,128)(2,1)S(1)}, bf16[208,224]{1,0:T(8,128)(2,1)}, u32[]{:S(2)}) copy-start(bf16[208,224]{1,0:T(8,128)(2,1)} %constant.10.clone.a1_ref) | copy-start | bytes 279556
  0.6 17.4 %copy-start.2 = (bf16[224,208]{1,0:T(8,128)(2,1)S(1)}, bf16[224,208]{1,0:T(8,128)(2,1)}, u32[]{:S(2)}) copy-start(bf16[224,208]{1,0:T(8,128)(2,1)} %constant.11.clone.a2_ref) | copy-start | bytes 279556
  2.4 4.4 %collective-permute-start = (f32[9,8,128]{2,1,0:T(8,128)S(1)}, f32[9,8,128]{2,1,0:T(8,128)S(1)}, u32[]{:S(2)}, u32[]{:S(2)}) collective-permute-start(f32[9,8,128]{2,1,0:T(8,128)S(1)} %get-tuple-element.43), channel_id=1, source_target_pairs={{0,1},{1,2},{2,3},{3,4},{4,5},{5,6},{6,7},{7,8},{8,9},{9,10},{10,1... | collective-permute-start | bytes 110600 | tf_op jit(solution)/shard_map/ppermute | solution.py:720
  4.0 4.0 %collective-permute-start.1 = (f32[9,8,128]{2,1,0:T(8,128)S(1)}, f32[9,8,128]{2,1,0:T(8,128)S(1)}, u32[]{:S(2)}, u32[]{:S(2)}) collective-permute-start(f32[9,8,128]{2,1,0:T(8,128)S(1)} %get-tuple-element.44), channel_id=1, source_target_pairs={{0,31},{1,0},{2,1},{3,2},{4,3},{5,4},{6,5},{7,6},{8,7},{9,8},{10,9... | collective-permute-start | bytes 110600 | tf_op jit(solution)/shard_map/ppermute | solution.py:720
  4.7 1.0 %copy-start = (f32[8,8,8,256]{3,2,1,0:T(8,128)S(1)}, f32[8,8,8,256]{3,2,1,0:T(8,128)}, u32[]{:S(2)}) copy-start(f32[8,8,8,256]{3,2,1,0:T(8,128)} %param.10) | copy-start | bytes 1572868
  8.0 7.6 %collective-permute-start.2 = (f32[20,8,128]{2,1,0:T(8,128)S(1)}, f32[20,8,128]{2,1,0:T(8,128)S(1)}, u32[]{:S(2)}, u32[]{:S(2)}) collective-permute-start(f32[20,8,128]{2,1,0:T(8,128)S(1)} %get-tuple-element.46), channel_id=1, source_target_pairs={{0,32},{1,0},{2,34},{3,2},{4,36},{5,4},{6,38},{7,6},{8,40},{9,8},{... | collective-permute-start | bytes 245768 | tf_op jit(solution)/shard_map/ppermute | solution.py:732
  13.6 4.4 %collective-permute-start.3 = (f32[20,8,128]{2,1,0:T(8,128)S(1)}, f32[20,8,128]{2,1,0:T(8,128)S(1)}, u32[]{:S(2)}, u32[]{:S(2)}) collective-permute-start(f32[20,8,128]{2,1,0:T(8,128)S(1)} %get-tuple-element.47), channel_id=1, source_target_pairs={{0,1},{1,33},{2,3},{3,35},{4,5},{5,37},{6,7},{7,39},{8,9},{9,41},{... | collective-permute-start | bytes 245768 | tf_op jit(solution)/shard_map/ppermute | solution.py:732
  19.5 5.0 %collective-permute-start.4 = (f32[10,3,8,128]{3,2,1,0:T(8,128)S(1)}, f32[10,3,8,128]{3,2,1,0:T(8,128)S(1)}, u32[]{:S(2)}, u32[]{:S(2)}) collective-permute-start(f32[10,3,8,128]{3,2,1,0:T(8,128)S(1)} %get-tuple-element.52), channel_id=1, source_target_pairs={{0,1},{1,2},{2,3},{3,4},{4,5},{5,6},{6,7},{7,8},{8,9},{9,10},{10,1... | collective-permute-start | bytes 368648 | tf_op jit(solution)/shard_map/ppermute | solution.py:720
  19.6 5.0 %collective-permute-start.5 = (f32[10,3,8,128]{3,2,1,0:T(8,128)S(1)}, f32[10,3,8,128]{3,2,1,0:T(8,128)S(1)}, u32[]{:S(2)}, u32[]{:S(2)}) collective-permute-start(f32[10,3,8,128]{3,2,1,0:T(8,128)S(1)} %get-tuple-element.53), channel_id=1, source_target_pairs={{0,31},{1,0},{2,1},{3,2},{4,3},{5,4},{6,5},{7,6},{8,7},{9,8},{10,9... | collective-permute-start | bytes 368648 | tf_op jit(solution)/shard_map/ppermute | solution.py:720
  24.6 8.3 %collective-permute-start.6 = (f32[3,20,8,128]{3,2,1,0:T(8,128)S(1)}, f32[3,20,8,128]{3,2,1,0:T(8,128)S(1)}, u32[]{:S(2)}, u32[]{:S(2)}) collective-permute-start(f32[3,20,8,128]{3,2,1,0:T(8,128)S(1)} %get-tuple-element.54), channel_id=1, source_target_pairs={{0,32},{1,0},{2,34},{3,2},{4,36},{5,4},{6,38},{7,6},{8,40},{9,8},{... | collective-permute-start | bytes 737288 | tf_op jit(solution)/shard_map/ppermute | solution.py:732
  29.2 6.2 %collective-permute-start.7 = (f32[3,20,8,128]{3,2,1,0:T(8,128)S(1)}, f32[3,20,8,128]{3,2,1,0:T(8,128)S(1)}, u32[]{:S(2)}, u32[]{:S(2)}) collective-permute-start(f32[3,20,8,128]{3,2,1,0:T(8,128)S(1)} %get-tuple-element.55), channel_id=1, source_target_pairs={{0,1},{1,33},{2,3},{3,35},{4,5},{5,37},{6,7},{7,39},{8,9},{9,41},{... | collective-permute-start | bytes 737288 | tf_op jit(solution)/shard_map/ppermute | solution.py:732
  35.4 2.9 %copy-start.3 = (bf16[16,512]{1,0:T(8,128)(2,1)S(1)}, bf16[16,512]{1,0:T(8,128)(2,1)}, u32[]{:S(2)}) copy-start(bf16[16,512]{1,0:T(8,128)(2,1)} %constant.13.clone.wm_ref) | copy-start | bytes 49156
  37.7 5.5 %copy-start.4 = (bf16[16,256]{1,0:T(8,128)(2,1)S(1)}, bf16[16,256]{1,0:T(8,128)(2,1)}, u32[]{:S(2)}) copy-start(bf16[16,256]{1,0:T(8,128)(2,1)} %constant.14.clone.wr_ref) | copy-start | bytes 24580
  37.7 2.8 %collective-permute-start.8 = (f32[2,18,8,128]{3,2,1,0:T(8,128)S(1)}, f32[2,18,8,128]{3,2,1,0:T(8,128)S(1)}, u32[]{:S(2)}, u32[]{:S(2)}) collective-permute-start(f32[2,18,8,128]{3,2,1,0:T(8,128)S(1)} %get-tuple-element.61), channel_id=1, source_target_pairs={{0,32},{1,0},{2,34},{3,2},{4,36},{5,4},{6,38},{7,6},{8,40},{9,8},{... | collective-permute-start | bytes 442376 | tf_op jit(solution)/shard_map/ppermute | solution.py:732
  37.8 5.4 %collective-permute-start.9 = (f32[2,18,8,128]{3,2,1,0:T(8,128)S(1)}, f32[2,18,8,128]{3,2,1,0:T(8,128)S(1)}, u32[]{:S(2)}, u32[]{:S(2)}) collective-permute-start(f32[2,18,8,128]{3,2,1,0:T(8,128)S(1)} %get-tuple-element.62), channel_id=1, source_target_pairs={{0,1},{1,33},{2,3},{3,35},{4,5},{5,37},{6,7},{7,39},{8,9},{9,41},{... | collective-permute-start | bytes 442376 | tf_op jit(solution)/shard_map/ppermute | solution.py:732
  43.8 19.3 %collective-permute-start.10 = (f32[2,8,8,128]{3,2,1,0:T(8,128)S(1)}, f32[2,8,8,128]{3,2,1,0:T(8,128)S(1)}, u32[]{:S(2)}, u32[]{:S(2)}) collective-permute-start(f32[2,8,8,128]{3,2,1,0:T(8,128)S(1)} %get-tuple-element.71), channel_id=1, source_target_pairs={{0,1},{1,2},{2,3},{3,4},{4,5},{5,6},{6,7},{7,8},{8,9},{9,10},{10,1... | collective-permute-start | bytes 196616 | tf_op jit(solution)/shard_map/ppermute | solution.py:720
  43.9 19.3 %collective-permute-start.11 = (f32[2,8,8,128]{3,2,1,0:T(8,128)S(1)}, f32[2,8,8,128]{3,2,1,0:T(8,128)S(1)}, u32[]{:S(2)}, u32[]{:S(2)}) collective-permute-start(f32[2,8,8,128]{3,2,1,0:T(8,128)S(1)} %get-tuple-element.72), channel_id=1, source_target_pairs={{0,31},{1,0},{2,1},{3,2},{4,3},{5,4},{6,5},{7,6},{8,7},{9,8},{10,9... | collective-permute-start | bytes 196616 | tf_op jit(solution)/shard_map/ppermute | solution.py:720

commit v9 on v8

--- a/solution.py
+++ b/solution.py
@@ -88,6 +88,16 @@
         return jnp.where(even_row(), self.refs[0][at], self.refs[1][at])
 
 
+def from_y(near, odd):
+    return Picked(odd, near), Picked(near, odd)
+
+
+def put_y(near_ref, odd_ref, at, down, up):
+    even = even_row()
+    near_ref[at] = jnp.where(even, up, down)
+    odd_ref[at] = jnp.where(even, down, up)
+
+
 def lane_up(x):
     lane = lax.broadcasted_iota(jnp.int32, x.shape, x.ndim - 1)
     return jnp.where(lane == LANES - 1, 0.0, pltpu.roll(x, LANES - 1, x.ndim - 1))
@@ -112,7 +122,7 @@
 
 def start_kernel(
     rhs_hbm, stretch_hbm, mass_hbm, slot_hbm, group_hbm,
-    coef_ref, to_down_ref, to_up_ref, slot_ref,
+    coef_ref, near_ref, odd_ref, slot_ref,
     face_ref, stretch_ref, mass_ref, group_ref, sems,
 ):
     pairs = (
@@ -128,11 +138,13 @@
         c.start()
     copies[0].wait()
     oh = onehot(slot_ref[...])
-    for k, out, b in ((1, to_down_ref, 0), (2, to_up_ref, 1)):
+    faces = []
+    for k, b in ((1, 0), (2, 1)):
         copies[k].wait()
         g = dot_t(jnp.concatenate(split3(face_ref[k - 1].reshape(64, 256)), 0), oh)
         g = g[0:64] + g[64:128] + g[128:192]
-        out[0:8] = g[:, b * LANES : (b + 1) * LANES].reshape(8, 8, LANES)
+        faces.append(g[:, b * LANES : (b + 1) * LANES].reshape(8, 8, LANES))
+    put_y(near_ref, odd_ref, slice(0, 8), *faces)
     for c in copies[3:]:
         c.wait()
     c = jnp.concatenate(
@@ -151,8 +163,9 @@
     coef_ref[0] = coef
     coef_ref[1] = gr
     pad = jnp.zeros((3, LANES), F32)
-    to_down_ref[8] = jnp.concatenate([coef[0:4], gr[0:1], pad], 0)
-    to_up_ref[8] = jnp.concatenate([coef[4:8], gr[1:2], pad], 0)
+    down = jnp.concatenate([coef[0:4], gr[0:1], pad], 0)
+    up = jnp.concatenate([coef[4:8], gr[1:2], pad], 0)
+    put_y(near_ref, odd_ref, 8, down, up)
 
 
 def place_kernel(lam_hbm, rhs_ref, slot_ref, coef_ref, src_ref, dinv_ref, lam_ref, sems):
@@ -177,6 +190,7 @@
 
 
 def rim_kernel(src_ref, coef_ref, yd_ref, yu_ref, to_a_ref, to_b_ref):
+    yd_ref, yu_ref = from_y(yd_ref, yu_ref)
     coef_y = jnp.concatenate([yd_ref[8, 0:4, :], yu_ref[8, 0:4, :]], 0)
     even = even_row()
     coef = coef_ref[0]
@@ -302,6 +316,7 @@
 
 
 def first_inner_kernel(src_ref, yd_ref, yu_ref, a1_ref, rin_ref, sin_ref, sout):
+    yd_ref, yu_ref = from_y(yd_ref, yu_ref)
     _, _, down, up = flags()
     for x in range(8):
         put_layer(rin_ref, x, yd_ref[x : x + 1] * down, src_ref[x], yu_ref[x : x + 1] * up)
@@ -311,7 +326,7 @@
 
 def first_kernel(
     xa_ref, xb_ref, sin_ref, dinv_ref, a1_ref, a2_ref,
-    rout_ref, wout, to_down_ref, to_up_ref, sout, spec,
+    rout_ref, wout, near_ref, odd_ref, sout, spec,
 ):
     left, right, down, up = flags()
     x_refs = Picked(xa_ref, xb_ref), Picked(xb_ref, xa_ref)
@@ -326,11 +341,11 @@
         sout[k] = forward(rout_ref, k * 192, a1_ref)
     finish_solves({0: ((sout, 0), (sout, 1))}, sin_ref, dinv_ref, a2_ref, spec, wout)
     for p in range(10):
-        to_down_ref[p] = get(wout, p, 0, 3)
-        to_up_ref[p] = get(wout, p, 15, 3)
+        put_y(near_ref, odd_ref, p, get(wout, p, 0, 3), get(wout, p, 15, 3))
 
 
 def edge_kernel(w_ref, d_ref, u_ref, a_ref, b_ref):
+    d_ref, u_ref = from_y(d_ref, u_ref)
     _, _, down, up = flags()
     even = even_row()
     for k in range(3):
@@ -392,6 +407,8 @@
 def second_inner_kernel(
     rin_ref, coef_ref, yd_ref, yu_ref, w_ref, d_ref, u_ref, a1_ref, h_ref, sin_ref, cb, r1, sout,
 ):
+    yd_ref, yu_ref = from_y(yd_ref, yu_ref)
+    d_ref, u_ref = from_y(d_ref, u_ref)
     left, right, down, up = flags()
     for x in range(3, 9):
         h_ref[x - 3] = with_rows(get(w_ref, x - 1, 0, 18), 3, d_ref[x - 1], u_ref[x - 1], down, up)
@@ -413,6 +430,8 @@
     hin_ref, sin_ref, dinv_ref, a1_ref, a2_ref,
     c_ref, to_a_ref, to_b_ref, own_down_ref, own_up_ref, h, cb, r1, sout, spec, wout,
 ):
+    yd_ref, yu_ref = from_y(yd_ref, yu_ref)
+    d_ref, u_ref = from_y(d_ref, u_ref)
     left, right, down, up = flags()
     l_ref, r_ref = Picked(a_ref, b_ref), Picked(b_ref, a_ref)
     for x in (0, 1, 2, 9, 10, 11):
@@ -521,6 +540,7 @@
     src_ref, coef_ref, yd_ref, yu_ref, c_ref, slot_ref, wm_ref,
     smooth_hbm, res_hbm, mr_ref, mom_ref, pick_ref, member_ref, h, smooth_ref, res_ref, sems,
 ):
+    yd_ref, yu_ref = from_y(yd_ref, yu_ref)
     _, _, down, up = flags()
     oh = onehot(slot_ref[...])
     copies = []
@@ -566,8 +586,9 @@
 def middle_kernel(
     src_ref, coef_ref, yd_ref, yu_ref, c_ref, a_ref, b_ref, own_down_ref, own_up_ref,
     mom_ref, pick_ref, member_ref, wm_ref, wr_ref,
-    u_ref, mr_ref, to_down_ref, to_up_ref, part_ref, h, rim, edge,
+    u_ref, mr_ref, near_ref, odd_ref, part_ref, h, rim, edge, slabs,
 ):
+    yd_ref, yu_ref = from_y(yd_ref, yu_ref)
     left, right, down, up = flags()
     l_ref, r_ref = Picked(a_ref, b_ref), Picked(b_ref, a_ref)
     for p in range(10):
@@ -590,8 +611,8 @@
             column_residual(get_h, src_ref, coefs[b], x, b, mr_ref, k)
     rim[...] = jnp.zeros((256, 256), F32)
     for k, out, far, near, tile, lanes, y_far, y_near in (
-        (0, to_down_ref, 0, 1, yd_ref, slice(0, LANES), 2, 3),
-        (1, to_up_ref, 1, 0, yu_ref, slice(LANES, 256), 1, 0),
+        (0, slabs.at[0], 0, 1, yd_ref, slice(0, LANES), 2, 3),
+        (1, slabs.at[1], 1, 0, yu_ref, slice(LANES, 256), 1, 0),
     ):
         slab = edge.at[k]
         cf = rows_of(tile[8], 0)
@@ -610,6 +631,8 @@
             rim[at : at + 8, lanes] = -res[0]
             at = (x * 4 + y_far) * 8
             rim[at : at + 8, lanes] = cf[1] * v[0]
+    for k in range(2):
+        put_y(near_ref, odd_ref, k, slabs[0, k], slabs[1, k])
     mom = mom_ref[...]
     mom = mom + moments(wm_ref, 0, mr_ref[0:2].reshape(128, 256))
     mom = mom + moments(wm_ref, 6, mr_ref[2:4].reshape(128, 256))
@@ -631,6 +654,7 @@
     arrived_ref,
     smooth_hbm, res_hbm, coarse_hbm, smooth_ref, res_ref, coarse_ref, sems,
 ):
+    d_ref, u_ref = from_y(d_ref, u_ref)
     _, _, down, up = flags()
     total = jnp.sum(arrived_ref[...], axis=0, keepdims=True)
     for v in range(8):
@@ -715,9 +739,16 @@
     return pltpu.VMEM(shape, F32)
 
 
-def ring(value, axis, by):
-    n = lax.axis_size(axis)
-    return lax.ppermute(value, axis, [(i, (i + by) % n) for i in range(n)])
+def swap_y(value, odd):
+    nx = lax.axis_size("sx")
+    ny = lax.axis_size("sy")
+    pairs = []
+    for i in range(nx):
+        for j in range(ny):
+            to = j + 1 if j % 2 == odd else j - 1
+            target = i * ny + to if 0 <= to < ny else (i ^ 1) * ny + j
+            pairs.append((i * ny + j, target))
+    return lax.ppermute(value, ("sx", "sy"), pairs)
 
 
 def snake(value, by):
@@ -761,7 +792,7 @@
     wr = jnp.asarray(W_RIM, BF16)
     row = pltpu.VMEM((1, 256), jnp.int32)
     rhs = right_side.reshape(8, 64, 256)
-    coef, to_d, to_u, slot = call(
+    coef, near, odd, slot = call(
         start_kernel,
         [vm(2, 8, LANES), vm(9, 8, LANES), vm(9, 8, LANES), row],
         (
@@ -775,8 +806,8 @@
         hbm_in=5,
         sems=6,
     )
-    yd = ring(to_u, "sy", 1)
-    yu = ring(to_d, "sy", -1)
+    yn = swap_y(near, 0)
+    yo = swap_y(odd, 1)
     src, dinv = call(
         place_kernel,
         [vm(8, 16, 8, LANES), vm(10, 104, 256)],
@@ -785,32 +816,32 @@
         hbm_in=1,
         sems=1,
     )
-    to_a, to_b = call(rim_kernel, [vm(20, 8, LANES)] * 2, (src, coef, yd, yu))
+    to_a, to_b = call(rim_kernel, [vm(20, 8, LANES)] * 2, (src, coef, yn, yo))
     xa = snake(to_a, 1)
     xb = snake(to_b, -1)
     rin, sin = call(
         first_inner_kernel,
         [vm(8 * 192, LANES), vm(10, 104, 256)],
-        (src, yd, yu, a1),
+        (src, yn, yo, a1),
         [(8, 104, 256)],
     )
 
     side = vm(10, 3, 8, LANES)
-    rout, w, to_d, to_u = call(
+    rout, w, near, odd = call(
         first_kernel,
         [vm(2 * 192, LANES), vm(1920, LANES), side, side],
         (xa, xb, sin, dinv, a1, a2),
         [(2, 104, 256), (10, 104, 256)],
     )
-    d = ring(to_u, "sy", 1)
-    u = ring(to_d, "sy", -1)
-    to_a, to_b = call(edge_kernel, [vm(3, 20, 8, LANES)] * 2, (w, d, u))
+    n = swap_y(near, 0)
+    o = swap_y(odd, 1)
+    to_a, to_b = call(edge_kernel, [vm(3, 20, 8, LANES)] * 2, (w, n, o))
     a = snake(to_a, 1)
     b = snake(to_b, -1)
     hin, sin = call(
         second_inner_kernel,
         [vm(6, 20, 8, LANES), vm(10, 104, 256)],
-        (rin, coef, yd, yu, w, d, u, a1),
+        (rin, coef, yn, yo, w, n, o, a1),
         [(4, 5, 8, LANES), (4 * 192, LANES), (4, 104, 256)],
     )
 
@@ -819,7 +850,7 @@
     c, to_a, to_b, own_d, own_u = call(
         second_kernel,
         [vm(10, 18, 8, LANES), slab, slab, side, side],
-        (rin, rout, coef, xa, xb, yd, yu, w, a, b, d, u, hin, sin, dinv, a1, a2),
+        (rin, rout, coef, xa, xb, yn, yo, w, a, b, n, o, hin, sin, dinv, a1, a2),
         [
             (6, 20, 8, LANES),
             (3, 4, 5, 8, LANES),
@@ -836,24 +867,24 @@
     smooth, res, rin, mom, pick, member = call(
         middle_inner_kernel,
         [sd(8, 64, 256), sd(8, 64, 256), vm(4, 64, 256), vm(16, 256), vm(ny, 512), vm(16, 512)],
-        (src, coef, yd, yu, c, slot, wm),
+        (src, coef, yn, yo, c, slot, wm),
         [(6, 18, 8, LANES), (6, 48, 256), (4, 32, 256)],
         hbm_out=2,
         sems=2,
     )
-    uout, rout, to_d, to_u, part = call(
+    uout, rout, near, odd, part = call(
         middle_kernel,
         [vm(2, 16, 8, LANES), vm(4, 64, 256), edge, edge, vm(ny, LANES)],
-        (src, coef, yd, yu, c, a, b, own_d, own_u, mom, pick, member, wm, wr),
-        [(10, 18, 8, LANES), (256, 256), (2, 10, 2, 8, LANES)],
-    )
-    d = ring(to_u, "sy", 1)
-    u = ring(to_d, "sy", -1)
+        (src, coef, yn, yo, c, a, b, own_d, own_u, mom, pick, member, wm, wr),
+        [(10, 18, 8, LANES), (256, 256), (2, 10, 2, 8, LANES), (2, 2, 8, 8, LANES)],
+    )
+    n = swap_y(near, 0)
+    o = swap_y(odd, 1)
     arrived = lax.all_to_all(part, "sy", split_axis=0, concat_axis=0, tiled=True)
     smooth, res, coarse = call(
         last_kernel,
         [sd(8, 64, 256), sd(8, 64, 256), sd(8, GRP_DEV)],
-        (smooth, res, c, uout, rin, rout, coef, d, u, slot, arrived),
+        (smooth, res, c, uout, rin, rout, coef, n, o, slot, arrived),
         [(8, 64, 256), (8, 64, 256), (8, GRP_DEV)],
         hbm_in=2,
         hbm_out=3,

time: 64.6 us -> 65.8 us (1.019)
  blocking collectives: 17.2 us -> 24.1 us
  starting transfers between devices: 17.2 us -> 12.7 us
  waiting for transfers between devices: 16.6 us -> 15.4 us
    ppermute x6, starting transfers between devices: 10.7 us -> 1.76 us  [snake(): return lax.ppermute(value, ('sx', 'sy'), pairs)]
    all_to_all x1, blocking collectives: 17.2 us -> 24.1 us  [on_device(): lax.all_to_all(part, 'sy', split_axis=0, concat_axis=0, tiled=True)]
    ppermute x6, starting transfers between devices: 6.46 us -> 10.9 us  [swap_y(): return lax.ppermute(value, ('sx', 'sy'), pairs)]
    ppermute x6, waiting for transfers between devices: 12.4 us -> 11.4 us  [snake(): return lax.ppermute(value, ('sx', 'sy'), pairs)]
where the time goes in v9:
time: 65.8 us; the launch traced here: 65.6 us
  blocking collectives  24.1 us (37%)
  waiting for transfers between devices  15.4 us (23%)
  starting transfers between devices  12.7 us (19%)
  Pallas kernels  11.5 us (17%)
  local copies, waits for them, and re-layouts  1.07 us (2%)
  between operations  0.78 us (1%)
    all_to_all x1, blocking collectives, on_device(): lax.all_to_all(part, 'sy', split_axis=0, concat_axis=0, tiled=True)  24.1 us
    pallas_call x11, Pallas kernels, call(): pl.pallas_call(kernel, out_shape=outs, in_specs=[hbm if k < hbm_in else v...  11.5 us
    ppermute x6, waiting for transfers between devices, snake(): return lax.ppermute(value, ('sx', 'sy'), pairs)  11.4 us
    ppermute x6, starting transfers between devices, swap_y(): return lax.ppermute(value, ('sx', 'sy'), pairs)  10.9 us
    ppermute x6, waiting for transfers between devices, swap_y(): return lax.ppermute(value, ('sx', 'sy'), pairs)  4 us
    ppermute x6, starting transfers between devices, snake(): return lax.ppermute(value, ('sx', 'sy'), pairs)  1.76 us
  transfers between devices with their start and end apart: 12, of which 9 were waited for; matrix products, arithmetic and copies ran while one was open for 0% of the time, Pallas kernels for 6%

profile of v9, /device:TPU:8, one launch (start us, length us, event | category | flops | bytes accessed | tf_op | source)
XLA Modules:
  0.0 65.6 jit_solution(18145691816165386243)
XLA Ops:
  0.6 0.0 copy-start.1
  0.6 0.0 copy-start.2
  0.7 1.7 %shard_map.121 = (f32[2,8,128]{2,1,0:T(8,128)S(1)}, f32[9,8,128]{2,1,0:T(8,128)S(1)}, f32[9,8,128]{2,1,0:T(8,128)S(1)}, s32[1,256]{1,0:T(1,128)S(1)}) custom-call(f32[8,64,256]{2,1,0:T(8,128)} %bitcast.10, f32[3,256]{1,0:T(4,128)} %stretch_hbm.1, f32[1,256]{1,0:T(1,128)} %bitcast.16, s32[1,256]{1,0:T(1,128)} %bitcast.17, s32[1,256]{1,0:T(1,128)} %bitcast.18), custom_call_target="tpu_custom_call" | custom-call | tf_op jit(solution)/shard_map/pallas_call | solution.py:776
  2.4 2.2 %collective-permute-start = (f32[9,8,128]{2,1,0:T(8,128)S(1)}, f32[9,8,128]{2,1,0:T(8,128)S(1)}, u32[]{:S(2)}, u32[]{:S(2)}) collective-permute-start(f32[9,8,128]{2,1,0:T(8,128)S(1)} %get-tuple-element.43), channel_id=1, source_target_pairs={{0,1},{1,0},{2,3},{3,2},{4,5},{5,4},{6,7},{7,6},{8,9},{9,8},{10,11... | collective-permute-start | bytes 110600 | tf_op jit(solution)/shard_map/ppermute | solution.py:751
  4.6 0.7 %collective-permute-start.1 = (f32[9,8,128]{2,1,0:T(8,128)S(1)}, f32[9,8,128]{2,1,0:T(8,128)S(1)}, u32[]{:S(2)}, u32[]{:S(2)}) collective-permute-start(f32[9,8,128]{2,1,0:T(8,128)S(1)} %get-tuple-element.44), channel_id=1, source_target_pairs={{0,32},{1,2},{2,1},{3,4},{4,3},{5,6},{6,5},{7,8},{8,7},{9,10},{10,... | collective-permute-start | bytes 110600 | tf_op jit(solution)/shard_map/ppermute | solution.py:751
  5.3 0.0 copy-start
  5.3 1.0 %copy-done = f32[8,8,8,256]{3,2,1,0:T(8,128)S(1)} copy-done((f32[8,8,8,256]{3,2,1,0:T(8,128)S(1)}, f32[8,8,8,256]{3,2,1,0:T(8,128)}, u32[]{:S(2)}) %copy-start) | copy-done | bytes 524312
  6.4 1.1 %shard_map.122 = (f32[8,16,8,128]{3,2,1,0:T(8,128)S(1)}, f32[10,104,256]{2,1,0:T(8,128)S(1)}) custom-call(f32[2,104,128]{2,1,0:T(8,128)} %constant.12.clone.lam_hbm, f32[8,64,256]{2,1,0:T(8,128)S(1)} %bitcast.11, s32[1,256]{1,0:T(1,128)S(1)} %get-tuple-element.40.slot_ref, f32[2,8,128]{2,1,0:T(8,128)S(1)} %get-tuple-element.41.coef_ref), custom_call_target="tpu_custom_call" | custom-call | tf_op jit(solution)/shard_map/pallas_call | solution.py:776
  7.4 0.0 collective-permute-done.yd_ref
  7.5 1.1 %collective-permute-done.1.yu_ref = f32[9,8,128]{2,1,0:T(8,128)S(1)} collective-permute-done((f32[9,8,128]{2,1,0:T(8,128)S(1)}, f32[9,8,128]{2,1,0:T(8,128)S(1)}, u32[]{:S(2)}, u32[]{:S(2)}) %collective-permute-start.1) | collective-permute-done | bytes 36896 | tf_op jit(solution)/shard_map/ppermute | solution.py:751
  8.6 0.1 collective-permute-start.2
  8.7 0.5 collective-permute-start.3
  9.2 0.0 copy-done.1
  9.2 0.9 %shard_map.123 = (f32[1536,128]{1,0:T(8,128)S(1)}, f32[10,104,256]{2,1,0:T(8,128)S(1)}) custom-call(f32[8,16,8,128]{3,2,1,0:T(8,128)S(1)} %get-tuple-element.42.src_ref, f32[9,8,128]{2,1,0:T(8,128)S(1)} %collective-permute-done.yd_ref, f32[9,8,128]{2,1,0:T(8,128)S(1)} %collective-permute-done.1.yu_ref, bf16[208,224]{1,0:T(8,128)(2,1)S(1)} %copy-done.1), custom_call_target="tpu_custom_call" | custom-call | tf_op jit(solution)/shard_map/pallas_call | solution.py:776
  10.2 0.6 collective-permute-done.2.xa_ref
  10.8 2.5 %collective-permute-done.3.xb_ref = f32[20,8,128]{2,1,0:T(8,128)S(1)} collective-permute-done((f32[20,8,128]{2,1,0:T(8,128)S(1)}, f32[20,8,128]{2,1,0:T(8,128)S(1)}, u32[]{:S(2)}, u32[]{:S(2)}) %collective-permute-start.3) | collective-permute-done | bytes 81952 | tf_op jit(solution)/shard_map/ppermute | solution.py:763
  13.2 0.0 copy-done.2
  13.2 1.5 %shard_map.125 = (f32[384,128]{1,0:T(8,128)S(1)}, f32[1920,128]{1,0:T(8,128)S(1)}, f32[10,3,8,128]{3,2,1,0:T(8,128)S(1)}, f32[10,3,8,128]{3,2,1,0:T(8,128)S(1)}) custom-call(f32[20,8,128]{2,1,0:T(8,128)S(1)} %collective-permute-done.2.xa_ref, f32[20,8,128]{2,1,0:T(8,128)S(1)} %collective-permute-done.3.xb_ref, ...), custom_call_target="tpu_custom_call" | custom-call | tf_op jit(solution)/shard_map/pallas_call | solution.py:776
  14.8 0.1 collective-permute-start.4
  14.9 3.5 %collective-permute-start.5 = (f32[10,3,8,128]{3,2,1,0:T(8,128)S(1)}, f32[10,3,8,128]{3,2,1,0:T(8,128)S(1)}, u32[]{:S(2)}, u32[]{:S(2)}) collective-permute-start(f32[10,3,8,128]{3,2,1,0:T(8,128)S(1)} %get-tuple-element.53), channel_id=1, source_target_pairs={{0,32},{1,2},{2,1},{3,4},{4,3},{5,6},{6,5},{7,8},{8,7},{9,10},{10,... | collective-permute-start | bytes 368648 | tf_op jit(solution)/shard_map/ppermute | solution.py:751
  18.4 1.3 %collective-permute-done.4.d_ref = f32[10,3,8,128]{3,2,1,0:T(8,128)S(1)} collective-permute-done((f32[10,3,8,128]{3,2,1,0:T(8,128)S(1)}, f32[10,3,8,128]{3,2,1,0:T(8,128)S(1)}, u32[]{:S(2)}, u32[]{:S(2)}) %collective-permute-start.4) | collective-permute-done | bytes 122912 | tf_op jit(solution)/shard_map/ppermute | solution.py:751
  19.8 1.5 %collective-permute-done.5.u_ref = f32[10,3,8,128]{3,2,1,0:T(8,128)S(1)} collective-permute-done((f32[10,3,8,128]{3,2,1,0:T(8,128)S(1)}, f32[10,3,8,128]{3,2,1,0:T(8,128)S(1)}, u32[]{:S(2)}, u32[]{:S(2)}) %collective-permute-start.5) | collective-permute-done | bytes 122912 | tf_op jit(solution)/shard_map/ppermute | solution.py:751
  21.3 0.1 shard_map.126
  21.3 0.1 collective-permute-start.6
  21.4 0.5 collective-permute-start.7
  21.9 1.0 %shard_map.127 = (f32[6,20,8,128]{3,2,1,0:T(8,128)S(1)}, f32[10,104,256]{2,1,0:T(8,128)S(1)}) custom-call(f32[1536,128]{1,0:T(8,128)S(1)} %get-tuple-element.45.rin_ref, f32[2,8,128]{2,1,0:T(8,128)S(1)} %get-tuple-element.41.coef_ref, f32[9,8,128]{2,1,0:T(8,128)S(1)} %collective-permute-done.yd_ref, f32[9,8,128]{2,1,0:T(8,128)S(1)} %collective-permute-done.1.yu_ref, ...), custom_call_target="tpu_custom_call" | custom-call | tf_op jit(solution)/shard_map/pallas_call | solution.py:776
  22.9 2.2 %collective-permute-done.6.a_ref = f32[3,20,8,128]{3,2,1,0:T(8,128)S(1)} collective-permute-done((f32[3,20,8,128]{3,2,1,0:T(8,128)S(1)}, f32[3,20,8,128]{3,2,1,0:T(8,128)S(1)}, u32[]{:S(2)}, u32[]{:S(2)}) %collective-permute-start.6) | collective-permute-done | bytes 245792 | tf_op jit(solution)/shard_map/ppermute | solution.py:763
  25.1 2.6 %collective-permute-done.7.b_ref = f32[3,20,8,128]{3,2,1,0:T(8,128)S(1)} collective-permute-done((f32[3,20,8,128]{3,2,1,0:T(8,128)S(1)}, f32[3,20,8,128]{3,2,1,0:T(8,128)S(1)}, u32[]{:S(2)}, u32[]{:S(2)}) %collective-permute-start.7) | collective-permute-done | bytes 245792 | tf_op jit(solution)/shard_map/ppermute | solution.py:763
  27.7 0.0 copy-start.3
  27.7 2.3 %shard_map.128 = (f32[10,18,8,128]{3,2,1,0:T(8,128)S(1)}, f32[2,18,8,128]{3,2,1,0:T(8,128)S(1)}, f32[2,18,8,128]{3,2,1,0:T(8,128)S(1)}, f32[10,2,8,128]{3,2,1,0:T(8,128)S(1)}, f32[10,2,8,128]{3,2,1,0:T(8,128)S(1)}) custom-call(f32[1536,128]{1,0:T(8,128)S(1)} %get-tuple-element.45.rin_ref, f32[384,128]{1,0:T(8,128)S(1)} %get-tuple-element.50.rout_ref, ...), custom_call_target="tpu_custom_call" | custom-call | tf_op jit(solution)/shard_map/pallas_call | solution.py:776
  30.0 0.0 copy-start.4
  30.0 0.1 collective-permute-start.8
  30.1 0.5 collective-permute-start.9
  30.6 0.0 copy-done.3
  30.6 1.2 %shard_map.129 = (f32[8,64,256]{2,1,0:T(8,128)}, f32[8,64,256]{2,1,0:T(8,128)}, f32[4,64,256]{2,1,0:T(8,128)S(1)}, f32[16,256]{1,0:T(8,128)S(1)}, f32[32,512]{1,0:T(8,128)S(1)}, /*index=5*/f32[16,512]{1,0:T(8,128)S(1)}) custom-call(f32[8,16,8,128]{3,2,1,0:T(8,128)S(1)} %get-tuple-element.42.src_ref, f32[2,8,128]{2,1,0:T(8,128)S(1)} %get-tuple-element.41.coef_ref, ...), custom_call_target="tpu_custom_call" | custom-call | tf_op jit(solution)/shard_map/pallas_call | solution.py:776
  31.8 1.0 %collective-permute-done.8.a_ref = f32[2,18,8,128]{3,2,1,0:T(8,128)S(1)} collective-permute-done((f32[2,18,8,128]{3,2,1,0:T(8,128)S(1)}, f32[2,18,8,128]{3,2,1,0:T(8,128)S(1)}, u32[]{:S(2)}, u32[]{:S(2)}) %collective-permute-start.8) | collective-permute-done | bytes 147488 | tf_op jit(solution)/shard_map/ppermute | solution.py:763
  32.8 2.6 %collective-permute-done.9.b_ref = f32[2,18,8,128]{3,2,1,0:T(8,128)S(1)} collective-permute-done((f32[2,18,8,128]{3,2,1,0:T(8,128)S(1)}, f32[2,18,8,128]{3,2,1,0:T(8,128)S(1)}, u32[]{:S(2)}, u32[]{:S(2)}) %collective-permute-start.9) | collective-permute-done | bytes 147488 | tf_op jit(solution)/shard_map/ppermute | solution.py:763
  35.4 0.0 copy-done.4
  35.4 0.6 shard_map.130
  36.0 0.0 collective-permute-start.10
  36.0 4.3 %collective-permute-start.11 = (f32[2,8,8,128]{3,2,1,0:T(8,128)S(1)}, f32[2,8,8,128]{3,2,1,0:T(8,128)S(1)}, u32[]{:S(2)}, u32[]{:S(2)}) collective-permute-start(f32[2,8,8,128]{3,2,1,0:T(8,128)S(1)} %get-tuple-element.72), channel_id=1, source_target_pairs={{0,32},{1,2},{2,1},{3,4},{4,3},{5,6},{6,5},{7,8},{8,7},{9,10},{10,... | collective-permute-start | bytes 196616 | tf_op jit(solution)/shard_map/ppermute | solution.py:751
  40.4 24.1 %all_to_all.11 = f32[32,1,128]{2,1,0:T(1,128)S(1)} all-to-all(f32[32,1,128]{2,1,0:T(1,128)S(1)} %bitcast.13), channel_id=1, replica_groups=mesh['sx'=8,'sy'=32] {'sy'}, dimensions={0} | all-to-all | bytes 32768 | tf_op jit(solution)/shard_map/all_to_all | solution.py:883
  64.5 0.0 collective-permute-done.10.d_ref
  64.5 0.0 collective-permute-done.11.u_ref
  64.5 1.1 %shard_map.131 = (f32[8,64,256]{2,1,0:T(8,128)}, f32[8,64,256]{2,1,0:T(8,128)}, f32[8,16]{1,0:T(8,128)}) custom-call(f32[8,64,256]{2,1,0:T(8,128)} %get-tuple-element.59.smooth_in, f32[8,64,256]{2,1,0:T(8,128)} %get-tuple-element.60.res_in, f32[10,18,8,128]{3,2,1,0:T(8,128)S(1)} %get-tuple-element.58.c_ref, ...), custom_call_target="tpu_custom_call", output_to_operand_aliasing={{0}: (0, {}), {1}: (1, {})} | custom-call | tf_op jit(solution)/shard_map/pallas_call | solution.py:776
  (1 shorter events, 0.0 us)
Async XLA Ops:
  0.6 8.6 %copy-start.1 = (bf16[208,224]{1,0:T(8,128)(2,1)S(1)}, bf16[208,224]{1,0:T(8,128)(2,1)}, u32[]{:S(2)}) copy-start(bf16[208,224]{1,0:T(8,128)(2,1)} %constant.10.clone.a1_ref) | copy-start | bytes 279556
  0.6 12.6 %copy-start.2 = (bf16[224,208]{1,0:T(8,128)(2,1)S(1)}, bf16[224,208]{1,0:T(8,128)(2,1)}, u32[]{:S(2)}) copy-start(bf16[224,208]{1,0:T(8,128)(2,1)} %constant.11.clone.a2_ref) | copy-start | bytes 279556
  2.4 5.1 %collective-permute-start = (f32[9,8,128]{2,1,0:T(8,128)S(1)}, f32[9,8,128]{2,1,0:T(8,128)S(1)}, u32[]{:S(2)}, u32[]{:S(2)}) collective-permute-start(f32[9,8,128]{2,1,0:T(8,128)S(1)} %get-tuple-element.43), channel_id=1, source_target_pairs={{0,1},{1,0},{2,3},{3,2},{4,5},{5,4},{6,7},{7,6},{8,9},{9,8},{10,11... | collective-permute-start | bytes 110600 | tf_op jit(solution)/shard_map/ppermute | solution.py:751
  4.6 4.0 %collective-permute-start.1 = (f32[9,8,128]{2,1,0:T(8,128)S(1)}, f32[9,8,128]{2,1,0:T(8,128)S(1)}, u32[]{:S(2)}, u32[]{:S(2)}) collective-permute-start(f32[9,8,128]{2,1,0:T(8,128)S(1)} %get-tuple-element.44), channel_id=1, source_target_pairs={{0,32},{1,2},{2,1},{3,4},{4,3},{5,6},{6,5},{7,8},{8,7},{9,10},{10,... | collective-permute-start | bytes 110600 | tf_op jit(solution)/shard_map/ppermute | solution.py:751
  5.3 1.0 %copy-start = (f32[8,8,8,256]{3,2,1,0:T(8,128)S(1)}, f32[8,8,8,256]{3,2,1,0:T(8,128)}, u32[]{:S(2)}) copy-start(f32[8,8,8,256]{3,2,1,0:T(8,128)} %param.10) | copy-start | bytes 1572868
  8.6 2.1 %collective-permute-start.2 = (f32[20,8,128]{2,1,0:T(8,128)S(1)}, f32[20,8,128]{2,1,0:T(8,128)S(1)}, u32[]{:S(2)}, u32[]{:S(2)}) collective-permute-start(f32[20,8,128]{2,1,0:T(8,128)S(1)} %get-tuple-element.46), channel_id=1, source_target_pairs={{0,32},{1,0},{2,34},{3,2},{4,36},{5,4},{6,38},{7,6},{8,40},{9,8},{... | collective-permute-start | bytes 245768 | tf_op jit(solution)/shard_map/ppermute | solution.py:763
  8.7 4.5 %collective-permute-start.3 = (f32[20,8,128]{2,1,0:T(8,128)S(1)}, f32[20,8,128]{2,1,0:T(8,128)S(1)}, u32[]{:S(2)}, u32[]{:S(2)}) collective-permute-start(f32[20,8,128]{2,1,0:T(8,128)S(1)} %get-tuple-element.47), channel_id=1, source_target_pairs={{0,1},{1,33},{2,3},{3,35},{4,5},{5,37},{6,7},{7,39},{8,9},{9,41},{... | collective-permute-start | bytes 245768 | tf_op jit(solution)/shard_map/ppermute | solution.py:763
  14.8 5.0 %collective-permute-start.4 = (f32[10,3,8,128]{3,2,1,0:T(8,128)S(1)}, f32[10,3,8,128]{3,2,1,0:T(8,128)S(1)}, u32[]{:S(2)}, u32[]{:S(2)}) collective-permute-start(f32[10,3,8,128]{3,2,1,0:T(8,128)S(1)} %get-tuple-element.52), channel_id=1, source_target_pairs={{0,1},{1,0},{2,3},{3,2},{4,5},{5,4},{6,7},{7,6},{8,9},{9,8},{10,11... | collective-permute-start | bytes 368648 | tf_op jit(solution)/shard_map/ppermute | solution.py:751
  14.9 6.4 %collective-permute-start.5 = (f32[10,3,8,128]{3,2,1,0:T(8,128)S(1)}, f32[10,3,8,128]{3,2,1,0:T(8,128)S(1)}, u32[]{:S(2)}, u32[]{:S(2)}) collective-permute-start(f32[10,3,8,128]{3,2,1,0:T(8,128)S(1)} %get-tuple-element.53), channel_id=1, source_target_pairs={{0,32},{1,2},{2,1},{3,4},{4,3},{5,6},{6,5},{7,8},{8,7},{9,10},{10,... | collective-permute-start | bytes 368648 | tf_op jit(solution)/shard_map/ppermute | solution.py:751
  21.3 3.8 %collective-permute-start.6 = (f32[3,20,8,128]{3,2,1,0:T(8,128)S(1)}, f32[3,20,8,128]{3,2,1,0:T(8,128)S(1)}, u32[]{:S(2)}, u32[]{:S(2)}) collective-permute-start(f32[3,20,8,128]{3,2,1,0:T(8,128)S(1)} %get-tuple-element.54), channel_id=1, source_target_pairs={{0,32},{1,0},{2,34},{3,2},{4,36},{5,4},{6,38},{7,6},{8,40},{9,8},{... | collective-permute-start | bytes 737288 | tf_op jit(solution)/shard_map/ppermute | solution.py:763
  21.4 6.3 %collective-permute-start.7 = (f32[3,20,8,128]{3,2,1,0:T(8,128)S(1)}, f32[3,20,8,128]{3,2,1,0:T(8,128)S(1)}, u32[]{:S(2)}, u32[]{:S(2)}) collective-permute-start(f32[3,20,8,128]{3,2,1,0:T(8,128)S(1)} %get-tuple-element.55), channel_id=1, source_target_pairs={{0,1},{1,33},{2,3},{3,35},{4,5},{5,37},{6,7},{7,39},{8,9},{9,41},{... | collective-permute-start | bytes 737288 | tf_op jit(solution)/shard_map/ppermute | solution.py:763
  27.7 2.9 %copy-start.3 = (bf16[16,512]{1,0:T(8,128)(2,1)S(1)}, bf16[16,512]{1,0:T(8,128)(2,1)}, u32[]{:S(2)}) copy-start(bf16[16,512]{1,0:T(8,128)(2,1)} %constant.13.clone.wm_ref) | copy-start | bytes 49156
  30.0 5.3 %copy-start.4 = (bf16[16,256]{1,0:T(8,128)(2,1)S(1)}, bf16[16,256]{1,0:T(8,128)(2,1)}, u32[]{:S(2)}) copy-start(bf16[16,256]{1,0:T(8,128)(2,1)} %constant.14.clone.wr_ref) | copy-start | bytes 24580
  30.0 2.8 %collective-permute-start.8 = (f32[2,18,8,128]{3,2,1,0:T(8,128)S(1)}, f32[2,18,8,128]{3,2,1,0:T(8,128)S(1)}, u32[]{:S(2)}, u32[]{:S(2)}) collective-permute-start(f32[2,18,8,128]{3,2,1,0:T(8,128)S(1)} %get-tuple-element.61), channel_id=1, source_target_pairs={{0,32},{1,0},{2,34},{3,2},{4,36},{5,4},{6,38},{7,6},{8,40},{9,8},{... | collective-permute-start | bytes 442376 | tf_op jit(solution)/shard_map/ppermute | solution.py:763
  30.1 5.2 %collective-permute-start.9 = (f32[2,18,8,128]{3,2,1,0:T(8,128)S(1)}, f32[2,18,8,128]{3,2,1,0:T(8,128)S(1)}, u32[]{:S(2)}, u32[]{:S(2)}) collective-permute-start(f32[2,18,8,128]{3,2,1,0:T(8,128)S(1)} %get-tuple-element.62), channel_id=1, source_target_pairs={{0,1},{1,33},{2,3},{3,35},{4,5},{5,37},{6,7},{7,39},{8,9},{9,41},{... | collective-permute-start | bytes 442376 | tf_op jit(solution)/shard_map/ppermute | solution.py:763
  36.0 28.5 %collective-permute-start.10 = (f32[2,8,8,128]{3,2,1,0:T(8,128)S(1)}, f32[2,8,8,128]{3,2,1,0:T(8,128)S(1)}, u32[]{:S(2)}, u32[]{:S(2)}) collective-permute-start(f32[2,8,8,128]{3,2,1,0:T(8,128)S(1)} %get-tuple-element.71), channel_id=1, source_target_pairs={{0,1},{1,0},{2,3},{3,2},{4,5},{5,4},{6,7},{7,6},{8,9},{9,8},{10,11... | collective-permute-start | bytes 196616 | tf_op jit(solution)/shard_map/ppermute | solution.py:751
  36.0 28.5 %collective-permute-start.11 = (f32[2,8,8,128]{3,2,1,0:T(8,128)S(1)}, f32[2,8,8,128]{3,2,1,0:T(8,128)S(1)}, u32[]{:S(2)}, u32[]{:S(2)}) collective-permute-start(f32[2,8,8,128]{3,2,1,0:T(8,128)S(1)} %get-tuple-element.72), channel_id=1, source_target_pairs={{0,32},{1,2},{2,1},{3,4},{4,3},{5,6},{6,5},{7,8},{8,7},{9,10},{10,... | collective-permute-start | bytes 196616 | tf_op jit(solution)/shard_map/ppermute | solution.py:751

commit v10 on v8

--- a/solution.py
+++ b/solution.py
@@ -217,25 +217,24 @@
     return acc
 
 
+HALVES = (slice(0, LANES), slice(LANES, 256))
+
+
 def partial_x(layers, out_ref):
-    for b in range(2):
-        lanes = slice(b * LANES, (b + 1) * LANES)
-
-        def chunk(t, carry):
-            row = pl.ds(pl.multiple_of(t * 8, 8), 8)
+    def chunk(t, carry):
+        row = pl.ds(pl.multiple_of(t * 8, 8), 8)
+        for lanes in HALVES:
             for i, v in enumerate(along_x(layers, None, row, lanes)):
                 out_ref[i, row, lanes] = v
-            return carry
-
-        lax.fori_loop(0, 13, chunk, 0)
+        return carry
+
+    lax.fori_loop(0, 13, chunk, 0, unroll=True)
 
 
 def finish_solves(layers, partial, dinv_ref, a2_ref, spec, wout):
-    for b in range(2):
-        lanes = slice(b * LANES, (b + 1) * LANES)
-
-        def chunk(t, carry):
-            row = pl.ds(pl.multiple_of(t * 8, 8), 8)
+    def chunk(t, carry):
+        row = pl.ds(pl.multiple_of(t * 8, 8), 8)
+        for lanes in HALVES:
             z = along_x(layers, partial, row, lanes)
             z = [z[i] * dinv_ref[i, row, lanes] for i in range(10)]
             for p in range(5):
@@ -246,9 +245,9 @@
                     o = o + z[i + 1] * float(SINES[i + 1, p])
                 spec[p, row, lanes] = e + o
                 spec[9 - p, row, lanes] = e - o
-            return carry
-
-        lax.fori_loop(0, 13, chunk, 0)
+        return carry
+
+    lax.fori_loop(0, 13, chunk, 0, unroll=True)
 
     for p in range(10):
         base = p * 192

time: 64.6 us -> 64.3 us (level)
  Pallas kernels: 11.5 us -> 10.8 us
    pallas_call x11, Pallas kernels: 11.5 us -> 10.8 us  [call(): pl.pallas_call(kernel, out_shape=outs, in_specs=[hbm if k < hbm_in else v...]
where the time goes in v10:
time: 64.3 us; the launch traced here: 64.1 us
  starting transfers between devices  17.3 us (27%)
  blocking collectives  17.2 us (27%)
  waiting for transfers between devices  16.8 us (26%)
  Pallas kernels  10.8 us (17%)
  local copies, waits for them, and re-layouts  1.07 us (2%)
  between operations  0.92 us (1%)
    all_to_all x1, blocking collectives, on_device(): lax.all_to_all(part, 'sy', split_axis=0, concat_axis=0, tiled=True)  17.2 us
    ppermute x6, waiting for transfers between devices, snake(): return lax.ppermute(value, ('sx', 'sy'), pairs)  12.6 us
    ppermute x6, starting transfers between devices, snake(): return lax.ppermute(value, ('sx', 'sy'), pairs)  10.9 us
    pallas_call x11, Pallas kernels, call(): pl.pallas_call(kernel, out_shape=outs, in_specs=[hbm if k < hbm_in else v...  10.8 us
    ppermute x6, starting transfers between devices, ring(): return lax.ppermute(value, axis, [(i, (i + by) % n) for i in range(n)])  6.46 us
    ppermute x6, waiting for transfers between devices, ring(): return lax.ppermute(value, axis, [(i, (i + by) % n) for i in range(n)])  4.12 us
  transfers between devices with their start and end apart: 12, of which 9 were waited for; matrix products, arithmetic and copies ran while one was open for 0% of the time, Pallas kernels for 6%

profile of v10, /device:TPU:8, one launch (start us, length us, event | category | flops | bytes accessed | tf_op | source)
XLA Modules:
  0.0 64.1 jit_solution(16556434509169668583)
XLA Ops:
  0.6 0.0 copy-start.1
  0.6 0.0 copy-start.2
  0.7 1.7 %shard_map.121 = (f32[2,8,128]{2,1,0:T(8,128)S(1)}, f32[9,8,128]{2,1,0:T(8,128)S(1)}, f32[9,8,128]{2,1,0:T(8,128)S(1)}, s32[1,256]{1,0:T(1,128)S(1)}) custom-call(f32[8,64,256]{2,1,0:T(8,128)} %bitcast.10, f32[3,256]{1,0:T(4,128)} %stretch_hbm.1, f32[1,256]{1,0:T(1,128)} %bitcast.16, s32[1,256]{1,0:T(1,128)} %bitcast.17, s32[1,256]{1,0:T(1,128)} %bitcast.18), custom_call_target="tpu_custom_call" | custom-call | tf_op jit(solution)/shard_map/pallas_call | solution.py:744
  2.4 1.7 %collective-permute-start = (f32[9,8,128]{2,1,0:T(8,128)S(1)}, f32[9,8,128]{2,1,0:T(8,128)S(1)}, u32[]{:S(2)}, u32[]{:S(2)}) collective-permute-start(f32[9,8,128]{2,1,0:T(8,128)S(1)} %get-tuple-element.43), channel_id=1, source_target_pairs={{0,1},{1,2},{2,3},{3,4},{4,5},{5,6},{6,7},{7,8},{8,9},{9,10},{10,1... | collective-permute-start | bytes 110600 | tf_op jit(solution)/shard_map/ppermute | solution.py:719
  4.0 0.7 %collective-permute-start.1 = (f32[9,8,128]{2,1,0:T(8,128)S(1)}, f32[9,8,128]{2,1,0:T(8,128)S(1)}, u32[]{:S(2)}, u32[]{:S(2)}) collective-permute-start(f32[9,8,128]{2,1,0:T(8,128)S(1)} %get-tuple-element.44), channel_id=1, source_target_pairs={{0,31},{1,0},{2,1},{3,2},{4,3},{5,4},{6,5},{7,6},{8,7},{9,8},{10,9... | collective-permute-start | bytes 110600 | tf_op jit(solution)/shard_map/ppermute | solution.py:719
  4.7 0.0 copy-start
  4.7 1.0 %copy-done = f32[8,8,8,256]{3,2,1,0:T(8,128)S(1)} copy-done((f32[8,8,8,256]{3,2,1,0:T(8,128)S(1)}, f32[8,8,8,256]{3,2,1,0:T(8,128)}, u32[]{:S(2)}) %copy-start) | copy-done | bytes 524312
  5.8 1.1 %shard_map.122 = (f32[8,16,8,128]{3,2,1,0:T(8,128)S(1)}, f32[10,104,256]{2,1,0:T(8,128)S(1)}) custom-call(f32[2,104,128]{2,1,0:T(8,128)} %constant.12.clone.lam_hbm, f32[8,64,256]{2,1,0:T(8,128)S(1)} %bitcast.11, s32[1,256]{1,0:T(1,128)S(1)} %get-tuple-element.40.slot_ref, f32[2,8,128]{2,1,0:T(8,128)S(1)} %get-tuple-element.41.coef_ref), custom_call_target="tpu_custom_call" | custom-call | tf_op jit(solution)/shard_map/pallas_call | solution.py:744
  6.8 0.0 collective-permute-done.yd_ref
  6.8 1.2 %collective-permute-done.1.yu_ref = f32[9,8,128]{2,1,0:T(8,128)S(1)} collective-permute-done((f32[9,8,128]{2,1,0:T(8,128)S(1)}, f32[9,8,128]{2,1,0:T(8,128)S(1)}, u32[]{:S(2)}, u32[]{:S(2)}) %collective-permute-start.1) | collective-permute-done | bytes 36896 | tf_op jit(solution)/shard_map/ppermute | solution.py:719
  8.0 5.5 %collective-permute-start.2 = (f32[20,8,128]{2,1,0:T(8,128)S(1)}, f32[20,8,128]{2,1,0:T(8,128)S(1)}, u32[]{:S(2)}, u32[]{:S(2)}) collective-permute-start(f32[20,8,128]{2,1,0:T(8,128)S(1)} %get-tuple-element.46), channel_id=1, source_target_pairs={{0,32},{1,0},{2,34},{3,2},{4,36},{5,4},{6,38},{7,6},{8,40},{9,8},{... | collective-permute-start | bytes 245768 | tf_op jit(solution)/shard_map/ppermute | solution.py:731
  13.6 0.0 collective-permute-start.3
  13.6 0.0 copy-done.1
  13.6 0.7 %shard_map.123 = (f32[1536,128]{1,0:T(8,128)S(1)}, f32[10,104,256]{2,1,0:T(8,128)S(1)}) custom-call(f32[8,16,8,128]{3,2,1,0:T(8,128)S(1)} %get-tuple-element.42.src_ref, f32[9,8,128]{2,1,0:T(8,128)S(1)} %collective-permute-done.yd_ref, f32[9,8,128]{2,1,0:T(8,128)S(1)} %collective-permute-done.1.yu_ref, bf16[208,224]{1,0:T(8,128)(2,1)S(1)} %copy-done.1), custom_call_target="tpu_custom_call" | custom-call | tf_op jit(solution)/shard_map/pallas_call | solution.py:744
  14.3 1.3 %collective-permute-done.2.xa_ref = f32[20,8,128]{2,1,0:T(8,128)S(1)} collective-permute-done((f32[20,8,128]{2,1,0:T(8,128)S(1)}, f32[20,8,128]{2,1,0:T(8,128)S(1)}, u32[]{:S(2)}, u32[]{:S(2)}) %collective-permute-start.2) | collective-permute-done | bytes 81952 | tf_op jit(solution)/shard_map/ppermute | solution.py:731
  15.6 2.4 %collective-permute-done.3.xb_ref = f32[20,8,128]{2,1,0:T(8,128)S(1)} collective-permute-done((f32[20,8,128]{2,1,0:T(8,128)S(1)}, f32[20,8,128]{2,1,0:T(8,128)S(1)}, u32[]{:S(2)}, u32[]{:S(2)}) %collective-permute-start.3) | collective-permute-done | bytes 81952 | tf_op jit(solution)/shard_map/ppermute | solution.py:731
  18.0 0.0 copy-done.2
  18.0 1.4 %shard_map.125 = (f32[384,128]{1,0:T(8,128)S(1)}, f32[1920,128]{1,0:T(8,128)S(1)}, f32[10,3,8,128]{3,2,1,0:T(8,128)S(1)}, f32[10,3,8,128]{3,2,1,0:T(8,128)S(1)}) custom-call(f32[20,8,128]{2,1,0:T(8,128)S(1)} %collective-permute-done.2.xa_ref, f32[20,8,128]{2,1,0:T(8,128)S(1)} %collective-permute-done.3.xb_ref, ...), custom_call_target="tpu_custom_call" | custom-call | tf_op jit(solution)/shard_map/pallas_call | solution.py:744
  19.4 0.1 collective-permute-start.4
  19.5 2.0 %collective-permute-start.5 = (f32[10,3,8,128]{3,2,1,0:T(8,128)S(1)}, f32[10,3,8,128]{3,2,1,0:T(8,128)S(1)}, u32[]{:S(2)}, u32[]{:S(2)}) collective-permute-start(f32[10,3,8,128]{3,2,1,0:T(8,128)S(1)} %get-tuple-element.53), channel_id=1, source_target_pairs={{0,31},{1,0},{2,1},{3,2},{4,3},{5,4},{6,5},{7,6},{8,7},{9,8},{10,9... | collective-permute-start | bytes 368648 | tf_op jit(solution)/shard_map/ppermute | solution.py:719
  21.5 2.9 %collective-permute-done.4.d_ref = f32[10,3,8,128]{3,2,1,0:T(8,128)S(1)} collective-permute-done((f32[10,3,8,128]{3,2,1,0:T(8,128)S(1)}, f32[10,3,8,128]{3,2,1,0:T(8,128)S(1)}, u32[]{:S(2)}, u32[]{:S(2)}) %collective-permute-start.4) | collective-permute-done | bytes 122912 | tf_op jit(solution)/shard_map/ppermute | solution.py:719
  24.3 0.1 collective-permute-done.5.u_ref
  24.5 4.6 %collective-permute-start.6 = (f32[3,20,8,128]{3,2,1,0:T(8,128)S(1)}, f32[3,20,8,128]{3,2,1,0:T(8,128)S(1)}, u32[]{:S(2)}, u32[]{:S(2)}) collective-permute-start(f32[3,20,8,128]{3,2,1,0:T(8,128)S(1)} %get-tuple-element.54), channel_id=1, source_target_pairs={{0,32},{1,0},{2,34},{3,2},{4,36},{5,4},{6,38},{7,6},{8,40},{9,8},{... | collective-permute-start | bytes 737288 | tf_op jit(solution)/shard_map/ppermute | solution.py:731
  29.1 0.0 collective-permute-start.7
  29.1 0.8 %shard_map.127 = (f32[6,20,8,128]{3,2,1,0:T(8,128)S(1)}, f32[10,104,256]{2,1,0:T(8,128)S(1)}) custom-call(f32[1536,128]{1,0:T(8,128)S(1)} %get-tuple-element.45.rin_ref, f32[2,8,128]{2,1,0:T(8,128)S(1)} %get-tuple-element.41.coef_ref, f32[9,8,128]{2,1,0:T(8,128)S(1)} %collective-permute-done.yd_ref, f32[9,8,128]{2,1,0:T(8,128)S(1)} %collective-permute-done.1.yu_ref, ...), custom_call_target="tpu_custom_call" | custom-call | tf_op jit(solution)/shard_map/pallas_call | solution.py:744
  29.8 2.9 %collective-permute-done.6.a_ref = f32[3,20,8,128]{3,2,1,0:T(8,128)S(1)} collective-permute-done((f32[3,20,8,128]{3,2,1,0:T(8,128)S(1)}, f32[3,20,8,128]{3,2,1,0:T(8,128)S(1)}, u32[]{:S(2)}, u32[]{:S(2)}) %collective-permute-start.6) | collective-permute-done | bytes 245792 | tf_op jit(solution)/shard_map/ppermute | solution.py:731
  32.8 2.5 %collective-permute-done.7.b_ref = f32[3,20,8,128]{3,2,1,0:T(8,128)S(1)} collective-permute-done((f32[3,20,8,128]{3,2,1,0:T(8,128)S(1)}, f32[3,20,8,128]{3,2,1,0:T(8,128)S(1)}, u32[]{:S(2)}, u32[]{:S(2)}) %collective-permute-start.7) | collective-permute-done | bytes 245792 | tf_op jit(solution)/shard_map/ppermute | solution.py:731
  35.2 0.0 copy-start.3
  35.2 2.1 %shard_map.128 = (f32[10,18,8,128]{3,2,1,0:T(8,128)S(1)}, f32[2,18,8,128]{3,2,1,0:T(8,128)S(1)}, f32[2,18,8,128]{3,2,1,0:T(8,128)S(1)}, f32[10,2,8,128]{3,2,1,0:T(8,128)S(1)}, f32[10,2,8,128]{3,2,1,0:T(8,128)S(1)}) custom-call(f32[1536,128]{1,0:T(8,128)S(1)} %get-tuple-element.45.rin_ref, f32[384,128]{1,0:T(8,128)S(1)} %get-tuple-element.50.rout_ref, ...), custom_call_target="tpu_custom_call" | custom-call | tf_op jit(solution)/shard_map/pallas_call | solution.py:744
  37.4 0.0 copy-start.4
  37.4 0.3 collective-permute-start.8
  37.7 0.5 collective-permute-start.9
  38.2 0.0 copy-done.3
  38.2 1.2 %shard_map.129 = (f32[8,64,256]{2,1,0:T(8,128)}, f32[8,64,256]{2,1,0:T(8,128)}, f32[4,64,256]{2,1,0:T(8,128)S(1)}, f32[16,256]{1,0:T(8,128)S(1)}, f32[32,512]{1,0:T(8,128)S(1)}, /*index=5*/f32[16,512]{1,0:T(8,128)S(1)}) custom-call(f32[8,16,8,128]{3,2,1,0:T(8,128)S(1)} %get-tuple-element.42.src_ref, f32[2,8,128]{2,1,0:T(8,128)S(1)} %get-tuple-element.41.coef_ref, ...), custom_call_target="tpu_custom_call" | custom-call | tf_op jit(solution)/shard_map/pallas_call | solution.py:744
  39.3 1.0 %collective-permute-done.8.a_ref = f32[2,18,8,128]{3,2,1,0:T(8,128)S(1)} collective-permute-done((f32[2,18,8,128]{3,2,1,0:T(8,128)S(1)}, f32[2,18,8,128]{3,2,1,0:T(8,128)S(1)}, u32[]{:S(2)}, u32[]{:S(2)}) %collective-permute-start.8) | collective-permute-done | bytes 147488 | tf_op jit(solution)/shard_map/ppermute | solution.py:731
  40.3 2.6 %collective-permute-done.9.b_ref = f32[2,18,8,128]{3,2,1,0:T(8,128)S(1)} collective-permute-done((f32[2,18,8,128]{3,2,1,0:T(8,128)S(1)}, f32[2,18,8,128]{3,2,1,0:T(8,128)S(1)}, u32[]{:S(2)}, u32[]{:S(2)}) %collective-permute-start.9) | collective-permute-done | bytes 147488 | tf_op jit(solution)/shard_map/ppermute | solution.py:731
  42.9 0.0 copy-done.4
  42.9 0.6 shard_map.130
  43.5 0.0 collective-permute-start.10
  43.5 2.0 %collective-permute-start.11 = (f32[2,8,8,128]{3,2,1,0:T(8,128)S(1)}, f32[2,8,8,128]{3,2,1,0:T(8,128)S(1)}, u32[]{:S(2)}, u32[]{:S(2)}) collective-permute-start(f32[2,8,8,128]{3,2,1,0:T(8,128)S(1)} %get-tuple-element.72), channel_id=1, source_target_pairs={{0,31},{1,0},{2,1},{3,2},{4,3},{5,4},{6,5},{7,6},{8,7},{9,8},{10,9... | collective-permute-start | bytes 196616 | tf_op jit(solution)/shard_map/ppermute | solution.py:719
  45.6 17.2 %all_to_all.11 = f32[32,1,128]{2,1,0:T(1,128)S(1)} all-to-all(f32[32,1,128]{2,1,0:T(1,128)S(1)} %bitcast.13), channel_id=1, replica_groups=mesh['sx'=8,'sy'=32] {'sy'}, dimensions={0} | all-to-all | bytes 32768 | tf_op jit(solution)/shard_map/all_to_all | solution.py:851
  62.8 0.0 collective-permute-done.10.d_ref
  62.8 0.0 collective-permute-done.11.u_ref
  62.8 1.1 %shard_map.131 = (f32[8,64,256]{2,1,0:T(8,128)}, f32[8,64,256]{2,1,0:T(8,128)}, f32[8,16]{1,0:T(8,128)}) custom-call(f32[8,64,256]{2,1,0:T(8,128)} %get-tuple-element.59.smooth_in, f32[8,64,256]{2,1,0:T(8,128)} %get-tuple-element.60.res_in, f32[10,18,8,128]{3,2,1,0:T(8,128)S(1)} %get-tuple-element.58.c_ref, ...), custom_call_target="tpu_custom_call", output_to_operand_aliasing={{0}: (0, {}), {1}: (1, {})} | custom-call | tf_op jit(solution)/shard_map/pallas_call | solution.py:744
  (2 shorter events, 0.1 us)
Async XLA Ops:
  0.6 12.9 %copy-start.1 = (bf16[208,224]{1,0:T(8,128)(2,1)S(1)}, bf16[208,224]{1,0:T(8,128)(2,1)}, u32[]{:S(2)}) copy-start(bf16[208,224]{1,0:T(8,128)(2,1)} %constant.10.clone.a1_ref) | copy-start | bytes 279556
  0.6 17.4 %copy-start.2 = (bf16[224,208]{1,0:T(8,128)(2,1)S(1)}, bf16[224,208]{1,0:T(8,128)(2,1)}, u32[]{:S(2)}) copy-start(bf16[224,208]{1,0:T(8,128)(2,1)} %constant.11.clone.a2_ref) | copy-start | bytes 279556
  2.4 4.4 %collective-permute-start = (f32[9,8,128]{2,1,0:T(8,128)S(1)}, f32[9,8,128]{2,1,0:T(8,128)S(1)}, u32[]{:S(2)}, u32[]{:S(2)}) collective-permute-start(f32[9,8,128]{2,1,0:T(8,128)S(1)} %get-tuple-element.43), channel_id=1, source_target_pairs={{0,1},{1,2},{2,3},{3,4},{4,5},{5,6},{6,7},{7,8},{8,9},{9,10},{10,1... | collective-permute-start | bytes 110600 | tf_op jit(solution)/shard_map/ppermute | solution.py:719
  4.0 4.0 %collective-permute-start.1 = (f32[9,8,128]{2,1,0:T(8,128)S(1)}, f32[9,8,128]{2,1,0:T(8,128)S(1)}, u32[]{:S(2)}, u32[]{:S(2)}) collective-permute-start(f32[9,8,128]{2,1,0:T(8,128)S(1)} %get-tuple-element.44), channel_id=1, source_target_pairs={{0,31},{1,0},{2,1},{3,2},{4,3},{5,4},{6,5},{7,6},{8,7},{9,8},{10,9... | collective-permute-start | bytes 110600 | tf_op jit(solution)/shard_map/ppermute | solution.py:719
  4.7 1.0 %copy-start = (f32[8,8,8,256]{3,2,1,0:T(8,128)S(1)}, f32[8,8,8,256]{3,2,1,0:T(8,128)}, u32[]{:S(2)}) copy-start(f32[8,8,8,256]{3,2,1,0:T(8,128)} %param.10) | copy-start | bytes 1572868
  8.0 7.6 %collective-permute-start.2 = (f32[20,8,128]{2,1,0:T(8,128)S(1)}, f32[20,8,128]{2,1,0:T(8,128)S(1)}, u32[]{:S(2)}, u32[]{:S(2)}) collective-permute-start(f32[20,8,128]{2,1,0:T(8,128)S(1)} %get-tuple-element.46), channel_id=1, source_target_pairs={{0,32},{1,0},{2,34},{3,2},{4,36},{5,4},{6,38},{7,6},{8,40},{9,8},{... | collective-permute-start | bytes 245768 | tf_op jit(solution)/shard_map/ppermute | solution.py:731
  13.6 4.4 %collective-permute-start.3 = (f32[20,8,128]{2,1,0:T(8,128)S(1)}, f32[20,8,128]{2,1,0:T(8,128)S(1)}, u32[]{:S(2)}, u32[]{:S(2)}) collective-permute-start(f32[20,8,128]{2,1,0:T(8,128)S(1)} %get-tuple-element.47), channel_id=1, source_target_pairs={{0,1},{1,33},{2,3},{3,35},{4,5},{5,37},{6,7},{7,39},{8,9},{9,41},{... | collective-permute-start | bytes 245768 | tf_op jit(solution)/shard_map/ppermute | solution.py:731
  19.4 5.0 %collective-permute-start.4 = (f32[10,3,8,128]{3,2,1,0:T(8,128)S(1)}, f32[10,3,8,128]{3,2,1,0:T(8,128)S(1)}, u32[]{:S(2)}, u32[]{:S(2)}) collective-permute-start(f32[10,3,8,128]{3,2,1,0:T(8,128)S(1)} %get-tuple-element.52), channel_id=1, source_target_pairs={{0,1},{1,2},{2,3},{3,4},{4,5},{5,6},{6,7},{7,8},{8,9},{9,10},{10,1... | collective-permute-start | bytes 368648 | tf_op jit(solution)/shard_map/ppermute | solution.py:719
  19.5 5.0 %collective-permute-start.5 = (f32[10,3,8,128]{3,2,1,0:T(8,128)S(1)}, f32[10,3,8,128]{3,2,1,0:T(8,128)S(1)}, u32[]{:S(2)}, u32[]{:S(2)}) collective-permute-start(f32[10,3,8,128]{3,2,1,0:T(8,128)S(1)} %get-tuple-element.53), channel_id=1, source_target_pairs={{0,31},{1,0},{2,1},{3,2},{4,3},{5,4},{6,5},{7,6},{8,7},{9,8},{10,9... | collective-permute-start | bytes 368648 | tf_op jit(solution)/shard_map/ppermute | solution.py:719
  24.5 8.3 %collective-permute-start.6 = (f32[3,20,8,128]{3,2,1,0:T(8,128)S(1)}, f32[3,20,8,128]{3,2,1,0:T(8,128)S(1)}, u32[]{:S(2)}, u32[]{:S(2)}) collective-permute-start(f32[3,20,8,128]{3,2,1,0:T(8,128)S(1)} %get-tuple-element.54), channel_id=1, source_target_pairs={{0,32},{1,0},{2,34},{3,2},{4,36},{5,4},{6,38},{7,6},{8,40},{9,8},{... | collective-permute-start | bytes 737288 | tf_op jit(solution)/shard_map/ppermute | solution.py:731
  29.1 6.2 %collective-permute-start.7 = (f32[3,20,8,128]{3,2,1,0:T(8,128)S(1)}, f32[3,20,8,128]{3,2,1,0:T(8,128)S(1)}, u32[]{:S(2)}, u32[]{:S(2)}) collective-permute-start(f32[3,20,8,128]{3,2,1,0:T(8,128)S(1)} %get-tuple-element.55), channel_id=1, source_target_pairs={{0,1},{1,33},{2,3},{3,35},{4,5},{5,37},{6,7},{7,39},{8,9},{9,41},{... | collective-permute-start | bytes 737288 | tf_op jit(solution)/shard_map/ppermute | solution.py:731
  35.2 2.9 %copy-start.3 = (bf16[16,512]{1,0:T(8,128)(2,1)S(1)}, bf16[16,512]{1,0:T(8,128)(2,1)}, u32[]{:S(2)}) copy-start(bf16[16,512]{1,0:T(8,128)(2,1)} %constant.13.clone.wm_ref) | copy-start | bytes 49156
  37.4 5.5 %copy-start.4 = (bf16[16,256]{1,0:T(8,128)(2,1)S(1)}, bf16[16,256]{1,0:T(8,128)(2,1)}, u32[]{:S(2)}) copy-start(bf16[16,256]{1,0:T(8,128)(2,1)} %constant.14.clone.wr_ref) | copy-start | bytes 24580
  37.4 2.9 %collective-permute-start.8 = (f32[2,18,8,128]{3,2,1,0:T(8,128)S(1)}, f32[2,18,8,128]{3,2,1,0:T(8,128)S(1)}, u32[]{:S(2)}, u32[]{:S(2)}) collective-permute-start(f32[2,18,8,128]{3,2,1,0:T(8,128)S(1)} %get-tuple-element.61), channel_id=1, source_target_pairs={{0,32},{1,0},{2,34},{3,2},{4,36},{5,4},{6,38},{7,6},{8,40},{9,8},{... | collective-permute-start | bytes 442376 | tf_op jit(solution)/shard_map/ppermute | solution.py:731
  37.7 5.2 %collective-permute-start.9 = (f32[2,18,8,128]{3,2,1,0:T(8,128)S(1)}, f32[2,18,8,128]{3,2,1,0:T(8,128)S(1)}, u32[]{:S(2)}, u32[]{:S(2)}) collective-permute-start(f32[2,18,8,128]{3,2,1,0:T(8,128)S(1)} %get-tuple-element.62), channel_id=1, source_target_pairs={{0,1},{1,33},{2,3},{3,35},{4,5},{5,37},{6,7},{7,39},{8,9},{9,41},{... | collective-permute-start | bytes 442376 | tf_op jit(solution)/shard_map/ppermute | solution.py:731
  43.5 19.3 %collective-permute-start.10 = (f32[2,8,8,128]{3,2,1,0:T(8,128)S(1)}, f32[2,8,8,128]{3,2,1,0:T(8,128)S(1)}, u32[]{:S(2)}, u32[]{:S(2)}) collective-permute-start(f32[2,8,8,128]{3,2,1,0:T(8,128)S(1)} %get-tuple-element.71), channel_id=1, source_target_pairs={{0,1},{1,2},{2,3},{3,4},{4,5},{5,6},{6,7},{7,8},{8,9},{9,10},{10,1... | collective-permute-start | bytes 196616 | tf_op jit(solution)/shard_map/ppermute | solution.py:719
  43.5 19.3 %collective-permute-start.11 = (f32[2,8,8,128]{3,2,1,0:T(8,128)S(1)}, f32[2,8,8,128]{3,2,1,0:T(8,128)S(1)}, u32[]{:S(2)}, u32[]{:S(2)}) collective-permute-start(f32[2,8,8,128]{3,2,1,0:T(8,128)S(1)} %get-tuple-element.72), channel_id=1, source_target_pairs={{0,31},{1,0},{2,1},{3,2},{4,3},{5,4},{6,5},{7,6},{8,7},{9,8},{10,9... | collective-permute-start | bytes 196616 | tf_op jit(solution)/shard_map/ppermute | solution.py:719

commit v11 on v10

--- a/solution.py
+++ b/solution.py
@@ -176,7 +176,7 @@
                 dinv_ref[i, row, lanes] = 1.0 / (d0 + cxl[i])
 
 
-def rim_kernel(src_ref, coef_ref, yd_ref, yu_ref, to_a_ref, to_b_ref):
+def rim_kernel(src_ref, coef_ref, yu_ref, yd_ref, to_a_ref, to_b_ref):
     coef_y = jnp.concatenate([yd_ref[8, 0:4, :], yu_ref[8, 0:4, :]], 0)
     even = even_row()
     coef = coef_ref[0]
@@ -329,7 +329,7 @@
         to_up_ref[p] = get(wout, p, 15, 3)
 
 
-def edge_kernel(w_ref, d_ref, u_ref, a_ref, b_ref):
+def edge_kernel(w_ref, u_ref, d_ref, a_ref, b_ref):
     _, _, down, up = flags()
     even = even_row()
     for k in range(3):
@@ -626,7 +626,7 @@
 
 
 def last_kernel(
-    smooth_in, res_in, c_ref, uout_ref, rin_ref, rout_ref, coef_ref, d_ref, u_ref, slot_ref,
+    smooth_in, res_in, c_ref, uout_ref, rin_ref, rout_ref, coef_ref, u_ref, d_ref, slot_ref,
     arrived_ref,
     smooth_hbm, res_hbm, coarse_hbm, smooth_ref, res_ref, coarse_ref, sems,
 ):
@@ -774,8 +774,8 @@
         hbm_in=5,
         sems=6,
     )
+    yu = ring(to_d, "sy", -1)
     yd = ring(to_u, "sy", 1)
-    yu = ring(to_d, "sy", -1)
     src, dinv = call(
         place_kernel,
         [vm(8, 16, 8, LANES), vm(10, 104, 256)],
@@ -784,7 +784,7 @@
         hbm_in=1,
         sems=1,
     )
-    to_a, to_b = call(rim_kernel, [vm(20, 8, LANES)] * 2, (src, coef, yd, yu))
+    to_a, to_b = call(rim_kernel, [vm(20, 8, LANES)] * 2, (src, coef, yu, yd))
     xa = snake(to_a, 1)
     xb = snake(to_b, -1)
     rin, sin = call(
@@ -801,9 +801,9 @@
         (xa, xb, sin, dinv, a1, a2),
         [(2, 104, 256), (10, 104, 256)],
     )
+    u = ring(to_d, "sy", -1)
     d = ring(to_u, "sy", 1)
-    u = ring(to_d, "sy", -1)
-    to_a, to_b = call(edge_kernel, [vm(3, 20, 8, LANES)] * 2, (w, d, u))
+    to_a, to_b = call(edge_kernel, [vm(3, 20, 8, LANES)] * 2, (w, u, d))
     a = snake(to_a, 1)
     b = snake(to_b, -1)
     hin, sin = call(
@@ -846,13 +846,13 @@
         (src, coef, yd, yu, c, a, b, own_d, own_u, mom, pick, member, wm, wr),
         [(10, 18, 8, LANES), (256, 256), (2, 10, 2, 8, LANES)],
     )
+    u = ring(to_d, "sy", -1)
     d = ring(to_u, "sy", 1)
-    u = ring(to_d, "sy", -1)
     arrived = lax.all_to_all(part, "sy", split_axis=0, concat_axis=0, tiled=True)
     smooth, res, coarse = call(
         last_kernel,
         [sd(8, 64, 256), sd(8, 64, 256), sd(8, GRP_DEV)],
-        (smooth, res, c, uout, rin, rout, coef, d, u, slot, arrived),
+        (smooth, res, c, uout, rin, rout, coef, u, d, slot, arrived),
         [(8, 64, 256), (8, 64, 256), (8, GRP_DEV)],
         hbm_in=2,
         hbm_out=3,

time: 64.3 us -> 66.5 us (1.034)
  waiting for transfers between devices: 16.8 us -> 19.9 us
  blocking collectives: 17.2 us -> 15.4 us
  starting transfers between devices: 17.3 us -> 18.2 us
    ppermute x6, waiting for transfers between devices: 4.12 us -> 7.24 us  [ring(): return lax.ppermute(value, axis, [(i, (i + by) % n) for i in range(n)])]
    all_to_all x1, blocking collectives: 17.2 us -> 15.4 us  [on_device(): lax.all_to_all(part, 'sy', split_axis=0, concat_axis=0, tiled=True)]
    ppermute x6, starting transfers between devices: 10.9 us -> 11.7 us  [snake(): return lax.ppermute(value, ('sx', 'sy'), pairs)]
where the time goes in v11:
time: 66.5 us; the launch traced here: 66.2 us
  waiting for transfers between devices  19.9 us (30%)
  starting transfers between devices  18.2 us (27%)
  blocking collectives  15.4 us (23%)
  Pallas kernels  10.8 us (16%)
  local copies, waits for them, and re-layouts  1.07 us (2%)
  between operations  0.92 us (1%)
    all_to_all x1, blocking collectives, on_device(): lax.all_to_all(part, 'sy', split_axis=0, concat_axis=0, tiled=True)  15.4 us
    ppermute x6, waiting for transfers between devices, snake(): return lax.ppermute(value, ('sx', 'sy'), pairs)  12.6 us
    ppermute x6, starting transfers between devices, snake(): return lax.ppermute(value, ('sx', 'sy'), pairs)  11.7 us
    pallas_call x11, Pallas kernels, call(): pl.pallas_call(kernel, out_shape=outs, in_specs=[hbm if k < hbm_in else v...  10.8 us
    ppermute x6, waiting for transfers between devices, ring(): return lax.ppermute(value, axis, [(i, (i + by) % n) for i in range(n)])  7.24 us
    ppermute x6, starting transfers between devices, ring(): return lax.ppermute(value, axis, [(i, (i + by) % n) for i in range(n)])  6.46 us
  transfers between devices with their start and end apart: 12, of which 9 were waited for; matrix products, arithmetic and copies ran while one was open for 0% of the time, Pallas kernels for 6%

profile of v11, /device:TPU:8, one launch (start us, length us, event | category | flops | bytes accessed | tf_op | source)
XLA Modules:
  0.0 66.2 jit_solution(7607236007279502088)
XLA Ops:
  0.6 0.0 copy-start.1
  0.6 0.0 copy-start.2
  0.7 1.7 %shard_map.121 = (f32[2,8,128]{2,1,0:T(8,128)S(1)}, f32[9,8,128]{2,1,0:T(8,128)S(1)}, f32[9,8,128]{2,1,0:T(8,128)S(1)}, s32[1,256]{1,0:T(1,128)S(1)}) custom-call(f32[8,64,256]{2,1,0:T(8,128)} %bitcast.10, f32[3,256]{1,0:T(4,128)} %stretch_hbm.1, f32[1,256]{1,0:T(1,128)} %bitcast.16, s32[1,256]{1,0:T(1,128)} %bitcast.17, s32[1,256]{1,0:T(1,128)} %bitcast.18), custom_call_target="tpu_custom_call" | custom-call | tf_op jit(solution)/shard_map/pallas_call | solution.py:744
  2.4 1.7 %collective-permute-start = (f32[9,8,128]{2,1,0:T(8,128)S(1)}, f32[9,8,128]{2,1,0:T(8,128)S(1)}, u32[]{:S(2)}, u32[]{:S(2)}) collective-permute-start(f32[9,8,128]{2,1,0:T(8,128)S(1)} %get-tuple-element.43), channel_id=1, source_target_pairs={{0,1},{1,2},{2,3},{3,4},{4,5},{5,6},{6,7},{7,8},{8,9},{9,10},{10,1... | collective-permute-start | bytes 110600 | tf_op jit(solution)/shard_map/ppermute | solution.py:719
  4.0 0.7 %collective-permute-start.1 = (f32[9,8,128]{2,1,0:T(8,128)S(1)}, f32[9,8,128]{2,1,0:T(8,128)S(1)}, u32[]{:S(2)}, u32[]{:S(2)}) collective-permute-start(f32[9,8,128]{2,1,0:T(8,128)S(1)} %get-tuple-element.44), channel_id=1, source_target_pairs={{0,31},{1,0},{2,1},{3,2},{4,3},{5,4},{6,5},{7,6},{8,7},{9,8},{10,9... | collective-permute-start | bytes 110600 | tf_op jit(solution)/shard_map/ppermute | solution.py:719
  4.7 0.0 copy-start
  4.7 1.0 %copy-done = f32[8,8,8,256]{3,2,1,0:T(8,128)S(1)} copy-done((f32[8,8,8,256]{3,2,1,0:T(8,128)S(1)}, f32[8,8,8,256]{3,2,1,0:T(8,128)}, u32[]{:S(2)}) %copy-start) | copy-done | bytes 524312
  5.8 1.1 %shard_map.122 = (f32[8,16,8,128]{3,2,1,0:T(8,128)S(1)}, f32[10,104,256]{2,1,0:T(8,128)S(1)}) custom-call(f32[2,104,128]{2,1,0:T(8,128)} %constant.12.clone.lam_hbm, f32[8,64,256]{2,1,0:T(8,128)S(1)} %bitcast.11, s32[1,256]{1,0:T(1,128)S(1)} %get-tuple-element.40.slot_ref, f32[2,8,128]{2,1,0:T(8,128)S(1)} %get-tuple-element.41.coef_ref), custom_call_target="tpu_custom_call" | custom-call | tf_op jit(solution)/shard_map/pallas_call | solution.py:744
  6.8 0.0 collective-permute-done.yd_ref
  6.8 1.2 %collective-permute-done.1.yu_ref = f32[9,8,128]{2,1,0:T(8,128)S(1)} collective-permute-done((f32[9,8,128]{2,1,0:T(8,128)S(1)}, f32[9,8,128]{2,1,0:T(8,128)S(1)}, u32[]{:S(2)}, u32[]{:S(2)}) %collective-permute-start.1) | collective-permute-done | bytes 36896 | tf_op jit(solution)/shard_map/ppermute | solution.py:719
  8.0 5.5 %collective-permute-start.2 = (f32[20,8,128]{2,1,0:T(8,128)S(1)}, f32[20,8,128]{2,1,0:T(8,128)S(1)}, u32[]{:S(2)}, u32[]{:S(2)}) collective-permute-start(f32[20,8,128]{2,1,0:T(8,128)S(1)} %get-tuple-element.46), channel_id=1, source_target_pairs={{0,32},{1,0},{2,34},{3,2},{4,36},{5,4},{6,38},{7,6},{8,40},{9,8},{... | collective-permute-start | bytes 245768 | tf_op jit(solution)/shard_map/ppermute | solution.py:731
  13.6 0.0 collective-permute-start.3
  13.6 0.0 copy-done.1
  13.6 0.7 %shard_map.123 = (f32[1536,128]{1,0:T(8,128)S(1)}, f32[10,104,256]{2,1,0:T(8,128)S(1)}) custom-call(f32[8,16,8,128]{3,2,1,0:T(8,128)S(1)} %get-tuple-element.42.src_ref, f32[9,8,128]{2,1,0:T(8,128)S(1)} %collective-permute-done.yd_ref, f32[9,8,128]{2,1,0:T(8,128)S(1)} %collective-permute-done.1.yu_ref, bf16[208,224]{1,0:T(8,128)(2,1)S(1)} %copy-done.1), custom_call_target="tpu_custom_call" | custom-call | tf_op jit(solution)/shard_map/pallas_call | solution.py:744
  14.3 1.3 %collective-permute-done.2.xa_ref = f32[20,8,128]{2,1,0:T(8,128)S(1)} collective-permute-done((f32[20,8,128]{2,1,0:T(8,128)S(1)}, f32[20,8,128]{2,1,0:T(8,128)S(1)}, u32[]{:S(2)}, u32[]{:S(2)}) %collective-permute-start.2) | collective-permute-done | bytes 81952 | tf_op jit(solution)/shard_map/ppermute | solution.py:731
  15.6 2.4 %collective-permute-done.3.xb_ref = f32[20,8,128]{2,1,0:T(8,128)S(1)} collective-permute-done((f32[20,8,128]{2,1,0:T(8,128)S(1)}, f32[20,8,128]{2,1,0:T(8,128)S(1)}, u32[]{:S(2)}, u32[]{:S(2)}) %collective-permute-start.3) | collective-permute-done | bytes 81952 | tf_op jit(solution)/shard_map/ppermute | solution.py:731
  18.0 0.0 copy-done.2
  18.0 1.4 %shard_map.125 = (f32[384,128]{1,0:T(8,128)S(1)}, f32[1920,128]{1,0:T(8,128)S(1)}, f32[10,3,8,128]{3,2,1,0:T(8,128)S(1)}, f32[10,3,8,128]{3,2,1,0:T(8,128)S(1)}) custom-call(f32[20,8,128]{2,1,0:T(8,128)S(1)} %collective-permute-done.2.xa_ref, f32[20,8,128]{2,1,0:T(8,128)S(1)} %collective-permute-done.3.xb_ref, ...), custom_call_target="tpu_custom_call" | custom-call | tf_op jit(solution)/shard_map/pallas_call | solution.py:744
  19.4 0.1 collective-permute-start.4
  19.5 2.0 %collective-permute-start.5 = (f32[10,3,8,128]{3,2,1,0:T(8,128)S(1)}, f32[10,3,8,128]{3,2,1,0:T(8,128)S(1)}, u32[]{:S(2)}, u32[]{:S(2)}) collective-permute-start(f32[10,3,8,128]{3,2,1,0:T(8,128)S(1)} %get-tuple-element.53), channel_id=1, source_target_pairs={{0,1},{1,2},{2,3},{3,4},{4,5},{5,6},{6,7},{7,8},{8,9},{9,10},{10,1... | collective-permute-start | bytes 368648 | tf_op jit(solution)/shard_map/ppermute | solution.py:719
  21.5 2.9 %collective-permute-done.4.u_ref = f32[10,3,8,128]{3,2,1,0:T(8,128)S(1)} collective-permute-done((f32[10,3,8,128]{3,2,1,0:T(8,128)S(1)}, f32[10,3,8,128]{3,2,1,0:T(8,128)S(1)}, u32[]{:S(2)}, u32[]{:S(2)}) %collective-permute-start.4) | collective-permute-done | bytes 122912 | tf_op jit(solution)/shard_map/ppermute | solution.py:719
  24.3 3.2 %collective-permute-done.5.d_ref = f32[10,3,8,128]{3,2,1,0:T(8,128)S(1)} collective-permute-done((f32[10,3,8,128]{3,2,1,0:T(8,128)S(1)}, f32[10,3,8,128]{3,2,1,0:T(8,128)S(1)}, u32[]{:S(2)}, u32[]{:S(2)}) %collective-permute-start.5) | collective-permute-done | bytes 122912 | tf_op jit(solution)/shard_map/ppermute | solution.py:719
  27.6 5.4 %collective-permute-start.6 = (f32[3,20,8,128]{3,2,1,0:T(8,128)S(1)}, f32[3,20,8,128]{3,2,1,0:T(8,128)S(1)}, u32[]{:S(2)}, u32[]{:S(2)}) collective-permute-start(f32[3,20,8,128]{3,2,1,0:T(8,128)S(1)} %get-tuple-element.54), channel_id=1, source_target_pairs={{0,32},{1,0},{2,34},{3,2},{4,36},{5,4},{6,38},{7,6},{8,40},{9,8},{... | collective-permute-start | bytes 737288 | tf_op jit(solution)/shard_map/ppermute | solution.py:731
  33.0 0.0 collective-permute-start.7
  33.0 0.8 %shard_map.127 = (f32[6,20,8,128]{3,2,1,0:T(8,128)S(1)}, f32[10,104,256]{2,1,0:T(8,128)S(1)}) custom-call(f32[1536,128]{1,0:T(8,128)S(1)} %get-tuple-element.45.rin_ref, f32[2,8,128]{2,1,0:T(8,128)S(1)} %get-tuple-element.41.coef_ref, f32[9,8,128]{2,1,0:T(8,128)S(1)} %collective-permute-done.yd_ref, f32[9,8,128]{2,1,0:T(8,128)S(1)} %collective-permute-done.1.yu_ref, ...), custom_call_target="tpu_custom_call" | custom-call | tf_op jit(solution)/shard_map/pallas_call | solution.py:744
  33.8 2.9 %collective-permute-done.6.a_ref = f32[3,20,8,128]{3,2,1,0:T(8,128)S(1)} collective-permute-done((f32[3,20,8,128]{3,2,1,0:T(8,128)S(1)}, f32[3,20,8,128]{3,2,1,0:T(8,128)S(1)}, u32[]{:S(2)}, u32[]{:S(2)}) %collective-permute-start.6) | collective-permute-done | bytes 245792 | tf_op jit(solution)/shard_map/ppermute | solution.py:731
  36.7 2.5 %collective-permute-done.7.b_ref = f32[3,20,8,128]{3,2,1,0:T(8,128)S(1)} collective-permute-done((f32[3,20,8,128]{3,2,1,0:T(8,128)S(1)}, f32[3,20,8,128]{3,2,1,0:T(8,128)S(1)}, u32[]{:S(2)}, u32[]{:S(2)}) %collective-permute-start.7) | collective-permute-done | bytes 245792 | tf_op jit(solution)/shard_map/ppermute | solution.py:731
  39.2 0.0 copy-start.3
  39.2 2.1 %shard_map.128 = (f32[10,18,8,128]{3,2,1,0:T(8,128)S(1)}, f32[2,18,8,128]{3,2,1,0:T(8,128)S(1)}, f32[2,18,8,128]{3,2,1,0:T(8,128)S(1)}, f32[10,2,8,128]{3,2,1,0:T(8,128)S(1)}, f32[10,2,8,128]{3,2,1,0:T(8,128)S(1)}) custom-call(f32[1536,128]{1,0:T(8,128)S(1)} %get-tuple-element.45.rin_ref, f32[384,128]{1,0:T(8,128)S(1)} %get-tuple-element.50.rout_ref, ...), custom_call_target="tpu_custom_call" | custom-call | tf_op jit(solution)/shard_map/pallas_call | solution.py:744
  41.3 0.0 copy-start.4
  41.3 0.3 collective-permute-start.8
  41.6 0.5 collective-permute-start.9
  42.1 0.0 copy-done.3
  42.1 1.2 %shard_map.129 = (f32[8,64,256]{2,1,0:T(8,128)}, f32[8,64,256]{2,1,0:T(8,128)}, f32[4,64,256]{2,1,0:T(8,128)S(1)}, f32[16,256]{1,0:T(8,128)S(1)}, f32[32,512]{1,0:T(8,128)S(1)}, /*index=5*/f32[16,512]{1,0:T(8,128)S(1)}) custom-call(f32[8,16,8,128]{3,2,1,0:T(8,128)S(1)} %get-tuple-element.42.src_ref, f32[2,8,128]{2,1,0:T(8,128)S(1)} %get-tuple-element.41.coef_ref, ...), custom_call_target="tpu_custom_call" | custom-call | tf_op jit(solution)/shard_map/pallas_call | solution.py:744
  43.3 1.0 %collective-permute-done.8.a_ref = f32[2,18,8,128]{3,2,1,0:T(8,128)S(1)} collective-permute-done((f32[2,18,8,128]{3,2,1,0:T(8,128)S(1)}, f32[2,18,8,128]{3,2,1,0:T(8,128)S(1)}, u32[]{:S(2)}, u32[]{:S(2)}) %collective-permute-start.8) | collective-permute-done | bytes 147488 | tf_op jit(solution)/shard_map/ppermute | solution.py:731
  44.3 2.6 %collective-permute-done.9.b_ref = f32[2,18,8,128]{3,2,1,0:T(8,128)S(1)} collective-permute-done((f32[2,18,8,128]{3,2,1,0:T(8,128)S(1)}, f32[2,18,8,128]{3,2,1,0:T(8,128)S(1)}, u32[]{:S(2)}, u32[]{:S(2)}) %collective-permute-start.9) | collective-permute-done | bytes 147488 | tf_op jit(solution)/shard_map/ppermute | solution.py:731
  46.9 0.0 copy-done.4
  46.9 0.6 shard_map.130
  47.5 0.0 collective-permute-start.10
  47.5 2.0 %collective-permute-start.11 = (f32[2,8,8,128]{3,2,1,0:T(8,128)S(1)}, f32[2,8,8,128]{3,2,1,0:T(8,128)S(1)}, u32[]{:S(2)}, u32[]{:S(2)}) collective-permute-start(f32[2,8,8,128]{3,2,1,0:T(8,128)S(1)} %get-tuple-element.72), channel_id=1, source_target_pairs={{0,1},{1,2},{2,3},{3,4},{4,5},{5,6},{6,7},{7,8},{8,9},{9,10},{10,1... | collective-permute-start | bytes 196616 | tf_op jit(solution)/shard_map/ppermute | solution.py:719
  49.5 15.4 %all_to_all.11 = f32[32,1,128]{2,1,0:T(1,128)S(1)} all-to-all(f32[32,1,128]{2,1,0:T(1,128)S(1)} %bitcast.13), channel_id=1, replica_groups=mesh['sx'=8,'sy'=32] {'sy'}, dimensions={0} | all-to-all | bytes 32768 | tf_op jit(solution)/shard_map/all_to_all | solution.py:851
  65.0 0.0 collective-permute-done.10.u_ref
  65.0 0.0 collective-permute-done.11.d_ref
  65.0 1.1 %shard_map.131 = (f32[8,64,256]{2,1,0:T(8,128)}, f32[8,64,256]{2,1,0:T(8,128)}, f32[8,16]{1,0:T(8,128)}) custom-call(f32[8,64,256]{2,1,0:T(8,128)} %get-tuple-element.59.smooth_in, f32[8,64,256]{2,1,0:T(8,128)} %get-tuple-element.60.res_in, f32[10,18,8,128]{3,2,1,0:T(8,128)S(1)} %get-tuple-element.58.c_ref, ...), custom_call_target="tpu_custom_call", output_to_operand_aliasing={{0}: (0, {}), {1}: (1, {})} | custom-call | tf_op jit(solution)/shard_map/pallas_call | solution.py:744
  (2 shorter events, 0.1 us)
Async XLA Ops:
  0.6 12.9 %copy-start.1 = (bf16[208,224]{1,0:T(8,128)(2,1)S(1)}, bf16[208,224]{1,0:T(8,128)(2,1)}, u32[]{:S(2)}) copy-start(bf16[208,224]{1,0:T(8,128)(2,1)} %constant.10.clone.a1_ref) | copy-start | bytes 279556
  0.6 17.4 %copy-start.2 = (bf16[224,208]{1,0:T(8,128)(2,1)S(1)}, bf16[224,208]{1,0:T(8,128)(2,1)}, u32[]{:S(2)}) copy-start(bf16[224,208]{1,0:T(8,128)(2,1)} %constant.11.clone.a2_ref) | copy-start | bytes 279556
  2.4 4.4 %collective-permute-start = (f32[9,8,128]{2,1,0:T(8,128)S(1)}, f32[9,8,128]{2,1,0:T(8,128)S(1)}, u32[]{:S(2)}, u32[]{:S(2)}) collective-permute-start(f32[9,8,128]{2,1,0:T(8,128)S(1)} %get-tuple-element.43), channel_id=1, source_target_pairs={{0,1},{1,2},{2,3},{3,4},{4,5},{5,6},{6,7},{7,8},{8,9},{9,10},{10,1... | collective-permute-start | bytes 110600 | tf_op jit(solution)/shard_map/ppermute | solution.py:719
  4.0 4.0 %collective-permute-start.1 = (f32[9,8,128]{2,1,0:T(8,128)S(1)}, f32[9,8,128]{2,1,0:T(8,128)S(1)}, u32[]{:S(2)}, u32[]{:S(2)}) collective-permute-start(f32[9,8,128]{2,1,0:T(8,128)S(1)} %get-tuple-element.44), channel_id=1, source_target_pairs={{0,31},{1,0},{2,1},{3,2},{4,3},{5,4},{6,5},{7,6},{8,7},{9,8},{10,9... | collective-permute-start | bytes 110600 | tf_op jit(solution)/shard_map/ppermute | solution.py:719
  4.7 1.0 %copy-start = (f32[8,8,8,256]{3,2,1,0:T(8,128)S(1)}, f32[8,8,8,256]{3,2,1,0:T(8,128)}, u32[]{:S(2)}) copy-start(f32[8,8,8,256]{3,2,1,0:T(8,128)} %param.10) | copy-start | bytes 1572868
  8.0 7.6 %collective-permute-start.2 = (f32[20,8,128]{2,1,0:T(8,128)S(1)}, f32[20,8,128]{2,1,0:T(8,128)S(1)}, u32[]{:S(2)}, u32[]{:S(2)}) collective-permute-start(f32[20,8,128]{2,1,0:T(8,128)S(1)} %get-tuple-element.46), channel_id=1, source_target_pairs={{0,32},{1,0},{2,34},{3,2},{4,36},{5,4},{6,38},{7,6},{8,40},{9,8},{... | collective-permute-start | bytes 245768 | tf_op jit(solution)/shard_map/ppermute | solution.py:731
  13.6 4.4 %collective-permute-start.3 = (f32[20,8,128]{2,1,0:T(8,128)S(1)}, f32[20,8,128]{2,1,0:T(8,128)S(1)}, u32[]{:S(2)}, u32[]{:S(2)}) collective-permute-start(f32[20,8,128]{2,1,0:T(8,128)S(1)} %get-tuple-element.47), channel_id=1, source_target_pairs={{0,1},{1,33},{2,3},{3,35},{4,5},{5,37},{6,7},{7,39},{8,9},{9,41},{... | collective-permute-start | bytes 245768 | tf_op jit(solution)/shard_map/ppermute | solution.py:731
  19.4 5.0 %collective-permute-start.4 = (f32[10,3,8,128]{3,2,1,0:T(8,128)S(1)}, f32[10,3,8,128]{3,2,1,0:T(8,128)S(1)}, u32[]{:S(2)}, u32[]{:S(2)}) collective-permute-start(f32[10,3,8,128]{3,2,1,0:T(8,128)S(1)} %get-tuple-element.52), channel_id=1, source_target_pairs={{0,31},{1,0},{2,1},{3,2},{4,3},{5,4},{6,5},{7,6},{8,7},{9,8},{10,9... | collective-permute-start | bytes 368648 | tf_op jit(solution)/shard_map/ppermute | solution.py:719
  19.5 8.1 %collective-permute-start.5 = (f32[10,3,8,128]{3,2,1,0:T(8,128)S(1)}, f32[10,3,8,128]{3,2,1,0:T(8,128)S(1)}, u32[]{:S(2)}, u32[]{:S(2)}) collective-permute-start(f32[10,3,8,128]{3,2,1,0:T(8,128)S(1)} %get-tuple-element.53), channel_id=1, source_target_pairs={{0,1},{1,2},{2,3},{3,4},{4,5},{5,6},{6,7},{7,8},{8,9},{9,10},{10,1... | collective-permute-start | bytes 368648 | tf_op jit(solution)/shard_map/ppermute | solution.py:719
  27.6 9.1 %collective-permute-start.6 = (f32[3,20,8,128]{3,2,1,0:T(8,128)S(1)}, f32[3,20,8,128]{3,2,1,0:T(8,128)S(1)}, u32[]{:S(2)}, u32[]{:S(2)}) collective-permute-start(f32[3,20,8,128]{3,2,1,0:T(8,128)S(1)} %get-tuple-element.54), channel_id=1, source_target_pairs={{0,32},{1,0},{2,34},{3,2},{4,36},{5,4},{6,38},{7,6},{8,40},{9,8},{... | collective-permute-start | bytes 737288 | tf_op jit(solution)/shard_map/ppermute | solution.py:731
  33.0 6.2 %collective-permute-start.7 = (f32[3,20,8,128]{3,2,1,0:T(8,128)S(1)}, f32[3,20,8,128]{3,2,1,0:T(8,128)S(1)}, u32[]{:S(2)}, u32[]{:S(2)}) collective-permute-start(f32[3,20,8,128]{3,2,1,0:T(8,128)S(1)} %get-tuple-element.55), channel_id=1, source_target_pairs={{0,1},{1,33},{2,3},{3,35},{4,5},{5,37},{6,7},{7,39},{8,9},{9,41},{... | collective-permute-start | bytes 737288 | tf_op jit(solution)/shard_map/ppermute | solution.py:731
  39.2 2.9 %copy-start.3 = (bf16[16,512]{1,0:T(8,128)(2,1)S(1)}, bf16[16,512]{1,0:T(8,128)(2,1)}, u32[]{:S(2)}) copy-start(bf16[16,512]{1,0:T(8,128)(2,1)} %constant.13.clone.wm_ref) | copy-start | bytes 49156
  41.3 5.5 %copy-start.4 = (bf16[16,256]{1,0:T(8,128)(2,1)S(1)}, bf16[16,256]{1,0:T(8,128)(2,1)}, u32[]{:S(2)}) copy-start(bf16[16,256]{1,0:T(8,128)(2,1)} %constant.14.clone.wr_ref) | copy-start | bytes 24580
  41.3 2.9 %collective-permute-start.8 = (f32[2,18,8,128]{3,2,1,0:T(8,128)S(1)}, f32[2,18,8,128]{3,2,1,0:T(8,128)S(1)}, u32[]{:S(2)}, u32[]{:S(2)}) collective-permute-start(f32[2,18,8,128]{3,2,1,0:T(8,128)S(1)} %get-tuple-element.61), channel_id=1, source_target_pairs={{0,32},{1,0},{2,34},{3,2},{4,36},{5,4},{6,38},{7,6},{8,40},{9,8},{... | collective-permute-start | bytes 442376 | tf_op jit(solution)/shard_map/ppermute | solution.py:731
  41.6 5.2 %collective-permute-start.9 = (f32[2,18,8,128]{3,2,1,0:T(8,128)S(1)}, f32[2,18,8,128]{3,2,1,0:T(8,128)S(1)}, u32[]{:S(2)}, u32[]{:S(2)}) collective-permute-start(f32[2,18,8,128]{3,2,1,0:T(8,128)S(1)} %get-tuple-element.62), channel_id=1, source_target_pairs={{0,1},{1,33},{2,3},{3,35},{4,5},{5,37},{6,7},{7,39},{8,9},{9,41},{... | collective-permute-start | bytes 442376 | tf_op jit(solution)/shard_map/ppermute | solution.py:731
  47.5 17.5 %collective-permute-start.10 = (f32[2,8,8,128]{3,2,1,0:T(8,128)S(1)}, f32[2,8,8,128]{3,2,1,0:T(8,128)S(1)}, u32[]{:S(2)}, u32[]{:S(2)}) collective-permute-start(f32[2,8,8,128]{3,2,1,0:T(8,128)S(1)} %get-tuple-element.71), channel_id=1, source_target_pairs={{0,31},{1,0},{2,1},{3,2},{4,3},{5,4},{6,5},{7,6},{8,7},{9,8},{10,9... | collective-permute-start | bytes 196616 | tf_op jit(solution)/shard_map/ppermute | solution.py:719
  47.5 17.4 %collective-permute-start.11 = (f32[2,8,8,128]{3,2,1,0:T(8,128)S(1)}, f32[2,8,8,128]{3,2,1,0:T(8,128)S(1)}, u32[]{:S(2)}, u32[]{:S(2)}) collective-permute-start(f32[2,8,8,128]{3,2,1,0:T(8,128)S(1)} %get-tuple-element.72), channel_id=1, source_target_pairs={{0,1},{1,2},{2,3},{3,4},{4,5},{5,6},{6,7},{7,8},{8,9},{9,10},{10,1... | collective-permute-start | bytes 196616 | tf_op jit(solution)/shard_map/ppermute | solution.py:719
